TPU v7x, 32 devices: a 4x2x2 block of a 4x4x8 slice. The times are simulated.
32 devices in a mesh: replica: 4 (over y, z), ep: 8 (over x, core).
Axes of the slice: x: 4, y: 2, z: 2, core: 2. Of those that a mesh axis runs over, the one named last changes fastest.
The devices are a block of a 4x4x8 slice.
Arguments:
- x: bfloat16 [32, 1024, 2048], P(('replica', 'ep')), parts along dimension 0
- wq: bfloat16 [2048, 2048], P('ep')
- wk: bfloat16 [2048, 2048], P('ep')
- wv: bfloat16 [2048, 2048], P('ep')
- wo: bfloat16 [2048, 2048], P('ep')
- wr: float32 [2048, 64], replicated
- w1: bfloat16 [64, 2048, 1024], P('ep')
- w3: bfloat16 [64, 2048, 1024], P('ep')
- w2: bfloat16 [64, 1024, 2048], P('ep')
- idx: int32 [32, 1024, 8], P(('replica', 'ep')), parts along dimension 0
Outputs:
- output: bfloat16 [32, 1024, 2048], P(('replica', 'ep')), parts along dimension 0
There are 4 independent parts. A program takes and returns all parts, laid end to end along the dimension named above; an argument that names none is the same for every part.
All inputs are finite; a program needn't handle non-finite values.
Results may differ from a plain program's by a relative error of at most 0.011257.
Values are sent between devices in bfloat16 or wider.
A program may use at most 768 MiB of HBM per device.

v0:
```python
import math
import jax
import jax.numpy as jnp
from jax import lax
from jax.sharding import PartitionSpec as P

HEAD = 128
BLOCK = 128
EPS = 1e-6
THETA = 10000.0


def rmsnorm(v):
    v = v.astype(jnp.float32)
    return v * lax.rsqrt(jnp.mean(v * v, axis=-1, keepdims=True) + EPS)


def rope(z):
    n = z.shape[-3]
    half = HEAD // 2
    freq = THETA ** (-jnp.arange(half, dtype=jnp.float32) / half)
    ang = jnp.arange(n, dtype=jnp.float32)[:, None] * freq
    c = jnp.cos(ang)[:, None, :]
    s = jnp.sin(ang)[:, None, :]
    z1, z2 = z[..., :half], z[..., half:]
    return jnp.concatenate([z1 * c - z2 * s, z2 * c + z1 * s], axis=-1)


def attention(x, s, wq, wk, wv, wo):
    t, d = x.shape
    nh = wq.shape[1] // HEAD
    a = rmsnorm(x).astype(jnp.bfloat16)

    def proj(w):
        return jnp.dot(a, w, preferred_element_type=jnp.float32).reshape(t // s, s, nh, HEAD)

    q = rope(proj(wq)).astype(jnp.bfloat16)
    k = rope(proj(wk)).astype(jnp.bfloat16)
    v = proj(wv).astype(jnp.bfloat16)
    sc = jnp.einsum('bqhe,bkhe->bhqk', q, k, preferred_element_type=jnp.float32) / math.sqrt(HEAD)
    sc = jnp.where(jnp.tril(jnp.ones((s, s), bool)), sc, -jnp.inf)
    p = jax.nn.softmax(sc, axis=-1).astype(jnp.bfloat16)
    o = jnp.einsum('bhqk,bkhe->bqhe', p, v, preferred_element_type=jnp.float32).astype(jnp.bfloat16)
    ao = jnp.dot(o.reshape(t, nh * HEAD), wo, preferred_element_type=jnp.float32)
    return (x.astype(jnp.float32) + ao).astype(jnp.bfloat16)


def router(h, wr, ids):
    r = rmsnorm(h)
    logits = jnp.dot(r, wr, precision=lax.Precision.HIGHEST, preferred_element_type=jnp.float32)
    g = jax.nn.softmax(jnp.take_along_axis(logits, ids, axis=1), axis=-1)
    return r.astype(jnp.bfloat16), g


def block_plan(eid, ne, cap):
    m = eid.shape[0]
    nb = (cap + ne * (BLOCK - 1)) // BLOCK + 1
    counts = jnp.bincount(eid, length=ne + 1)[:ne]
    nblk = (counts + BLOCK - 1) // BLOCK
    bend = jnp.cumsum(nblk)
    first = jnp.cumsum(counts) - counts
    order = jnp.argsort(eid)
    se = eid[order]
    sc = jnp.minimum(se, ne - 1)
    slot = jnp.where(se < ne, (bend[sc] - nblk[sc]) * BLOCK + jnp.arange(m) - first[sc], nb * BLOCK)
    cand = jnp.full((nb * BLOCK,), m, jnp.int32).at[slot].set(order.astype(jnp.int32), mode='drop')
    blk_e = jnp.minimum(jnp.searchsorted(bend, jnp.arange(nb), side='right'), ne - 1)
    return cand.reshape(nb, BLOCK), blk_e, bend[-1]


def expert_sum(rows, eid, gates, k, w1, w3, w2, cap):
    n, d = rows.shape
    ne = w1.shape[0]
    m = n * k
    cand, blk_e, nused = block_plan(eid, ne, cap)
    ok = cand < m
    row = jnp.where(ok, cand // k, 0)
    gate = jnp.where(ok, gates[jnp.minimum(cand, m - 1)], 0.0)

    def body(acc, xs):
        b, rb, gb, e = xs

        def work(acc):
            xb = rows[rb]
            a1 = jnp.dot(xb, w1[e], preferred_element_type=jnp.float32)
            a3 = jnp.dot(xb, w3[e], preferred_element_type=jnp.float32)
            act = (jax.nn.silu(a1) * a3).astype(jnp.bfloat16)
            o = jnp.dot(act, w2[e], preferred_element_type=jnp.float32).astype(jnp.bfloat16)
            return acc.at[rb].add(gb[:, None] * o.astype(jnp.float32))

        return lax.cond(b < nused, work, lambda acc: acc, acc), None

    acc, _ = lax.scan(body, jnp.zeros((n, d), jnp.float32), (jnp.arange(cand.shape[0]), row, gate, blk_e))
    return acc


def solution(mesh):
    nd = mesh.shape['ep']
    tok = P(('replica', 'ep'), None, None)
    rows_ep = P('ep', None)
    by_expert = P('ep', None, None)

    def a2a(v):
        return lax.all_to_all(v, 'ep', 0, 0, tiled=True)

    def local(x, wq, wk, wv, wo, wr, w1, w3, w2, idx):
        b, s, d = x.shape
        t, k, ne = b * s, idx.shape[-1], w1.shape[0]
        wq, wk, wv, wo = [lax.all_gather(w, 'ep', axis=0, tiled=True) for w in (wq, wk, wv, wo)]
        h = attention(x.reshape(t, d), s, wq, wk, wv, wo)
        ids = idx.reshape(t, k)
        u, g = router(h, wr, ids)
        dev = jnp.arange(nd)
        hit = jnp.any(ids[None] // ne == dev[:, None, None], axis=-1)
        pos = jnp.where(hit, jnp.cumsum(hit, axis=1) - 1, t)
        src = jnp.full((nd, t), t, jnp.int32).at[dev[:, None], pos].set(
            jnp.broadcast_to(jnp.arange(t, dtype=jnp.int32), (nd, t)), mode='drop')
        ok = src < t
        src = jnp.minimum(src, t - 1)
        mine = (ids[src] // ne == dev[:, None, None]) & ok[..., None]
        recv_x = a2a(jnp.where(ok[..., None], u[src], jnp.zeros((), jnp.bfloat16)))
        recv_e = a2a(jnp.where(mine, ids[src] % ne, ne))
        recv_g = a2a(jnp.where(mine, g[src], 0.0))
        n = nd * t
        part = expert_sum(recv_x.reshape(n, d), recv_e.reshape(-1), recv_g.reshape(-1), k,
                          w1, w3, w2, n * min(k, ne))
        back = a2a(part.astype(jnp.bfloat16).reshape(nd, t, d))
        moe = jnp.zeros((t, d), jnp.float32).at[src].add(
            jnp.where(ok[..., None], back.astype(jnp.float32), 0.0))
        return (h.astype(jnp.float32) + moe).astype(jnp.bfloat16).reshape(b, s, d)

    return jax.shard_map(local, mesh=mesh,
                         in_specs=(tok, rows_ep, rows_ep, rows_ep, rows_ep, P(None, None),
                                   by_expert, by_expert, by_expert, tok),
                         out_specs=tok, check_vma=False)
```

profile of v0, /device:TPU:113, one launch (start us, length us, event | category | flops | bytes accessed | tf_op | source)
XLA Modules:
  0.0 13822.5 jit_solution(13287392250067524511)
XLA Ops:
  15.2 30.5 scatter_custom_fusion.4
  46.4 28.0 gather_fusion.1
  99.4 25.5 sort.17
  124.9 362.7 %gather_fusion.2 = s32[65536]{0:T(1024)S(1)} fusion(s32[65536]{0:T(1024)S(1)} %reshape.434, s32[65536]{0:T(1024)S(1)} %fusion.82), kind=kCustom, calls=%fused_computation.2 | custom fusion | bytes 786432 | tf_op jit(solution)/shard_map/gather | solution.py:63
  494.7 452.1 %scatter_custom_fusion.1 = s32[9]{0:T(128)S(1)} fusion(s32[65536]{0:T(1024)S(1)} %reshape.578, s32[65536]{0:T(1024)S(1)} %broadcast.479, s32[]{:T(128)} %copy.95), kind=kCustom, calls=%fused_computation.191 | custom fusion | flops 65536 | bytes 40 | tf_op jit(solution)/shard_map/scatter-add | solution.py:58
  1027.7 35.6 fusion.118
  1063.3 31.5 fusion.65
  1115.1 64.1 gather_fusion.5
  1189.0 65.8 gather_fusion.6
  1256.1 28.0 gather_fusion.3
  1334.7 240.1 %scatter_custom_fusion.2 = s32[66560]{0:T(1024)S(1)} fusion(s32[65536]{0:T(1024)S(1)} %bitcast.239, s32[65536]{0:T(1024)} %copy-done.21, s32[]{:T(128)} %constant.195.clone.1), kind=kCustom, calls=%fused_computation.138 | custom fusion | bytes 266752 | tf_op jit(solution)/shard_map/scatter | solution.py:66
  1604.9 368.4 %gather_fusion.4 = f32[66560]{0:T(1024)S(1)} fusion(f32[65536]{0:T(1024)S(1)} %reshape.440, s32[66560]{0:T(1024)S(1)} %fusion.77), kind=kCustom, calls=%fused_computation.4 | custom fusion | bytes 798720 | tf_op jit(solution)/shard_map/gather | solution.py:78
  1994.6 2490.4 %while.37 = (s32[]{:T(128)}, f32[8192,2048]{1,0:T(8,128)}, s32[520]{0:T(1024)S(1)}, s32[]{:T(128)}, s32[520,128]{1,0:T(8,128)S(1)}, /*index=5*/f32[520,128]{1,0:...) while((s32[]{:T(128)}, f32[8192,2048]{1,0:T(8,128)}, ...), condition=%wide.region_21.22_spmd, body=%wide.region_17.21_spmd.sunk | while | flops 1612449152 | bytes 19932440 | solution.py:93
  1996.5 36.2 conditional.2
  2034.6 36.3 conditional.2
  2072.8 36.5 conditional.2
  2111.1 36.1 conditional.2
  2149.0 42.2 conditional.2
  2193.1 36.2 conditional.2
  2231.2 36.3 conditional.2
  2269.3 36.1 conditional.2
  2307.3 36.0 conditional.2
  2345.2 44.3 conditional.2
  2364.2 25.3 scatter_fusion
  2391.4 36.2 conditional.2
  2429.4 36.4 conditional.2
  2467.6 36.1 conditional.2
  2505.6 36.3 conditional.2
  2543.8 44.1 conditional.2
  2562.6 25.3 scatter_fusion
  2589.7 36.2 conditional.2
  2627.8 36.2 conditional.2
  2665.8 36.2 conditional.2
  2703.9 36.2 conditional.2
  2742.0 44.2 conditional.2
  2760.8 25.4 scatter_fusion
  2788.1 36.2 conditional.2
  2826.1 36.2 conditional.2
  2864.1 36.3 conditional.2
  2902.3 36.0 conditional.2
  2940.2 43.3 conditional.2
  2958.5 25.0 scatter_fusion
  2985.3 36.2 conditional.2
  3023.4 36.4 conditional.2
  3061.6 36.3 conditional.2
  3099.8 36.3 conditional.2
  3137.9 45.8 conditional.2
  3158.0 25.8 scatter_fusion
  3185.6 36.2 conditional.2
  3223.7 36.4 conditional.2
  3261.9 36.1 conditional.2
  3299.8 36.1 conditional.2
  3337.8 45.3 conditional.2
  3357.3 25.8 scatter_fusion
  3384.9 36.1 conditional.2
  3422.9 36.1 conditional.2
  3460.9 36.2 conditional.2
  3499.0 36.1 conditional.2
  3536.9 39.9 conditional.2
  4485.0 32.4 convert_element_type.116
  4517.4 8787.5 %all-to-all-start.3 = ((bf16[8,1024,2048]{2,1,0:T(8,128)(2,1)}), bf16[8,1024,2048]{2,1,0:T(8,128)(2,1)}, u32[]{:S(2)}, u32[]{:S(2)}) async-start(bf16[8,1024,2048]{2,1,0:T(8,128)(2,1)} %bitcast.223), calls=%async_computation.3 | async-start | bytes 67108864 | tf_op jit(solution)/shard_map/all_to_all | solution.py:104
  13305.0 364.0 %all-to-all-done.3 = bf16[8,1024,2048]{2,1,0:T(8,128)(2,1)} async-done(((bf16[8,1024,2048]{2,1,0:T(8,128)(2,1)}), bf16[8,1024,2048]{2,1,0:T(8,128)(2,1)}, u32[]{:S(2)}, u32[]{:S(2)}) %all-to-all-start.3) | async-done | bytes 33554464 | tf_op jit(solution)/shard_map/all_to_all | solution.py:104
  13669.0 32.4 convert_select_fusion
  13701.3 108.4 scatter_fusion.1
  (1482 shorter events, 1864.1 us)
Async XLA Ops:
  6.5 1172.6 %copy-start = (f32[2048,64]{0,1:T(8,128)S(1)}, f32[2048,64]{0,1:T(8,128)}, u32[]{:S(2)}) copy-start(f32[2048,64]{0,1:T(8,128)} %param.21) | copy-start | bytes 1572868
  6.6 950.8 %all-gather.9.cloned.1.call-start = ((), (), s32[]{:S(2)}) async-start(), calls=%async_computation.6 | async-start | bytes 9437184 | tf_op jit(solution)/shard_map/all_gather | solution.py:109
  7.3 962.7 %all-gather.7.cloned.1.call-start = ((), (), s32[]{:S(2)}) async-start(), calls=%async_computation.5 | async-start | bytes 9437184 | tf_op jit(solution)/shard_map/all_gather | solution.py:109
  8.1 974.2 %all-gather.5.cloned.1.call-start = ((), (), s32[]{:S(2)}) async-start(), calls=%async_computation.4 | async-start | bytes 9437184 | tf_op jit(solution)/shard_map/all_gather | solution.py:109
  9.9 64.5 copy-start.2
  45.7 31.4 copy-start.23
  45.8 0.6 copy-start.18
  46.4 28.0 copy-start.14
  46.4 37.6 copy-start.17
  77.2 15.7 copy-start.7
  78.2 14.7 all-to-all-start
  83.4 1011.4 %all-gather.11.cloned.1.call-start = ((), (), s32[]{:S(2)}) async-start(), calls=%async_computation.7 | async-start | bytes 9437184 | tf_op jit(solution)/shard_map/all_gather | solution.py:109
  124.8 362.8 %copy-start.21 = (s32[65536]{0:T(1024)}, s32[65536]{0:T(1024)S(1)}, u32[]{:S(2)}) copy-start(s32[65536]{0:T(1024)S(1)} %get-tuple-element.210) | copy-start | bytes 786436
  947.8 22.2 copy-start.11
  955.2 0.7 copy-start.9
  994.7 12.8 copy-start.6
  1110.4 2.0 copy-start.5
  1110.4 4.7 copy-start.15
  1115.1 73.9 copy-start.4
  1189.0 66.1 copy-start.3
  1189.0 67.1 copy-start.16
  1256.1 30.8 copy-start.8
  1256.1 30.8 copy-start.24
  1287.8 27.2 all-to-all-start.1
  1315.0 7.5 copy-start.10
  1315.0 17.2 copy-start.13
  1315.0 17.2 copy-start.20
  1315.0 19.0 copy-start.22
  1315.0 259.8 %copy-start.12 = (s32[8,1]{0,1:T(1,128)S(1)}, s32[8,1]{0,1:T(1,128)}, u32[]{:S(2)}) copy-start(s32[8,1]{0,1:T(1,128)} %copy-done.11) | copy-start | bytes 100
  1315.0 259.8 %copy-start.26 = (u32[520]{0:T(1024)S(1)}, u32[520]{0:T(1024)}, u32[]{:S(2)}) copy-start(u32[520]{0:T(1024)} %custom-call.3) | copy-start | bytes 6244
  1315.0 259.8 %copy-start.27 = (u32[520]{0:T(1024)S(1)}, u32[520]{0:T(1024)}, u32[]{:S(2)}) copy-start(u32[520]{0:T(1024)} %custom-call.2) | copy-start | bytes 6244
  1315.0 658.3 %all-to-all-start.2 = ((bf16[8,1024,2048]{2,1,0:T(8,128)(2,1)}), bf16[8,1024,2048]{2,1,0:T(8,128)(2,1)}, u32[]{:S(2)}, u32[]{:S(2)}) async-start(bf16[8,1024,2048]{2,1,0:T(8,128)(2,1)} %broadcast_select_fusion), calls=%async_computation.2 | async-start | bytes 67108864 | tf_op jit(solution)/shard_map/all_to_all | solution.py:104
  4517.4 8787.6 %copy-start.19 = (s32[1,8,8,128]{3,2,1,0:T(8,128)S(1)}, s32[1,8,8,128]{3,2,1,0:T(8,128)}, u32[]{:S(2)}) copy-start(s32[1,8,8,128]{3,2,1,0:T(8,128)} %copy-done.18) | copy-start | bytes 98308
  4517.4 9151.6 %copy-start.25 = (pred[8,1024]{1,0:T(8,128)(4,1)S(1)}, pred[8,1024]{1,0:T(8,128)(4,1)}, u32[]{:S(2)}) copy-start(pred[8,1024]{1,0:T(8,128)(4,1)} %copy-done.23) | copy-start | bytes 24580
  4517.4 9151.5 %all-to-all-start.3 = ((bf16[8,1024,2048]{2,1,0:T(8,128)(2,1)}), bf16[8,1024,2048]{2,1,0:T(8,128)(2,1)}, u32[]{:S(2)}, u32[]{:S(2)}) async-start(bf16[8,1024,2048]{2,1,0:T(8,128)(2,1)} %bitcast.223), calls=%async_computation.3 | async-start | bytes 67108864 | tf_op jit(solution)/shard_map/all_to_all | solution.py:104
  13701.3 114.5 copy-start.1
Sparse Core Ops, SparseCore 0:
  9.0 48.9 all-gather.8
  59.5 49.4 all-gather.6
  110.6 46.6 all-gather.4
  158.8 46.6 all-gather.10
where the time goes:
time: 14100 us; the launch traced here: 13800 us
  starting transfers between devices  8800 us (62%)
  local copies, waits for them, and re-layouts  1760 us (12%)
  other arithmetic  1680 us (12%)
  loops' own time  763 us (5%)
  matrix products  431 us (3%)
  waiting for transfers between devices  369 us (3%)
    all_to_all x4, starting transfers between devices, a2a(): return lax.all_to_all(v, 'ep', 0, 0, tiled=True)  8800 us
    scatter-add x40, other arithmetic, work(): return acc.at[rb].add(gb[:, None] * o.astype(jnp.float32))  935 us
    another operation x1, loops' own time, expert_sum(): lax.scan(body, jnp.zeros((n, d), jnp.float32), (jnp.arange(cand.shape[0])...  673 us
    scatter-add x1, other arithmetic, block_plan(): counts = jnp.bincount(eid, length=ne + 1)[:ne]  452 us
    gather x1, local copies, waits for them, and re-layouts, expert_sum(): gate = jnp.where(ok, gates[jnp.minimum(cand, m - 1)], 0.0)  368 us
    all_to_all x4, waiting for transfers between devices, a2a(): return lax.all_to_all(v, 'ep', 0, 0, tiled=True)  366 us
    gather x1, local copies, waits for them, and re-layouts, block_plan(): se = eid[order]  363 us
    dynamic_slice x560, local copies, waits for them, and re-layouts, expert_sum(): lax.scan(body, jnp.zeros((n, d), jnp.float32), (jnp.arange(cand.shape[0])...  332 us
  transfers between devices with their start and end apart: 8, of which 2 were waited for; matrix products, arithmetic and copies ran while one was open for 13% of the time, Pallas kernels for 0%

commit v1 on v0

v1 whole, which is shorter than its diff:
```python
import functools
import math
import jax
import jax.numpy as jnp
from jax import lax
from jax.experimental import pallas as pl
from jax.experimental.pallas import tpu as pltpu
from jax.sharding import PartitionSpec as P

HEAD = 128
EPS = 1e-6
THETA = 10000.0
PIECE = 16
CHUNK = 256
MT = 384
HM = 256
VMEM = 66_000_000
BF, F32, I32 = jnp.bfloat16, jnp.float32, jnp.int32


def rmsnorm(v):
    v = v.astype(F32)
    return v * lax.rsqrt(jnp.mean(v * v, axis=-1, keepdims=True) + EPS)


def dot(a, b):
    return jnp.dot(a, b, preferred_element_type=F32)


def params(**kw):
    return pltpu.CompilerParams(vmem_limit_bytes=VMEM, **kw)


def proj_kernel(rope, a_ref, w_ref, c_ref, s_ref, o_ref):
    tm = min(512, a_ref.shape[0])

    @pl.loop(0, a_ref.shape[0] // tm)
    def _(i):
        rows = pl.ds(pl.multiple_of(i * tm, tm), tm)
        z = dot(a_ref[rows, :], w_ref[...])
        for j in range(z.shape[1] // HEAD):
            zj = z[:, j * HEAD:(j + 1) * HEAD]
            if rope:
                zj = zj * c_ref[rows, :] + pltpu.roll(zj, HEAD // 2, 1) * s_ref[rows, :]
            o_ref[rows, j * HEAD:(j + 1) * HEAD] = zj.astype(BF)


def proj(a, w, cos, sin, rope):
    t, d = a.shape
    n = w.shape[1]
    tn = min(512, n)
    whole = lambda i: (0, 0)
    return pl.pallas_call(
        functools.partial(proj_kernel, rope),
        grid=(n // tn,),
        in_specs=[pl.BlockSpec((t, d), whole), pl.BlockSpec((d, tn), lambda i: (0, i)),
                  pl.BlockSpec((t, HEAD), whole), pl.BlockSpec((t, HEAD), whole)],
        out_specs=pl.BlockSpec((t, tn), lambda i: (0, i)),
        out_shape=jax.ShapeDtypeStruct((t, n), BF),
        compiler_params=params(),
        cost_estimate=pl.CostEstimate(flops=2 * t * d * n, bytes_accessed=2 * (t * d + d * n + t * n), transcendentals=0),
    )(a, w, cos, sin)


def attn_kernel(tq, q_ref, k_ref, v_ref, o_ref):
    t = q_ref.shape[0]
    scale = 1.0 / math.sqrt(HEAD)
    nt = (((1,), (1,)), ((), ()))
    row = lax.broadcasted_iota(I32, (tq, tq), 0)
    col = lax.broadcasted_iota(I32, (tq, tq), 1)
    for j in range(q_ref.shape[1] // HEAD):
        hs = slice(j * HEAD, (j + 1) * HEAD)
        for i in range(t // tq):
            q = q_ref[i * tq:(i + 1) * tq, hs]
            sd = lax.dot_general(q, k_ref[i * tq:(i + 1) * tq, hs], nt, preferred_element_type=F32)
            sd = jnp.where(col <= row, sd, -jnp.inf)
            m = jnp.max(sd, axis=1, keepdims=True)
            if i:
                so = lax.dot_general(q, k_ref[:i * tq, hs], nt, preferred_element_type=F32)
                m = jnp.maximum(m, jnp.max(so, axis=1, keepdims=True))
            pd = jnp.exp((sd - m) * scale)
            l = jnp.sum(pd, axis=1, keepdims=True)
            if i:
                po = jnp.exp((so - m) * scale)
                l = l + jnp.sum(po, axis=1, keepdims=True)
            inv = 1.0 / l
            o = dot((pd * inv).astype(BF), v_ref[i * tq:(i + 1) * tq, hs])
            if i:
                o = o + dot((po * inv).astype(BF), v_ref[:i * tq, hs])
            o_ref[i * tq:(i + 1) * tq, hs] = o.astype(BF)


def attn(q, k, v):
    t, n = q.shape
    tn = min(256, n)
    spec = pl.BlockSpec((t, tn), lambda i: (0, i))
    return pl.pallas_call(
        functools.partial(attn_kernel, min(256, t)),
        grid=(n // tn,), in_specs=[spec] * 3, out_specs=spec,
        out_shape=jax.ShapeDtypeStruct((t, n), BF),
        compiler_params=params(),
        cost_estimate=pl.CostEstimate(flops=4 * t * t * n, bytes_accessed=8 * t * n, transcendentals=t * t * n // HEAD),
    )(q, k, v)


def wo_kernel(o_ref, w_ref, x_ref, h_ref):
    tm = min(512, o_ref.shape[0])

    @pl.loop(0, o_ref.shape[0] // tm)
    def _(i):
        rows = pl.ds(pl.multiple_of(i * tm, tm), tm)
        h_ref[rows, :] = (x_ref[rows, :].astype(F32) + dot(o_ref[rows, :], w_ref[...])).astype(BF)


def wo_proj(o, w, x):
    t, n = o.shape
    d = w.shape[1]
    tn = min(512, d)
    return pl.pallas_call(
        wo_kernel,
        grid=(d // tn,),
        in_specs=[pl.BlockSpec((t, n), lambda i: (0, 0)), pl.BlockSpec((n, tn), lambda i: (0, i)),
                  pl.BlockSpec((t, tn), lambda i: (0, i))],
        out_specs=pl.BlockSpec((t, tn), lambda i: (0, i)),
        out_shape=jax.ShapeDtypeStruct((t, d), BF),
        compiler_params=params(),
        cost_estimate=pl.CostEstimate(flops=2 * t * d * n, bytes_accessed=2 * (t * n + d * n + 2 * t * d), transcendentals=0),
    )(o, w, x)


def fetch_expert(l, slot, own, other, bufs, sem):
    ne = own[0].shape[0]

    @pl.when(l < ne)
    def _():
        for src, dst in zip(own, bufs):
            pltpu.make_async_copy(src.at[l], dst.at[slot], sem.at[slot]).start()

    @pl.when(l >= ne)
    def _():
        for src, dst in zip(other, bufs):
            pltpu.make_async_copy(src.at[l - ne], dst.at[slot], sem.at[slot]).start()


def wait_expert(slot, own, bufs, sem):
    for src, dst in zip(own, bufs):
        pltpu.make_async_copy(src.at[0], dst.at[slot], sem.at[slot]).wait()


def ffn(x, w1, w3, w2):
    a1 = dot(x, w1)
    a3 = dot(x, w3)
    act = (jax.nn.silu(a1) * a3).astype(BF)
    return dot(act, w2).astype(BF)


def hot_kernel(has_acc, nh_ref, hl_ref, g_ref, ut_ref, ub_ref, *refs):
    if has_acc:
        acc_in, refs = refs[0], refs[1:]
    own, other, (ot_ref, ob_ref), refs = refs[:3], refs[3:6], refs[6:8], refs[8:]
    bufs, (ubuf, acc, sem, usem, asem) = refs[:3], refs[3:]
    half = ut_ref.shape[0]
    nh = nh_ref[0]
    tm = min(HM, half)

    @pl.when(nh > 0)
    def _():
        fetch_expert(hl_ref[0], 0, own, other, bufs, sem)

    ucp = [pltpu.make_async_copy(v, ubuf.at[pl.ds(p * half, half), :], usem) for p, v in enumerate((ut_ref, ub_ref))]
    for cp in ucp:
        cp.start()
    if has_acc:
        acp = pltpu.make_async_copy(acc_in, acc, asem)
        acp.start()
    else:
        acc[...] = jnp.zeros_like(acc)
    for cp in ucp:
        cp.wait()
    if has_acc:
        acp.wait()

    @pl.loop(0, nh)
    def _(i):
        slot = lax.rem(i, 2)
        wait_expert(slot, own, bufs, sem)

        @pl.when(i + 1 < nh)
        def _():
            fetch_expert(hl_ref[i + 1], 1 - slot, own, other, bufs, sem)

        e = hl_ref[i]

        @pl.loop(0, 2 * half // tm)
        def _(m):
            rows = pl.ds(pl.multiple_of(m * tm, tm), tm)
            z = ffn(ubuf[rows, :], bufs[0][slot], bufs[1][slot], bufs[2][slot])
            g = g_ref[rows, :]
            lane = lax.broadcasted_iota(I32, g.shape, 1)
            gc = jnp.sum(jnp.where(lane == e, g, 0.0), axis=1, keepdims=True)
            acc[rows, :] += gc * z.astype(F32)

    ot_ref[...] = acc[:half, :].astype(ot_ref.dtype)
    ob_ref[...] = acc[half:, :].astype(ob_ref.dtype)


def hot(nh, hl, ut, ub, g, acc, own, other, dtype):
    half, d = ut.shape
    ff = own[0].shape[2]
    vm = pl.BlockSpec(memory_space=pltpu.VMEM)
    sm = pl.BlockSpec(memory_space=pltpu.SMEM)
    hb = pl.BlockSpec(memory_space=pl.ANY)
    has = acc is not None
    out = jax.ShapeDtypeStruct((half, d), dtype)
    return pl.pallas_call(
        functools.partial(hot_kernel, has),
        in_specs=[sm, sm, vm] + [hb] * (9 if has else 8),
        out_specs=[vm, vm], out_shape=[out, out],
        scratch_shapes=[pltpu.VMEM((2, d, ff), BF), pltpu.VMEM((2, d, ff), BF), pltpu.VMEM((2, ff, d), BF),
                        pltpu.VMEM((2 * half, d), BF), pltpu.VMEM((2 * half, d), F32),
                        pltpu.SemaphoreType.DMA((2,)), pltpu.SemaphoreType.DMA, pltpu.SemaphoreType.DMA],
        compiler_params=params(),
        cost_estimate=pl.CostEstimate(flops=half * d, bytes_accessed=6 * d * ff, transcendentals=0),
    )(nh, hl, g, ut, ub, *([acc] if has else []), *own, *other)


def split3(g):
    hi = g.astype(BF)
    r = g - hi.astype(F32)
    mid = r.astype(BF)
    lo = (r - mid.astype(F32)).astype(BF)
    return hi, mid, lo


def selection(i, eg_ref, pos_ref, write):
    t = pos_ref.shape[1]
    it = lax.broadcasted_iota(I32, (PIECE, t), 0)

    @pl.loop(0, CHUNK // PIECE)
    def _(p):
        l = eg_ref[i * (CHUNK // PIECE) + p]
        row0 = i * CHUNK + p * PIECE
        write(pl.ds(pl.multiple_of(p * PIECE, PIECE), PIECE), pos_ref[pl.ds(l, 1), :] - row0 == it, l)


def gather_kernel(nch_ref, eg_ref, pos_ref, ut_ref, ub_ref, x_ref, pbuf, xbuf, sem):
    half = ut_ref.shape[0]
    nch = nch_ref[0]

    def out(i, slot):
        return pltpu.make_async_copy(xbuf.at[slot], x_ref.at[pl.ds(pl.multiple_of(i * CHUNK, CHUNK), CHUNK), :], sem.at[slot])

    def put(rows, hit, l):
        pbuf[rows, :] = jnp.where(hit, 1.0, 0.0).astype(BF)

    @pl.loop(0, nch)
    def _(i):
        slot = lax.rem(i, 2)

        @pl.when(i >= 2)
        def _():
            out(i - 2, slot).wait()

        selection(i, eg_ref, pos_ref, put)
        x = dot(pbuf[:, :half], ut_ref[...]) + dot(pbuf[:, half:], ub_ref[...])
        xbuf[slot] = x.astype(BF)
        out(i, slot).start()

    for k in (2, 1):
        @pl.when(nch >= k)
        def _():
            out(nch - k, lax.rem(nch - k, 2)).wait()


def gather(nch, eg, pos, ut, ub):
    half, d = ut.shape
    rows = eg.shape[0] * PIECE
    vm = pl.BlockSpec(memory_space=pltpu.VMEM)
    sm = pl.BlockSpec(memory_space=pltpu.SMEM)
    return pl.pallas_call(
        gather_kernel,
        in_specs=[sm, sm] + [vm] * 3,
        out_specs=pl.BlockSpec(memory_space=pl.ANY),
        out_shape=jax.ShapeDtypeStruct((rows, d), BF),
        scratch_shapes=[pltpu.VMEM((CHUNK, 2 * half), BF), pltpu.VMEM((2, CHUNK, d), BF), pltpu.SemaphoreType.DMA((2,))],
        compiler_params=params(),
        cost_estimate=pl.CostEstimate(flops=2 * CHUNK * half * d, bytes_accessed=4 * CHUNK * d, transcendentals=0),
    )(nch, eg, pos, ut, ub)


def cold_kernel(nb, nt_ref, tl_ref, tp_ref, tn_ref, tw_ref, tf_ref, nx_ref, pc_ref, *refs):
    xs, own, other, zs, refs = refs[:nb], refs[nb:nb + 3], refs[nb + 3:nb + 6], refs[nb + 6:2 * nb + 6], refs[2 * nb + 6:]
    bufs, (xbuf, zbuf, wsem, xsem, zsem) = refs[:3], refs[3:]
    nt = nt_ref[0]
    npb = xs[0].shape[0] // PIECE

    def pieces(q, fn):
        p0, n = tp_ref[q], tn_ref[q]

        @pl.loop(0, n)
        def _(i):
            c = pc_ref[p0 + i]
            for b in range(nb):
                @pl.when(jnp.logical_and(c >= b * npb, c < (b + 1) * npb))
                def _():
                    fn(b, pl.multiple_of((c - b * npb) * PIECE, PIECE), pl.multiple_of(i * PIECE, PIECE))

    def xin(q, slot):
        pieces(q, lambda b, src, dst: pltpu.make_async_copy(
            xs[b].at[pl.ds(src, PIECE), :], xbuf.at[slot, pl.ds(dst, PIECE), :], xsem.at[slot]).start())

    def zout(q, slot):
        pieces(q, lambda b, src, dst: pltpu.make_async_copy(
            zbuf.at[slot, pl.ds(dst, PIECE), :], zs[b].at[pl.ds(src, PIECE), :], zsem.at[slot]).start())

    def xwait(q, slot):
        @pl.loop(0, tn_ref[q])
        def _(i):
            pltpu.make_async_copy(xs[0].at[pl.ds(0, PIECE), :], xbuf.at[slot, pl.ds(0, PIECE), :], xsem.at[slot]).wait()

    def zwait(q, slot):
        @pl.loop(0, tn_ref[q])
        def _(i):
            pltpu.make_async_copy(zbuf.at[slot, pl.ds(0, PIECE), :], zs[0].at[pl.ds(0, PIECE), :], zsem.at[slot]).wait()

    @pl.when(nt > 0)
    def _():
        fetch_expert(tl_ref[0], 0, own, other, bufs, wsem)
        xin(0, 0)

    @pl.loop(0, nt)
    def _(q):
        slot = lax.rem(q, 2)
        ws = lax.rem(tw_ref[q], 2)

        @pl.when(tf_ref[q] == 1)
        def _():
            wait_expert(ws, own, bufs, wsem)

            @pl.when(nx_ref[q] >= 0)
            def _():
                fetch_expert(nx_ref[q], 1 - ws, own, other, bufs, wsem)

        @pl.when(q + 1 < nt)
        def _():
            xin(q + 1, 1 - slot)

        xwait(q, slot)

        @pl.when(q >= 2)
        def _():
            zwait(q - 2, slot)

        zbuf[slot] = ffn(xbuf[slot], bufs[0][ws], bufs[1][ws], bufs[2][ws])
        zout(q, slot)

    for k in (2, 1):
        @pl.when(nt >= k)
        def _():
            zwait(nt - k, lax.rem(nt - k, 2))


def cold(plan, xs, own, other):
    nb = len(xs)
    d, ff = own[0].shape[1:]
    sm = pl.BlockSpec(memory_space=pltpu.SMEM)
    hb = pl.BlockSpec(memory_space=pl.ANY)
    return pl.pallas_call(
        functools.partial(cold_kernel, nb),
        in_specs=[sm] * len(plan) + [hb] * (nb + 6),
        out_specs=[hb] * nb,
        out_shape=[jax.ShapeDtypeStruct(x.shape, BF) for x in xs],
        scratch_shapes=[pltpu.VMEM((2, d, ff), BF), pltpu.VMEM((2, d, ff), BF), pltpu.VMEM((2, ff, d), BF),
                        pltpu.VMEM((2, MT, d), BF), pltpu.VMEM((2, MT, d), BF),
                        pltpu.SemaphoreType.DMA((2,)), pltpu.SemaphoreType.DMA((2,)), pltpu.SemaphoreType.DMA((2,))],
        input_output_aliases={len(plan) + b: b for b in range(nb)},
        compiler_params=params(),
        cost_estimate=pl.CostEstimate(flops=6 * 16 * MT * d * ff, bytes_accessed=96 * d * ff, transcendentals=0),
    )(*plan, *xs, *own, *other)


def combine_kernel(nch_ref, eg_ref, pos_ref, gt_ref, z_ref, acc_ref, cbuf, zbuf, sem):
    t = acc_ref.shape[0]
    nch = nch_ref[0]
    tm = min(256, t)

    def get(i, slot):
        return pltpu.make_async_copy(z_ref.at[pl.ds(pl.multiple_of(i * CHUNK, CHUNK), CHUNK), :], zbuf.at[slot], sem.at[slot])

    def put(rows, hit, l):
        for j, g in enumerate(split3(gt_ref[pl.ds(l, 1), :])):
            cbuf[j, rows, :] = jnp.where(hit, g.astype(F32), 0.0).astype(BF)

    get(0, 0).start()
    acc_ref[...] = jnp.zeros_like(acc_ref)

    @pl.loop(0, nch)
    def _(i):
        slot = lax.rem(i, 2)

        @pl.when(i + 1 < nch)
        def _():
            get(i + 1, 1 - slot).start()

        selection(i, eg_ref, pos_ref, put)
        get(i, slot).wait()

        @pl.loop(0, t // tm)
        def _(m):
            ts = pl.ds(pl.multiple_of(m * tm, tm), tm)
            z = zbuf[slot]
            c = jnp.concatenate([cbuf[j, :, ts] for j in range(3)], axis=0)
            acc_ref[ts, :] += lax.dot_general(c, jnp.concatenate([z, z, z], axis=0), (((0,), (0,)), ((), ())),
                                              preferred_element_type=F32)


def combine(nch, eg, pos, gt, z):
    d = z.shape[1]
    t = pos.shape[1]
    vm = pl.BlockSpec(memory_space=pltpu.VMEM)
    sm = pl.BlockSpec(memory_space=pltpu.SMEM)
    return pl.pallas_call(
        combine_kernel,
        in_specs=[sm, sm, vm, vm, pl.BlockSpec(memory_space=pl.ANY)],
        out_specs=vm,
        out_shape=jax.ShapeDtypeStruct((t, d), F32),
        scratch_shapes=[pltpu.VMEM((3, CHUNK, t), BF), pltpu.VMEM((2, CHUNK, d), BF), pltpu.SemaphoreType.DMA((2,))],
        compiler_params=params(),
        cost_estimate=pl.CostEstimate(flops=t * d, bytes_accessed=4 * CHUNK * d, transcendentals=0),
    )(nch, eg, pos, gt, z)


def routing_plan(lid, local, nl):
    nb, t, k = lid.shape
    le = jnp.arange(nl, dtype=I32)
    hit = jnp.any((lid[:, None] == le[:, None, None]) & local[:, None], axis=-1)
    tri = (jnp.arange(t)[:, None] <= jnp.arange(t)[None, :]).astype(BF)
    rank = lax.dot_general(hit.astype(BF), tri, (((2,), (0,)), ((), ())), preferred_element_type=F32).astype(I32)
    cnt = rank[:, :, -1]
    hotm = cnt >= t // 2
    scnt = jnp.where(hotm, 0, cnt)
    pcs = (scnt + PIECE - 1) // PIECE
    pend = jnp.cumsum(pcs, axis=1)
    base = (pend - pcs) * PIECE
    pos = jnp.where(hit & ~hotm[..., None], base[..., None] + rank - 1, -1)
    rows = t * k + nl * PIECE
    npb = -(-rows // CHUNK) * CHUNK // PIECE
    nch = jnp.maximum(-(-pend[:, -1] * PIECE // CHUNK), 1)
    below = lambda ends, q: jnp.sum((ends <= q).astype(I32), axis=-1)
    eg = jnp.minimum(below(pend[:, None, :], jnp.arange(npb, dtype=I32)[None, :, None]), nl - 1)
    flat = pcs.T.reshape(-1)
    fend = jnp.cumsum(flat)
    p = jnp.arange(nb * npb, dtype=I32)[:, None]
    seg = jnp.minimum(below(fend[None, :], p), nl * nb - 1)
    inseg = seg[:, None] == jnp.arange(nl * nb, dtype=I32)
    shift_ = jnp.tile(jnp.arange(nb, dtype=I32) * npb, nl) + (pend - pcs).T.reshape(-1) - (fend - flat)
    pc = jnp.clip(p[:, 0] + jnp.sum(jnp.where(inseg, shift_, 0), axis=1), 0, nb * npb - 1)
    ppt = MT // PIECE
    ptot = jnp.sum(pcs, axis=0)
    pstart = jnp.cumsum(ptot) - ptot
    tiles = (ptot + ppt - 1) // ppt
    tend = jnp.cumsum(tiles)
    nq = -(-(nb * npb) // ppt) + nl
    q = jnp.arange(nq, dtype=I32)
    tl = jnp.minimum(below(tend[None, :], q[:, None]), nl - 1)
    one = tl[:, None] == le
    pick = lambda v: jnp.sum(jnp.where(one, v[None, :], 0), axis=1)
    ti = q - pick(tend - tiles)
    tp = pick(pstart) + ti * ppt
    tn = jnp.clip(pick(ptot) - ti * ppt, 0, ppt)
    active = (tiles > 0).astype(I32)
    tw = pick(jnp.cumsum(active) - active)
    tf = (ti == 0).astype(I32)
    later = (le[None, :] > tl[:, None]) & (active[None, :] > 0)
    nxt = jnp.min(jnp.where(later, le[None, :], nl), axis=1)
    nxt = jnp.where(nxt < nl, nxt, -1)
    plan = tuple(v.astype(I32) for v in (tend[-1:], tl, tp, tn, tw, tf, nxt, pc))
    hend = jnp.cumsum(hotm.astype(I32), axis=1)
    hl = jnp.minimum(below(hend[:, None, :], le[None, :, None]), nl - 1)
    return hend[:, -1], hl, nch, eg, pos, plan


def solution(mesh):
    nd = mesh.shape['ep']
    nx = nd // 2
    tok_spec = P(('replica', 'ep'), None, None)
    rows_ep = P('ep', None)
    by_expert = P('ep', None, None)

    def shift(v, s):
        return lax.ppermute(v, 'ep', [(2 * i + c, 2 * ((i + s) % nx) + c) for i in range(nx) for c in range(2)])

    def partner(v):
        return lax.ppermute(v, 'ep', [(i, i ^ 1) for i in range(nd)])

    def local(x, wq, wk, wv, wo, wr, w1, w3, w2, idx):
        b, s, d = x.shape
        t, k, ne = b * s, idx.shape[-1], w1.shape[0]
        nl = 2 * ne
        half = t // 2
        me = lax.axis_index('ep')
        x = x.reshape(t, d)
        ids = idx.reshape(t, k)

        wq, wk, wv, wo = [lax.all_gather(w, 'ep', axis=0, tiled=True) for w in (wq, wk, wv, wo)]
        own = (w1, w3, w2)
        other = tuple(partner(w) for w in own)

        ids4 = jnp.stack([ids, shift(ids, 1), shift(ids, -1), shift(ids, 2)])
        is_local = ids4 // nl == me // 2
        lid = (ids4 - me * ne) % nl
        nh, hl, nch, eg, pos, plan = routing_plan(lid, is_local, nl)

        hd = HEAD // 2
        freq = THETA ** (-jnp.arange(hd, dtype=F32) / hd)
        ang = (jnp.arange(t) % s).astype(F32)[:, None] * freq
        c, sn = jnp.cos(ang), jnp.sin(ang)
        cos, sin = jnp.concatenate([c, c], axis=1), jnp.concatenate([-sn, sn], axis=1)
        a = rmsnorm(x).astype(BF)
        q = proj(a, wq, cos, sin, True)
        kk = proj(a, wk, cos, sin, True)
        v = proj(a, wv, cos, sin, False)
        o = attn(q, kk, v)
        h = wo_proj(o, wo, x)

        r = rmsnorm(h)
        logits = jnp.dot(r, wr, precision=lax.Precision.HIGHEST, preferred_element_type=F32)
        oh = ids[..., None] == jnp.arange(wr.shape[1], dtype=I32)
        g = jax.nn.softmax(jnp.sum(jnp.where(oh, logits[:, None, :], 0.0), axis=-1), axis=-1)
        u = r.astype(BF)

        ut, ub = u[:half], u[half:]
        u1t, u2b = shift(ut, 1), shift(ub, -1)
        u1b, u2t = shift(ub, 1), shift(ut, -1)
        g4 = jnp.stack([g, shift(g, 1), shift(g, -1), shift(g, 2)])
        ohl = (lid[:, None] == jnp.arange(nl, dtype=I32)[:, None, None]) & is_local[:, None]
        gt = jnp.sum(jnp.where(ohl, g4[:, None], 0.0), axis=3)
        gd = jnp.swapaxes(gt, 1, 2)

        acc0 = hot(nh[0:1], hl[0], ut, ub, gd[0], None, own, other, F32)
        x0 = gather(nch[0:1], eg[0], pos[0], ut, ub)
        acc0, x0, u1t, u2b = lax.optimization_barrier((acc0, x0, u1t, u2b))
        u3t, u3b = shift(u1t, 1), shift(u2b, -1)
        us = [(ut, ub), (u1t, u1b), (u2t, u2b), (u3t, u3b)]
        xg = [x0] + [gather(nch[j:j + 1], eg[j], pos[j], *us[j]) for j in range(1, 4)]
        z = cold(plan, xg, own, other)

        def part(j, pj):
            accj = combine(nch[j:j + 1], eg[j], pj, gt[j], z[j])
            return hot(nh[j:j + 1], hl[j], *us[j], gd[j], accj, own, other, BF)

        b3t, b3b = part(3, pos[3])
        p1, b3t, b3b = lax.optimization_barrier((pos[1], b3t, b3b))
        r3t, r3b = shift(b3t, 1), shift(b3b, -1)
        b1 = part(1, p1)
        p2, b1, r3t, r3b = lax.optimization_barrier((pos[2], b1, r3t, r3b))
        r1 = [shift(v, -1) for v in b1]
        r3 = [shift(r3t, 1), shift(r3b, -1)]
        b2 = part(2, p2)
        p0, b2 = lax.optimization_barrier((pos[0], b2))
        r2 = [shift(v, 1) for v in b2]
        acc1 = combine(nch[0:1], eg[0], p0, gt[0], z[0])
        ys = []
        for p in range(2):
            rs = slice(p * half, (p + 1) * half)
            y = h[rs].astype(F32) + acc0[p] + acc1[rs]
            for v in (r1[p], r2[p], r3[p]):
                y = y + v.astype(F32)
            ys.append(y.astype(BF))
        return jnp.concatenate(ys, axis=0).reshape(b, s, d)

    return jax.shard_map(local, mesh=mesh,
                         in_specs=(tok_spec, rows_ep, rows_ep, rows_ep, rows_ep, P(None, None),
                                   by_expert, by_expert, by_expert, tok_spec),
                         out_specs=tok_spec, check_vma=False)
```

time: 14100 us -> 915 us (0.06); the launches traced: 13800 us -> 907 us
  starting transfers between devices: 8800 us -> 25.8 us
  local copies, waits for them, and re-layouts: 1760 us -> 11.3 us
  other arithmetic: 1680 us -> 39.6 us
  loops' own time: 763 us -> 0 us
  Pallas kernels: 0 us -> 581 us
  matrix products: 431 us -> 9.11 us
  waiting for transfers between devices: 369 us -> 226 us
    all_to_all x4 -> x0, starting transfers between devices: 8800 us -> none  [a2a(): return lax.all_to_all(v, 'ep', 0, 0, tiled=True)]
    scatter-add x42 -> x0, other arithmetic: 1500 us -> none  [the longest x40 935 us: work(): return acc.at[rb].add(gb[:, None] * o.astype(jnp.float32))]
    gather x58 -> x0, local copies, waits for them, and re-layouts: 1080 us -> none  [the longest x1 368 us: expert_sum(): gate = jnp.where(ok, gates[jnp.minimum(cand, m - 1)], 0.0)]
    another operation x522 -> x0, loops' own time: 763 us -> none  [the longest x1 673 us: expert_sum(): lax.scan(body, jnp.zeros((n, d), jnp.float32), (jnp.arange(cand.shape[0])...]
    pallas_call x0 -> x18, Pallas kernels: none -> 581 us  [the longest x4 268 us: hot(): pl.pallas_call(functools.partial(hot_kernel, has), in_specs=[sm, sm, vm]...]
    dot_general x85 -> x2, matrix products: 395 us -> 9.11 us  [the longest x1 8.73 us: local(): jnp.dot(r, wr, precision=lax.Precision.HIGHEST, preferred_element_type=F32)]
    all_to_all x4 -> x0, waiting for transfers between devices: 366 us -> none  [a2a(): return lax.all_to_all(v, 'ep', 0, 0, tiled=True)]
    dynamic_slice x560 -> x0, local copies, waits for them, and re-layouts: 332 us -> none  [expert_sum(): lax.scan(body, jnp.zeros((n, d), jnp.float32), (jnp.arange(cand.shape[0])...]
  transfers between devices with their start and end apart: 8 -> 27, of which waited for: 2 -> 9; matrix products, arithmetic and copies ran while one was open for 13% -> 5% of each run, Pallas kernels for 0% -> 34%
where the time goes in v1:
time: 915 us; the launch traced here: 907 us
  Pallas kernels  581 us (63%)
  waiting for transfers between devices  226 us (25%)
  other arithmetic  39.6 us (4%)
  starting transfers between devices  25.8 us (3%)
  between operations  13.9 us (2%)
  local copies, waits for them, and re-layouts  11.3 us (1%)
    pallas_call x4, Pallas kernels, hot(): pl.pallas_call(functools.partial(hot_kernel, has), in_specs=[sm, sm, vm]...  268 us
    ppermute x20, waiting for transfers between devices, shift(): lax.ppermute(v, 'ep', [(2 * i + c, 2 * ((i + s) % nx) + c) for i in range...  136 us
    pallas_call x4, Pallas kernels, combine(): pl.pallas_call(combine_kernel, in_specs=[sm, sm, vm, vm, pl.BlockSpec(mem...  99.1 us
    all_gather x4, waiting for transfers between devices, local(): lax.all_gather(w, 'ep', axis=0, tiled=True)  88.1 us
    pallas_call x1, Pallas kernels, cold(): pl.pallas_call(functools.partial(cold_kernel, nb), in_specs=[sm] * len(pl...  77.7 us
    pallas_call x3, Pallas kernels, proj(): pl.pallas_call(functools.partial(proj_kernel, rope), grid=(n // tn,), in_...  45.8 us
    pallas_call x4, Pallas kernels, gather(): pl.pallas_call(gather_kernel, in_specs=[sm, sm] + [vm] * 3, out_specs=pl....  40.3 us
    pallas_call x1, Pallas kernels, attn(): pl.pallas_call(functools.partial(attn_kernel, min(256, t)), grid=(n // tn...  35.7 us
  transfers between devices with their start and end apart: 27, of which 9 were waited for; matrix products, arithmetic and copies ran while one was open for 5% of the time, Pallas kernels for 34%

profile of v1, /device:TPU:113, one launch (start us, length us, event | category | flops | bytes accessed | tf_op | source)
XLA Modules:
  0.0 907.0 jit_solution(17509676873894205308)
XLA Ops:
  6.6 0.7 all-gather.9.cloned.1.call-update
  7.4 0.7 all-gather.7.cloned.1.call-update
  8.2 0.7 all-gather.5.cloned.1.call-update
  9.0 0.7 collective-permute-start.6
  10.3 3.1 collective-permute-start.2
  13.4 0.7 collective-permute-start.1
  14.1 3.1 fusion.2
  17.2 1.9 fusion.22
  19.1 2.8 fusion.3.a_ref
  21.9 1.3 pad_maximum_fusion
  23.2 0.9 collective-permute-start
  24.1 4.5 collective-permute-done
  28.8 0.9 fusion.18
  29.7 0.6 copy-done.5
  33.6 0.7 fusion.53
  34.4 0.7 convert_reduce_fusion.3
  35.4 0.6 slice_reduce_fusion.1
  37.4 21.7 %all-gather.9.cloned.1.call-done.w_ref = bf16[2048,2048]{1,0:T(8,128)(2,1)} async-done(((bf16[256,2048]{1,0:T(8,128)(2,1)}), bf16[2048,2048]{1,0:T(8,128)(2,1)}) %all-gather.9.cloned.1.call-update) | async-done | bytes 8388624 | tf_op jit(solution)/shard_map/all_gather | solution.py:505
  59.2 14.2 %shard_map.102.v_ref = bf16[1024,2048]{1,0:T(8,128)(2,1)} custom-call(bf16[1024,2048]{1,0:T(8,128)(2,1)} %fusion.3.a_ref, bf16[2048,2048]{1,0:T(8,128)(2,1)} %all-gather.9.cloned.1.call-done.w_ref, f32[1024,128]{1,0:T(8,128)} %get-tuple-element.108.c_ref, f32[1024,128]{1,0:T(8,128)} %get-tuple-element.109.s_ref), custom_call_target="tpu_custom_call" | custom-call | flops 8589934592 | bytes 16777216 | tf_op jit(solution)/shard_map/pallas_call | solution.py:53
  73.3 33.7 %all-gather.7.cloned.1.call-done.w_ref = bf16[2048,2048]{1,0:T(8,128)(2,1)} async-done(((bf16[256,2048]{1,0:T(8,128)(2,1)}), bf16[2048,2048]{1,0:T(8,128)(2,1)}) %all-gather.7.cloned.1.call-update) | async-done | bytes 8388624 | tf_op jit(solution)/shard_map/all_gather | solution.py:505
  107.0 15.8 %shard_map.101.k_ref = bf16[1024,2048]{1,0:T(8,128)(2,1)} custom-call(bf16[1024,2048]{1,0:T(8,128)(2,1)} %fusion.3.a_ref, bf16[2048,2048]{1,0:T(8,128)(2,1)} %all-gather.7.cloned.1.call-done.w_ref, f32[1024,128]{1,0:T(8,128)} %get-tuple-element.108.c_ref, f32[1024,128]{1,0:T(8,128)} %get-tuple-element.109.s_ref), custom_call_target="tpu_custom_call" | custom-call | flops 8589934592 | bytes 16777216 | tf_op jit(solution)/shard_map/pallas_call | solution.py:53
  122.8 32.7 %all-gather.5.cloned.1.call-done.w_ref = bf16[2048,2048]{1,0:T(8,128)(2,1)} async-done(((bf16[256,2048]{1,0:T(8,128)(2,1)}), bf16[2048,2048]{1,0:T(8,128)(2,1)}) %all-gather.5.cloned.1.call-update) | async-done | bytes 8388624 | tf_op jit(solution)/shard_map/all_gather | solution.py:505
  155.5 15.8 %shard_map.100.q_ref = bf16[1024,2048]{1,0:T(8,128)(2,1)} custom-call(bf16[1024,2048]{1,0:T(8,128)(2,1)} %fusion.3.a_ref, bf16[2048,2048]{1,0:T(8,128)(2,1)} %all-gather.5.cloned.1.call-done.w_ref, f32[1024,128]{1,0:T(8,128)} %get-tuple-element.108.c_ref, f32[1024,128]{1,0:T(8,128)} %get-tuple-element.109.s_ref), custom_call_target="tpu_custom_call" | custom-call | flops 8589934592 | bytes 16777216 | tf_op jit(solution)/shard_map/pallas_call | solution.py:53
  171.3 35.7 %shard_map.103.o_ref = bf16[1024,2048]{1,0:T(8,128)(2,1)} custom-call(bf16[1024,2048]{1,0:T(8,128)(2,1)} %shard_map.100.q_ref, bf16[1024,2048]{1,0:T(8,128)(2,1)} %shard_map.101.k_ref, bf16[1024,2048]{1,0:T(8,128)(2,1)} %shard_map.102.v_ref), custom_call_target="tpu_custom_call" | custom-call | flops 8589934592 | bytes 16777216 | tf_op jit(solution)/shard_map/pallas_call | solution.py:97
  207.1 14.5 %shard_map.104 = bf16[1024,2048]{1,0:T(8,128)(2,1)} custom-call(bf16[1024,2048]{1,0:T(8,128)(2,1)} %shard_map.103.o_ref, bf16[2048,2048]{1,0:T(8,128)(2,1)} %all-gather.11.cloned.1.call-done.w_ref, bf16[1024,2048]{1,0:T(8,128)(2,1)} %bitcast.71), custom_call_target="tpu_custom_call" | custom-call | flops 8589934592 | bytes 20971520 | tf_op jit(solution)/shard_map/pallas_call | solution.py:119
  221.6 3.2 fusion.4
  225.0 8.7 fusion.1
  234.1 1.5 collective-permute-start.5
  235.6 1.2 collective-permute-start.4
  236.8 2.9 fusion
  240.1 2.6 fusion.52
  242.7 2.4 collective-permute-start.10
  245.1 0.7 fusion.54
  246.5 0.7 slice_bitcast_fusion.8
  247.2 10.0 %shard_map.106.refs_0_ = bf16[8448,2048]{1,0:T(8,128)(2,1)} custom-call(s32[1]{0:T(128)} %get-tuple-element.107.nch_ref, s32[528]{0:T(1024)} %get-tuple-element.64.eg_ref, s32[16,1024]{1,0:T(8,128)} %get-tuple-element.52.pos_ref, bf16[512,2048]{1,0:T(8,128)(2,1)} %get-tuple-element.77.ut_ref, bf16[512,2048]{1,0:T(8,128)(2,1)} %get-tuple-element.76.ub_ref), custom_call_target="tpu_custom_call" | custom-call | flops 536870912 | bytes 2097152 | tf_op jit(solution)/shard_map/pallas_call | solution.py:280
  257.3 0.8 select_reduce_fusion
  258.8 4.3 collective-permute-start.11
  263.1 1.3 slice_bitcast_fusion
  264.4 66.2 %shard_map.105 = (f32[512,2048]{1,0:T(8,128)}, f32[512,2048]{1,0:T(8,128)}) custom-call(s32[1]{0:T(128)} %bitcast.6.nh_ref, s32[16]{0:T(128)} %get-tuple-element.96.hl_ref, f32[1024,16]{1,0:T(8,128)} %get-tuple-element.81.g_ref, bf16[512,2048]{1,0:T(8,128)(2,1)} %get-tuple-element.77.ut_ref, bf16[512,2048]{1,0:T(8,128)(2,1)} %get-tuple-element.76.ub_ref, ...), custom_call_target="tpu_custom_call" | custom-call | flops 1048576 | bytes 12582912 | tf_op jit(solution)/shard_map/pallas_call | solution.py:215
  330.8 1.4 collective-permute-start.13
  332.2 0.6 select_reduce_fusion.3
  334.8 0.6 add_clamp_fusion.pc_ref
  335.4 0.7 slice_bitcast_fusion.4
  336.1 10.0 %shard_map.108.refs_2_ = bf16[8448,2048]{1,0:T(8,128)(2,1)} custom-call(s32[1]{0:T(128)} %get-tuple-element.106.nch_ref, s32[528]{0:T(1024)} %get-tuple-element.63.eg_ref, s32[16,1024]{1,0:T(8,128)} %get-tuple-element.48.pos_ref, bf16[512,2048]{1,0:T(8,128)(2,1)} %collective-permute-done.11.ut_ref, bf16[512,2048]{1,0:T(8,128)(2,1)} %collective-permute-done.10.ub_ref), custom_call_target="tpu_custom_call" | custom-call | flops 536870912 | bytes 2097152 | tf_op jit(solution)/shard_map/pallas_call | solution.py:280
  346.1 10.1 %shard_map.107.refs_1_ = bf16[8448,2048]{1,0:T(8,128)(2,1)} custom-call(s32[1]{0:T(128)} %get-tuple-element.105.nch_ref, s32[528]{0:T(1024)} %get-tuple-element.62.eg_ref, s32[16,1024]{1,0:T(8,128)} %get-tuple-element.42.pos_ref, bf16[512,2048]{1,0:T(8,128)(2,1)} %collective-permute-done.9.ut_ref, bf16[512,2048]{1,0:T(8,128)(2,1)} %collective-permute-done.12.ub_ref), custom_call_target="tpu_custom_call" | custom-call | flops 536870912 | bytes 2097152 | tf_op jit(solution)/shard_map/pallas_call | solution.py:280
  356.2 23.0 %collective-permute-done.14.ub_ref = bf16[512,2048]{1,0:T(8,128)(2,1)} collective-permute-done((bf16[512,2048]{1,0:T(8,128)(2,1)}, bf16[512,2048]{1,0:T(8,128)(2,1)}, u32[]{:S(2)}, u32[]{:S(2)}) %collective-permute-start.14) | collective-permute-done | bytes 2097184 | tf_op jit(solution)/shard_map/ppermute | solution.py:491
  379.2 3.1 collective-permute-done.13.ut_ref
  382.3 10.1 %shard_map.109.refs_3_ = bf16[8448,2048]{1,0:T(8,128)(2,1)} custom-call(s32[1]{0:T(128)} %get-tuple-element.104.nch_ref, s32[528]{0:T(1024)} %get-tuple-element.61.eg_ref, s32[16,1024]{1,0:T(8,128)} %get-tuple-element.86.pos_ref, bf16[512,2048]{1,0:T(8,128)(2,1)} %collective-permute-done.13.ut_ref, bf16[512,2048]{1,0:T(8,128)(2,1)} %collective-permute-done.14.ub_ref), custom_call_target="tpu_custom_call" | custom-call | flops 536870912 | bytes 2097152 | tf_op jit(solution)/shard_map/pallas_call | solution.py:280
  392.4 77.7 %shard_map.110 = (bf16[8448,2048]{1,0:T(8,128)(2,1)}, bf16[8448,2048]{1,0:T(8,128)(2,1)}, bf16[8448,2048]{1,0:T(8,128)(2,1)}, bf16[8448,2048]{1,0:T(8,128)(2,1)}) custom-call(s32[1]{0:T(128)} %bitcast.30.nt_ref, s32[104]{0:T(128)} %copy-done.7, ...), custom_call_target="tpu_custom_call", output_to_operand_aliasing={{0}: (8, {}), {1}: (9, {}), {2}: (10, {}), {3}: (11, {})} | custom-call | flops 77309411328 | bytes 201326592 | tf_op jit(solution)/shard_map/pallas_call | solution.py:368
  470.2 24.8 %shard_map.111.refs_0_ = f32[1024,2048]{1,0:T(8,128)} custom-call(s32[1]{0:T(128)} %get-tuple-element.104.nch_ref, s32[528]{0:T(1024)} %get-tuple-element.61.eg_ref, s32[16,1024]{1,0:T(8,128)} %get-tuple-element.86.pos_ref, f32[16,1024]{1,0:T(8,128)} %get-tuple-element.85.gt_ref, bf16[8448,2048]{1,0:T(8,128)(2,1)} %get-tuple-element.39.z_ref), custom_call_target="tpu_custom_call" | custom-call | flops 2097152 | bytes 2097152 | tf_op jit(solution)/shard_map/pallas_call | solution.py:422
  495.0 67.3 %shard_map.112 = (bf16[512,2048]{1,0:T(8,128)(2,1)}, bf16[512,2048]{1,0:T(8,128)(2,1)}) custom-call(s32[1]{0:T(128)} %bitcast.24.nh_ref, s32[16]{0:T(128)} %get-tuple-element.93.hl_ref, f32[1024,16]{1,0:T(8,128)} %get-tuple-element.78.g_ref, bf16[512,2048]{1,0:T(8,128)(2,1)} %collective-permute-done.13.ut_ref, ...), custom_call_target="tpu_custom_call" | custom-call | flops 1048576 | bytes 12582912 | tf_op jit(solution)/shard_map/pallas_call | solution.py:215
  562.4 2.6 collective-permute-start.16
  565.0 24.8 %shard_map.113.refs_0_ = f32[1024,2048]{1,0:T(8,128)} custom-call(s32[1]{0:T(128)} %get-tuple-element.105.nch_ref, s32[528]{0:T(1024)} %get-tuple-element.62.eg_ref, s32[16,1024]{1,0:T(8,128)} %get-tuple-element.42.pos_ref, f32[16,1024]{1,0:T(8,128)} %get-tuple-element.84.gt_ref, bf16[8448,2048]{1,0:T(8,128)(2,1)} %get-tuple-element.43.z_ref), custom_call_target="tpu_custom_call" | custom-call | flops 2097152 | bytes 2097152 | tf_op jit(solution)/shard_map/pallas_call | solution.py:422
  589.8 67.4 %shard_map.114 = (bf16[512,2048]{1,0:T(8,128)(2,1)}, bf16[512,2048]{1,0:T(8,128)(2,1)}) custom-call(s32[1]{0:T(128)} %bitcast.20.nh_ref, s32[16]{0:T(128)} %get-tuple-element.94.hl_ref, f32[1024,16]{1,0:T(8,128)} %get-tuple-element.79.g_ref, bf16[512,2048]{1,0:T(8,128)(2,1)} %collective-permute-done.9.ut_ref, ...), custom_call_target="tpu_custom_call" | custom-call | flops 1048576 | bytes 12582912 | tf_op jit(solution)/shard_map/pallas_call | solution.py:215
  657.3 24.8 %shard_map.115.refs_0_ = f32[1024,2048]{1,0:T(8,128)} custom-call(s32[1]{0:T(128)} %get-tuple-element.106.nch_ref, s32[528]{0:T(1024)} %get-tuple-element.63.eg_ref, s32[16,1024]{1,0:T(8,128)} %get-tuple-element.48.pos_ref, f32[16,1024]{1,0:T(8,128)} %get-tuple-element.83.gt_ref, bf16[8448,2048]{1,0:T(8,128)(2,1)} %get-tuple-element.49.z_ref), custom_call_target="tpu_custom_call" | custom-call | flops 2097152 | bytes 2097152 | tf_op jit(solution)/shard_map/pallas_call | solution.py:422
  682.1 67.2 %shard_map.116 = (bf16[512,2048]{1,0:T(8,128)(2,1)}, bf16[512,2048]{1,0:T(8,128)(2,1)}) custom-call(s32[1]{0:T(128)} %bitcast.16.nh_ref, s32[16]{0:T(128)} %get-tuple-element.95.hl_ref, f32[1024,16]{1,0:T(8,128)} %get-tuple-element.80.g_ref, bf16[512,2048]{1,0:T(8,128)(2,1)} %collective-permute-done.11.ut_ref, ...), custom_call_target="tpu_custom_call" | custom-call | flops 1048576 | bytes 12582912 | tf_op jit(solution)/shard_map/pallas_call | solution.py:215
  749.5 2.6 collective-permute-start.17
  752.2 2.7 collective-permute-start.20
  754.8 40.1 %collective-permute-done.18 = bf16[512,2048]{1,0:T(8,128)(2,1)} collective-permute-done((bf16[512,2048]{1,0:T(8,128)(2,1)}, bf16[512,2048]{1,0:T(8,128)(2,1)}, u32[]{:S(2)}, u32[]{:S(2)}) %collective-permute-start.18) | collective-permute-done | bytes 2097184 | tf_op jit(solution)/shard_map/ppermute | solution.py:491
  794.9 24.7 %shard_map.117 = f32[1024,2048]{1,0:T(8,128)} custom-call(s32[1]{0:T(128)} %get-tuple-element.107.nch_ref, s32[528]{0:T(1024)} %get-tuple-element.64.eg_ref, s32[16,1024]{1,0:T(8,128)} %get-tuple-element.52.pos_ref, f32[16,1024]{1,0:T(8,128)} %get-tuple-element.82.gt_ref, bf16[8448,2048]{1,0:T(8,128)(2,1)} %get-tuple-element.53.z_ref), custom_call_target="tpu_custom_call" | custom-call | flops 2097152 | bytes 2097152 | tf_op jit(solution)/shard_map/pallas_call | solution.py:422
  819.7 20.2 %collective-permute-done.21 = bf16[512,2048]{1,0:T(8,128)(2,1)} collective-permute-done((bf16[512,2048]{1,0:T(8,128)(2,1)}, bf16[512,2048]{1,0:T(8,128)(2,1)}, u32[]{:S(2)}, u32[]{:S(2)}) %collective-permute-start.21) | collective-permute-done | bytes 2097184 | tf_op jit(solution)/shard_map/ppermute | solution.py:491
  839.9 44.9 %collective-permute-done.19 = bf16[512,2048]{1,0:T(8,128)(2,1)} collective-permute-done((bf16[512,2048]{1,0:T(8,128)(2,1)}, bf16[512,2048]{1,0:T(8,128)(2,1)}, u32[]{:S(2)}, u32[]{:S(2)}) %collective-permute-start.19) | collective-permute-done | bytes 2097184 | tf_op jit(solution)/shard_map/ppermute | solution.py:491
  884.8 12.9 %fusion.12 = (bf16[512,2048]{1,0:T(8,128)(2,1)S(1)}, bf16[512,2048]{1,0:T(8,128)(2,1)S(1)}) fusion(f32[1024,2048]{1,0:T(8,128)} %shard_map.117, bf16[512,2048]{1,0:T(8,128)(2,1)} %collective-permute-done.19, bf16[512,2048]{1,0:T(8,128)(2,1)} %collective-permute-done.18, bf16[512,2048]{1,0:T(8,128)(2,1)} %collective-permute-done.17, ...), kind=kLoop, calls=%fused_computation.18 | loop fusion | flops 20971520 | bytes 37748736 | tf_op jit(solution)/shard_map/convert_element_type | solution.py:569
  897.7 2.5 maximum_bitcast_fusion
  (119 shorter events, 10.8 us)
Async XLA Ops:
  6.5 218.2 %copy-start = (f32[2048,64]{0,1:T(8,128)S(1)}, f32[2048,64]{0,1:T(8,128)}, u32[]{:S(2)}) copy-start(f32[2048,64]{0,1:T(8,128)} %param.15) | copy-start | bytes 1572868
  6.6 3.7 copy-start.4
  6.6 52.6 %all-gather.9.cloned.1.call-start = ((), (), s32[]{:S(2)}) async-start(), calls=%async_computation.2 | async-start | bytes 9437184 | tf_op jit(solution)/shard_map/all_gather | solution.py:505
  7.3 99.7 %all-gather.7.cloned.1.call-start = ((), (), s32[]{:S(2)}) async-start(), calls=%async_computation.1 | async-start | bytes 9437184 | tf_op jit(solution)/shard_map/all_gather | solution.py:505
  8.1 147.4 %all-gather.5.cloned.1.call-start = ((), (), s32[]{:S(2)}) async-start(), calls=%async_computation | async-start | bytes 9437184 | tf_op jit(solution)/shard_map/all_gather | solution.py:505
  8.9 198.2 %all-gather.11.cloned.1.call-start = ((), (), s32[]{:S(2)}) async-start(), calls=%async_computation.3 | async-start | bytes 9437184 | tf_op jit(solution)/shard_map/all_gather | solution.py:505
  9.0 249.8 %collective-permute-start.6 = (bf16[8,2048,1024]{2,1,0:T(8,128)(2,1)}, bf16[8,2048,1024]{2,1,0:T(8,128)(2,1)}, u32[]{:S(2)}, u32[]{:S(2)}) collective-permute-start(bf16[8,2048,1024]{2,1,0:T(8,128)(2,1)} %refs_1_.7), channel_id=1, source_target_pairs={{0,1},{1,0},{2,3},{3,2},{4,5},{5,4},{6,7},{7,6},{8,9},{9,8},{10,11... | collective-permute-start | bytes 100663304 | tf_op jit(solution)/shard_map/ppermute | solution.py:494
  9.7 254.7 %collective-permute-start.7 = (bf16[8,2048,1024]{2,1,0:T(8,128)(2,1)}, bf16[8,2048,1024]{2,1,0:T(8,128)(2,1)}, u32[]{:S(2)}, u32[]{:S(2)}) collective-permute-start(bf16[8,2048,1024]{2,1,0:T(8,128)(2,1)} %refs_2_.7), channel_id=1, source_target_pairs={{0,1},{1,0},{2,3},{3,2},{4,5},{5,4},{6,7},{7,6},{8,9},{9,8},{10,11... | collective-permute-start | bytes 100663304 | tf_op jit(solution)/shard_map/ppermute | solution.py:494
  9.8 254.6 %collective-permute-start.8 = (bf16[8,1024,2048]{2,1,0:T(8,128)(2,1)}, bf16[8,1024,2048]{2,1,0:T(8,128)(2,1)}, u32[]{:S(2)}, u32[]{:S(2)}) collective-permute-start(bf16[8,1024,2048]{2,1,0:T(8,128)(2,1)} %refs_3_.5), channel_id=1, source_target_pairs={{0,1},{1,0},{2,3},{3,2},{4,5},{5,4},{6,7},{7,6},{8,9},{9,8},{10,11... | collective-permute-start | bytes 100663304 | tf_op jit(solution)/shard_map/ppermute | solution.py:494
  10.3 8.9 copy-start.3
  10.3 12.9 %collective-permute-start.2 = (s32[1024,8]{0,1:T(8,128)S(1)}, s32[1024,8]{0,1:T(8,128)S(1)}, u32[]{:S(2)}, u32[]{:S(2)}) collective-permute-start(s32[1024,8]{0,1:T(8,128)S(1)} %bitcast.73), channel_id=1, source_target_pairs={{0,4},{1,5},{2,6},{3,7},{4,0},{5,1},{6,2},{7,3},{8,12},{9,13},{10,... | collective-permute-start | bytes 98312 | tf_op jit(solution)/shard_map/ppermute | solution.py:491
  13.4 10.7 %collective-permute-start.1 = (s32[1024,8]{0,1:T(8,128)S(1)}, s32[1024,8]{0,1:T(8,128)S(1)}, u32[]{:S(2)}, u32[]{:S(2)}) collective-permute-start(s32[1024,8]{0,1:T(8,128)S(1)} %bitcast.74), channel_id=1, source_target_pairs={{0,6},{1,7},{2,0},{3,1},{4,2},{5,3},{6,4},{7,5},{8,14},{9,15},{10,... | collective-permute-start | bytes 98312 | tf_op jit(solution)/shard_map/ppermute | solution.py:491
  23.2 5.4 collective-permute-start
  29.7 0.6 copy-start.5
  36.5 0.5 copy-start.8
  221.5 3.5 copy-start.2
  234.1 5.7 collective-permute-start.5
  235.6 7.1 collective-permute-start.4
  239.7 6.0 copy-start.9
  239.7 6.6 copy-start.6
  239.8 5.3 collective-permute-start.3
  242.7 88.0 %collective-permute-start.10 = (bf16[512,2048]{1,0:T(8,128)(2,1)}, bf16[512,2048]{1,0:T(8,128)(2,1)}, u32[]{:S(2)}, u32[]{:S(2)}) collective-permute-start(bf16[512,2048]{1,0:T(8,128)(2,1)} %get-tuple-element.76.ub_ref), channel_id=1, source_target_pairs={{0,6},{1,7},{2,0},{3,1},{4,2},{5,3},{6,4},{7,5},{8,14},{9,15},{10,... | collective-permute-start | bytes 6291464 | tf_op jit(solution)/shard_map/ppermute | solution.py:491
  245.1 85.6 %collective-permute-start.9 = (bf16[512,2048]{1,0:T(8,128)(2,1)}, bf16[512,2048]{1,0:T(8,128)(2,1)}, u32[]{:S(2)}, u32[]{:S(2)}) collective-permute-start(bf16[512,2048]{1,0:T(8,128)(2,1)} %get-tuple-element.77.ut_ref), channel_id=1, source_target_pairs={{0,2},{1,3},{2,4},{3,5},{4,6},{5,7},{6,0},{7,1},{8,10},{9,11},{10,... | collective-permute-start | bytes 6291464 | tf_op jit(solution)/shard_map/ppermute | solution.py:491
  258.8 77.3 %collective-permute-start.11 = (bf16[512,2048]{1,0:T(8,128)(2,1)}, bf16[512,2048]{1,0:T(8,128)(2,1)}, u32[]{:S(2)}, u32[]{:S(2)}) collective-permute-start(bf16[512,2048]{1,0:T(8,128)(2,1)} %get-tuple-element.77.ut_ref), channel_id=1, source_target_pairs={{0,6},{1,7},{2,0},{3,1},{4,2},{5,3},{6,4},{7,5},{8,14},{9,15},{10,... | collective-permute-start | bytes 6291464 | tf_op jit(solution)/shard_map/ppermute | solution.py:491
  264.4 81.7 %collective-permute-start.12 = (bf16[512,2048]{1,0:T(8,128)(2,1)}, bf16[512,2048]{1,0:T(8,128)(2,1)}, u32[]{:S(2)}, u32[]{:S(2)}) collective-permute-start(bf16[512,2048]{1,0:T(8,128)(2,1)} %get-tuple-element.76.ub_ref), channel_id=1, source_target_pairs={{0,2},{1,3},{2,4},{3,5},{4,6},{5,7},{6,0},{7,1},{8,10},{9,11},{10,... | collective-permute-start | bytes 6291464 | tf_op jit(solution)/shard_map/ppermute | solution.py:491
  264.4 67.8 %copy-start.11 = (s32[104]{0:T(128)S(1)}, s32[104]{0:T(128)}, u32[]{:S(2)}) copy-start(s32[104]{0:T(128)} %convert_reduce_fusion.3) | copy-start | bytes 1252
  264.4 67.8 %copy-start.10 = (pred[16]{0:T(512)(128)(4,1)S(1)}, pred[16]{0:T(512)(128)(4,1)}, u32[]{:S(2)}) copy-start(pred[16]{0:T(512)(128)(4,1)} %fusion.47) | copy-start | bytes 52
  330.7 48.5 %collective-permute-start.14 = (bf16[512,2048]{1,0:T(8,128)(2,1)}, bf16[512,2048]{1,0:T(8,128)(2,1)}, u32[]{:S(2)}, u32[]{:S(2)}) collective-permute-start(bf16[512,2048]{1,0:T(8,128)(2,1)} %collective-permute-done.10.ub_ref), channel_id=1, source_target_pairs={{0,6},{1,7},{2,0},{3,1},{4,2},{5,3},{6,4},{7,5},{8,14},{9,15},{10,... | collective-permute-start | bytes 6291464 | tf_op jit(solution)/shard_map/ppermute | solution.py:491
  330.8 51.5 %collective-permute-start.13 = (bf16[512,2048]{1,0:T(8,128)(2,1)}, bf16[512,2048]{1,0:T(8,128)(2,1)}, u32[]{:S(2)}, u32[]{:S(2)}) collective-permute-start(bf16[512,2048]{1,0:T(8,128)(2,1)} %collective-permute-done.9.ut_ref), channel_id=1, source_target_pairs={{0,2},{1,3},{2,4},{3,5},{4,6},{5,7},{6,0},{7,1},{8,10},{9,11},{10,... | collective-permute-start | bytes 6291464 | tf_op jit(solution)/shard_map/ppermute | solution.py:491
  332.2 13.9 %copy-start.7 = (s32[104]{0:T(128)}, s32[104]{0:T(128)S(1)}, u32[]{:S(2)}) copy-start(s32[104]{0:T(128)S(1)} %broadcast_minimum_fusion.3.tl_ref) | copy-start | bytes 1252
  562.2 95.0 %collective-permute-start.15 = (bf16[512,2048]{1,0:T(8,128)(2,1)}, bf16[512,2048]{1,0:T(8,128)(2,1)}, u32[]{:S(2)}, u32[]{:S(2)}) collective-permute-start(bf16[512,2048]{1,0:T(8,128)(2,1)} %get-tuple-element.46), channel_id=1, source_target_pairs={{0,2},{1,3},{2,4},{3,5},{4,6},{5,7},{6,0},{7,1},{8,10},{9,11},{10,... | collective-permute-start | bytes 6291464 | tf_op jit(solution)/shard_map/ppermute | solution.py:491
  562.4 94.9 %collective-permute-start.16 = (bf16[512,2048]{1,0:T(8,128)(2,1)}, bf16[512,2048]{1,0:T(8,128)(2,1)}, u32[]{:S(2)}, u32[]{:S(2)}) collective-permute-start(bf16[512,2048]{1,0:T(8,128)(2,1)} %get-tuple-element.47), channel_id=1, source_target_pairs={{0,6},{1,7},{2,0},{3,1},{4,2},{5,3},{6,4},{7,5},{8,14},{9,15},{10,... | collective-permute-start | bytes 6291464 | tf_op jit(solution)/shard_map/ppermute | solution.py:491
  749.3 45.7 %collective-permute-start.18 = (bf16[512,2048]{1,0:T(8,128)(2,1)}, bf16[512,2048]{1,0:T(8,128)(2,1)}, u32[]{:S(2)}, u32[]{:S(2)}) collective-permute-start(bf16[512,2048]{1,0:T(8,128)(2,1)} %get-tuple-element.55), channel_id=1, source_target_pairs={{0,2},{1,3},{2,4},{3,5},{4,6},{5,7},{6,0},{7,1},{8,10},{9,11},{10,... | collective-permute-start | bytes 6291464 | tf_op jit(solution)/shard_map/ppermute | solution.py:491
  749.4 90.5 %collective-permute-start.21 = (bf16[512,2048]{1,0:T(8,128)(2,1)}, bf16[512,2048]{1,0:T(8,128)(2,1)}, u32[]{:S(2)}, u32[]{:S(2)}) collective-permute-start(bf16[512,2048]{1,0:T(8,128)(2,1)} %get-tuple-element.59), channel_id=1, source_target_pairs={{0,2},{1,3},{2,4},{3,5},{4,6},{5,7},{6,0},{7,1},{8,10},{9,11},{10,... | collective-permute-start | bytes 6291464 | tf_op jit(solution)/shard_map/ppermute | solution.py:491
  749.5 90.4 %collective-permute-start.17 = (bf16[512,2048]{1,0:T(8,128)(2,1)}, bf16[512,2048]{1,0:T(8,128)(2,1)}, u32[]{:S(2)}, u32[]{:S(2)}) collective-permute-start(bf16[512,2048]{1,0:T(8,128)(2,1)} %get-tuple-element.54), channel_id=1, source_target_pairs={{0,6},{1,7},{2,0},{3,1},{4,2},{5,3},{6,4},{7,5},{8,14},{9,15},{10,... | collective-permute-start | bytes 6291464 | tf_op jit(solution)/shard_map/ppermute | solution.py:491
  752.1 132.7 %collective-permute-start.19 = (bf16[512,2048]{1,0:T(8,128)(2,1)}, bf16[512,2048]{1,0:T(8,128)(2,1)}, u32[]{:S(2)}, u32[]{:S(2)}) collective-permute-start(bf16[512,2048]{1,0:T(8,128)(2,1)} %collective-permute-done.15), channel_id=1, source_target_pairs={{0,2},{1,3},{2,4},{3,5},{4,6},{5,7},{6,0},{7,1},{8,10},{9,11},{10,... | collective-permute-start | bytes 6291464 | tf_op jit(solution)/shard_map/ppermute | solution.py:491
  752.2 132.7 %collective-permute-start.20 = (bf16[512,2048]{1,0:T(8,128)(2,1)}, bf16[512,2048]{1,0:T(8,128)(2,1)}, u32[]{:S(2)}, u32[]{:S(2)}) collective-permute-start(bf16[512,2048]{1,0:T(8,128)(2,1)} %get-tuple-element.58), channel_id=1, source_target_pairs={{0,6},{1,7},{2,0},{3,1},{4,2},{5,3},{6,4},{7,5},{8,14},{9,15},{10,... | collective-permute-start | bytes 6291464 | tf_op jit(solution)/shard_map/ppermute | solution.py:491
  794.9 89.9 %collective-permute-start.22 = (bf16[512,2048]{1,0:T(8,128)(2,1)}, bf16[512,2048]{1,0:T(8,128)(2,1)}, u32[]{:S(2)}, u32[]{:S(2)}) collective-permute-start(bf16[512,2048]{1,0:T(8,128)(2,1)} %collective-permute-done.16), channel_id=1, source_target_pairs={{0,6},{1,7},{2,0},{3,1},{4,2},{5,3},{6,4},{7,5},{8,14},{9,15},{10,... | collective-permute-start | bytes 6291464 | tf_op jit(solution)/shard_map/ppermute | solution.py:491
  897.7 2.5 copy-start.1
Sparse Core Ops, SparseCore 0:
  9.0 50.1 all-gather.8
  60.8 46.1 all-gather.6
  108.6 46.8 all-gather.4
  157.0 46.5 all-gather.10

commit v2 on v1

v2 whole, which is shorter than its diff:
```python
import functools
import math
import typing
import jax
import jax.numpy as jnp
from jax import lax
from jax.experimental import pallas as pl
from jax.experimental.pallas import tpu as pltpu
from jax.sharding import PartitionSpec as P

HEAD = 128
EPS = 1e-6
THETA = 10000.0
PIECE = 16
CHUNK = 256
MT = 416
HM = 256
VMEM = 66_000_000
BF, F32, I32 = jnp.bfloat16, jnp.float32, jnp.int32


def rmsnorm(v):
    v = v.astype(F32)
    return v * lax.rsqrt(jnp.mean(v * v, axis=-1, keepdims=True) + EPS)


def dot(a, b):
    return jnp.dot(a, b, preferred_element_type=F32)


def params(**kw):
    return pltpu.CompilerParams(vmem_limit_bytes=VMEM, **kw)


def proj_kernel(rope, a_ref, w_ref, c_ref, s_ref, o_ref):
    tm = min(512, a_ref.shape[0])

    @pl.loop(0, a_ref.shape[0] // tm)
    def _(i):
        rows = pl.ds(pl.multiple_of(i * tm, tm), tm)
        z = dot(a_ref[rows, :], w_ref[...])
        for j in range(z.shape[1] // HEAD):
            zj = z[:, j * HEAD:(j + 1) * HEAD]
            if rope:
                zj = zj * c_ref[rows, :] + pltpu.roll(zj, HEAD // 2, 1) * s_ref[rows, :]
            o_ref[rows, j * HEAD:(j + 1) * HEAD] = zj.astype(BF)


def proj(a, w, cos, sin, rope):
    t, d = a.shape
    n = w.shape[1]
    tn = min(512, n)
    whole = lambda i: (0, 0)
    return pl.pallas_call(
        functools.partial(proj_kernel, rope),
        grid=(n // tn,),
        in_specs=[pl.BlockSpec((t, d), whole), pl.BlockSpec((d, tn), lambda i: (0, i)),
                  pl.BlockSpec((t, HEAD), whole), pl.BlockSpec((t, HEAD), whole)],
        out_specs=pl.BlockSpec((t, tn), lambda i: (0, i)),
        out_shape=jax.ShapeDtypeStruct((t, n), BF),
        compiler_params=params(),
        cost_estimate=pl.CostEstimate(flops=2 * t * d * n, bytes_accessed=2 * (t * d + d * n + t * n), transcendentals=0),
    )(a, w, cos, sin)


def attn_kernel(tq, q_ref, k_ref, v_ref, o_ref):
    t = q_ref.shape[0]
    scale = 1.0 / math.sqrt(HEAD)
    nt = (((1,), (1,)), ((), ()))
    row = lax.broadcasted_iota(I32, (tq, tq), 0)
    col = lax.broadcasted_iota(I32, (tq, tq), 1)
    for j in range(q_ref.shape[1] // HEAD):
        hs = slice(j * HEAD, (j + 1) * HEAD)
        for i in range(t // tq):
            q = q_ref[i * tq:(i + 1) * tq, hs]
            sd = lax.dot_general(q, k_ref[i * tq:(i + 1) * tq, hs], nt, preferred_element_type=F32)
            sd = jnp.where(col <= row, sd, -jnp.inf)
            m = jnp.max(sd, axis=1, keepdims=True)
            if i:
                so = lax.dot_general(q, k_ref[:i * tq, hs], nt, preferred_element_type=F32)
                m = jnp.maximum(m, jnp.max(so, axis=1, keepdims=True))
            pd = jnp.exp((sd - m) * scale)
            l = jnp.sum(pd, axis=1, keepdims=True)
            if i:
                po = jnp.exp((so - m) * scale)
                l = l + jnp.sum(po, axis=1, keepdims=True)
            inv = 1.0 / l
            o = dot((pd * inv).astype(BF), v_ref[i * tq:(i + 1) * tq, hs])
            if i:
                o = o + dot((po * inv).astype(BF), v_ref[:i * tq, hs])
            o_ref[i * tq:(i + 1) * tq, hs] = o.astype(BF)


def attn(q, k, v):
    t, n = q.shape
    tn = min(256, n)
    spec = pl.BlockSpec((t, tn), lambda i: (0, i))
    return pl.pallas_call(
        functools.partial(attn_kernel, min(256, t)),
        grid=(n // tn,), in_specs=[spec] * 3, out_specs=spec,
        out_shape=jax.ShapeDtypeStruct((t, n), BF),
        compiler_params=params(),
        cost_estimate=pl.CostEstimate(flops=4 * t * t * n, bytes_accessed=8 * t * n, transcendentals=t * t * n // HEAD),
    )(q, k, v)


def wo_kernel(o_ref, w_ref, x_ref, h_ref):
    tm = min(512, o_ref.shape[0])

    @pl.loop(0, o_ref.shape[0] // tm)
    def _(i):
        rows = pl.ds(pl.multiple_of(i * tm, tm), tm)
        h_ref[rows, :] = (x_ref[rows, :].astype(F32) + dot(o_ref[rows, :], w_ref[...])).astype(BF)


def wo_proj(o, w, x):
    t, n = o.shape
    d = w.shape[1]
    tn = min(512, d)
    return pl.pallas_call(
        wo_kernel,
        grid=(d // tn,),
        in_specs=[pl.BlockSpec((t, n), lambda i: (0, 0)), pl.BlockSpec((n, tn), lambda i: (0, i)),
                  pl.BlockSpec((t, tn), lambda i: (0, i))],
        out_specs=pl.BlockSpec((t, tn), lambda i: (0, i)),
        out_shape=jax.ShapeDtypeStruct((t, d), BF),
        compiler_params=params(),
        cost_estimate=pl.CostEstimate(flops=2 * t * d * n, bytes_accessed=2 * (t * n + d * n + 2 * t * d), transcendentals=0),
    )(o, w, x)


def fetch_expert(l, slot, own, other, bufs, sem):
    ne = own[0].shape[0]

    @pl.when(l < ne)
    def _():
        for src, dst in zip(own, bufs):
            pltpu.make_async_copy(src.at[l], dst.at[slot], sem.at[slot]).start()

    @pl.when(l >= ne)
    def _():
        for src, dst in zip(other, bufs):
            pltpu.make_async_copy(src.at[l - ne], dst.at[slot], sem.at[slot]).start()


def wait_expert(slot, own, bufs, sem):
    for src, dst in zip(own, bufs):
        pltpu.make_async_copy(src.at[0], dst.at[slot], sem.at[slot]).wait()


def ffn(x, w1, w3, w2):
    a1 = dot(x, w1)
    a3 = dot(x, w3)
    act = (jax.nn.silu(a1) * a3).astype(BF)
    return dot(act, w2).astype(BF)


def block_kernel(js, has_acc, comb, dense, *refs):
    refs = list(refs)
    nblk = len(js)
    take = lambda n: [refs.pop(0) for _ in range(n)]
    if dense:
        n_ref, ent_ref = take(2)
    gt_ref, = take(1)
    if comb:
        nch_ref, eg_ref, pos_ref, z_ref = take(4)
        cap = z_ref.shape[0] // pos_ref.shape[0]
    if dense:
        us = take(nblk)
        own, other = take(3), take(3)
        nl = 2 * own[0].shape[0]
    accs = [take(1)[0] if h else None for h in has_acc]
    outs = take(nblk)
    acc, asem = take(2)
    if comb:
        cbuf, zbuf, zsem = take(3)
    if dense:
        bufs, (ubuf, sem, usem) = take(3), take(3)
    t, d = outs[0].shape

    if dense:
        n = n_ref[0]

        @pl.when(n > 0)
        def _():
            fetch_expert(lax.rem(ent_ref[0], nl), 0, own, other, bufs, sem)

        ucp = [pltpu.make_async_copy(us[p], ubuf.at[pl.ds(p * t, t), :], usem) for p in range(nblk)]
        for cp in ucp:
            cp.start()
    for p in range(nblk):
        rows = pl.ds(p * t, t)
        if has_acc[p]:
            pltpu.make_async_copy(accs[p], acc.at[rows, :], asem.at[p]).start()
        else:
            acc[rows, :] = jnp.zeros((t, d), F32)
    for p in range(nblk):
        if has_acc[p]:
            pltpu.make_async_copy(accs[p], acc.at[pl.ds(p * t, t), :], asem.at[p]).wait()

    if comb:
        for p, j in enumerate(js):
            nch = nch_ref[j]

            def get(i, slot):
                src = pl.multiple_of(j * cap + i * CHUNK, CHUNK)
                return pltpu.make_async_copy(z_ref.at[pl.ds(src, CHUNK), :], zbuf.at[slot], zsem.at[slot])

            get(0, 0).start()

            @pl.loop(0, nch)
            def _(i):
                slot = lax.rem(i, 2)

                @pl.when(i + 1 < nch)
                def _():
                    get(i + 1, 1 - slot).start()

                for q, (hit, l) in enumerate(selection(j, i, eg_ref, pos_ref)):
                    for k, g in enumerate(split3(gt_ref[j, pl.ds(l, 1), :])):
                        cbuf[pl.ds(k * CHUNK + q * PIECE, PIECE), :] = jnp.where(hit, g.astype(F32), 0.0).astype(BF)
                get(i, slot).wait()
                tn = min(1024, d)

                @pl.loop(0, d // tn)
                def _(m):
                    cs = pl.ds(pl.multiple_of(m * tn, tn), tn)
                    z = zbuf[slot, :, cs]
                    acc[p * t:(p + 1) * t, cs] += lax.dot_general(
                        cbuf[...], jnp.concatenate([z, z, z], axis=0), (((0,), (0,)), ((), ())), preferred_element_type=F32)

    if dense:
        for cp in ucp:
            cp.wait()
        tm = min(HM, t)

        @pl.loop(0, n)
        def _(i):
            slot = lax.rem(i, 2)
            wait_expert(slot, own, bufs, sem)

            @pl.when(i + 1 < n)
            def _():
                fetch_expert(lax.rem(ent_ref[i + 1], nl), 1 - slot, own, other, bufs, sem)

            e = lax.rem(ent_ref[i], nl)
            p = lax.div(ent_ref[i], nl)
            blk = jnp.where(p == 0, js[0], js[-1])

            @pl.loop(0, t // tm)
            def _(m):
                rows = pl.ds(pl.multiple_of(p * t + m * tm, tm), tm)
                z = ffn(ubuf[rows, :], bufs[0][slot], bufs[1][slot], bufs[2][slot])
                g = gt_ref[blk, pl.ds(e, 1), pl.ds(pl.multiple_of(m * tm, tm), tm)]
                eye = lax.broadcasted_iota(I32, (tm, tm), 0) == lax.broadcasted_iota(I32, (tm, tm), 1)
                gc = jnp.sum(jnp.where(eye, g, 0.0), axis=1, keepdims=True)
                acc[rows, :] += gc * z.astype(F32)

    for p in range(nblk):
        outs[p][...] = acc[p * t:(p + 1) * t, :].astype(outs[p].dtype)


def block(js, r, z, us, accs, own, other, dtype, comb=True, ents=None):
    nblk = len(js)
    t = r.pos.shape[2]
    d = own[0].shape[1]
    ff = own[0].shape[2]
    dense = ents is not None
    vm = pl.BlockSpec(memory_space=pltpu.VMEM)
    sm = pl.BlockSpec(memory_space=pltpu.SMEM)
    hb = pl.BlockSpec(memory_space=pl.ANY)
    args, specs, scratch = [], [], []
    if dense:
        args += list(ents)
        specs += [sm, sm]
    args += [r.gt]
    specs += [vm]
    if comb:
        args += [r.nch, r.eg.reshape(-1), r.pos, z]
        specs += [sm, sm, vm, hb]
    if dense:
        args += list(us) + list(own) + list(other)
        specs += [hb] * (nblk + 6)
    args += [v for v in accs if v is not None]
    specs += [hb for v in accs if v is not None]
    scratch += [pltpu.VMEM((nblk * t, d), F32), pltpu.SemaphoreType.DMA((nblk,))]
    if comb:
        scratch += [pltpu.VMEM((3 * CHUNK, t), BF), pltpu.VMEM((2, CHUNK, d), BF), pltpu.SemaphoreType.DMA((2,))]
    if dense:
        scratch += [pltpu.VMEM((2, d, ff), BF), pltpu.VMEM((2, d, ff), BF), pltpu.VMEM((2, ff, d), BF),
                    pltpu.VMEM((nblk * t, d), BF), pltpu.SemaphoreType.DMA((2,)), pltpu.SemaphoreType.DMA]
    out = jax.ShapeDtypeStruct((t, d), dtype)
    return pl.pallas_call(
        functools.partial(block_kernel, js, [v is not None for v in accs], comb, dense),
        in_specs=specs, out_specs=[vm] * nblk, out_shape=[out] * nblk, scratch_shapes=scratch,
        compiler_params=params(),
        cost_estimate=pl.CostEstimate(flops=t * d, bytes_accessed=6 * d * ff, transcendentals=0),
    )(*args)


def split3(g):
    hi = g.astype(BF)
    r = g - hi.astype(F32)
    mid = r.astype(BF)
    lo = (r - mid.astype(F32)).astype(BF)
    return hi, mid, lo


def selection(j, i, eg_ref, pos_ref):
    t = pos_ref.shape[2]
    it = lax.broadcasted_iota(I32, (PIECE, t), 0)
    npc = CHUNK // PIECE
    npb = eg_ref.shape[0] // pos_ref.shape[0]
    for q in range(npc):
        l = eg_ref[j * npb + i * npc + q]
        yield pos_ref[j, pl.ds(l, 1), :] - (i * CHUNK + q * PIECE) == it, l


def gather_kernel(js, nch_ref, eg_ref, pos_ref, *refs):
    us = refs[:len(js)]
    x_ref, xbuf, sem = refs[-3:]
    cap = x_ref.shape[0] // pos_ref.shape[0]
    for p, j in enumerate(js):
        nch = nch_ref[j]

        def out(i, slot):
            dst = pl.multiple_of(j * cap + i * CHUNK, CHUNK)
            return pltpu.make_async_copy(xbuf.at[slot], x_ref.at[pl.ds(dst, CHUNK), :], sem.at[slot])

        @pl.loop(0, nch)
        def _(i):
            slot = lax.rem(i, 2)

            @pl.when(i >= 2)
            def _():
                out(i - 2, slot).wait()

            pm = jnp.concatenate([jnp.where(hit, 1.0, 0.0).astype(BF) for hit, _ in selection(j, i, eg_ref, pos_ref)], axis=0)
            xbuf[slot] = dot(pm, us[p][...]).astype(BF)
            out(i, slot).start()

        for k in (2, 1):
            @pl.when(nch >= k)
            def _():
                out(nch - k, lax.rem(nch - k, 2)).wait()


def gather(js, r, us, x):
    nblk = len(js)
    t, d = us[0].shape
    nb = r.eg.shape[0]
    cap = r.eg.shape[1] * PIECE
    vm = pl.BlockSpec(memory_space=pltpu.VMEM)
    sm = pl.BlockSpec(memory_space=pltpu.SMEM)
    hb = pl.BlockSpec(memory_space=pl.ANY)
    return pl.pallas_call(
        functools.partial(gather_kernel, js),
        in_specs=[sm, sm, vm] + [vm] * nblk + ([hb] if x is not None else []),
        out_specs=hb,
        out_shape=jax.ShapeDtypeStruct((nb * cap, d), BF),
        input_output_aliases={3 + nblk: 0} if x is not None else {},
        scratch_shapes=[pltpu.VMEM((2, CHUNK, d), BF), pltpu.SemaphoreType.DMA((2,))],
        compiler_params=params(),
        cost_estimate=pl.CostEstimate(flops=t * d, bytes_accessed=4 * CHUNK * d, transcendentals=0),
    )(r.nch, r.eg.reshape(-1), r.pos, *us, *([x] if x is not None else []))


def cold_kernel(nt_ref, tl_ref, tp_ref, tn_ref, tw_ref, tf_ref, nx_ref, pc_ref, x_ref, *refs):
    own, other, z_ref, refs = refs[:3], refs[3:6], refs[6], refs[7:]
    bufs, (xbuf, zbuf, wsem, xsem, zsem) = refs[:3], refs[3:]
    nt = nt_ref[0]

    def xin(q, slot):
        p0 = tp_ref[q]

        @pl.loop(0, tn_ref[q])
        def _(i):
            src = pl.ds(pl.multiple_of(pc_ref[p0 + i] * PIECE, PIECE), PIECE)
            dst = pl.ds(pl.multiple_of(i * PIECE, PIECE), PIECE)
            pltpu.make_async_copy(x_ref.at[src, :], xbuf.at[slot, dst, :], xsem.at[slot]).start()

    def zout(q, slot):
        p0 = tp_ref[q]

        @pl.loop(0, tn_ref[q])
        def _(i):
            src = pl.ds(pl.multiple_of(i * PIECE, PIECE), PIECE)
            dst = pl.ds(pl.multiple_of(pc_ref[p0 + i] * PIECE, PIECE), PIECE)
            pltpu.make_async_copy(zbuf.at[slot, src, :], z_ref.at[dst, :], zsem.at[slot]).start()

    def xwait(q, slot):
        @pl.loop(0, tn_ref[q])
        def _(i):
            pltpu.make_async_copy(x_ref.at[pl.ds(0, PIECE), :], xbuf.at[slot, pl.ds(0, PIECE), :], xsem.at[slot]).wait()

    def zwait(q, slot):
        @pl.loop(0, tn_ref[q])
        def _(i):
            pltpu.make_async_copy(zbuf.at[slot, pl.ds(0, PIECE), :], z_ref.at[pl.ds(0, PIECE), :], zsem.at[slot]).wait()

    @pl.when(nt > 0)
    def _():
        fetch_expert(tl_ref[0], 0, own, other, bufs, wsem)
        xin(0, 0)

    @pl.loop(0, nt)
    def _(q):
        slot = lax.rem(q, 2)
        ws = lax.rem(tw_ref[q], 2)

        @pl.when(tf_ref[q] == 1)
        def _():
            wait_expert(ws, own, bufs, wsem)

            @pl.when(nx_ref[q] >= 0)
            def _():
                fetch_expert(nx_ref[q], 1 - ws, own, other, bufs, wsem)

        @pl.when(q + 1 < nt)
        def _():
            xin(q + 1, 1 - slot)

        xwait(q, slot)

        @pl.when(q >= 2)
        def _():
            zwait(q - 2, slot)

        zbuf[slot] = ffn(xbuf[slot], bufs[0][ws], bufs[1][ws], bufs[2][ws])
        zout(q, slot)

    for k in (2, 1):
        @pl.when(nt >= k)
        def _():
            zwait(nt - k, lax.rem(nt - k, 2))


def cold(plan, x, own, other):
    d, ff = own[0].shape[1:]
    sm = pl.BlockSpec(memory_space=pltpu.SMEM)
    hb = pl.BlockSpec(memory_space=pl.ANY)
    return pl.pallas_call(
        cold_kernel,
        in_specs=[sm] * len(plan) + [hb] * 7,
        out_specs=hb,
        out_shape=jax.ShapeDtypeStruct(x.shape, BF),
        scratch_shapes=[pltpu.VMEM((2, d, ff), BF), pltpu.VMEM((2, d, ff), BF), pltpu.VMEM((2, ff, d), BF),
                        pltpu.VMEM((2, MT, d), BF), pltpu.VMEM((2, MT, d), BF),
                        pltpu.SemaphoreType.DMA((2,)), pltpu.SemaphoreType.DMA((2,)), pltpu.SemaphoreType.DMA((2,))],
        input_output_aliases={len(plan): 0},
        compiler_params=params(),
        cost_estimate=pl.CostEstimate(flops=6 * 16 * MT * d * ff, bytes_accessed=96 * d * ff, transcendentals=0),
    )(*plan, x, *own, *other)


def final_kernel(h_ref, *refs):
    y_ref = refs[-1]
    acc, parts = refs[0], refs[1:-1]
    y = h_ref[...].astype(F32) + acc[...]
    for v in parts:
        y = y + v[...].astype(F32)
    y_ref[...] = y.astype(BF)


def final(h, accs, parts):
    t, d = h.shape
    half = t // 2
    tm = min(128, half)
    n = half // tm

    def body(h_ref, *refs):
        for p in range(2):
            @pl.when(pl.program_id(0) // n == p)
            def _():
                final_kernel(h_ref, refs[p], *refs[2 + p:-1:2], refs[-1])

    spec = lambda p: pl.BlockSpec((tm, d), lambda i: (jnp.minimum(i, n - 1) if p == 0 else jnp.maximum(i - n, 0), 0))
    return pl.pallas_call(
        body, grid=(2 * n,),
        in_specs=[pl.BlockSpec((tm, d), lambda i: (i, 0))] + [spec(0), spec(1)] * (1 + len(parts)),
        out_specs=pl.BlockSpec((tm, d), lambda i: (i, 0)),
        out_shape=jax.ShapeDtypeStruct((t, d), BF),
        compiler_params=params(),
        cost_estimate=pl.CostEstimate(flops=6 * t * d, bytes_accessed=20 * t * d, transcendentals=0),
    )(h, *accs, *[v for part in parts for v in part])


def entries(nh, hl):
    nblk, nl = hl.shape
    end = jnp.cumsum(nh)
    i = jnp.arange(nblk * nl, dtype=I32)
    p = jnp.minimum(jnp.sum((end[None, :] <= i[:, None]).astype(I32), axis=1), nblk - 1)
    mine = p[:, None] == jnp.arange(nblk)
    k = i - jnp.sum(jnp.where(mine, (end - nh)[None, :], 0), axis=1)
    row = jnp.sum(jnp.where(mine[..., None], hl[None], 0), axis=1)
    e = jnp.sum(jnp.where(jnp.arange(nl)[None, :] == k[:, None], row, 0), axis=1)
    return end[-1:].astype(I32), (p * nl + e).astype(I32)


class Routing(typing.NamedTuple):
    nh: typing.Any
    hl: typing.Any
    nch: typing.Any
    eg: typing.Any
    pos: typing.Any
    gt: typing.Any


def routing_plan(lid, local, nl):
    nb, t, k = lid.shape
    le = jnp.arange(nl, dtype=I32)
    hit = jnp.any((lid[:, None] == le[:, None, None]) & local[:, None], axis=-1)
    tri = (jnp.arange(t)[:, None] <= jnp.arange(t)[None, :]).astype(BF)
    rank = lax.dot_general(hit.astype(BF), tri, (((2,), (0,)), ((), ())), preferred_element_type=F32).astype(I32)
    cnt = rank[:, :, -1]
    hotm = cnt >= t // 2
    scnt = jnp.where(hotm, 0, cnt)
    pcs = (scnt + PIECE - 1) // PIECE
    pend = jnp.cumsum(pcs, axis=1)
    base = (pend - pcs) * PIECE
    pos = jnp.where(hit & ~hotm[..., None], base[..., None] + rank - 1, -1)
    rows = t * k + nl * PIECE
    npb = -(-rows // CHUNK) * CHUNK // PIECE
    nch = jnp.maximum(-(-pend[:, -1] * PIECE // CHUNK), 1)
    below = lambda ends, q: jnp.sum((ends <= q).astype(I32), axis=-1)
    eg = jnp.minimum(below(pend[:, None, :], jnp.arange(npb, dtype=I32)[None, :, None]), nl - 1)
    flat = pcs.T.reshape(-1)
    fend = jnp.cumsum(flat)
    p = jnp.arange(nb * npb, dtype=I32)[:, None]
    seg = jnp.minimum(below(fend[None, :], p), nl * nb - 1)
    inseg = seg[:, None] == jnp.arange(nl * nb, dtype=I32)
    shift_ = jnp.tile(jnp.arange(nb, dtype=I32) * npb, nl) + (pend - pcs).T.reshape(-1) - (fend - flat)
    pc = jnp.clip(p[:, 0] + jnp.sum(jnp.where(inseg, shift_, 0), axis=1), 0, nb * npb - 1)
    ppt = MT // PIECE
    ptot = jnp.sum(pcs, axis=0)
    pstart = jnp.cumsum(ptot) - ptot
    tiles = (ptot + ppt - 1) // ppt
    tend = jnp.cumsum(tiles)
    nq = -(-(nb * npb) // ppt) + nl
    q = jnp.arange(nq, dtype=I32)
    tl = jnp.minimum(below(tend[None, :], q[:, None]), nl - 1)
    one = tl[:, None] == le
    pick = lambda v: jnp.sum(jnp.where(one, v[None, :], 0), axis=1)
    ti = q - pick(tend - tiles)
    tp = pick(pstart) + ti * ppt
    tn = jnp.clip(pick(ptot) - ti * ppt, 0, ppt)
    active = (tiles > 0).astype(I32)
    tw = pick(jnp.cumsum(active) - active)
    tf = (ti == 0).astype(I32)
    later = (le[None, :] > tl[:, None]) & (active[None, :] > 0)
    nxt = jnp.min(jnp.where(later, le[None, :], nl), axis=1)
    nxt = jnp.where(nxt < nl, nxt, -1)
    plan = tuple(v.astype(I32) for v in (tend[-1:], tl, tp, tn, tw, tf, nxt, pc))
    hend = jnp.cumsum(hotm.astype(I32), axis=1)
    hl = jnp.minimum(below(hend[:, None, :], le[None, :, None]), nl - 1)
    return Routing(hend[:, -1], hl, nch, eg, pos, None), plan


def solution(mesh):
    nd = mesh.shape['ep']
    nx = nd // 2
    tok_spec = P(('replica', 'ep'), None, None)
    rows_ep = P('ep', None)
    by_expert = P('ep', None, None)

    def shift(v, s):
        return lax.ppermute(v, 'ep', [(2 * i + c, 2 * ((i + s) % nx) + c) for i in range(nx) for c in range(2)])

    def partner(v):
        return lax.ppermute(v, 'ep', [(i, i ^ 1) for i in range(nd)])

    def local(x, wq, wk, wv, wo, wr, w1, w3, w2, idx):
        b, s, d = x.shape
        t, k, ne = b * s, idx.shape[-1], w1.shape[0]
        nl = 2 * ne
        half = t // 2
        me = lax.axis_index('ep')
        x = x.reshape(t, d)
        ids = idx.reshape(t, k)

        wq, wk, wv, wo = [lax.all_gather(w, 'ep', axis=0, tiled=True) for w in (wq, wk, wv, wo)]
        own = (w1, w3, w2)
        other = tuple(partner(w) for w in own)

        halves = lambda v: v.reshape(2 * v.shape[0], half, *v.shape[2:])
        ids4 = jnp.stack([ids, shift(ids, 1), shift(ids, -1), shift(ids, 2)])
        is_local = halves(ids4 // nl == me // 2)
        lid = halves((ids4 - me * ne) % nl)
        r, plan = routing_plan(lid, is_local, nl)
        ohl = (lid[:, None] == jnp.arange(nl, dtype=I32)[:, None, None]) & is_local[:, None]
        A, R, L, O = (0, 1), (2, 3), (4, 5), (6, 7)
        solo = lambda j: entries(r.nh[j:j + 1], r.hl[j:j + 1])
        ents = {j: solo(j) for j in (0, 2, 3, 4, 5)}
        ents[1] = entries(jnp.where(jnp.arange(2) == 1, r.nh[:2], 0), r.hl[:2])
        ents[6] = entries(r.nh[6:8], r.hl[6:8])
        ra = Routing(None, None, None, None, r.pos[:2], None)

        hd = HEAD // 2
        freq = THETA ** (-jnp.arange(hd, dtype=F32) / hd)
        ang = (jnp.arange(t) % s).astype(F32)[:, None] * freq
        c, sn = jnp.cos(ang), jnp.sin(ang)
        cos, sin = jnp.concatenate([c, c], axis=1), jnp.concatenate([-sn, sn], axis=1)
        a = rmsnorm(x).astype(BF)
        a, cos, sin, r, plan, ents, ids4 = lax.optimization_barrier((a, cos, sin, r._replace(gt=ohl), plan, ents, ids4))
        ohl = r.gt
        q = proj(a, wq, cos, sin, True)
        kk = proj(a, wk, cos, sin, True)
        v = proj(a, wv, cos, sin, False)
        o = attn(q, kk, v)
        h = wo_proj(o, wo, x)

        rn = rmsnorm(h)
        logits = jnp.dot(rn, wr, precision=lax.Precision.HIGHEST, preferred_element_type=F32)
        oh = ids[..., None] == jnp.arange(wr.shape[1], dtype=I32)
        g = jax.nn.softmax(jnp.sum(jnp.where(oh, logits[:, None, :], 0.0), axis=-1), axis=-1)
        u = rn.astype(BF)

        ut, ub = u[:half], u[half:]
        u1t, u2b = shift(ut, 1), shift(ub, -1)
        ut2, ub2, g = lax.optimization_barrier((ut, ub, g))
        g4 = [g, shift(g, 1), shift(g, -1), shift(g, 2)]
        u1b, u2t = shift(ub2, 1), shift(ut2, -1)
        spread = lambda o, v: jnp.sum(jnp.where(o, halves(v)[:, None], 0.0), axis=3)
        ra = ra._replace(gt=spread(ohl[:2], g[None]))
        r = r._replace(gt=spread(ohl, jnp.stack(g4)))

        x = gather(A, r, (ut, ub), None)
        a0, = block((0,), ra, None, (ut,), (None,), own, other, F32, comb=False, ents=ents[0])
        a0, x, u1t, u2b = lax.optimization_barrier((a0, x, u1t, u2b))
        u3t, u3b = shift(u1t, 1), shift(u2b, -1)
        d2, = block((2,), r, None, (u1t,), (None,), own, other, F32, comb=False, ents=ents[2])
        u1b, d2 = lax.optimization_barrier((u1b, d2))
        x = gather(R, r, (u1t, u1b), x)
        x = gather(L, r, (u2t, u2b), x)
        u2bx, x = lax.optimization_barrier((u2b, x))
        d5, = block((5,), r, None, (u2bx,), (None,), own, other, F32, comb=False, ents=ents[5])
        u3t, d5 = lax.optimization_barrier((u3t, d5))
        x = gather(O, r, (u3t, u3b), x)
        z = cold(plan, x, own, other)

        tie = lambda r, *v: (lambda w: (r._replace(nch=w[0]), *w[1:]))(lax.optimization_barrier((r.nch, *v)))
        b6, b7 = block(O, r, z, (u3t, u3b), (None, None), own, other, BF, ents=ents[6])
        r, b6, b7 = tie(r, b6, b7)
        c6, c7 = shift(b6, 1), shift(b7, -1)
        b2, b5 = block((2, 5), r, z, (), (d2, d5), own, other, BF)
        r, b2, b5 = tie(r, b2, b5)
        b2, b5 = shift(b2, -1), shift(b5, 1)
        b3, = block((3,), r, z, (u1b,), (None,), own, other, BF, ents=ents[3])
        r, b3, c6, c7 = tie(r, b3, c6, c7)
        b6, b7 = shift(c6, 1), shift(c7, -1)
        b3 = shift(b3, -1)
        b4, = block((4,), r, z, (u2t,), (None,), own, other, BF, ents=ents[4])
        r, b4 = tie(r, b4)
        b4 = shift(b4, 1)
        accs = block(A, r, z, (ut, ub), (a0, None), own, other, F32, ents=ents[1])
        y = final(h, accs, [(b2, b3), (b4, b5), (b6, b7)])
        return y.reshape(b, s, d)

    return jax.shard_map(local, mesh=mesh,
                         in_specs=(tok_spec, rows_ep, rows_ep, rows_ep, rows_ep, P(None, None),
                                   by_expert, by_expert, by_expert, tok_spec),
                         out_specs=tok_spec, check_vma=False)
```

time: 915 us -> 861 us (0.941)
  the two profiles are of different devices: /device:TPU:113 before, /device:TPU:81 now
where the time goes in v2:
time: 861 us; the launch traced here: 853 us
  Pallas kernels  355 us (41%)
  waiting for transfers between devices  257 us (30%)
  starting transfers between devices  173 us (20%)
  other arithmetic  36.8 us (4%)
  between operations  14.2 us (2%)
  matrix products  10.5 us (1%)
    ppermute x20, waiting for transfers between devices, shift(): lax.ppermute(v, 'ep', [(2 * i + c, 2 * ((i + s) % nx) + c) for i in range...  180 us
    ppermute x20, starting transfers between devices, shift(): lax.ppermute(v, 'ep', [(2 * i + c, 2 * ((i + s) % nx) + c) for i in range...  170 us
    pallas_call x8, Pallas kernels, block(): pl.pallas_call(functools.partial(block_kernel, js, [v is not None for v i...  106 us
    pallas_call x1, Pallas kernels, cold(): pl.pallas_call(cold_kernel, in_specs=[sm] * len(plan) + [hb] * 7, out_spe...  103 us
    all_gather x4, waiting for transfers between devices, local(): lax.all_gather(w, 'ep', axis=0, tiled=True)  75.1 us
    pallas_call x3, Pallas kernels, proj(): pl.pallas_call(functools.partial(proj_kernel, rope), grid=(n // tn,), in_...  46 us
    pallas_call x4, Pallas kernels, gather(): pl.pallas_call(functools.partial(gather_kernel, js), in_specs=[sm, sm, vm...  36.6 us
    pallas_call x1, Pallas kernels, attn(): pl.pallas_call(functools.partial(attn_kernel, min(256, t)), grid=(n // tn...  35.7 us
  transfers between devices with their start and end apart: 27, of which 15 were waited for; matrix products, arithmetic and copies ran while one was open for 6% of the time, Pallas kernels for 25%

profile of v2, /device:TPU:81, one launch (start us, length us, event | category | flops | bytes accessed | tf_op | source)
XLA Modules:
  0.0 853.2 jit_solution(13536790273624451166)
XLA Ops:
  6.6 0.7 all-gather.9.cloned.1.call-update
  9.0 2.1 collective-permute-start.6
  11.6 0.8 collective-permute-start
  12.4 1.9 collective-permute-start.1
  14.4 3.2 fusion.2
  17.6 1.9 fusion.9
  19.6 2.9 fusion.3.a_ref
  22.4 1.3 pad_maximum_fusion
  23.8 1.1 collective-permute-start.2
  24.9 4.3 collective-permute-done.2
  29.4 1.2 fusion.6
  43.7 1.1 multiply_add_fusion.1.refs_1_
  44.8 1.1 multiply_add_fusion.2.refs_1_
  46.0 1.3 multiply_add_fusion.3.refs_1_
  47.2 1.1 multiply_add_fusion.4.refs_1_
  48.3 1.1 multiply_add_fusion.6.refs_1_
  52.2 0.8 add_select_fusion.pos_ref.refs_5_.refs_3_
  53.0 8.2 all-gather.9.cloned.1.call-done.w_ref
  61.2 14.4 %shard_map.102.v_ref = bf16[1024,2048]{1,0:T(8,128)(2,1)} custom-call(bf16[1024,2048]{1,0:T(8,128)(2,1)} %fusion.3.a_ref, bf16[2048,2048]{1,0:T(8,128)(2,1)} %all-gather.9.cloned.1.call-done.w_ref, f32[1024,128]{1,0:T(8,128)} %get-tuple-element.66.c_ref, f32[1024,128]{1,0:T(8,128)} %get-tuple-element.67.s_ref), custom_call_target="tpu_custom_call" | custom-call | flops 8589934592 | bytes 16777216 | tf_op jit(solution)/shard_map/pallas_call | solution.py:54
  75.6 34.2 %all-gather.7.cloned.1.call-done.w_ref = bf16[2048,2048]{1,0:T(8,128)(2,1)} async-done(((bf16[256,2048]{1,0:T(8,128)(2,1)}), bf16[2048,2048]{1,0:T(8,128)(2,1)}) %all-gather.7.cloned.1.call-update) | async-done | bytes 8388624 | tf_op jit(solution)/shard_map/all_gather | solution.py:581
  109.8 15.8 %shard_map.101.k_ref = bf16[1024,2048]{1,0:T(8,128)(2,1)} custom-call(bf16[1024,2048]{1,0:T(8,128)(2,1)} %fusion.3.a_ref, bf16[2048,2048]{1,0:T(8,128)(2,1)} %all-gather.7.cloned.1.call-done.w_ref, f32[1024,128]{1,0:T(8,128)} %get-tuple-element.66.c_ref, f32[1024,128]{1,0:T(8,128)} %get-tuple-element.67.s_ref), custom_call_target="tpu_custom_call" | custom-call | flops 8589934592 | bytes 16777216 | tf_op jit(solution)/shard_map/pallas_call | solution.py:54
  125.6 32.7 %all-gather.5.cloned.1.call-done.w_ref = bf16[2048,2048]{1,0:T(8,128)(2,1)} async-done(((bf16[256,2048]{1,0:T(8,128)(2,1)}), bf16[2048,2048]{1,0:T(8,128)(2,1)}) %all-gather.5.cloned.1.call-update) | async-done | bytes 8388624 | tf_op jit(solution)/shard_map/all_gather | solution.py:581
  158.3 15.8 %shard_map.100.q_ref = bf16[1024,2048]{1,0:T(8,128)(2,1)} custom-call(bf16[1024,2048]{1,0:T(8,128)(2,1)} %fusion.3.a_ref, bf16[2048,2048]{1,0:T(8,128)(2,1)} %all-gather.5.cloned.1.call-done.w_ref, f32[1024,128]{1,0:T(8,128)} %get-tuple-element.66.c_ref, f32[1024,128]{1,0:T(8,128)} %get-tuple-element.67.s_ref), custom_call_target="tpu_custom_call" | custom-call | flops 8589934592 | bytes 16777216 | tf_op jit(solution)/shard_map/pallas_call | solution.py:54
  174.1 35.7 %shard_map.103.o_ref = bf16[1024,2048]{1,0:T(8,128)(2,1)} custom-call(bf16[1024,2048]{1,0:T(8,128)(2,1)} %shard_map.100.q_ref, bf16[1024,2048]{1,0:T(8,128)(2,1)} %shard_map.101.k_ref, bf16[1024,2048]{1,0:T(8,128)(2,1)} %shard_map.102.v_ref), custom_call_target="tpu_custom_call" | custom-call | flops 8589934592 | bytes 16777216 | tf_op jit(solution)/shard_map/pallas_call | solution.py:98
  209.8 14.3 %shard_map.104.h_ref = bf16[1024,2048]{1,0:T(8,128)(2,1)} custom-call(bf16[1024,2048]{1,0:T(8,128)(2,1)} %shard_map.103.o_ref, bf16[2048,2048]{1,0:T(8,128)(2,1)} %all-gather.11.cloned.1.call-done.w_ref, bf16[1024,2048]{1,0:T(8,128)(2,1)} %bitcast.51), custom_call_target="tpu_custom_call" | custom-call | flops 8589934592 | bytes 20971520 | tf_op jit(solution)/shard_map/pallas_call | solution.py:120
  224.1 3.2 fusion.4
  228.3 2.5 fusion.51
  231.4 0.9 collective-permute-start.9
  233.0 10.3 %fusion = f32[1024,64]{0,1:T(8,128)S(1)} fusion(f32[2048,64]{0,1:T(8,128)S(1)} %copy-done, bf16[1024,2048]{1,0:T(8,128)(2,1)} %shard_map.104.h_ref, f32[1024]{0:T(1024)S(1)} %add_rsqrt_fusion), kind=kOutput, calls=%fused_computation.4 | convolution fusion | flops 1614807040 | bytes 4984832 | tf_op jit(solution)/shard_map/dot_general | solution.py:613
  243.6 1.7 select_reduce_fusion.3.refs_2_
  245.5 9.2 %shard_map.106.refs_2_ = bf16[34816,2048]{1,0:T(8,128)(2,1)} custom-call(s32[8]{0:T(128)} %negate_maximum_fusion.nch_ref.refs_3_.refs_1_, s32[2176]{0:T(1024)} %reshape.691.eg_ref.refs_4_.refs_2_, s32[8,16,512]{2,1,0:T(8,128)} %add_select_fusion.pos_ref.refs_5_.refs_3_, bf16[512,2048]{1,0:T(8,128)(2,1)} %get-tuple-element.91.refs_3_.refs_0_.refs_7_, ...), custom_call_target="tpu_custom_call" | custom-call | flops 1048576 | bytes 2097152 | tf_op jit(solution)/shard_map/pallas_call | solution.py:356
  254.7 2.6 collective-permute-start.12
  257.3 5.4 shard_map.105.refs_15_
  262.7 15.3 %collective-permute-done.10.refs_1_.refs_3_ = bf16[512,2048]{1,0:T(8,128)(2,1)} collective-permute-done((bf16[512,2048]{1,0:T(8,128)(2,1)}, bf16[512,2048]{1,0:T(8,128)(2,1)}, u32[]{:S(2)}, u32[]{:S(2)}) %collective-permute-start.10) | collective-permute-done | bytes 2097184 | tf_op jit(solution)/shard_map/ppermute | solution.py:567
  278.0 1.5 collective-permute-done.9.refs_3_.refs_0_
  279.5 13.5 %collective-permute-start.11 = (bf16[512,2048]{1,0:T(8,128)(2,1)}, bf16[512,2048]{1,0:T(8,128)(2,1)}, u32[]{:S(2)}, u32[]{:S(2)}) collective-permute-start(bf16[512,2048]{1,0:T(8,128)(2,1)} %collective-permute-done.9.refs_3_.refs_0_), channel_id=1, source_target_pairs={{0,2},{1,3},{2,4},{3,5},{4,6},{5,7},{6,0},{7,1},{8,10},{9,11},{10,... | collective-permute-start | bytes 6291464 | tf_op jit(solution)/shard_map/ppermute | solution.py:567
  293.0 1.5 collective-permute-start.3
  294.5 75.6 %collective-permute-done.3 = f32[1024,8]{0,1:T(8,128)S(1)} collective-permute-done((f32[1024,8]{0,1:T(8,128)S(1)}, f32[1024,8]{0,1:T(8,128)S(1)}, u32[]{:S(2)}, u32[]{:S(2)}) %collective-permute-start.3) | collective-permute-done | bytes 32800 | tf_op jit(solution)/shard_map/ppermute | solution.py:567
  370.1 2.7 collective-permute-done.4
  373.1 4.0 collective-permute-done.5
  377.2 1.4 select_reduce_fusion.refs_2_.refs_0_
  378.6 5.5 shard_map.107.refs_5_
  384.1 9.1 %shard_map.108.refs_2_ = bf16[34816,2048]{1,0:T(8,128)(2,1)} custom-call(s32[8]{0:T(128)} %negate_maximum_fusion.nch_ref.refs_3_.refs_1_, s32[2176]{0:T(1024)} %reshape.691.eg_ref.refs_4_.refs_2_, s32[8,16,512]{2,1,0:T(8,128)} %add_select_fusion.pos_ref.refs_5_.refs_3_, ...), custom_call_target="tpu_custom_call", output_to_operand_aliasing={{}: (5, {})} | custom-call | flops 1048576 | bytes 2097152 | tf_op jit(solution)/shard_map/pallas_call | solution.py:356
  393.2 9.2 %shard_map.109.refs_2_ = bf16[34816,2048]{1,0:T(8,128)(2,1)} custom-call(s32[8]{0:T(128)} %negate_maximum_fusion.nch_ref.refs_3_.refs_1_, s32[2176]{0:T(1024)} %reshape.691.eg_ref.refs_4_.refs_2_, s32[8,16,512]{2,1,0:T(8,128)} %add_select_fusion.pos_ref.refs_5_.refs_3_, ...), custom_call_target="tpu_custom_call", output_to_operand_aliasing={{}: (5, {})} | custom-call | flops 1048576 | bytes 2097152 | tf_op jit(solution)/shard_map/pallas_call | solution.py:356
  402.4 5.4 shard_map.110.refs_6_
  407.8 9.2 %shard_map.111.x_ref = bf16[34816,2048]{1,0:T(8,128)(2,1)} custom-call(s32[8]{0:T(128)} %negate_maximum_fusion.nch_ref.refs_3_.refs_1_, s32[2176]{0:T(1024)} %reshape.691.eg_ref.refs_4_.refs_2_, s32[8,16,512]{2,1,0:T(8,128)} %add_select_fusion.pos_ref.refs_5_.refs_3_, ...), custom_call_target="tpu_custom_call", output_to_operand_aliasing={{}: (5, {})} | custom-call | flops 1048576 | bytes 2097152 | tf_op jit(solution)/shard_map/pallas_call | solution.py:356
  417.0 103.4 %shard_map.112.refs_6_.refs_4_ = bf16[34816,2048]{1,0:T(8,128)(2,1)} custom-call(s32[1]{0:T(128)} %bitcast.9.nt_ref, s32[100]{0:T(128)} %copy-done.6, s32[100]{0:T(128)} %get-tuple-element.79.tp_ref, s32[100]{0:T(128)} %get-tuple-element.80.tn_ref, s32[100]{0:T(128)} %get-tuple-element.81.tw_ref, ...), custom_call_target="tpu_custom_call", output_to_operand_aliasing={{}: (8, {})} | custom-call | flops 83751862272 | bytes 201326592 | tf_op jit(solution)/shard_map/pallas_call | solution.py:442
  520.4 20.7 %shard_map.113 = (bf16[512,2048]{1,0:T(8,128)(2,1)}, bf16[512,2048]{1,0:T(8,128)(2,1)}) custom-call(s32[1]{0:T(128)} %bitcast.28.refs_0_, s32[32]{0:T(128)} %multiply_add_fusion.refs_1_, f32[8,16,512]{2,1,0:T(8,128)} %select_reduce_fusion.refs_2_.refs_0_, s32[8]{0:T(128)} %negate_maximum_fusion.nch_ref.refs_3_.refs_1_, ...), custom_call_target="tpu_custom_call" | custom-call | flops 1048576 | bytes 12582912 | tf_op jit(solution)/shard_map/pallas_call | solution.py:293
  541.1 92.9 %collective-permute-start.15 = (bf16[512,2048]{1,0:T(8,128)(2,1)}, bf16[512,2048]{1,0:T(8,128)(2,1)}, u32[]{:S(2)}, u32[]{:S(2)}) collective-permute-start(bf16[512,2048]{1,0:T(8,128)(2,1)} %get-tuple-element.110), channel_id=1, source_target_pairs={{0,2},{1,3},{2,4},{3,5},{4,6},{5,7},{6,0},{7,1},{8,10},{9,11},{10,... | collective-permute-start | bytes 6291464 | tf_op jit(solution)/shard_map/ppermute | solution.py:567
  634.0 22.3 %shard_map.114 = (bf16[512,2048]{1,0:T(8,128)(2,1)}, bf16[512,2048]{1,0:T(8,128)(2,1)}) custom-call(f32[8,16,512]{2,1,0:T(8,128)} %select_reduce_fusion.refs_2_.refs_0_, s32[8]{0:T(128)} %negate_maximum_fusion.nch_ref.refs_3_.refs_1_, s32[2176]{0:T(1024)} %reshape.691.eg_ref.refs_4_.refs_2_, s32[8,16,512]{2,1,0:T(8,128)} %add_select_fusion.pos_ref.refs_5_.refs_3_, ...), custom_call_target="tpu_custom_call" | custom-call | flops 1048576 | bytes 12582912 | tf_op jit(solution)/shard_map/pallas_call | solution.py:293
  656.4 1.5 collective-permute-start.20
  658.0 11.8 %shard_map.115 = bf16[512,2048]{1,0:T(8,128)(2,1)} custom-call(s32[1]{0:T(128)} %bitcast.19.refs_0_, s32[16]{0:T(128)} %multiply_add_fusion.3.refs_1_, f32[8,16,512]{2,1,0:T(8,128)} %select_reduce_fusion.refs_2_.refs_0_, s32[8]{0:T(128)} %negate_maximum_fusion.nch_ref.refs_3_.refs_1_, s32[2176]{0:T(1024)} %reshape.691.eg_ref.refs_4_.refs_2_, ...), custom_call_target="tpu_custom_call" | custom-call | flops 1048576 | bytes 12582912 | tf_op jit(solution)/shard_map/pallas_call | solution.py:293
  669.7 10.1 %collective-permute-done.15 = bf16[512,2048]{1,0:T(8,128)(2,1)} collective-permute-done((bf16[512,2048]{1,0:T(8,128)(2,1)}, bf16[512,2048]{1,0:T(8,128)(2,1)}, u32[]{:S(2)}, u32[]{:S(2)}) %collective-permute-start.15) | collective-permute-done | bytes 2097184 | tf_op jit(solution)/shard_map/ppermute | solution.py:567
  679.8 2.2 collective-permute-done.16
  682.0 11.6 %shard_map.116 = bf16[512,2048]{1,0:T(8,128)(2,1)} custom-call(s32[1]{0:T(128)} %bitcast.22.refs_0_, s32[16]{0:T(128)} %multiply_add_fusion.2.refs_1_, f32[8,16,512]{2,1,0:T(8,128)} %select_reduce_fusion.refs_2_.refs_0_, s32[8]{0:T(128)} %negate_maximum_fusion.nch_ref.refs_3_.refs_1_, s32[2176]{0:T(1024)} %reshape.691.eg_ref.refs_4_.refs_2_, ...), custom_call_target="tpu_custom_call" | custom-call | flops 1048576 | bytes 12582912 | tf_op jit(solution)/shard_map/pallas_call | solution.py:293
  693.6 49.3 %collective-permute-start.19 = (bf16[512,2048]{1,0:T(8,128)(2,1)}, bf16[512,2048]{1,0:T(8,128)(2,1)}, u32[]{:S(2)}, u32[]{:S(2)}) collective-permute-start(bf16[512,2048]{1,0:T(8,128)(2,1)} %shard_map.116), channel_id=1, source_target_pairs={{0,2},{1,3},{2,4},{3,5},{4,6},{5,7},{6,0},{7,1},{8,10},{9,11},{10,... | collective-permute-start | bytes 6291464 | tf_op jit(solution)/shard_map/ppermute | solution.py:567
  742.9 1.5 collective-permute-start.21
  744.4 1.2 collective-permute-start.22
  745.6 23.8 %shard_map.117 = (f32[512,2048]{1,0:T(8,128)}, f32[512,2048]{1,0:T(8,128)}) custom-call(s32[1]{0:T(128)} %bitcast.15.refs_0_, s32[32]{0:T(128)} %multiply_add_fusion.5.refs_1_, f32[8,16,512]{2,1,0:T(8,128)} %select_reduce_fusion.refs_2_.refs_0_, s32[8]{0:T(128)} %negate_maximum_fusion.nch_ref.refs_3_.refs_1_, s32[2176]{0:T(1024)} %reshape.691.eg_ref.refs_4_.refs_2_, ...), custom_call_target="tpu_custom_call" | custom-call | flops 1048576 | bytes 12582912 | tf_op jit(solution)/shard_map/pallas_call | solution.py:293
  769.4 19.3 %collective-permute-done.19.refs_4_ = bf16[512,2048]{1,0:T(8,128)(2,1)} collective-permute-done((bf16[512,2048]{1,0:T(8,128)(2,1)}, bf16[512,2048]{1,0:T(8,128)(2,1)}, u32[]{:S(2)}, u32[]{:S(2)}) %collective-permute-start.19) | collective-permute-done | bytes 2097184 | tf_op jit(solution)/shard_map/ppermute | solution.py:567
  788.7 2.2 collective-permute-done.18.refs_3_
  790.9 40.5 %collective-permute-done.21.refs_6_ = bf16[512,2048]{1,0:T(8,128)(2,1)} collective-permute-done((bf16[512,2048]{1,0:T(8,128)(2,1)}, bf16[512,2048]{1,0:T(8,128)(2,1)}, u32[]{:S(2)}, u32[]{:S(2)}) %collective-permute-start.21) | collective-permute-done | bytes 2097184 | tf_op jit(solution)/shard_map/ppermute | solution.py:567
  831.4 2.2 collective-permute-done.22.refs_7_
  833.6 12.6 %shard_map.118 = bf16[1024,2048]{1,0:T(8,128)(2,1)} custom-call(bf16[1024,2048]{1,0:T(8,128)(2,1)} %shard_map.104.h_ref, f32[512,2048]{1,0:T(8,128)} %get-tuple-element.117.refs_0_, f32[512,2048]{1,0:T(8,128)} %get-tuple-element.118.refs_1_, bf16[512,2048]{1,0:T(8,128)(2,1)} %collective-permute-done.17.refs_2_, ...), custom_call_target="tpu_custom_call" | custom-call | flops 12582912 | bytes 41943040 | tf_op jit(solution)/shard_map/pallas_call | solution.py:478
  (141 shorter events, 21.2 us)
Async XLA Ops:
  6.5 226.4 %copy-start = (f32[2048,64]{0,1:T(8,128)S(1)}, f32[2048,64]{0,1:T(8,128)}, u32[]{:S(2)}) copy-start(f32[2048,64]{0,1:T(8,128)} %param.15) | copy-start | bytes 1572868
  6.6 54.7 %all-gather.9.cloned.1.call-start = ((), (), s32[]{:S(2)}) async-start(), calls=%async_computation.2 | async-start | bytes 9437184 | tf_op jit(solution)/shard_map/all_gather | solution.py:581
  7.3 102.4 %all-gather.7.cloned.1.call-start = ((), (), s32[]{:S(2)}) async-start(), calls=%async_computation.1 | async-start | bytes 9437184 | tf_op jit(solution)/shard_map/all_gather | solution.py:581
  8.1 150.2 %all-gather.5.cloned.1.call-start = ((), (), s32[]{:S(2)}) async-start(), calls=%async_computation | async-start | bytes 9437184 | tf_op jit(solution)/shard_map/all_gather | solution.py:581
  8.9 200.9 %all-gather.11.cloned.1.call-start = ((), (), s32[]{:S(2)}) async-start(), calls=%async_computation.3 | async-start | bytes 9437184 | tf_op jit(solution)/shard_map/all_gather | solution.py:581
  9.0 236.4 %collective-permute-start.6 = (bf16[8,2048,1024]{2,1,0:T(8,128)(2,1)}, bf16[8,2048,1024]{2,1,0:T(8,128)(2,1)}, u32[]{:S(2)}, u32[]{:S(2)}) collective-permute-start(bf16[8,2048,1024]{2,1,0:T(8,128)(2,1)} %refs_9_.7), channel_id=1, source_target_pairs={{0,1},{1,0},{2,3},{3,2},{4,5},{5,4},{6,7},{7,6},{8,9},{9,8},{10,11... | collective-permute-start | bytes 100663304 | tf_op jit(solution)/shard_map/ppermute | solution.py:570
  11.1 243.6 %collective-permute-start.7 = (bf16[8,2048,1024]{2,1,0:T(8,128)(2,1)}, bf16[8,2048,1024]{2,1,0:T(8,128)(2,1)}, u32[]{:S(2)}, u32[]{:S(2)}) collective-permute-start(bf16[8,2048,1024]{2,1,0:T(8,128)(2,1)} %refs_10_.7), channel_id=1, source_target_pairs={{0,1},{1,0},{2,3},{3,2},{4,5},{5,4},{6,7},{7,6},{8,9},{9,8},{10,11... | collective-permute-start | bytes 100663304 | tf_op jit(solution)/shard_map/ppermute | solution.py:570
  11.2 246.1 %collective-permute-start.8 = (bf16[8,1024,2048]{2,1,0:T(8,128)(2,1)}, bf16[8,1024,2048]{2,1,0:T(8,128)(2,1)}, u32[]{:S(2)}, u32[]{:S(2)}) collective-permute-start(bf16[8,1024,2048]{2,1,0:T(8,128)(2,1)} %refs_11_.3), channel_id=1, source_target_pairs={{0,1},{1,0},{2,3},{3,2},{4,5},{5,4},{6,7},{7,6},{8,9},{9,8},{10,11... | collective-permute-start | bytes 100663304 | tf_op jit(solution)/shard_map/ppermute | solution.py:570
  11.6 12.2 %collective-permute-start = (s32[1024,8]{0,1:T(8,128)}, s32[1024,8]{0,1:T(8,128)S(1)}, u32[]{:S(2)}, u32[]{:S(2)}) collective-permute-start(s32[1024,8]{0,1:T(8,128)} %bitcast.57), channel_id=1, source_target_pairs={{0,2},{1,3},{2,4},{3,5},{4,6},{5,7},{6,0},{7,1},{8,10},{9,11},{10,... | collective-permute-start | bytes 98312 | tf_op jit(solution)/shard_map/ppermute | solution.py:567
  12.4 12.5 %collective-permute-start.1 = (s32[1024,8]{0,1:T(8,128)}, s32[1024,8]{0,1:T(8,128)S(1)}, u32[]{:S(2)}, u32[]{:S(2)}) collective-permute-start(s32[1024,8]{0,1:T(8,128)} %bitcast.58), channel_id=1, source_target_pairs={{0,6},{1,7},{2,0},{3,1},{4,2},{5,3},{6,4},{7,5},{8,14},{9,15},{10,... | collective-permute-start | bytes 98312 | tf_op jit(solution)/shard_map/ppermute | solution.py:567
  14.4 5.2 copy-start.3
  19.5 4.2 copy-start.5
  23.8 5.4 collective-permute-start.2
  41.2 1.0 copy-start.6
  224.1 3.4 copy-start.2
  230.8 47.2 %collective-permute-start.10 = (bf16[512,2048]{1,0:T(8,128)(2,1)}, bf16[512,2048]{1,0:T(8,128)(2,1)}, u32[]{:S(2)}, u32[]{:S(2)}) collective-permute-start(bf16[512,2048]{1,0:T(8,128)(2,1)} %get-tuple-element.92.refs_1_.refs_8_), channel_id=1, source_target_pairs={{0,6},{1,7},{2,0},{3,1},{4,2},{5,3},{6,4},{7,5},{8,14},{9,15},{10,... | collective-permute-start | bytes 6291464 | tf_op jit(solution)/shard_map/ppermute | solution.py:567
  231.4 48.1 %collective-permute-start.9 = (bf16[512,2048]{1,0:T(8,128)(2,1)}, bf16[512,2048]{1,0:T(8,128)(2,1)}, u32[]{:S(2)}, u32[]{:S(2)}) collective-permute-start(bf16[512,2048]{1,0:T(8,128)(2,1)} %get-tuple-element.91.refs_3_.refs_0_.refs_7_), channel_id=1, source_target_pairs={{0,2},{1,3},{2,4},{3,5},{4,6},{5,7},{6,0},{7,1},{8,10},{9,11},{10,... | collective-permute-start | bytes 6291464 | tf_op jit(solution)/shard_map/ppermute | solution.py:567
  245.3 138.7 %collective-permute-start.13 = (bf16[512,2048]{1,0:T(8,128)(2,1)}, bf16[512,2048]{1,0:T(8,128)(2,1)}, u32[]{:S(2)}, u32[]{:S(2)}) collective-permute-start(bf16[512,2048]{1,0:T(8,128)(2,1)} %get-tuple-element.92.refs_1_.refs_8_), channel_id=1, source_target_pairs={{0,2},{1,3},{2,4},{3,5},{4,6},{5,7},{6,0},{7,1},{8,10},{9,11},{10,... | collective-permute-start | bytes 6291464 | tf_op jit(solution)/shard_map/ppermute | solution.py:567
  254.7 122.4 %copy-start.4 = (pred[8,16,512,8]{2,3,1,0:T(8,128)(4,1)S(1)}, pred[8,16,512,8]{2,3,1,0:T(8,128)(4,1)}, u32[]{:S(2)}) copy-start(pred[8,16,512,8]{2,3,1,0:T(8,128)(4,1)} %get-tuple-element.70) | copy-start | bytes 1572868
  254.7 138.4 %collective-permute-start.12 = (bf16[512,2048]{1,0:T(8,128)(2,1)}, bf16[512,2048]{1,0:T(8,128)(2,1)}, u32[]{:S(2)}, u32[]{:S(2)}) collective-permute-start(bf16[512,2048]{1,0:T(8,128)(2,1)} %get-tuple-element.91.refs_3_.refs_0_.refs_7_), channel_id=1, source_target_pairs={{0,6},{1,7},{2,0},{3,1},{4,2},{5,3},{6,4},{7,5},{8,14},{9,15},{10,... | collective-permute-start | bytes 6291464 | tf_op jit(solution)/shard_map/ppermute | solution.py:567
  279.5 128.2 %collective-permute-start.11 = (bf16[512,2048]{1,0:T(8,128)(2,1)}, bf16[512,2048]{1,0:T(8,128)(2,1)}, u32[]{:S(2)}, u32[]{:S(2)}) collective-permute-start(bf16[512,2048]{1,0:T(8,128)(2,1)} %collective-permute-done.9.refs_3_.refs_0_), channel_id=1, source_target_pairs={{0,2},{1,3},{2,4},{3,5},{4,6},{5,7},{6,0},{7,1},{8,10},{9,11},{10,... | collective-permute-start | bytes 6291464 | tf_op jit(solution)/shard_map/ppermute | solution.py:567
  293.0 114.7 %collective-permute-start.14 = (bf16[512,2048]{1,0:T(8,128)(2,1)}, bf16[512,2048]{1,0:T(8,128)(2,1)}, u32[]{:S(2)}, u32[]{:S(2)}) collective-permute-start(bf16[512,2048]{1,0:T(8,128)(2,1)} %collective-permute-done.10.refs_1_.refs_3_), channel_id=1, source_target_pairs={{0,6},{1,7},{2,0},{3,1},{4,2},{5,3},{6,4},{7,5},{8,14},{9,15},{10,... | collective-permute-start | bytes 6291464 | tf_op jit(solution)/shard_map/ppermute | solution.py:567
  293.0 77.1 %collective-permute-start.3 = (f32[1024,8]{0,1:T(8,128)S(1)}, f32[1024,8]{0,1:T(8,128)S(1)}, u32[]{:S(2)}, u32[]{:S(2)}) collective-permute-start(f32[1024,8]{0,1:T(8,128)S(1)} %fusion.21), channel_id=1, source_target_pairs={{0,2},{1,3},{2,4},{3,5},{4,6},{5,7},{6,0},{7,1},{8,10},{9,11},{10,... | collective-permute-start | bytes 98312 | tf_op jit(solution)/shard_map/ppermute | solution.py:567
  370.1 2.8 collective-permute-start.4
  372.9 4.3 collective-permute-start.5
  541.1 138.7 %collective-permute-start.15 = (bf16[512,2048]{1,0:T(8,128)(2,1)}, bf16[512,2048]{1,0:T(8,128)(2,1)}, u32[]{:S(2)}, u32[]{:S(2)}) collective-permute-start(bf16[512,2048]{1,0:T(8,128)(2,1)} %get-tuple-element.110), channel_id=1, source_target_pairs={{0,2},{1,3},{2,4},{3,5},{4,6},{5,7},{6,0},{7,1},{8,10},{9,11},{10,... | collective-permute-start | bytes 6291464 | tf_op jit(solution)/shard_map/ppermute | solution.py:567
  634.0 48.0 %collective-permute-start.16 = (bf16[512,2048]{1,0:T(8,128)(2,1)}, bf16[512,2048]{1,0:T(8,128)(2,1)}, u32[]{:S(2)}, u32[]{:S(2)}) collective-permute-start(bf16[512,2048]{1,0:T(8,128)(2,1)} %get-tuple-element.111), channel_id=1, source_target_pairs={{0,6},{1,7},{2,0},{3,1},{4,2},{5,3},{6,4},{7,5},{8,14},{9,15},{10,... | collective-permute-start | bytes 6291464 | tf_op jit(solution)/shard_map/ppermute | solution.py:567
  656.3 88.1 %collective-permute-start.17 = (bf16[512,2048]{1,0:T(8,128)(2,1)}, bf16[512,2048]{1,0:T(8,128)(2,1)}, u32[]{:S(2)}, u32[]{:S(2)}) collective-permute-start(bf16[512,2048]{1,0:T(8,128)(2,1)} %get-tuple-element.119), channel_id=1, source_target_pairs={{0,6},{1,7},{2,0},{3,1},{4,2},{5,3},{6,4},{7,5},{8,14},{9,15},{10,... | collective-permute-start | bytes 6291464 | tf_op jit(solution)/shard_map/ppermute | solution.py:567
  656.4 113.0 %collective-permute-start.20 = (bf16[512,2048]{1,0:T(8,128)(2,1)}, bf16[512,2048]{1,0:T(8,128)(2,1)}, u32[]{:S(2)}, u32[]{:S(2)}) collective-permute-start(bf16[512,2048]{1,0:T(8,128)(2,1)} %get-tuple-element.122), channel_id=1, source_target_pairs={{0,2},{1,3},{2,4},{3,5},{4,6},{5,7},{6,0},{7,1},{8,10},{9,11},{10,... | collective-permute-start | bytes 6291464 | tf_op jit(solution)/shard_map/ppermute | solution.py:567
  693.6 95.1 %collective-permute-start.19 = (bf16[512,2048]{1,0:T(8,128)(2,1)}, bf16[512,2048]{1,0:T(8,128)(2,1)}, u32[]{:S(2)}, u32[]{:S(2)}) collective-permute-start(bf16[512,2048]{1,0:T(8,128)(2,1)} %shard_map.116), channel_id=1, source_target_pairs={{0,2},{1,3},{2,4},{3,5},{4,6},{5,7},{6,0},{7,1},{8,10},{9,11},{10,... | collective-permute-start | bytes 6291464 | tf_op jit(solution)/shard_map/ppermute | solution.py:567
  742.9 48.0 %collective-permute-start.18 = (bf16[512,2048]{1,0:T(8,128)(2,1)}, bf16[512,2048]{1,0:T(8,128)(2,1)}, u32[]{:S(2)}, u32[]{:S(2)}) collective-permute-start(bf16[512,2048]{1,0:T(8,128)(2,1)} %shard_map.115), channel_id=1, source_target_pairs={{0,6},{1,7},{2,0},{3,1},{4,2},{5,3},{6,4},{7,5},{8,14},{9,15},{10,... | collective-permute-start | bytes 6291464 | tf_op jit(solution)/shard_map/ppermute | solution.py:567
  742.9 88.5 %collective-permute-start.21 = (bf16[512,2048]{1,0:T(8,128)(2,1)}, bf16[512,2048]{1,0:T(8,128)(2,1)}, u32[]{:S(2)}, u32[]{:S(2)}) collective-permute-start(bf16[512,2048]{1,0:T(8,128)(2,1)} %collective-permute-done.15), channel_id=1, source_target_pairs={{0,2},{1,3},{2,4},{3,5},{4,6},{5,7},{6,0},{7,1},{8,10},{9,11},{10,... | collective-permute-start | bytes 6291464 | tf_op jit(solution)/shard_map/ppermute | solution.py:567
  744.4 89.2 %collective-permute-start.22 = (bf16[512,2048]{1,0:T(8,128)(2,1)}, bf16[512,2048]{1,0:T(8,128)(2,1)}, u32[]{:S(2)}, u32[]{:S(2)}) collective-permute-start(bf16[512,2048]{1,0:T(8,128)(2,1)} %collective-permute-done.16), channel_id=1, source_target_pairs={{0,6},{1,7},{2,0},{3,1},{4,2},{5,3},{6,4},{7,5},{8,14},{9,15},{10,... | collective-permute-start | bytes 6291464 | tf_op jit(solution)/shard_map/ppermute | solution.py:567
  833.6 12.6 %copy-start.1 = (f32[2048,64]{0,1:T(8,128)S(1)}, f32[2048,64]{0,1:T(8,128)}, u32[]{:S(2)}) copy-start(f32[2048,64]{0,1:T(8,128)} %param.15) | copy-start | bytes 1572868
Sparse Core Ops, SparseCore 0:
  9.0 52.1 all-gather.8
  62.8 46.8 all-gather.6
  111.4 46.8 all-gather.4
  159.8 46.5 all-gather.10

commit v3 on v2

v3 whole, which is shorter than its diff:
```python
import functools
import math
import typing
import jax
import jax.numpy as jnp
from jax import lax
from jax.experimental import pallas as pl
from jax.experimental.pallas import tpu as pltpu
from jax.sharding import PartitionSpec as P

HEAD = 128
EPS = 1e-6
THETA = 10000.0
PIECE = 16
CHUNK = 256
MT = 416
HM = 256
VMEM = 66_000_000
BF, F32, I32 = jnp.bfloat16, jnp.float32, jnp.int32


def rmsnorm(v):
    v = v.astype(F32)
    return v * lax.rsqrt(jnp.mean(v * v, axis=-1, keepdims=True) + EPS)


def dot(a, b):
    return jnp.dot(a, b, preferred_element_type=F32)


NT = (((1,), (1,)), ((), ()))
DMA2 = pltpu.SemaphoreType.DMA((2,))


def cost(flops, bytes_):
    return pl.CostEstimate(flops=flops, bytes_accessed=bytes_, transcendentals=0)


def parity(i):
    return lax.rem(i, 2)


def expert_buffers(d, ff):
    return [pltpu.VMEM((2, *v), BF) for v in ((d, ff), (d, ff), (ff, d))]


def loop(n):
    return pl.loop(0, n)


def params(**kw):
    return pltpu.CompilerParams(vmem_limit_bytes=VMEM, **kw)


LT, LB, RT, RB, OT, OB, PO, PASS = 0, 1, 2, 3, 4, 5, 6, 7
MESH = pl.DeviceIdType.MESH


def layer_kernel(nx, x_ref, wv_ref, wk_ref, wq_ref, wo_ref, cos_ref, sin_ref, w1_ref, w3_ref, h_ref, ut_ref, ub_ref,
                 o1_ref, o3_ref, w_ref, ab, qb, kb, vb, ssem, rsem, lsem, iosem, swap_send, swap_recv):
    shards = (wv_ref, wk_ref, wq_ref, wo_ref)
    sh = wv_ref.shape[0]
    hs = sh // 2
    t, d = ab.shape
    me = lax.axis_index("ep")
    chip, core = me // 2, me % 2
    right, left, opp = [2 * ((chip + k) % nx) + core for k in (1, nx - 1, 2)]
    partner = 2 * chip + 1 - core

    barrier = pltpu.get_barrier_semaphore()
    for dev in (right, left, partner):
        pl.semaphore_signal(barrier, inc=1, device_id={"ep": dev}, device_id_type=MESH)
    pl.semaphore_wait(barrier, 3)

    def rows(e, half=None):
        if half is None:
            return pl.ds(pl.multiple_of(e * sh, sh), sh)
        return pl.ds(pl.multiple_of(e * sh + half * hs, hs), hs)

    def remote(w, src, dst, dev, s, r):
        return pltpu.make_async_remote_copy(src_ref=src, dst_ref=w_ref.at[w, dst, :], send_sem=ssem.at[w, s],
                                            recv_sem=rsem.at[w, r], device_id={"ep": dev}, device_id_type=MESH)

    def own(w):
        src = shards[w]
        top, bot = src.at[pl.ds(0, hs), :], src.at[pl.ds(hs, hs), :]
        return [remote(w, top, rows(me, 0), right, 0, LT), remote(w, bot, rows(me, 1), left, 1, RB),
                remote(w, bot, rows(me, 1), right, 2, LB), remote(w, top, rows(me, 0), left, 3, RT),
                remote(w, src, rows(me), partner, 6, PO)]

    def mine(w):
        return pltpu.make_async_copy(shards[w], w_ref.at[w, rows(me), :], lsem.at[w])

    where = {LT: (left, 0), LB: (left, 1), RT: (right, 0), RB: (right, 1), OT: (opp, 0), OB: (opp, 1)}

    def onward(w, k):
        e, half = where[LT if k == OT else RB]
        return remote(w, w_ref.at[w, rows(e, half), :], rows(e, half), right if k == OT else left, 4 if k == OT else 5, k)

    def across(w, k):
        r = rows(*where[k])
        return remote(w, w_ref.at[w, r, :], r, partner, PASS + k, PASS + k)

    def arrive(w, k):
        r = rows(me) if k == PO else rows(*where[k % PASS])
        remote(w, w_ref.at[w, r, :], r, partner, 0, k).wait_recv()

    def begin(w):
        for c in own(w):
            c.start()
        mine(w).start()

    def stage_a(w):
        arrive(w, LT)
        onward(w, OT).start()
        arrive(w, RB)
        onward(w, OB).start()
        if w + 1 < 4:
            begin(w + 1)
        across(w, LT).start()
        across(w, RB).start()
        swap()

    def stage_b(w):
        for k in (LB, RT):
            arrive(w, k)
            across(w, k).start()
        swap()

    def stage_c(w):
        for k in (OT, OB):
            arrive(w, k)
            across(w, k).start()
        swap()

    def stage_d(w):
        for k in (PO, PASS + LT, PASS + RB, PASS + LB, PASS + RT, PASS + OT, PASS + OB):
            arrive(w, k)
        mine(w).wait()

    pieces = [(src.at[e], dst.at[e]) for e in range(w1_ref.shape[0]) for src, dst in ((w1_ref, o1_ref), (w3_ref, o3_ref))]
    swaps = [pltpu.make_async_remote_copy(src_ref=src, dst_ref=dst, send_sem=swap_send.at[i], recv_sem=swap_recv.at[i],
                                          device_id={"ep": partner}, device_id_type=MESH) for i, (src, dst) in enumerate(pieces)]
    waiting = list(swaps)

    def swap():
        if waiting:
            waiting.pop(0).start()

    begin(0)
    swap()
    xin = pltpu.make_async_copy(x_ref, kb, iosem.at[0])
    xin.start()
    xin.wait()
    rb = min(128, t)

    @loop(t // rb)
    def _(i):
        r = pl.ds(pl.multiple_of(i * rb, rb), rb)
        ab[r, :] = rmsnorm(kb[r, :]).astype(BF)

    tm, tn = min(512, t), min(512, d)

    def project(w, dst, rope):
        @loop(d // tn)
        def _(n):
            @loop(t // tm)
            def _(m):
                r = pl.ds(pl.multiple_of(m * tm, tm), tm)
                z = dot(ab[r, :], w_ref[w, :, pl.ds(pl.multiple_of(n * tn, tn), tn)])
                for j in range(tn // HEAD):
                    zj = z[:, j * HEAD:(j + 1) * HEAD]
                    if rope:
                        zj = zj * cos_ref[r, :] + pltpu.roll(zj, HEAD // 2, 1) * sin_ref[r, :]
                    dst[r, pl.ds(pl.multiple_of(n * tn + j * HEAD, HEAD), HEAD)] = zj.astype(BF)

    for w, (dst, rope) in enumerate(((vb, False), (kb, True), (qb, True))):
        stage_a(w)
        stage_b(w)
        stage_c(w)
        stage_d(w)
        swap()
        project(w, dst, rope)
    stage_a(3)

    tq = min(256, t)
    scale = 1.0 / math.sqrt(HEAD)
    causal = lax.broadcasted_iota(I32, (tq, tq), 1) <= lax.broadcasted_iota(I32, (tq, tq), 0)

    def heads(lo, hi):
        @pl.loop(lo, hi)
        def _(j):
            c = pl.ds(pl.multiple_of(j * HEAD, HEAD), HEAD)
            for i in range(t // tq):
                r = slice(i * tq, (i + 1) * tq)
                q = qb[r, c]
                sd = lax.dot_general(q, kb[r, c], NT, preferred_element_type=F32)
                sd = jnp.where(causal, sd, -jnp.inf)
                m = jnp.max(sd, axis=1, keepdims=True)
                if i:
                    so = lax.dot_general(q, kb[:i * tq, c], NT, preferred_element_type=F32)
                    m = jnp.maximum(m, jnp.max(so, axis=1, keepdims=True))
                pd = jnp.exp((sd - m) * scale)
                l = jnp.sum(pd, axis=1, keepdims=True)
                if i:
                    po = jnp.exp((so - m) * scale)
                    l = l + jnp.sum(po, axis=1, keepdims=True)
                inv = 1.0 / l
                o = dot((pd * inv).astype(BF), vb[r, c])
                if i:
                    o = o + dot((po * inv).astype(BF), vb[:i * tq, c])
                qb[r, c] = o.astype(BF)

    nh = d // HEAD
    cut1, cut2 = nh * 3 // 8, nh * 3 // 4
    heads(0, cut1)
    stage_b(3)
    heads(cut1, cut2)
    stage_c(3)
    heads(cut2, nh)
    xin = pltpu.make_async_copy(x_ref, vb, iosem.at[0])
    xin.start()
    stage_d(3)
    xin.wait()

    @loop(d // tn)
    def _(n):
        c = pl.ds(pl.multiple_of(n * tn, tn), tn)

        @loop(t // tm)
        def _(m):
            r = pl.ds(pl.multiple_of(m * tm, tm), tm)
            ab[r, c] = (vb[r, c].astype(F32) + dot(qb[r, :], w_ref[3, :, c])).astype(BF)

    hout = pltpu.make_async_copy(ab, h_ref, iosem.at[0])
    hout.start()

    @loop(t // rb)
    def _(i):
        r = pl.ds(pl.multiple_of(i * rb, rb), rb)
        kb[r, :] = rmsnorm(ab[r, :]).astype(BF)

    uout = [pltpu.make_async_copy(kb.at[pl.ds(p * t // 2, t // 2), :], o, iosem.at[1 + p]) for p, o in enumerate((ut_ref, ub_ref))]
    for c in uout:
        c.start()
    while waiting:
        swap()
    for c in swaps:
        c.wait()
    for w in range(4):
        for c in own(w) + [onward(w, OT), onward(w, OB)] + [across(w, k) for k in where]:
            c.wait_send()
    hout.wait()
    for c in uout:
        c.wait()


def attention_layer(nx, x, wv, wk, wq, wo, cos, sin, w1, w3):
    t, d = x.shape
    hb = pl.BlockSpec(memory_space=pl.ANY)
    vm = pl.BlockSpec(memory_space=pltpu.VMEM)
    half = jax.ShapeDtypeStruct((t // 2, d), BF)
    act = pltpu.VMEM((t, d), BF)
    return pl.pallas_call(
        functools.partial(layer_kernel, nx),
        in_specs=[hb] * 5 + [vm] * 2 + [hb] * 2,
        out_specs=[hb] * 5,
        out_shape=[jax.ShapeDtypeStruct((t, d), BF), half, half, jax.ShapeDtypeStruct(w1.shape, BF),
                   jax.ShapeDtypeStruct(w3.shape, BF)],
        scratch_shapes=[pltpu.VMEM((4, d, d), BF), act, act, act, act,
                        pltpu.SemaphoreType.DMA((4, 13)), pltpu.SemaphoreType.DMA((4, 13)),
                        pltpu.SemaphoreType.DMA((4,)), pltpu.SemaphoreType.DMA((3,)),
                        pltpu.SemaphoreType.DMA((2 * w1.shape[0],)), pltpu.SemaphoreType.DMA((2 * w1.shape[0],))],
        compiler_params=params(collective_id=0, has_side_effects=True),
        cost_estimate=cost(8 * t * d * d, 24 * t * d),
    )(x, wv, wk, wq, wo, cos, sin, w1, w3)


def fetch_expert(l, slot, own, other, bufs, sem):
    ne = own[0].shape[0]

    @pl.when(l < ne)
    def _():
        for src, dst in zip(own, bufs):
            pltpu.make_async_copy(src.at[l], dst.at[slot], sem.at[slot]).start()

    @pl.when(l >= ne)
    def _():
        for src, dst in zip(other, bufs):
            pltpu.make_async_copy(src.at[l - ne], dst.at[slot], sem.at[slot]).start()


def wait_expert(slot, own, bufs, sem):
    for src, dst in zip(own, bufs):
        pltpu.make_async_copy(src.at[0], dst.at[slot], sem.at[slot]).wait()


def ffn(x, w1, w3, w2):
    a1 = dot(x, w1)
    a3 = dot(x, w3)
    act = (jax.nn.silu(a1) * a3).astype(BF)
    return dot(act, w2).astype(BF)


def block_kernel(js, has_acc, comb, dense, *refs):
    refs = list(refs)
    nblk = len(js)
    take = lambda n: [refs.pop(0) for _ in range(n)]
    if any(dense):
        nh_ref, hl_ref = take(2)
    gt_ref, = take(1)
    if comb:
        nch_ref, eg_ref, pos_ref, z_ref = take(4)
        cap = z_ref.shape[0] // pos_ref.shape[0]
    if any(dense):
        us = take(nblk)
        own, other = take(3), take(3)
        nl = 2 * own[0].shape[0]
    accs = [take(1)[0] if h else None for h in has_acc]
    outs = take(nblk)
    acc, asem = take(2)
    if comb:
        cbuf, zbuf, zsem = take(3)
    if any(dense):
        bufs, (ubuf, sem, usem) = take(3), take(3)
    t, d = outs[0].shape

    if any(dense):
        ns = [nh_ref[j] if on else 0 for j, on in zip(js, dense)]
        n = sum(ns)

        def entry(i):
            p = jnp.where(i < ns[0], 0, nblk - 1)
            return p, hl_ref[jnp.where(p == 0, js[0], js[-1]) * nl + i - jnp.where(p == 0, 0, ns[0])]

        @pl.when(n > 0)
        def _():
            fetch_expert(entry(0)[1], 0, own, other, bufs, sem)

        ucp = [pltpu.make_async_copy(us[p], ubuf.at[pl.ds(p * t, t), :], usem) for p in range(nblk)]
        for cp in ucp:
            cp.start()
    for p in range(nblk):
        rows = pl.ds(p * t, t)
        if has_acc[p]:
            pltpu.make_async_copy(accs[p], acc.at[rows, :], asem.at[p]).start()
        else:
            acc[rows, :] = jnp.zeros((t, d), F32)
    for p in range(nblk):
        if has_acc[p]:
            pltpu.make_async_copy(accs[p], acc.at[pl.ds(p * t, t), :], asem.at[p]).wait()

    if comb:
        for p, j in enumerate(js):
            nch = nch_ref[j]

            def get(i, slot):
                src = pl.multiple_of(j * cap + i * CHUNK, CHUNK)
                return pltpu.make_async_copy(z_ref.at[pl.ds(src, CHUNK), :], zbuf.at[slot], zsem.at[slot])

            get(0, 0).start()
            nl = gt_ref.shape[1]
            lane = lax.broadcasted_iota(I32, (1, CHUNK), 1)
            ti = lax.broadcasted_iota(I32, (PIECE, t), 1)
            si = lax.broadcasted_iota(I32, (PIECE, t), 0)
            tparts = jnp.where(si == 0, ti % 256, jnp.where(si == 1, ti // 256, 0)).astype(F32).astype(BF)
            table = jnp.concatenate([*split3(gt_ref[j]), tparts], axis=0)

            @loop(nch)
            def _(i):
                slot = parity(i)

                @pl.when(i + 1 < nch)
                def _():
                    get(i + 1, 1 - slot).start()

                ps, el = [], jnp.zeros((1, CHUNK), I32)
                for q, (hit, l) in enumerate(selection(j, i, eg_ref, pos_ref)):
                    ps.append(jnp.where(hit, 1.0, 0.0).astype(BF))
                    el = jnp.where(lane // PIECE == q, l, el)
                sel = lax.dot_general(table, jnp.concatenate(ps, axis=0), NT, preferred_element_type=F32)
                tok = (sel[3 * nl:3 * nl + 1] + 256.0 * sel[3 * nl + 1:3 * nl + 2]).astype(I32)
                hot_ = lax.broadcasted_iota(I32, (t, CHUNK), 0) == tok
                sub = lax.broadcasted_iota(I32, (nl, CHUNK), 0) == el
                for k in range(3):
                    gk = jnp.sum(jnp.where(sub, sel[k * nl:(k + 1) * nl], 0.0), axis=0, keepdims=True)
                    cbuf[:, k * CHUNK:(k + 1) * CHUNK] = jnp.where(hot_, gk, 0.0).astype(BF)
                get(i, slot).wait()
                tn = min(1024, d)

                @loop(d // tn)
                def _(m):
                    cs = pl.ds(pl.multiple_of(m * tn, tn), tn)
                    z = zbuf[slot, :, cs]
                    acc[p * t:(p + 1) * t, cs] += dot(cbuf[:], jnp.concatenate([z, z, z], axis=0))

    if any(dense):
        for cp in ucp:
            cp.wait()
        tm = min(HM, t)

        @loop(n)
        def _(i):
            slot = parity(i)
            wait_expert(slot, own, bufs, sem)

            @pl.when(i + 1 < n)
            def _():
                fetch_expert(entry(i + 1)[1], 1 - slot, own, other, bufs, sem)

            p, e = entry(i)
            blk = jnp.where(p == 0, js[0], js[-1])

            @loop(t // tm)
            def _(m):
                rows = pl.ds(pl.multiple_of(p * t + m * tm, tm), tm)
                z = ffn(ubuf[rows, :], bufs[0][slot], bufs[1][slot], bufs[2][slot])
                g = gt_ref[blk, pl.ds(e, 1), pl.ds(pl.multiple_of(m * tm, tm), tm)]
                eye = lax.broadcasted_iota(I32, (tm, tm), 0) == lax.broadcasted_iota(I32, (tm, tm), 1)
                gc = jnp.sum(jnp.where(eye, g, 0.0), axis=1, keepdims=True)
                acc[rows, :] += gc * z.astype(F32)

    for p in range(nblk):
        outs[p][:] = acc[p * t:(p + 1) * t, :].astype(outs[p].dtype)


def block(js, r, z, us, accs, own, other, dtype, dense, comb=True):
    nblk = len(js)
    t = r.pos.shape[2]
    d = own[0].shape[1]
    ff = own[0].shape[2]
    vm = pl.BlockSpec(memory_space=pltpu.VMEM)
    sm = pl.BlockSpec(memory_space=pltpu.SMEM)
    hb = pl.BlockSpec(memory_space=pl.ANY)
    args, specs, scratch = [], [], []
    if any(dense):
        args += [r.nh, r.hl.reshape(-1)]
        specs += [sm, sm]
    args += [r.gt]
    specs += [vm]
    if comb:
        args += [r.nch, r.eg.reshape(-1), r.pos, z]
        specs += [sm, sm, vm, hb]
    if any(dense):
        args += list(us) + list(own) + list(other)
        specs += [hb] * (nblk + 6)
    args += [v for v in accs if v is not None]
    specs += [hb for v in accs if v is not None]
    scratch += [pltpu.VMEM((nblk * t, d), F32), pltpu.SemaphoreType.DMA((nblk,))]
    if comb:
        scratch += [pltpu.VMEM((t, 3 * CHUNK), BF), pltpu.VMEM((2, CHUNK, d), BF), DMA2]
    if any(dense):
        scratch += [*expert_buffers(d, ff),
                    pltpu.VMEM((nblk * t, d), BF), DMA2, pltpu.SemaphoreType.DMA]
    out = jax.ShapeDtypeStruct((t, d), dtype)
    return pl.pallas_call(
        functools.partial(block_kernel, js, [v is not None for v in accs], comb, dense),
        in_specs=specs, out_specs=[vm] * nblk, out_shape=[out] * nblk, scratch_shapes=scratch,
        compiler_params=params(),
        cost_estimate=cost(t * d, 6 * d * ff),
    )(*args)


def split3(g):
    hi = g.astype(BF)
    r = g - hi.astype(F32)
    mid = r.astype(BF)
    lo = (r - mid.astype(F32)).astype(BF)
    return hi, mid, lo


def selection(j, i, eg_ref, pos_ref):
    t = pos_ref.shape[2]
    it = lax.broadcasted_iota(I32, (PIECE, t), 0)
    npc = CHUNK // PIECE
    npb = eg_ref.shape[0] // pos_ref.shape[0]
    for q in range(npc):
        l = eg_ref[j * npb + i * npc + q]
        yield pos_ref[j, pl.ds(l, 1), :] - (i * CHUNK + q * PIECE) == it, l


def gather_kernel(js, nch_ref, eg_ref, pos_ref, *refs):
    us = refs[:len(js)]
    x_ref, xbuf, sem = refs[-3:]
    cap = x_ref.shape[0] // pos_ref.shape[0]
    for p, j in enumerate(js):
        nch = nch_ref[j]

        def out(i, slot):
            dst = pl.multiple_of(j * cap + i * CHUNK, CHUNK)
            return pltpu.make_async_copy(xbuf.at[slot], x_ref.at[pl.ds(dst, CHUNK), :], sem.at[slot])

        @loop(nch)
        def _(i):
            slot = parity(i)

            @pl.when(i >= 2)
            def _():
                out(i - 2, slot).wait()

            pm = jnp.concatenate([jnp.where(hit, 1.0, 0.0).astype(BF) for hit, _ in selection(j, i, eg_ref, pos_ref)], axis=0)
            xbuf[slot] = dot(pm, us[p][:]).astype(BF)
            out(i, slot).start()

        for k in (2, 1):
            @pl.when(nch >= k)
            def _():
                out(nch - k, parity(nch - k)).wait()


def gather(js, r, us, x):
    nblk = len(js)
    t, d = us[0].shape
    nb = r.eg.shape[0]
    cap = r.eg.shape[1] * PIECE
    vm = pl.BlockSpec(memory_space=pltpu.VMEM)
    sm = pl.BlockSpec(memory_space=pltpu.SMEM)
    hb = pl.BlockSpec(memory_space=pl.ANY)
    return pl.pallas_call(
        functools.partial(gather_kernel, js),
        in_specs=[sm, sm, vm] + [vm] * nblk + ([hb] if x is not None else []),
        out_specs=hb,
        out_shape=jax.ShapeDtypeStruct((nb * cap, d), BF),
        input_output_aliases={3 + nblk: 0} if x is not None else {},
        scratch_shapes=[pltpu.VMEM((2, CHUNK, d), BF), DMA2],
        compiler_params=params(),
        cost_estimate=cost(t * d, 4 * CHUNK * d),
    )(r.nch, r.eg.reshape(-1), r.pos, *us, *([x] if x is not None else []))


def cold_kernel(nt_ref, tl_ref, tp_ref, tn_ref, tw_ref, tf_ref, nx_ref, pc_ref, x_ref, *refs):
    own, other, z_ref, refs = refs[:3], refs[3:6], refs[6], refs[7:]
    bufs, (xbuf, zbuf, wsem, xsem, zsem) = refs[:3], refs[3:]
    nt = nt_ref[0]

    def xin(q, slot):
        p0 = tp_ref[q]

        @loop(tn_ref[q])
        def _(i):
            src = pl.ds(pl.multiple_of(pc_ref[p0 + i] * PIECE, PIECE), PIECE)
            dst = pl.ds(pl.multiple_of(i * PIECE, PIECE), PIECE)
            pltpu.make_async_copy(x_ref.at[src, :], xbuf.at[slot, dst, :], xsem.at[slot]).start()

    def zout(q, slot):
        p0 = tp_ref[q]

        @loop(tn_ref[q])
        def _(i):
            src = pl.ds(pl.multiple_of(i * PIECE, PIECE), PIECE)
            dst = pl.ds(pl.multiple_of(pc_ref[p0 + i] * PIECE, PIECE), PIECE)
            pltpu.make_async_copy(zbuf.at[slot, src, :], z_ref.at[dst, :], zsem.at[slot]).start()

    def drain(n, fn):
        bit = 1
        while bit <= MT // PIECE:
            @pl.when(lax.rem(lax.div(n, bit), 2) == 1)
            def _(bit=bit):
                fn(pl.ds(0, bit * PIECE))

            bit *= 2

    def xwait(q, slot):
        drain(tn_ref[q], lambda r: pltpu.make_async_copy(x_ref.at[r, :], xbuf.at[slot, r, :], xsem.at[slot]).wait())

    def zwait(q, slot):
        drain(tn_ref[q], lambda r: pltpu.make_async_copy(zbuf.at[slot, r, :], z_ref.at[r, :], zsem.at[slot]).wait())

    @pl.when(nt > 0)
    def _():
        fetch_expert(tl_ref[0], 0, own, other, bufs, wsem)
        xin(0, 0)

    @loop(nt)
    def _(q):
        slot = parity(q)
        ws = parity(tw_ref[q])

        @pl.when(tf_ref[q] == 1)
        def _():
            wait_expert(ws, own, bufs, wsem)

            @pl.when(nx_ref[q] >= 0)
            def _():
                fetch_expert(nx_ref[q], 1 - ws, own, other, bufs, wsem)

        @pl.when(q + 1 < nt)
        def _():
            xin(q + 1, 1 - slot)

        xwait(q, slot)

        @pl.when(q >= 2)
        def _():
            zwait(q - 2, slot)

        zbuf[slot] = ffn(xbuf[slot], bufs[0][ws], bufs[1][ws], bufs[2][ws])
        zout(q, slot)

    for k in (2, 1):
        @pl.when(nt >= k)
        def _():
            zwait(nt - k, parity(nt - k))


def cold(plan, x, own, other):
    d, ff = own[0].shape[1:]
    sm = pl.BlockSpec(memory_space=pltpu.SMEM)
    hb = pl.BlockSpec(memory_space=pl.ANY)
    return pl.pallas_call(
        cold_kernel,
        in_specs=[sm] * len(plan) + [hb] * 7,
        out_specs=hb,
        out_shape=jax.ShapeDtypeStruct(x.shape, BF),
        scratch_shapes=[*expert_buffers(d, ff),
                        pltpu.VMEM((2, MT, d), BF), pltpu.VMEM((2, MT, d), BF),
                        DMA2, DMA2, DMA2],
        input_output_aliases={len(plan): 0},
        compiler_params=params(),
        cost_estimate=cost(6 * 16 * MT * d * ff, 96 * d * ff),
    )(*plan, x, *own, *other)


def final_kernel(h_ref, *refs):
    y_ref = refs[-1]
    acc, parts = refs[0], refs[1:-1]
    y = h_ref[:].astype(F32) + acc[:]
    for v in parts:
        y = y + v[:].astype(F32)
    y_ref[:] = y.astype(BF)


def final(h, accs, parts):
    t, d = h.shape
    half = t // 2
    tm = min(128, half)
    n = half // tm

    def body(h_ref, *refs):
        for p in range(2):
            @pl.when(pl.program_id(0) // n == p)
            def _():
                final_kernel(h_ref, refs[p], *refs[2 + p:-1:2], refs[-1])

    spec = lambda p: pl.BlockSpec((tm, d), lambda i: (jnp.minimum(i, n - 1) if p == 0 else jnp.maximum(i - n, 0), 0))
    return pl.pallas_call(
        body, grid=(2 * n,),
        in_specs=[pl.BlockSpec((tm, d), lambda i: (i, 0))] + [spec(0), spec(1)] * (1 + len(parts)),
        out_specs=pl.BlockSpec((tm, d), lambda i: (i, 0)),
        out_shape=jax.ShapeDtypeStruct((t, d), BF),
        compiler_params=params(),
        cost_estimate=cost(6 * t * d, 20 * t * d),
    )(h, *accs, *[v for part in parts for v in part])


class Routing(typing.NamedTuple):
    nh: typing.Any
    hl: typing.Any
    nch: typing.Any
    eg: typing.Any
    pos: typing.Any
    gt: typing.Any


def routing_plan(lid, local, nl):
    nb, t, k = lid.shape
    le = jnp.arange(nl, dtype=I32)
    hit = jnp.any((lid[:, None] == le[:, None, None]) & local[:, None], axis=-1)
    tri = (jnp.arange(t)[:, None] <= jnp.arange(t)[None, :]).astype(BF)
    rank = lax.dot_general(hit.astype(BF), tri, (((2,), (0,)), ((), ())), preferred_element_type=F32).astype(I32)
    cnt = rank[:, :, -1]
    hotm = cnt >= t // 2
    scnt = jnp.where(hotm, 0, cnt)
    pcs = (scnt + PIECE - 1) // PIECE
    pend = jnp.cumsum(pcs, axis=1)
    base = (pend - pcs) * PIECE
    pos = jnp.where(hit & ~hotm[..., None], base[..., None] + rank - 1, -1)
    rows = t * k + nl * PIECE
    npb = -(-rows // CHUNK) * CHUNK // PIECE
    nch = jnp.maximum(-(-pend[:, -1] * PIECE // CHUNK), 1)
    below = lambda ends, q: jnp.sum((ends <= q).astype(I32), axis=-1)
    eg = jnp.minimum(below(pend[:, None, :], jnp.arange(npb, dtype=I32)[None, :, None]), nl - 1)
    flat = pcs.T.reshape(-1)
    fend = jnp.cumsum(flat)
    p = jnp.arange(nb * npb, dtype=I32)[:, None]
    seg = jnp.minimum(below(fend[None, :], p), nl * nb - 1)
    inseg = seg[:, None] == jnp.arange(nl * nb, dtype=I32)
    shift_ = jnp.tile(jnp.arange(nb, dtype=I32) * npb, nl) + (pend - pcs).T.reshape(-1) - (fend - flat)
    pc = jnp.clip(p[:, 0] + jnp.sum(jnp.where(inseg, shift_, 0), axis=1), 0, nb * npb - 1)
    ppt = MT // PIECE
    ptot = jnp.sum(pcs, axis=0)
    pstart = jnp.cumsum(ptot) - ptot
    tiles = (ptot + ppt - 1) // ppt
    tend = jnp.cumsum(tiles)
    nq = -(-(nb * npb) // ppt) + nl
    q = jnp.arange(nq, dtype=I32)
    tl = jnp.minimum(below(tend[None, :], q[:, None]), nl - 1)
    one = tl[:, None] == le
    pick = lambda v: jnp.sum(jnp.where(one, v[None, :], 0), axis=1)
    ti = q - pick(tend - tiles)
    tp = pick(pstart) + ti * ppt
    tn = jnp.clip(pick(ptot) - ti * ppt, 0, ppt)
    active = (tiles > 0).astype(I32)
    tw = pick(jnp.cumsum(active) - active)
    tf = (ti == 0).astype(I32)
    later = (le[None, :] > tl[:, None]) & (active[None, :] > 0)
    nxt = jnp.min(jnp.where(later, le[None, :], nl), axis=1)
    nxt = jnp.where(nxt < nl, nxt, -1)
    plan = tuple(v.astype(I32) for v in (tend[-1:], tl, tp, tn, tw, tf, nxt, pc))
    hend = jnp.cumsum(hotm.astype(I32), axis=1)
    hl = jnp.minimum(below(hend[:, None, :], le[None, :, None]), nl - 1)
    return Routing(hend[:, -1], hl, nch, eg, pos, None), plan


ON = (True,)


def solution(mesh):
    nd = mesh.shape['ep']
    nx = nd // 2
    tok_spec = P(('replica', 'ep'), None, None)
    rows_ep = P('ep', None)
    by_expert = P('ep', None, None)

    def shift(v, s):
        return lax.ppermute(v, 'ep', [(2 * i + c, 2 * ((i + s) % nx) + c) for i in range(nx) for c in range(2)])

    def partner(v):
        return lax.ppermute(v, 'ep', [(i, i ^ 1) for i in range(nd)])

    def local(x, wq, wk, wv, wo, wr, w1, w3, w2, idx):
        b, s, d = x.shape
        t, k, ne = b * s, idx.shape[-1], w1.shape[0]
        nl = 2 * ne
        half = t // 2
        me = lax.axis_index('ep')
        x = x.reshape(t, d)
        ids = idx.reshape(t, k)

        ids4 = jnp.stack([ids, shift(ids, 1), shift(ids, -1), shift(ids, 2)])
        hd = HEAD // 2
        freq = THETA ** (-jnp.arange(hd, dtype=F32) / hd)
        ang = (jnp.arange(t) % s).astype(F32)[:, None] * freq
        c, sn = jnp.cos(ang), jnp.sin(ang)
        cos, sin = jnp.concatenate([c, c], axis=1), jnp.concatenate([-sn, sn], axis=1)
        x, cos, sin, ids4 = lax.optimization_barrier((x, cos, sin, ids4))
        h, ut, ub, o1, o3 = attention_layer(nx, x, wv, wk, wq, wo, cos, sin, w1, w3)
        ids4, w2, ut, ub = lax.optimization_barrier((ids4, w2, ut, ub))
        o2 = partner(w2)
        own, other = (w1, w3, w2), (o1, o3, o2)

        halves = lambda v: v.reshape(2 * v.shape[0], half, *v.shape[2:])
        is_local = halves(ids4 // nl == me // 2)
        lid = halves((ids4 - me * ne) % nl)
        r, plan = routing_plan(lid, is_local, nl)
        ohl = (lid[:, None] == jnp.arange(nl, dtype=I32)[:, None, None]) & is_local[:, None]
        A, R, L, O = (0, 1), (2, 3), (4, 5), (6, 7)
        ra = r._replace(pos=r.pos[:2])

        u1t, u2b = shift(ut, 1), shift(ub, -1)
        logits = jnp.dot(rmsnorm(h), wr, precision=lax.Precision.HIGHEST, preferred_element_type=F32)
        oh = ids[..., None] == jnp.arange(wr.shape[1], dtype=I32)
        g = jax.nn.softmax(jnp.sum(jnp.where(oh, logits[:, None, :], 0.0), axis=-1), axis=-1)
        ut2, ub2, g = lax.optimization_barrier((ut, ub, g))
        g4 = [g, shift(g, 1), shift(g, -1), shift(g, 2)]
        u1b, u2t = shift(ub2, 1), shift(ut2, -1)
        spread = lambda o, v: jnp.sum(jnp.where(o, halves(v)[:, None], 0.0), axis=3)
        ra = ra._replace(gt=spread(ohl[:2], g[None]))
        r = r._replace(gt=spread(ohl, jnp.stack(g4)))

        x = gather(A, r, (ut, ub), None)
        a0, = block((0,), ra, None, (ut,), (None,), own, other, F32, ON, comb=False)
        a0, x, u1t, u2b = lax.optimization_barrier((a0, x, u1t, u2b))
        u3t, u3b = shift(u1t, 1), shift(u2b, -1)
        d2, = block((2,), r, None, (u1t,), (None,), own, other, F32, ON, comb=False)
        u1b, d2 = lax.optimization_barrier((u1b, d2))
        x = gather(R, r, (u1t, u1b), x)
        x = gather(L, r, (u2t, u2b), x)
        u2bx, x = lax.optimization_barrier((u2b, x))
        d5, = block((5,), r, None, (u2bx,), (None,), own, other, F32, ON, comb=False)
        u3t, d5 = lax.optimization_barrier((u3t, d5))
        x = gather(O, r, (u3t, u3b), x)
        z = cold(plan, x, own, other)

        tie = lambda r, *v: (lambda w: (r._replace(nch=w[0]), *w[1:]))(lax.optimization_barrier((r.nch, *v)))
        b6, b7 = block(O, r, z, (u3t, u3b), (None, None), own, other, BF, 2 * ON)
        r, b6, b7 = tie(r, b6, b7)
        c6, c7 = shift(b6, 1), shift(b7, -1)
        b2, b5 = block((2, 5), r, z, (), (d2, d5), own, other, BF, (False, False))
        r, b2, b5 = tie(r, b2, b5)
        b2, b5 = shift(b2, -1), shift(b5, 1)
        b3, = block((3,), r, z, (u1b,), (None,), own, other, BF, ON)
        r, b3, c6, c7 = tie(r, b3, c6, c7)
        b6, b7 = shift(c6, 1), shift(c7, -1)
        b3 = shift(b3, -1)
        b4, = block((4,), r, z, (u2t,), (None,), own, other, BF, ON)
        r, b4 = tie(r, b4)
        b4 = shift(b4, 1)
        accs = block(A, r, z, (ut, ub), (a0, None), own, other, F32, (False, True))
        y = final(h, accs, [(b2, b3), (b4, b5), (b6, b7)])
        return y.reshape(b, s, d)

    return jax.shard_map(local, mesh=mesh,
                         in_specs=(tok_spec, rows_ep, rows_ep, rows_ep, rows_ep, P(None, None),
                                   by_expert, by_expert, by_expert, tok_spec),
                         out_specs=tok_spec, check_vma=False)
```

time: 861 us -> 796 us (0.925)
  the two profiles are of different devices: /device:TPU:81 before, /device:TPU:122 now
where the time goes in v3:
time: 796 us; the launch traced here: 792 us
  Pallas kernels  427 us (54%)
  starting transfers between devices  199 us (25%)
  waiting for transfers between devices  134 us (17%)
  other arithmetic  19.3 us (2%)
  matrix products  8.98 us (1%)
    ppermute x20, starting transfers between devices, shift(): lax.ppermute(v, 'ep', [(2 * i + c, 2 * ((i + s) % nx) + c) for i in range...  197 us
    pallas_call x1, Pallas kernels, attention_layer(): pl.pallas_call(functools.partial(layer_kernel, nx), in_specs=[hb] * 5 + [...  173 us
    ppermute x20, waiting for transfers between devices, shift(): lax.ppermute(v, 'ep', [(2 * i + c, 2 * ((i + s) % nx) + c) for i in range...  122 us
    pallas_call x8, Pallas kernels, block(): pl.pallas_call(functools.partial(block_kernel, js, [v is not None for v i...  104 us
    pallas_call x1, Pallas kernels, cold(): pl.pallas_call(cold_kernel, in_specs=[sm] * len(plan) + [hb] * 7, out_spe...  100 us
    pallas_call x4, Pallas kernels, gather(): pl.pallas_call(functools.partial(gather_kernel, js), in_specs=[sm, sm, vm...  36.6 us
  transfers between devices with their start and end apart: 21, of which 10 were waited for; matrix products, arithmetic and copies ran while one was open for 4% of the time, Pallas kernels for 14%

profile of v3, /device:TPU:122, one launch (start us, length us, event | category | flops | bytes accessed | tf_op | source)
XLA Modules:
  0.0 792.2 jit_solution(7810961908749298277)
XLA Ops:
  0.0 2.4 collective-permute-start.2
  2.4 1.3 collective-permute-start.1
  3.7 0.7 collective-permute-start
  4.5 1.9 fusion.6
  6.4 1.3 pad_maximum_fusion
  7.8 172.9 %shard_map.100 = (bf16[1024,2048]{1,0:T(8,128)(2,1)}, bf16[512,2048]{1,0:T(8,128)(2,1)}, bf16[512,2048]{1,0:T(8,128)(2,1)}, bf16[8,2048,1024]{2,1,0:T(8,128)(2,1)}, bf16[8,2048,1024]{2,1,0:T(8,128)(2,1)}) custom-call(bf16[1024,2048]{1,0:T(8,128)(2,1)} %bitcast.48, bf16[256,2048]{1,0:T(8,128)(2,1)} %wv_ref.1, bf16[256,2048]{1,0:T(8,128)(2,1)} %wk_ref.1, ...), custom_call_target="tpu_custom_call" | custom-call | flops 34359738368 | bytes 50331648 | tf_op jit(solution)/shard_map/pallas_call | solution.py:264
  180.7 2.3 collective-permute-start.6
  183.0 2.1 collective-permute-start.8
  185.1 0.5 collective-permute-start.7
  185.6 3.2 fusion
  189.1 8.7 %fusion.1 = f32[1024,64]{0,1:T(8,128)S(1)} fusion(f32[2048,64]{0,1:T(8,128)S(1)} %copy-done, bf16[1024,2048]{1,0:T(8,128)(2,1)S(1)} %copy-done.2, f32[1024]{0:T(1024)S(1)} %add_rsqrt_fusion), kind=kOutput, calls=%fused_computation.3 | convolution fusion | flops 1614807040 | bytes 4984832 | tf_op jit(solution)/shard_map/dot_general | solution.py:761
  197.8 0.3 select_reduce_fusion.1
  198.2 2.6 collective-permute-start.5
  200.9 1.2 fusion.3
  202.1 0.2 convolution_convert_fusion
  202.4 0.3 slice_reduce_fusion
  203.4 0.7 min.52.refs_1_
  204.8 0.7 min.55.eg_ref.refs_4_.refs_2_
  205.6 0.5 collective-permute-start.10
  206.3 0.3 fusion.17
  206.6 0.3 fusion.15
  206.9 0.5 negate_maximum_fusion.nch_ref.refs_3_.refs_1_
  207.4 0.8 add_select_fusion.pos_ref.refs_5_.refs_3_
  208.2 9.2 %shard_map.102.refs_2_ = bf16[34816,2048]{1,0:T(8,128)(2,1)} custom-call(s32[8]{0:T(128)} %negate_maximum_fusion.nch_ref.refs_3_.refs_1_, s32[2176]{0:T(1024)} %min.55.eg_ref.refs_4_.refs_2_, s32[8,16,512]{2,1,0:T(8,128)} %add_select_fusion.pos_ref.refs_5_.refs_3_, bf16[512,2048]{1,0:T(8,128)(2,1)} %get-tuple-element.65.refs_3_.refs_0_.refs_7_, ...), custom_call_target="tpu_custom_call" | custom-call | flops 1048576 | bytes 2097152 | tf_op jit(solution)/shard_map/pallas_call | solution.py:519
  217.4 0.7 slice_reduce_fusion.1.refs_0_
  218.2 1.7 select_reduce_fusion.3.refs_2_
  220.0 12.1 %collective-permute-done.6.refs_9_.refs_5_.refs_14_.refs_13_ = bf16[8,1024,2048]{2,1,0:T(8,128)(2,1)} collective-permute-done((bf16[8,1024,2048]{2,1,0:T(8,128)(2,1)}, bf16[8,1024,2048]{2,1,0:T(8,128)(2,1)}, u32[]{:S(2)}, u32[]{:S(2)}) %collective-permute-start.6) | collective-permute-done | bytes 33554464 | tf_op jit(solution)/shard_map/ppermute | solution.py:729
  232.1 1.0 collective-permute-start.11
  233.2 4.8 shard_map.101.refs_15_
  238.0 32.3 %collective-permute-start.9 = (bf16[512,2048]{1,0:T(8,128)(2,1)}, bf16[512,2048]{1,0:T(8,128)(2,1)}, u32[]{:S(2)}, u32[]{:S(2)}) collective-permute-start(bf16[512,2048]{1,0:T(8,128)(2,1)} %collective-permute-done.7.refs_3_.refs_0_), channel_id=1, source_target_pairs={{0,2},{1,3},{2,4},{3,5},{4,6},{5,7},{6,0},{7,1},{8,10},{9,11},{10,... | collective-permute-start | bytes 6291464 | tf_op jit(solution)/shard_map/ppermute | solution.py:726
  271.0 0.7 select_reduce_fusion.4
  271.7 0.4 convert_reduce_fusion
  272.1 0.7 select_reduce_fusion.2
  272.8 0.6 add_clamp_fusion.pc_ref
  273.4 0.6 subtract_clamp_fusion
  274.0 0.5 compare_convert_fusion.1.tf_ref
  274.5 47.7 %collective-permute-done.4 = f32[1024,8]{0,1:T(8,128)S(1)} collective-permute-done((f32[1024,8]{0,1:T(8,128)S(1)}, f32[1024,8]{0,1:T(8,128)S(1)}, u32[]{:S(2)}, u32[]{:S(2)}) %collective-permute-start.4) | collective-permute-done | bytes 32800 | tf_op jit(solution)/shard_map/ppermute | solution.py:726
  322.2 0.8 collective-permute-start.3
  323.0 0.6 compare_select_fusion.2.nx_ref
  323.6 0.5 slice.25
  324.1 2.3 collective-permute-done.3
  326.4 1.6 select_reduce_fusion.refs_2_.refs_0_
  328.0 4.8 shard_map.103.refs_5_
  332.8 9.1 %shard_map.104.refs_2_ = bf16[34816,2048]{1,0:T(8,128)(2,1)} custom-call(s32[8]{0:T(128)} %negate_maximum_fusion.nch_ref.refs_3_.refs_1_, s32[2176]{0:T(1024)} %min.55.eg_ref.refs_4_.refs_2_, s32[8,16,512]{2,1,0:T(8,128)} %add_select_fusion.pos_ref.refs_5_.refs_3_, ...), custom_call_target="tpu_custom_call", output_to_operand_aliasing={{}: (5, {})} | custom-call | flops 1048576 | bytes 2097152 | tf_op jit(solution)/shard_map/pallas_call | solution.py:519
  341.9 9.2 %shard_map.105.refs_2_ = bf16[34816,2048]{1,0:T(8,128)(2,1)} custom-call(s32[8]{0:T(128)} %negate_maximum_fusion.nch_ref.refs_3_.refs_1_, s32[2176]{0:T(1024)} %min.55.eg_ref.refs_4_.refs_2_, s32[8,16,512]{2,1,0:T(8,128)} %add_select_fusion.pos_ref.refs_5_.refs_3_, ...), custom_call_target="tpu_custom_call", output_to_operand_aliasing={{}: (5, {})} | custom-call | flops 1048576 | bytes 2097152 | tf_op jit(solution)/shard_map/pallas_call | solution.py:519
  351.1 5.0 shard_map.106.refs_6_
  356.2 9.2 %shard_map.107.x_ref = bf16[34816,2048]{1,0:T(8,128)(2,1)} custom-call(s32[8]{0:T(128)} %negate_maximum_fusion.nch_ref.refs_3_.refs_1_, s32[2176]{0:T(1024)} %min.55.eg_ref.refs_4_.refs_2_, s32[8,16,512]{2,1,0:T(8,128)} %add_select_fusion.pos_ref.refs_5_.refs_3_, ...), custom_call_target="tpu_custom_call", output_to_operand_aliasing={{}: (5, {})} | custom-call | flops 1048576 | bytes 2097152 | tf_op jit(solution)/shard_map/pallas_call | solution.py:519
  365.3 100.2 %shard_map.108.refs_6_.refs_4_ = bf16[34816,2048]{1,0:T(8,128)(2,1)} custom-call(s32[1]{0:T(128)} %bitcast.15.nt_ref, s32[100]{0:T(128)} %copy-done.4, s32[100]{0:T(128)} %get-tuple-element.108.tp_ref, s32[100]{0:T(128)} %get-tuple-element.107.tn_ref, s32[100]{0:T(128)} %get-tuple-element.94.tw_ref, ...), custom_call_target="tpu_custom_call", output_to_operand_aliasing={{}: (8, {})} | custom-call | flops 83751862272 | bytes 201326592 | tf_op jit(solution)/shard_map/pallas_call | solution.py:610
  465.6 20.9 %shard_map.109 = (bf16[512,2048]{1,0:T(8,128)(2,1)}, bf16[512,2048]{1,0:T(8,128)(2,1)}) custom-call(s32[8]{0:T(128)} %slice_reduce_fusion.1.refs_0_, s32[128]{0:T(128)} %min.52.refs_1_, f32[8,16,512]{2,1,0:T(8,128)} %select_reduce_fusion.refs_2_.refs_0_, s32[8]{0:T(128)} %negate_maximum_fusion.nch_ref.refs_3_.refs_1_, s32[2176]{0:T(1024)} %min.55.eg_ref.refs_4_.refs_2_, ...), custom_call_target="tpu_custom_call" | custom-call | flops 1048576 | bytes 12582912 | tf_op jit(solution)/shard_map/pallas_call | solution.py:456
  486.5 96.6 %collective-permute-start.13 = (bf16[512,2048]{1,0:T(8,128)(2,1)}, bf16[512,2048]{1,0:T(8,128)(2,1)}, u32[]{:S(2)}, u32[]{:S(2)}) collective-permute-start(bf16[512,2048]{1,0:T(8,128)(2,1)} %get-tuple-element.80), channel_id=1, source_target_pairs={{0,2},{1,3},{2,4},{3,5},{4,6},{5,7},{6,0},{7,1},{8,10},{9,11},{10,... | collective-permute-start | bytes 6291464 | tf_op jit(solution)/shard_map/ppermute | solution.py:726
  583.0 22.6 %shard_map.110 = (bf16[512,2048]{1,0:T(8,128)(2,1)}, bf16[512,2048]{1,0:T(8,128)(2,1)}) custom-call(f32[8,16,512]{2,1,0:T(8,128)} %select_reduce_fusion.refs_2_.refs_0_, s32[8]{0:T(128)} %negate_maximum_fusion.nch_ref.refs_3_.refs_1_, s32[2176]{0:T(1024)} %min.55.eg_ref.refs_4_.refs_2_, s32[8,16,512]{2,1,0:T(8,128)} %add_select_fusion.pos_ref.refs_5_.refs_3_, ...), custom_call_target="tpu_custom_call" | custom-call | flops 1048576 | bytes 12582912 | tf_op jit(solution)/shard_map/pallas_call | solution.py:456
  605.8 2.1 collective-permute-start.18
  607.9 11.2 %shard_map.111 = bf16[512,2048]{1,0:T(8,128)(2,1)} custom-call(s32[8]{0:T(128)} %slice_reduce_fusion.1.refs_0_, s32[128]{0:T(128)} %min.52.refs_1_, f32[8,16,512]{2,1,0:T(8,128)} %select_reduce_fusion.refs_2_.refs_0_, s32[8]{0:T(128)} %negate_maximum_fusion.nch_ref.refs_3_.refs_1_, s32[2176]{0:T(1024)} %min.55.eg_ref.refs_4_.refs_2_, ...), custom_call_target="tpu_custom_call" | custom-call | flops 1048576 | bytes 12582912 | tf_op jit(solution)/shard_map/pallas_call | solution.py:456
  619.1 10.2 %collective-permute-done.13 = bf16[512,2048]{1,0:T(8,128)(2,1)} collective-permute-done((bf16[512,2048]{1,0:T(8,128)(2,1)}, bf16[512,2048]{1,0:T(8,128)(2,1)}, u32[]{:S(2)}, u32[]{:S(2)}) %collective-permute-start.13) | collective-permute-done | bytes 2097184 | tf_op jit(solution)/shard_map/ppermute | solution.py:726
  629.3 2.5 collective-permute-done.14
  631.8 11.4 %shard_map.112 = bf16[512,2048]{1,0:T(8,128)(2,1)} custom-call(s32[8]{0:T(128)} %slice_reduce_fusion.1.refs_0_, s32[128]{0:T(128)} %min.52.refs_1_, f32[8,16,512]{2,1,0:T(8,128)} %select_reduce_fusion.refs_2_.refs_0_, s32[8]{0:T(128)} %negate_maximum_fusion.nch_ref.refs_3_.refs_1_, s32[2176]{0:T(1024)} %min.55.eg_ref.refs_4_.refs_2_, ...), custom_call_target="tpu_custom_call" | custom-call | flops 1048576 | bytes 12582912 | tf_op jit(solution)/shard_map/pallas_call | solution.py:456
  643.3 51.7 %collective-permute-start.17 = (bf16[512,2048]{1,0:T(8,128)(2,1)}, bf16[512,2048]{1,0:T(8,128)(2,1)}, u32[]{:S(2)}, u32[]{:S(2)}) collective-permute-start(bf16[512,2048]{1,0:T(8,128)(2,1)} %shard_map.112), channel_id=1, source_target_pairs={{0,2},{1,3},{2,4},{3,5},{4,6},{5,7},{6,0},{7,1},{8,10},{9,11},{10,... | collective-permute-start | bytes 6291464 | tf_op jit(solution)/shard_map/ppermute | solution.py:726
  695.0 2.0 collective-permute-start.19
  697.0 23.5 %shard_map.113 = (f32[512,2048]{1,0:T(8,128)}, f32[512,2048]{1,0:T(8,128)}) custom-call(s32[8]{0:T(128)} %slice_reduce_fusion.1.refs_0_, s32[128]{0:T(128)} %min.52.refs_1_, f32[8,16,512]{2,1,0:T(8,128)} %select_reduce_fusion.refs_2_.refs_0_, s32[8]{0:T(128)} %negate_maximum_fusion.nch_ref.refs_3_.refs_1_, s32[2176]{0:T(1024)} %min.55.eg_ref.refs_4_.refs_2_, ...), custom_call_target="tpu_custom_call" | custom-call | flops 1048576 | bytes 12582912 | tf_op jit(solution)/shard_map/pallas_call | solution.py:456
  720.5 20.8 %collective-permute-done.17.refs_4_ = bf16[512,2048]{1,0:T(8,128)(2,1)} collective-permute-done((bf16[512,2048]{1,0:T(8,128)(2,1)}, bf16[512,2048]{1,0:T(8,128)(2,1)}, u32[]{:S(2)}, u32[]{:S(2)}) %collective-permute-start.17) | collective-permute-done | bytes 2097184 | tf_op jit(solution)/shard_map/ppermute | solution.py:726
  741.3 2.5 collective-permute-done.16.refs_3_
  743.8 33.4 %collective-permute-done.19.refs_6_ = bf16[512,2048]{1,0:T(8,128)(2,1)} collective-permute-done((bf16[512,2048]{1,0:T(8,128)(2,1)}, bf16[512,2048]{1,0:T(8,128)(2,1)}, u32[]{:S(2)}, u32[]{:S(2)}) %collective-permute-start.19) | collective-permute-done | bytes 2097184 | tf_op jit(solution)/shard_map/ppermute | solution.py:726
  777.2 2.2 collective-permute-done.20.refs_7_
  779.4 12.6 %shard_map.114 = bf16[1024,2048]{1,0:T(8,128)(2,1)} custom-call(bf16[1024,2048]{1,0:T(8,128)(2,1)} %get-tuple-element.52.h_ref, f32[512,2048]{1,0:T(8,128)} %get-tuple-element.85.refs_0_, f32[512,2048]{1,0:T(8,128)} %get-tuple-element.86.refs_1_, bf16[512,2048]{1,0:T(8,128)(2,1)} %collective-permute-done.15.refs_2_, ...), custom_call_target="tpu_custom_call" | custom-call | flops 12582912 | bytes 41943040 | tf_op jit(solution)/shard_map/pallas_call | solution.py:646
  (75 shorter events, 3.4 us)
Async XLA Ops:
  0.0 188.9 %copy-start = (f32[2048,64]{0,1:T(8,128)S(1)}, f32[2048,64]{0,1:T(8,128)}, u32[]{:S(2)}) copy-start(f32[2048,64]{0,1:T(8,128)} %param.15) | copy-start | bytes 1572868
  0.0 7.7 collective-permute-start.2
  2.4 5.3 collective-permute-start.1
  3.7 4.1 collective-permute-start
  4.4 3.4 copy-start.3
  180.7 51.4 %collective-permute-start.6 = (bf16[8,1024,2048]{2,1,0:T(8,128)(2,1)}, bf16[8,1024,2048]{2,1,0:T(8,128)(2,1)}, u32[]{:S(2)}, u32[]{:S(2)}) collective-permute-start(bf16[8,1024,2048]{2,1,0:T(8,128)(2,1)} %refs_11_.1), channel_id=1, source_target_pairs={{0,1},{1,0},{2,3},{3,2},{4,5},{5,4},{6,7},{7,6},{8,9},{9,8},{10,11... | collective-permute-start | bytes 100663304 | tf_op jit(solution)/shard_map/ppermute | solution.py:729
  183.0 54.9 %collective-permute-start.8 = (bf16[512,2048]{1,0:T(8,128)(2,1)}, bf16[512,2048]{1,0:T(8,128)(2,1)}, u32[]{:S(2)}, u32[]{:S(2)}) collective-permute-start(bf16[512,2048]{1,0:T(8,128)(2,1)} %get-tuple-element.66.refs_1_.refs_8_), channel_id=1, source_target_pairs={{0,6},{1,7},{2,0},{3,1},{4,2},{5,3},{6,4},{7,5},{8,14},{9,15},{10,... | collective-permute-start | bytes 6291464 | tf_op jit(solution)/shard_map/ppermute | solution.py:726
  185.1 52.9 %collective-permute-start.7 = (bf16[512,2048]{1,0:T(8,128)(2,1)}, bf16[512,2048]{1,0:T(8,128)(2,1)}, u32[]{:S(2)}, u32[]{:S(2)}) collective-permute-start(bf16[512,2048]{1,0:T(8,128)(2,1)} %get-tuple-element.65.refs_3_.refs_0_.refs_7_), channel_id=1, source_target_pairs={{0,2},{1,3},{2,4},{3,5},{4,6},{5,7},{6,0},{7,1},{8,10},{9,11},{10,... | collective-permute-start | bytes 6291464 | tf_op jit(solution)/shard_map/ppermute | solution.py:726
  185.6 3.5 copy-start.2
  198.2 75.8 %collective-permute-start.5 = (f32[1024,8]{0,1:T(8,128)S(1)}, f32[1024,8]{0,1:T(8,128)S(1)}, u32[]{:S(2)}, u32[]{:S(2)}) collective-permute-start(f32[1024,8]{0,1:T(8,128)S(1)} %fusion.18), channel_id=1, source_target_pairs={{0,4},{1,5},{2,6},{3,7},{4,0},{5,1},{6,2},{7,3},{8,12},{9,13},{10,... | collective-permute-start | bytes 98312 | tf_op jit(solution)/shard_map/ppermute | solution.py:726
  205.6 136.3 %collective-permute-start.10 = (bf16[512,2048]{1,0:T(8,128)(2,1)}, bf16[512,2048]{1,0:T(8,128)(2,1)}, u32[]{:S(2)}, u32[]{:S(2)}) collective-permute-start(bf16[512,2048]{1,0:T(8,128)(2,1)} %get-tuple-element.65.refs_3_.refs_0_.refs_7_), channel_id=1, source_target_pairs={{0,6},{1,7},{2,0},{3,1},{4,2},{5,3},{6,4},{7,5},{8,14},{9,15},{10,... | collective-permute-start | bytes 6291464 | tf_op jit(solution)/shard_map/ppermute | solution.py:726
  232.1 100.7 %collective-permute-start.11 = (bf16[512,2048]{1,0:T(8,128)(2,1)}, bf16[512,2048]{1,0:T(8,128)(2,1)}, u32[]{:S(2)}, u32[]{:S(2)}) collective-permute-start(bf16[512,2048]{1,0:T(8,128)(2,1)} %get-tuple-element.66.refs_1_.refs_8_), channel_id=1, source_target_pairs={{0,2},{1,3},{2,4},{3,5},{4,6},{5,7},{6,0},{7,1},{8,10},{9,11},{10,... | collective-permute-start | bytes 6291464 | tf_op jit(solution)/shard_map/ppermute | solution.py:726
  238.0 118.2 %collective-permute-start.9 = (bf16[512,2048]{1,0:T(8,128)(2,1)}, bf16[512,2048]{1,0:T(8,128)(2,1)}, u32[]{:S(2)}, u32[]{:S(2)}) collective-permute-start(bf16[512,2048]{1,0:T(8,128)(2,1)} %collective-permute-done.7.refs_3_.refs_0_), channel_id=1, source_target_pairs={{0,2},{1,3},{2,4},{3,5},{4,6},{5,7},{6,0},{7,1},{8,10},{9,11},{10,... | collective-permute-start | bytes 6291464 | tf_op jit(solution)/shard_map/ppermute | solution.py:726
  270.3 85.8 %collective-permute-start.12 = (bf16[512,2048]{1,0:T(8,128)(2,1)}, bf16[512,2048]{1,0:T(8,128)(2,1)}, u32[]{:S(2)}, u32[]{:S(2)}) collective-permute-start(bf16[512,2048]{1,0:T(8,128)(2,1)} %collective-permute-done.8.refs_1_.refs_3_), channel_id=1, source_target_pairs={{0,6},{1,7},{2,0},{3,1},{4,2},{5,3},{6,4},{7,5},{8,14},{9,15},{10,... | collective-permute-start | bytes 6291464 | tf_op jit(solution)/shard_map/ppermute | solution.py:726
  270.3 62.5 %copy-start.4 = (s32[100]{0:T(128)}, s32[100]{0:T(128)S(1)}, u32[]{:S(2)}) copy-start(s32[100]{0:T(128)S(1)} %broadcast_minimum_fusion.3.tl_ref) | copy-start | bytes 1204
  274.0 48.2 %collective-permute-start.4 = (f32[1024,8]{0,1:T(8,128)S(1)}, f32[1024,8]{0,1:T(8,128)S(1)}, u32[]{:S(2)}, u32[]{:S(2)}) collective-permute-start(f32[1024,8]{0,1:T(8,128)S(1)} %fusion.18), channel_id=1, source_target_pairs={{0,6},{1,7},{2,0},{3,1},{4,2},{5,3},{6,4},{7,5},{8,14},{9,15},{10,... | collective-permute-start | bytes 98312 | tf_op jit(solution)/shard_map/ppermute | solution.py:726
  322.2 4.2 collective-permute-start.3
  486.5 142.9 %collective-permute-start.13 = (bf16[512,2048]{1,0:T(8,128)(2,1)}, bf16[512,2048]{1,0:T(8,128)(2,1)}, u32[]{:S(2)}, u32[]{:S(2)}) collective-permute-start(bf16[512,2048]{1,0:T(8,128)(2,1)} %get-tuple-element.80), channel_id=1, source_target_pairs={{0,2},{1,3},{2,4},{3,5},{4,6},{5,7},{6,0},{7,1},{8,10},{9,11},{10,... | collective-permute-start | bytes 6291464 | tf_op jit(solution)/shard_map/ppermute | solution.py:726
  583.0 48.8 %collective-permute-start.14 = (bf16[512,2048]{1,0:T(8,128)(2,1)}, bf16[512,2048]{1,0:T(8,128)(2,1)}, u32[]{:S(2)}, u32[]{:S(2)}) collective-permute-start(bf16[512,2048]{1,0:T(8,128)(2,1)} %get-tuple-element.81), channel_id=1, source_target_pairs={{0,6},{1,7},{2,0},{3,1},{4,2},{5,3},{6,4},{7,5},{8,14},{9,15},{10,... | collective-permute-start | bytes 6291464 | tf_op jit(solution)/shard_map/ppermute | solution.py:726
  605.6 91.3 %collective-permute-start.15 = (bf16[512,2048]{1,0:T(8,128)(2,1)}, bf16[512,2048]{1,0:T(8,128)(2,1)}, u32[]{:S(2)}, u32[]{:S(2)}) collective-permute-start(bf16[512,2048]{1,0:T(8,128)(2,1)} %get-tuple-element.87), channel_id=1, source_target_pairs={{0,6},{1,7},{2,0},{3,1},{4,2},{5,3},{6,4},{7,5},{8,14},{9,15},{10,... | collective-permute-start | bytes 6291464 | tf_op jit(solution)/shard_map/ppermute | solution.py:726
  605.8 114.7 %collective-permute-start.18 = (bf16[512,2048]{1,0:T(8,128)(2,1)}, bf16[512,2048]{1,0:T(8,128)(2,1)}, u32[]{:S(2)}, u32[]{:S(2)}) collective-permute-start(bf16[512,2048]{1,0:T(8,128)(2,1)} %get-tuple-element.90), channel_id=1, source_target_pairs={{0,2},{1,3},{2,4},{3,5},{4,6},{5,7},{6,0},{7,1},{8,10},{9,11},{10,... | collective-permute-start | bytes 6291464 | tf_op jit(solution)/shard_map/ppermute | solution.py:726
  643.3 98.0 %collective-permute-start.17 = (bf16[512,2048]{1,0:T(8,128)(2,1)}, bf16[512,2048]{1,0:T(8,128)(2,1)}, u32[]{:S(2)}, u32[]{:S(2)}) collective-permute-start(bf16[512,2048]{1,0:T(8,128)(2,1)} %shard_map.112), channel_id=1, source_target_pairs={{0,2},{1,3},{2,4},{3,5},{4,6},{5,7},{6,0},{7,1},{8,10},{9,11},{10,... | collective-permute-start | bytes 6291464 | tf_op jit(solution)/shard_map/ppermute | solution.py:726
  694.9 48.8 %collective-permute-start.16 = (bf16[512,2048]{1,0:T(8,128)(2,1)}, bf16[512,2048]{1,0:T(8,128)(2,1)}, u32[]{:S(2)}, u32[]{:S(2)}) collective-permute-start(bf16[512,2048]{1,0:T(8,128)(2,1)} %shard_map.111), channel_id=1, source_target_pairs={{0,6},{1,7},{2,0},{3,1},{4,2},{5,3},{6,4},{7,5},{8,14},{9,15},{10,... | collective-permute-start | bytes 6291464 | tf_op jit(solution)/shard_map/ppermute | solution.py:726
  695.0 82.2 %collective-permute-start.19 = (bf16[512,2048]{1,0:T(8,128)(2,1)}, bf16[512,2048]{1,0:T(8,128)(2,1)}, u32[]{:S(2)}, u32[]{:S(2)}) collective-permute-start(bf16[512,2048]{1,0:T(8,128)(2,1)} %collective-permute-done.13), channel_id=1, source_target_pairs={{0,2},{1,3},{2,4},{3,5},{4,6},{5,7},{6,0},{7,1},{8,10},{9,11},{10,... | collective-permute-start | bytes 6291464 | tf_op jit(solution)/shard_map/ppermute | solution.py:726
  697.0 82.4 %collective-permute-start.20 = (bf16[512,2048]{1,0:T(8,128)(2,1)}, bf16[512,2048]{1,0:T(8,128)(2,1)}, u32[]{:S(2)}, u32[]{:S(2)}) collective-permute-start(bf16[512,2048]{1,0:T(8,128)(2,1)} %collective-permute-done.14), channel_id=1, source_target_pairs={{0,6},{1,7},{2,0},{3,1},{4,2},{5,3},{6,4},{7,5},{8,14},{9,15},{10,... | collective-permute-start | bytes 6291464 | tf_op jit(solution)/shard_map/ppermute | solution.py:726
  779.4 12.6 %copy-start.1 = (f32[2048,64]{0,1:T(8,128)S(1)}, f32[2048,64]{0,1:T(8,128)}, u32[]{:S(2)}) copy-start(f32[2048,64]{0,1:T(8,128)} %param.15) | copy-start | bytes 1572868

commit v4 on v3

--- a/solution.py
+++ b/solution.py
@@ -11,9 +11,9 @@
 HEAD = 128
 EPS = 1e-6
 THETA = 10000.0
-PIECE = 16
+PIECE = 8
 CHUNK = 256
-MT = 416
+MT = 352
 HM = 256
 VMEM = 66_000_000
 BF, F32, I32 = jnp.bfloat16, jnp.float32, jnp.int32
@@ -29,6 +29,7 @@
 
 
 NT = (((1,), (1,)), ((), ()))
+TN = (((0,), (0,)), ((), ()))
 DMA2 = pltpu.SemaphoreType.DMA((2,))
 
 
@@ -125,13 +126,17 @@
         for k in (LB, RT):
             arrive(w, k)
             across(w, k).start()
-        swap()
+        if w != 2:
+            swap()
+        if w == 3:
+            swap()
 
     def stage_c(w):
         for k in (OT, OB):
             arrive(w, k)
             across(w, k).start()
-        swap()
+        if w != 2:
+            swap()
 
     def stage_d(w):
         for k in (PO, PASS + LT, PASS + RB, PASS + LB, PASS + RT, PASS + OT, PASS + OB):
@@ -180,44 +185,37 @@
         stage_c(w)
         stage_d(w)
         swap()
+        if w == 2:
+            swap()
         project(w, dst, rope)
     stage_a(3)
 
     tq = min(256, t)
-    scale = 1.0 / math.sqrt(HEAD)
-    causal = lax.broadcasted_iota(I32, (tq, tq), 1) <= lax.broadcasted_iota(I32, (tq, tq), 0)
-
-    def heads(lo, hi):
-        @pl.loop(lo, hi)
-        def _(j):
-            c = pl.ds(pl.multiple_of(j * HEAD, HEAD), HEAD)
+    scale = math.log2(math.e) / math.sqrt(HEAD)
+    causal = lax.broadcasted_iota(I32, (tq, tq), 0) <= lax.broadcasted_iota(I32, (tq, tq), 1)
+    group = min(4, d // HEAD)
+    steps = d // HEAD // group
+    marks = {1: stage_b, steps - 1: stage_c}
+    if len(marks) > steps - 1:
+        marks = {}
+        stage_b(3)
+        stage_c(3)
+
+    @loop(steps)
+    def _(jj):
+        for at, stage in marks.items():
+            pl.when(jj == at)(functools.partial(stage, 3))
+        for j in range(group):
+            c = pl.ds(pl.multiple_of((jj * group + j) * HEAD, HEAD), HEAD)
             for i in range(t // tq):
-                r = slice(i * tq, (i + 1) * tq)
-                q = qb[r, c]
-                sd = lax.dot_general(q, kb[r, c], NT, preferred_element_type=F32)
-                sd = jnp.where(causal, sd, -jnp.inf)
-                m = jnp.max(sd, axis=1, keepdims=True)
-                if i:
-                    so = lax.dot_general(q, kb[:i * tq, c], NT, preferred_element_type=F32)
-                    m = jnp.maximum(m, jnp.max(so, axis=1, keepdims=True))
-                pd = jnp.exp((sd - m) * scale)
-                l = jnp.sum(pd, axis=1, keepdims=True)
-                if i:
-                    po = jnp.exp((so - m) * scale)
-                    l = l + jnp.sum(po, axis=1, keepdims=True)
-                inv = 1.0 / l
-                o = dot((pd * inv).astype(BF), vb[r, c])
-                if i:
-                    o = o + dot((po * inv).astype(BF), vb[:i * tq, c])
-                qb[r, c] = o.astype(BF)
-
-    nh = d // HEAD
-    cut1, cut2 = nh * 3 // 8, nh * 3 // 4
-    heads(0, cut1)
-    stage_b(3)
-    heads(cut1, cut2)
-    stage_c(3)
-    heads(cut2, nh)
+                r, n = slice(i * tq, (i + 1) * tq), (i + 1) * tq
+                sc = lax.dot_general(kb[:n, c], qb[r, c], NT, preferred_element_type=F32)
+                diag = jnp.where(causal, sc[i * tq:], -jnp.inf)
+                sc = jnp.concatenate([sc[:i * tq], diag], axis=0) if i else diag
+                p = jnp.exp2((sc - jnp.max(sc, axis=0, keepdims=True)) * scale)
+                p = (p * (1.0 / jnp.sum(p, axis=0, keepdims=True))).astype(BF)
+                qb[r, c] = lax.dot_general(p, vb[:n, c], TN, preferred_element_type=F32).astype(BF)
+
     xin = pltpu.make_async_copy(x_ref, vb, iosem.at[0])
     xin.start()
     stage_d(3)
@@ -361,8 +359,8 @@
             get(0, 0).start()
             nl = gt_ref.shape[1]
             lane = lax.broadcasted_iota(I32, (1, CHUNK), 1)
-            ti = lax.broadcasted_iota(I32, (PIECE, t), 1)
-            si = lax.broadcasted_iota(I32, (PIECE, t), 0)
+            ti = lax.broadcasted_iota(I32, (16, t), 1)
+            si = lax.broadcasted_iota(I32, (16, t), 0)
             tparts = jnp.where(si == 0, ti % 256, jnp.where(si == 1, ti // 256, 0)).astype(F32).astype(BF)
             table = jnp.concatenate([*split3(gt_ref[j]), tparts], axis=0)
 
@@ -374,11 +372,11 @@
                 def _():
                     get(i + 1, 1 - slot).start()
 
-                ps, el = [], jnp.zeros((1, CHUNK), I32)
-                for q, (hit, l) in enumerate(selection(j, i, eg_ref, pos_ref)):
-                    ps.append(jnp.where(hit, 1.0, 0.0).astype(BF))
+                pm, ls = selection(j, i, eg_ref, pos_ref)
+                el = jnp.zeros_like(lane)
+                for q, l in enumerate(ls):
                     el = jnp.where(lane // PIECE == q, l, el)
-                sel = lax.dot_general(table, jnp.concatenate(ps, axis=0), NT, preferred_element_type=F32)
+                sel = lax.dot_general(table, pm, NT, preferred_element_type=F32)
                 tok = (sel[3 * nl:3 * nl + 1] + 256.0 * sel[3 * nl + 1:3 * nl + 2]).astype(I32)
                 hot_ = lax.broadcasted_iota(I32, (t, CHUNK), 0) == tok
                 sub = lax.broadcasted_iota(I32, (nl, CHUNK), 0) == el
@@ -420,8 +418,15 @@
                 gc = jnp.sum(jnp.where(eye, g, 0.0), axis=1, keepdims=True)
                 acc[rows, :] += gc * z.astype(F32)
 
-    for p in range(nblk):
-        outs[p][:] = acc[p * t:(p + 1) * t, :].astype(outs[p].dtype)
+    if outs[0].dtype == F32:
+        done = [pltpu.make_async_copy(acc.at[pl.ds(p * t, t), :], outs[p], asem.at[p]) for p in range(nblk)]
+        for cp in done:
+            cp.start()
+        for cp in done:
+            cp.wait()
+    else:
+        for p in range(nblk):
+            outs[p][:] = acc[p * t:(p + 1) * t, :].astype(BF)
 
 
 def block(js, r, z, us, accs, own, other, dtype, dense, comb=True):
@@ -455,7 +460,7 @@
     out = jax.ShapeDtypeStruct((t, d), dtype)
     return pl.pallas_call(
         functools.partial(block_kernel, js, [v is not None for v in accs], comb, dense),
-        in_specs=specs, out_specs=[vm] * nblk, out_shape=[out] * nblk, scratch_shapes=scratch,
+        in_specs=specs, out_specs=[hb if dtype == F32 else vm] * nblk, out_shape=[out] * nblk, scratch_shapes=scratch,
         compiler_params=params(),
         cost_estimate=cost(t * d, 6 * d * ff),
     )(*args)
@@ -471,12 +476,16 @@
 
 def selection(j, i, eg_ref, pos_ref):
     t = pos_ref.shape[2]
-    it = lax.broadcasted_iota(I32, (PIECE, t), 0)
+    it = lax.broadcasted_iota(I32, (2 * PIECE, t), 0)
     npc = CHUNK // PIECE
-    npb = eg_ref.shape[0] // pos_ref.shape[0]
-    for q in range(npc):
-        l = eg_ref[j * npb + i * npc + q]
-        yield pos_ref[j, pl.ds(l, 1), :] - (i * CHUNK + q * PIECE) == it, l
+    first = (j * (eg_ref.shape[0] // pos_ref.shape[0] // npc) + i) * npc
+    ls = [eg_ref[first + q] for q in range(npc)]
+    hits = []
+    for q in range(0, npc, 2):
+        own, nxt = [pos_ref[j, pl.ds(l, 1), :] for l in ls[q:q + 2]]
+        hit = jnp.where(it < PIECE, own, nxt) - (i * CHUNK + q * PIECE) == it
+        hits.append(jnp.where(hit, 1.0, 0.0).astype(BF))
+    return jnp.concatenate(hits, axis=0), ls
 
 
 def gather_kernel(js, nch_ref, eg_ref, pos_ref, *refs):
@@ -498,8 +507,7 @@
             def _():
                 out(i - 2, slot).wait()
 
-            pm = jnp.concatenate([jnp.where(hit, 1.0, 0.0).astype(BF) for hit, _ in selection(j, i, eg_ref, pos_ref)], axis=0)
-            xbuf[slot] = dot(pm, us[p][:]).astype(BF)
+            xbuf[slot] = dot(selection(j, i, eg_ref, pos_ref)[0], us[p][:]).astype(BF)
             out(i, slot).start()
 
         for k in (2, 1):
@@ -533,23 +541,35 @@
     bufs, (xbuf, zbuf, wsem, xsem, zsem) = refs[:3], refs[3:]
     nt = nt_ref[0]
 
+    def each(n, fn):
+        @loop(lax.div(n, 2))
+        def _(i):
+            fn(2 * i)
+            fn(2 * i + 1)
+
+        @pl.when(parity(n) == 1)
+        def _():
+            fn(n - 1)
+
     def xin(q, slot):
         p0 = tp_ref[q]
 
-        @loop(tn_ref[q])
-        def _(i):
+        def one(i):
             src = pl.ds(pl.multiple_of(pc_ref[p0 + i] * PIECE, PIECE), PIECE)
             dst = pl.ds(pl.multiple_of(i * PIECE, PIECE), PIECE)
             pltpu.make_async_copy(x_ref.at[src, :], xbuf.at[slot, dst, :], xsem.at[slot]).start()
 
+        each(tn_ref[q], one)
+
     def zout(q, slot):
         p0 = tp_ref[q]
 
-        @loop(tn_ref[q])
-        def _(i):
+        def one(i):
             src = pl.ds(pl.multiple_of(i * PIECE, PIECE), PIECE)
             dst = pl.ds(pl.multiple_of(pc_ref[p0 + i] * PIECE, PIECE), PIECE)
             pltpu.make_async_copy(zbuf.at[slot, src, :], z_ref.at[dst, :], zsem.at[slot]).start()
+
+        each(tn_ref[q], one)
 
     def drain(n, fn):
         bit = 1
@@ -772,30 +792,28 @@
         a0, = block((0,), ra, None, (ut,), (None,), own, other, F32, ON, comb=False)
         a0, x, u1t, u2b = lax.optimization_barrier((a0, x, u1t, u2b))
         u3t, u3b = shift(u1t, 1), shift(u2b, -1)
-        d2, = block((2,), r, None, (u1t,), (None,), own, other, F32, ON, comb=False)
+        d2, d5 = block((2, 5), r, None, (u1t, u2b), (None, None), own, other, F32, 2 * ON, comb=False)
         u1b, d2 = lax.optimization_barrier((u1b, d2))
         x = gather(R, r, (u1t, u1b), x)
         x = gather(L, r, (u2t, u2b), x)
-        u2bx, x = lax.optimization_barrier((u2b, x))
-        d5, = block((5,), r, None, (u2bx,), (None,), own, other, F32, ON, comb=False)
-        u3t, d5 = lax.optimization_barrier((u3t, d5))
+        u3t, x = lax.optimization_barrier((u3t, x))
         x = gather(O, r, (u3t, u3b), x)
         z = cold(plan, x, own, other)
 
         tie = lambda r, *v: (lambda w: (r._replace(nch=w[0]), *w[1:]))(lax.optimization_barrier((r.nch, *v)))
+        b2, b5 = block((2, 5), r, z, (), (d2, d5), own, other, BF, (False, False))
+        r, b2, b5 = tie(r, b2, b5)
+        b2, b5 = shift(b2, -1), shift(b5, 1)
         b6, b7 = block(O, r, z, (u3t, u3b), (None, None), own, other, BF, 2 * ON)
         r, b6, b7 = tie(r, b6, b7)
         c6, c7 = shift(b6, 1), shift(b7, -1)
-        b2, b5 = block((2, 5), r, z, (), (d2, d5), own, other, BF, (False, False))
-        r, b2, b5 = tie(r, b2, b5)
-        b2, b5 = shift(b2, -1), shift(b5, 1)
         b3, = block((3,), r, z, (u1b,), (None,), own, other, BF, ON)
-        r, b3, c6, c7 = tie(r, b3, c6, c7)
-        b6, b7 = shift(c6, 1), shift(c7, -1)
+        r, b3 = tie(r, b3)
         b3 = shift(b3, -1)
         b4, = block((4,), r, z, (u2t,), (None,), own, other, BF, ON)
-        r, b4 = tie(r, b4)
+        r, b4, c6, c7 = tie(r, b4, c6, c7)
         b4 = shift(b4, 1)
+        b6, b7 = shift(c6, 1), shift(c7, -1)
         accs = block(A, r, z, (ut, ub), (a0, None), own, other, F32, (False, True))
         y = final(h, accs, [(b2, b3), (b4, b5), (b6, b7)])
         return y.reshape(b, s, d)

time: 796 us -> 772 us (0.970)
  the two profiles are of different devices: /device:TPU:122 before, /device:TPU:113 now
where the time goes in v4:
time: 772 us; the launch traced here: 767 us
  Pallas kernels  601 us (78%)
  waiting for transfers between devices  108 us (14%)
  starting transfers between devices  23.3 us (3%)
  other arithmetic  21.3 us (3%)
  matrix products  8.98 us (1%)
    pallas_call x7, Pallas kernels, block(): pl.pallas_call(functools.partial(block_kernel, js, [v is not None for v i...  322 us
    pallas_call x1, Pallas kernels, attention_layer(): pl.pallas_call(functools.partial(layer_kernel, nx), in_specs=[hb] * 5 + [...  168 us
    ppermute x20, waiting for transfers between devices, shift(): lax.ppermute(v, 'ep', [(2 * i + c, 2 * ((i + s) % nx) + c) for i in range...  92 us
    pallas_call x1, Pallas kernels, cold(): pl.pallas_call(cold_kernel, in_specs=[sm] * len(plan) + [hb] * 7, out_spe...  70 us
    pallas_call x4, Pallas kernels, gather(): pl.pallas_call(functools.partial(gather_kernel, js), in_specs=[sm, sm, vm...  29.1 us
    ppermute x20, starting transfers between devices, shift(): lax.ppermute(v, 'ep', [(2 * i + c, 2 * ((i + s) % nx) + c) for i in range...  22.2 us
    ppermute x1, waiting for transfers between devices, partner(): return lax.ppermute(v, 'ep', [(i, i ^ 1) for i in range(nd)])  15.9 us
  transfers between devices with their start and end apart: 21, of which 5 were waited for; matrix products, arithmetic and copies ran while one was open for 4% of the time, Pallas kernels for 33%

profile of v4, /device:TPU:113, one launch (start us, length us, event | category | flops | bytes accessed | tf_op | source)
XLA Modules:
  0.0 766.9 jit_solution(9233764613915791342)
XLA Ops:
  0.0 1.3 collective-permute-start
  1.4 1.6 collective-permute-start.1
  3.0 1.5 collective-permute-start.2
  4.5 1.9 fusion.6
  6.4 1.3 pad_maximum_fusion
  7.8 167.9 %shard_map.100 = (bf16[1024,2048]{1,0:T(8,128)(2,1)}, bf16[512,2048]{1,0:T(8,128)(2,1)}, bf16[512,2048]{1,0:T(8,128)(2,1)}, bf16[8,2048,1024]{2,1,0:T(8,128)(2,1)}, bf16[8,2048,1024]{2,1,0:T(8,128)(2,1)}) custom-call(bf16[1024,2048]{1,0:T(8,128)(2,1)} %bitcast.48, bf16[256,2048]{1,0:T(8,128)(2,1)} %wv_ref.1, bf16[256,2048]{1,0:T(8,128)(2,1)} %wk_ref.1, ...), custom_call_target="tpu_custom_call" | custom-call | flops 34359738368 | bytes 50331648 | tf_op jit(solution)/shard_map/pallas_call | solution.py:262
  175.7 1.1 collective-permute-start.6
  177.0 1.2 fusion.3
  178.2 0.2 convolution_convert_fusion
  178.4 0.3 slice_reduce_fusion
  178.7 0.2 reduce_window_sum.38
  178.9 0.2 reduce_window_sum.37
  179.1 0.5 collective-permute-start.7
  179.5 2.3 collective-permute-start.8
  181.8 3.1 fusion
  184.9 8.7 %fusion.1 = f32[1024,64]{0,1:T(8,128)S(1)} fusion(f32[2048,64]{0,1:T(8,128)S(1)} %copy-done, bf16[1024,2048]{1,0:T(8,128)(2,1)S(1)} %copy-done.2, f32[1024]{0:T(1024)S(1)} %add_rsqrt_fusion), kind=kOutput, calls=%fused_computation.3 | convolution fusion | flops 1614807040 | bytes 4984832 | tf_op jit(solution)/shard_map/dot_general | solution.py:781
  193.6 0.3 select_reduce_fusion.2
  193.9 0.2 convert_reduce_fusion.2
  194.5 0.7 min.55.eg_ref.refs_2_.refs_4_
  195.2 0.6 min.52.refs_1_
  195.8 0.4 collective-permute-start.4
  196.2 1.0 collective-permute-start.11
  198.0 0.2 multiply_reduce_fusion
  198.2 0.3 fusion.17
  198.5 0.3 fusion.15
  198.8 0.5 negate_maximum_fusion.nch_ref.refs_1_.refs_3_
  199.3 0.8 add_select_fusion.pos_ref.refs_3_.refs_5_
  200.2 7.2 shard_map.102.refs_2_
  207.4 0.7 slice_reduce_fusion.1.refs_0_
  208.2 1.7 select_reduce_fusion.3.refs_2_
  210.0 15.9 %collective-permute-done.6.refs_9_.refs_10_.refs_5_.refs_14_.refs_13_ = bf16[8,1024,2048]{2,1,0:T(8,128)(2,1)} collective-permute-done((bf16[8,1024,2048]{2,1,0:T(8,128)(2,1)}, bf16[8,1024,2048]{2,1,0:T(8,128)(2,1)}, u32[]{:S(2)}, u32[]{:S(2)}) %collective-permute-start.6) | collective-permute-done | bytes 33554464 | tf_op jit(solution)/shard_map/ppermute | solution.py:749
  225.9 1.6 collective-permute-start.10
  227.5 35.7 %shard_map.101.refs_15_ = f32[512,2048]{1,0:T(8,128)} custom-call(s32[8]{0:T(128)} %slice_reduce_fusion.1.refs_0_, s32[128]{0:T(128)} %min.52.refs_1_, f32[2,16,512]{2,1,0:T(8,128)} %select_reduce_fusion.3.refs_2_, bf16[512,2048]{1,0:T(8,128)(2,1)} %get-tuple-element.64.refs_3_.refs_0_.refs_7_, bf16[8,2048,1024]{2,1,0:T(8,128)(2,1)} %refs_9_.7, ...), custom_call_target="tpu_custom_call" | custom-call | flops 1048576 | bytes 12582912 | tf_op jit(solution)/shard_map/pallas_call | solution.py:461
  263.4 2.6 collective-permute-start.12
  266.5 0.2 reduce-window.32
  266.7 0.7 select_reduce_fusion.4
  267.4 0.6 convert_reduce_fusion
  268.1 2.6 select_reduce_fusion
  270.7 0.6 add_clamp_fusion.pc_ref
  271.3 0.5 subtract_clamp_fusion
  271.8 0.6 compare_convert_fusion.1.tf_ref
  272.4 45.7 %collective-permute-done.5 = f32[1024,8]{0,1:T(8,128)S(1)} collective-permute-done((f32[1024,8]{0,1:T(8,128)S(1)}, f32[1024,8]{0,1:T(8,128)S(1)}, u32[]{:S(2)}, u32[]{:S(2)}) %collective-permute-start.5) | collective-permute-done | bytes 32800 | tf_op jit(solution)/shard_map/ppermute | solution.py:746
  318.1 1.7 collective-permute-start.3
  319.8 0.5 compare_select_fusion.2.nx_ref
  320.3 0.5 slice.25
  320.8 1.2 collective-permute-done.3
  322.1 1.6 select_reduce_fusion.1.refs_2_.refs_0_
  323.6 65.3 %shard_map.103 = (f32[512,2048]{1,0:T(8,128)}, f32[512,2048]{1,0:T(8,128)}) custom-call(s32[8]{0:T(128)} %slice_reduce_fusion.1.refs_0_, s32[128]{0:T(128)} %min.52.refs_1_, f32[8,16,512]{2,1,0:T(8,128)} %select_reduce_fusion.1.refs_2_.refs_0_, bf16[512,2048]{1,0:T(8,128)(2,1)} %collective-permute-done.7.refs_3_.refs_0_, ...), custom_call_target="tpu_custom_call" | custom-call | flops 1048576 | bytes 12582912 | tf_op jit(solution)/shard_map/pallas_call | solution.py:461
  388.9 7.2 shard_map.104.refs_2_
  396.2 7.5 shard_map.105.refs_2_
  403.6 7.2 shard_map.106.x_ref
  410.9 70.0 %shard_map.107.refs_4_.refs_6_ = bf16[34816,2048]{1,0:T(8,128)(2,1)} custom-call(s32[1]{0:T(128)} %bitcast.15.nt_ref, s32[115]{0:T(128)} %copy-done.4, s32[115]{0:T(128)} %get-tuple-element.108.tp_ref, s32[115]{0:T(128)} %get-tuple-element.107.tn_ref, s32[115]{0:T(128)} %get-tuple-element.94.tw_ref, ...), custom_call_target="tpu_custom_call", output_to_operand_aliasing={{}: (8, {})} | custom-call | flops 70866960384 | bytes 201326592 | tf_op jit(solution)/shard_map/pallas_call | solution.py:630
  480.9 17.9 %shard_map.108 = (bf16[512,2048]{1,0:T(8,128)(2,1)}, bf16[512,2048]{1,0:T(8,128)(2,1)}) custom-call(f32[8,16,512]{2,1,0:T(8,128)} %select_reduce_fusion.1.refs_2_.refs_0_, s32[8]{0:T(128)} %negate_maximum_fusion.nch_ref.refs_1_.refs_3_, s32[4352]{0:T(1024)} %min.55.eg_ref.refs_2_.refs_4_, s32[8,16,512]{2,1,0:T(8,128)} %add_select_fusion.pos_ref.refs_3_.refs_5_, ...), custom_call_target="tpu_custom_call" | custom-call | flops 1048576 | bytes 12582912 | tf_op jit(solution)/shard_map/pallas_call | solution.py:461
  498.7 73.0 %shard_map.109 = (bf16[512,2048]{1,0:T(8,128)(2,1)}, bf16[512,2048]{1,0:T(8,128)(2,1)}) custom-call(s32[8]{0:T(128)} %slice_reduce_fusion.1.refs_0_, s32[128]{0:T(128)} %min.52.refs_1_, f32[8,16,512]{2,1,0:T(8,128)} %select_reduce_fusion.1.refs_2_.refs_0_, s32[8]{0:T(128)} %negate_maximum_fusion.nch_ref.refs_1_.refs_3_, s32[4352]{0:T(1024)} %min.55.eg_ref.refs_2_.refs_4_, ...), custom_call_target="tpu_custom_call" | custom-call | flops 1048576 | bytes 12582912 | tf_op jit(solution)/shard_map/pallas_call | solution.py:461
  571.9 2.6 collective-permute-start.14
  574.6 40.1 %shard_map.110 = bf16[512,2048]{1,0:T(8,128)(2,1)} custom-call(s32[8]{0:T(128)} %slice_reduce_fusion.1.refs_0_, s32[128]{0:T(128)} %min.52.refs_1_, f32[8,16,512]{2,1,0:T(8,128)} %select_reduce_fusion.1.refs_2_.refs_0_, s32[8]{0:T(128)} %negate_maximum_fusion.nch_ref.refs_1_.refs_3_, s32[4352]{0:T(1024)} %min.55.eg_ref.refs_2_.refs_4_, ...), custom_call_target="tpu_custom_call" | custom-call | flops 1048576 | bytes 12582912 | tf_op jit(solution)/shard_map/pallas_call | solution.py:461
  614.9 1.4 collective-permute-start.18
  616.4 40.1 %shard_map.111 = bf16[512,2048]{1,0:T(8,128)(2,1)} custom-call(s32[8]{0:T(128)} %slice_reduce_fusion.1.refs_0_, s32[128]{0:T(128)} %min.52.refs_1_, f32[8,16,512]{2,1,0:T(8,128)} %select_reduce_fusion.1.refs_2_.refs_0_, s32[8]{0:T(128)} %negate_maximum_fusion.nch_ref.refs_1_.refs_3_, s32[4352]{0:T(1024)} %min.55.eg_ref.refs_2_.refs_4_, ...), custom_call_target="tpu_custom_call" | custom-call | flops 1048576 | bytes 12582912 | tf_op jit(solution)/shard_map/pallas_call | solution.py:461
  656.6 0.3 collective-permute-start.19
  656.9 5.8 collective-permute-done.16.refs_3_
  662.7 2.7 collective-permute-start.20
  665.4 49.4 %shard_map.112 = (f32[512,2048]{1,0:T(8,128)}, f32[512,2048]{1,0:T(8,128)}) custom-call(s32[8]{0:T(128)} %slice_reduce_fusion.1.refs_0_, s32[128]{0:T(128)} %min.52.refs_1_, f32[8,16,512]{2,1,0:T(8,128)} %select_reduce_fusion.1.refs_2_.refs_0_, s32[8]{0:T(128)} %negate_maximum_fusion.nch_ref.refs_1_.refs_3_, s32[4352]{0:T(1024)} %min.55.eg_ref.refs_2_.refs_4_, ...), custom_call_target="tpu_custom_call" | custom-call | flops 1048576 | bytes 12582912 | tf_op jit(solution)/shard_map/pallas_call | solution.py:461
  714.8 39.2 %collective-permute-done.19.refs_6_ = bf16[512,2048]{1,0:T(8,128)(2,1)} collective-permute-done((bf16[512,2048]{1,0:T(8,128)(2,1)}, bf16[512,2048]{1,0:T(8,128)(2,1)}, u32[]{:S(2)}, u32[]{:S(2)}) %collective-permute-start.19) | collective-permute-done | bytes 2097184 | tf_op jit(solution)/shard_map/ppermute | solution.py:746
  754.1 12.6 %shard_map.113 = bf16[1024,2048]{1,0:T(8,128)(2,1)} custom-call(bf16[1024,2048]{1,0:T(8,128)(2,1)} %get-tuple-element.52.h_ref, f32[512,2048]{1,0:T(8,128)} %get-tuple-element.85.refs_0_, f32[512,2048]{1,0:T(8,128)} %get-tuple-element.86.refs_1_, bf16[512,2048]{1,0:T(8,128)(2,1)} %collective-permute-done.15.refs_2_, ...), custom_call_target="tpu_custom_call" | custom-call | flops 12582912 | bytes 41943040 | tf_op jit(solution)/shard_map/pallas_call | solution.py:666
  (74 shorter events, 2.6 us)
Async XLA Ops:
  0.0 184.9 %copy-start = (f32[2048,64]{0,1:T(8,128)S(1)}, f32[2048,64]{0,1:T(8,128)}, u32[]{:S(2)}) copy-start(f32[2048,64]{0,1:T(8,128)} %param.15) | copy-start | bytes 1572868
  0.0 7.8 %copy-start.3 = (s32[1,1024,8]{1,2,0:T(8,128)S(1)}, s32[1,1024,8]{1,2,0:T(8,128)}, u32[]{:S(2)}) copy-start(s32[1,1024,8]{1,2,0:T(8,128)} %param.19) | copy-start | bytes 98308
  0.0 7.7 %collective-permute-start = (s32[1024,8]{0,1:T(8,128)}, s32[1024,8]{0,1:T(8,128)S(1)}, u32[]{:S(2)}, u32[]{:S(2)}) collective-permute-start(s32[1024,8]{0,1:T(8,128)} %bitcast.35), channel_id=1, source_target_pairs={{0,2},{1,3},{2,4},{3,5},{4,6},{5,7},{6,0},{7,1},{8,10},{9,11},{10,... | collective-permute-start | bytes 98312 | tf_op jit(solution)/shard_map/ppermute | solution.py:746
  1.4 6.4 collective-permute-start.1
  3.0 4.7 collective-permute-start.2
  175.7 50.2 %collective-permute-start.6 = (bf16[8,1024,2048]{2,1,0:T(8,128)(2,1)}, bf16[8,1024,2048]{2,1,0:T(8,128)(2,1)}, u32[]{:S(2)}, u32[]{:S(2)}) collective-permute-start(bf16[8,1024,2048]{2,1,0:T(8,128)(2,1)} %refs_11_.1), channel_id=1, source_target_pairs={{0,1},{1,0},{2,3},{3,2},{4,5},{5,4},{6,7},{7,6},{8,9},{9,8},{10,11... | collective-permute-start | bytes 100663304 | tf_op jit(solution)/shard_map/ppermute | solution.py:749
  179.1 5.8 copy-start.2
  179.1 84.2 %collective-permute-start.7 = (bf16[512,2048]{1,0:T(8,128)(2,1)}, bf16[512,2048]{1,0:T(8,128)(2,1)}, u32[]{:S(2)}, u32[]{:S(2)}) collective-permute-start(bf16[512,2048]{1,0:T(8,128)(2,1)} %get-tuple-element.64.refs_3_.refs_0_.refs_7_), channel_id=1, source_target_pairs={{0,2},{1,3},{2,4},{3,5},{4,6},{5,7},{6,0},{7,1},{8,10},{9,11},{10,... | collective-permute-start | bytes 6291464 | tf_op jit(solution)/shard_map/ppermute | solution.py:746
  179.5 83.7 %collective-permute-start.8 = (bf16[512,2048]{1,0:T(8,128)(2,1)}, bf16[512,2048]{1,0:T(8,128)(2,1)}, u32[]{:S(2)}, u32[]{:S(2)}) collective-permute-start(bf16[512,2048]{1,0:T(8,128)(2,1)} %get-tuple-element.66.refs_1_.refs_8_), channel_id=1, source_target_pairs={{0,6},{1,7},{2,0},{3,1},{4,2},{5,3},{6,4},{7,5},{8,14},{9,15},{10,... | collective-permute-start | bytes 6291464 | tf_op jit(solution)/shard_map/ppermute | solution.py:746
  195.8 76.0 %collective-permute-start.4 = (f32[1024,8]{0,1:T(8,128)S(1)}, f32[1024,8]{0,1:T(8,128)S(1)}, u32[]{:S(2)}, u32[]{:S(2)}) collective-permute-start(f32[1024,8]{0,1:T(8,128)S(1)} %fusion.18), channel_id=1, source_target_pairs={{0,6},{1,7},{2,0},{3,1},{4,2},{5,3},{6,4},{7,5},{8,14},{9,15},{10,... | collective-permute-start | bytes 98312 | tf_op jit(solution)/shard_map/ppermute | solution.py:746
  196.2 192.7 %collective-permute-start.11 = (bf16[512,2048]{1,0:T(8,128)(2,1)}, bf16[512,2048]{1,0:T(8,128)(2,1)}, u32[]{:S(2)}, u32[]{:S(2)}) collective-permute-start(bf16[512,2048]{1,0:T(8,128)(2,1)} %get-tuple-element.66.refs_1_.refs_8_), channel_id=1, source_target_pairs={{0,2},{1,3},{2,4},{3,5},{4,6},{5,7},{6,0},{7,1},{8,10},{9,11},{10,... | collective-permute-start | bytes 6291464 | tf_op jit(solution)/shard_map/ppermute | solution.py:746
  225.9 170.2 %collective-permute-start.10 = (bf16[512,2048]{1,0:T(8,128)(2,1)}, bf16[512,2048]{1,0:T(8,128)(2,1)}, u32[]{:S(2)}, u32[]{:S(2)}) collective-permute-start(bf16[512,2048]{1,0:T(8,128)(2,1)} %get-tuple-element.64.refs_3_.refs_0_.refs_7_), channel_id=1, source_target_pairs={{0,6},{1,7},{2,0},{3,1},{4,2},{5,3},{6,4},{7,5},{8,14},{9,15},{10,... | collective-permute-start | bytes 6291464 | tf_op jit(solution)/shard_map/ppermute | solution.py:746
  263.3 140.3 %collective-permute-start.9 = (bf16[512,2048]{1,0:T(8,128)(2,1)}, bf16[512,2048]{1,0:T(8,128)(2,1)}, u32[]{:S(2)}, u32[]{:S(2)}) collective-permute-start(bf16[512,2048]{1,0:T(8,128)(2,1)} %collective-permute-done.7.refs_3_.refs_0_), channel_id=1, source_target_pairs={{0,2},{1,3},{2,4},{3,5},{4,6},{5,7},{6,0},{7,1},{8,10},{9,11},{10,... | collective-permute-start | bytes 6291464 | tf_op jit(solution)/shard_map/ppermute | solution.py:746
  263.4 140.2 %collective-permute-start.12 = (bf16[512,2048]{1,0:T(8,128)(2,1)}, bf16[512,2048]{1,0:T(8,128)(2,1)}, u32[]{:S(2)}, u32[]{:S(2)}) collective-permute-start(bf16[512,2048]{1,0:T(8,128)(2,1)} %collective-permute-done.8.refs_4_.refs_1_), channel_id=1, source_target_pairs={{0,6},{1,7},{2,0},{3,1},{4,2},{5,3},{6,4},{7,5},{8,14},{9,15},{10,... | collective-permute-start | bytes 6291464 | tf_op jit(solution)/shard_map/ppermute | solution.py:746
  266.1 122.9 %copy-start.4 = (s32[115]{0:T(128)}, s32[115]{0:T(128)S(1)}, u32[]{:S(2)}) copy-start(s32[115]{0:T(128)S(1)} %broadcast_minimum_fusion.3.tl_ref) | copy-start | bytes 1384
  271.8 46.3 %collective-permute-start.5 = (f32[1024,8]{0,1:T(8,128)S(1)}, f32[1024,8]{0,1:T(8,128)S(1)}, u32[]{:S(2)}, u32[]{:S(2)}) collective-permute-start(f32[1024,8]{0,1:T(8,128)S(1)} %fusion.18), channel_id=1, source_target_pairs={{0,4},{1,5},{2,6},{3,7},{4,0},{5,1},{6,2},{7,3},{8,12},{9,13},{10,... | collective-permute-start | bytes 98312 | tf_op jit(solution)/shard_map/ppermute | solution.py:746
  318.1 4.0 collective-permute-start.3
  571.8 84.7 %collective-permute-start.13 = (bf16[512,2048]{1,0:T(8,128)(2,1)}, bf16[512,2048]{1,0:T(8,128)(2,1)}, u32[]{:S(2)}, u32[]{:S(2)}) collective-permute-start(bf16[512,2048]{1,0:T(8,128)(2,1)} %get-tuple-element.81), channel_id=1, source_target_pairs={{0,2},{1,3},{2,4},{3,5},{4,6},{5,7},{6,0},{7,1},{8,10},{9,11},{10,... | collective-permute-start | bytes 6291464 | tf_op jit(solution)/shard_map/ppermute | solution.py:746
  571.9 84.6 %collective-permute-start.14 = (bf16[512,2048]{1,0:T(8,128)(2,1)}, bf16[512,2048]{1,0:T(8,128)(2,1)}, u32[]{:S(2)}, u32[]{:S(2)}) collective-permute-start(bf16[512,2048]{1,0:T(8,128)(2,1)} %get-tuple-element.82), channel_id=1, source_target_pairs={{0,6},{1,7},{2,0},{3,1},{4,2},{5,3},{6,4},{7,5},{8,14},{9,15},{10,... | collective-permute-start | bytes 6291464 | tf_op jit(solution)/shard_map/ppermute | solution.py:746
  614.7 48.1 %collective-permute-start.16 = (bf16[512,2048]{1,0:T(8,128)(2,1)}, bf16[512,2048]{1,0:T(8,128)(2,1)}, u32[]{:S(2)}, u32[]{:S(2)}) collective-permute-start(bf16[512,2048]{1,0:T(8,128)(2,1)} %shard_map.110), channel_id=1, source_target_pairs={{0,6},{1,7},{2,0},{3,1},{4,2},{5,3},{6,4},{7,5},{8,14},{9,15},{10,... | collective-permute-start | bytes 6291464 | tf_op jit(solution)/shard_map/ppermute | solution.py:746
  614.8 100.0 %collective-permute-start.15 = (bf16[512,2048]{1,0:T(8,128)(2,1)}, bf16[512,2048]{1,0:T(8,128)(2,1)}, u32[]{:S(2)}, u32[]{:S(2)}) collective-permute-start(bf16[512,2048]{1,0:T(8,128)(2,1)} %get-tuple-element.87), channel_id=1, source_target_pairs={{0,6},{1,7},{2,0},{3,1},{4,2},{5,3},{6,4},{7,5},{8,14},{9,15},{10,... | collective-permute-start | bytes 6291464 | tf_op jit(solution)/shard_map/ppermute | solution.py:746
  614.9 99.9 %collective-permute-start.18 = (bf16[512,2048]{1,0:T(8,128)(2,1)}, bf16[512,2048]{1,0:T(8,128)(2,1)}, u32[]{:S(2)}, u32[]{:S(2)}) collective-permute-start(bf16[512,2048]{1,0:T(8,128)(2,1)} %get-tuple-element.90), channel_id=1, source_target_pairs={{0,2},{1,3},{2,4},{3,5},{4,6},{5,7},{6,0},{7,1},{8,10},{9,11},{10,... | collective-permute-start | bytes 6291464 | tf_op jit(solution)/shard_map/ppermute | solution.py:746
  656.5 58.3 %collective-permute-start.17 = (bf16[512,2048]{1,0:T(8,128)(2,1)}, bf16[512,2048]{1,0:T(8,128)(2,1)}, u32[]{:S(2)}, u32[]{:S(2)}) collective-permute-start(bf16[512,2048]{1,0:T(8,128)(2,1)} %shard_map.111), channel_id=1, source_target_pairs={{0,2},{1,3},{2,4},{3,5},{4,6},{5,7},{6,0},{7,1},{8,10},{9,11},{10,... | collective-permute-start | bytes 6291464 | tf_op jit(solution)/shard_map/ppermute | solution.py:746
  656.6 97.4 %collective-permute-start.19 = (bf16[512,2048]{1,0:T(8,128)(2,1)}, bf16[512,2048]{1,0:T(8,128)(2,1)}, u32[]{:S(2)}, u32[]{:S(2)}) collective-permute-start(bf16[512,2048]{1,0:T(8,128)(2,1)} %collective-permute-done.13), channel_id=1, source_target_pairs={{0,2},{1,3},{2,4},{3,5},{4,6},{5,7},{6,0},{7,1},{8,10},{9,11},{10,... | collective-permute-start | bytes 6291464 | tf_op jit(solution)/shard_map/ppermute | solution.py:746
  662.7 91.3 %collective-permute-start.20 = (bf16[512,2048]{1,0:T(8,128)(2,1)}, bf16[512,2048]{1,0:T(8,128)(2,1)}, u32[]{:S(2)}, u32[]{:S(2)}) collective-permute-start(bf16[512,2048]{1,0:T(8,128)(2,1)} %collective-permute-done.14), channel_id=1, source_target_pairs={{0,6},{1,7},{2,0},{3,1},{4,2},{5,3},{6,4},{7,5},{8,14},{9,15},{10,... | collective-permute-start | bytes 6291464 | tf_op jit(solution)/shard_map/ppermute | solution.py:746
  754.1 12.6 %copy-start.1 = (f32[2048,64]{0,1:T(8,128)S(1)}, f32[2048,64]{0,1:T(8,128)}, u32[]{:S(2)}) copy-start(f32[2048,64]{0,1:T(8,128)} %param.15) | copy-start | bytes 1572868

commit v5 on v4

--- a/solution.py
+++ b/solution.py
@@ -3,6 +3,7 @@
 import typing
 import jax
 import jax.numpy as jnp
+import numpy as np
 from jax import lax
 from jax.experimental import pallas as pl
 from jax.experimental.pallas import tpu as pltpu
@@ -53,12 +54,21 @@
     return pltpu.CompilerParams(vmem_limit_bytes=VMEM, **kw)
 
 
+def split3(g):
+    hi = g.astype(BF)
+    r = g - hi.astype(F32)
+    mid = r.astype(BF)
+    lo = (r - mid.astype(F32)).astype(BF)
+    return hi, mid, lo
+
+
 LT, LB, RT, RB, OT, OB, PO, PASS = 0, 1, 2, 3, 4, 5, 6, 7
 MESH = pl.DeviceIdType.MESH
 
 
-def layer_kernel(nx, x_ref, wv_ref, wk_ref, wq_ref, wo_ref, cos_ref, sin_ref, w1_ref, w3_ref, h_ref, ut_ref, ub_ref,
-                 o1_ref, o3_ref, w_ref, ab, qb, kb, vb, ssem, rsem, lsem, iosem, swap_send, swap_recv):
+def layer_kernel(nx, x_ref, wv_ref, wk_ref, wq_ref, wo_ref, cos_ref, sin_ref, w1_ref, w3_ref, wr_ref, id_ref,
+                 h_ref, ut_ref, ub_ref, o1_ref, o3_ref, lg_ref, id4_ref,
+                 w_ref, ab, qb, kb, vb, rb3, ssem, rsem, lsem, iosem, swap_send, swap_recv, id_send, id_recv):
     shards = (wv_ref, wk_ref, wq_ref, wo_ref)
     sh = wv_ref.shape[0]
     hs = sh // 2
@@ -69,9 +79,10 @@
     partner = 2 * chip + 1 - core
 
     barrier = pltpu.get_barrier_semaphore()
-    for dev in (right, left, partner):
+    around = (right, left, opp)
+    for dev in (*around, partner):
         pl.semaphore_signal(barrier, inc=1, device_id={"ep": dev}, device_id_type=MESH)
-    pl.semaphore_wait(barrier, 3)
+    pl.semaphore_wait(barrier, 4)
 
     def rows(e, half=None):
         if half is None:
@@ -152,12 +163,18 @@
         if waiting:
             waiting.pop(0).start()
 
+    ids = [pltpu.make_async_remote_copy(src_ref=id_ref, dst_ref=id4_ref.at[k + 1], send_sem=id_send.at[k], recv_sem=id_recv.at[k],
+                                        device_id={"ep": dev}, device_id_type=MESH) for k, dev in enumerate(around)]
+    ids.append(pltpu.make_async_copy(id_ref, id4_ref.at[0], id_send.at[3]))
     begin(0)
+    for c in ids:
+        c.start()
     swap()
     xin = pltpu.make_async_copy(x_ref, kb, iosem.at[0])
     xin.start()
     xin.wait()
-    rb = min(128, t)
+    rb = min(256, t)
+    rb3[:] = jnp.concatenate([*split3(wr_ref[:]), jnp.zeros(wr_ref.shape, BF)], axis=1)
 
     @loop(t // rb)
     def _(i):
@@ -236,14 +253,19 @@
     @loop(t // rb)
     def _(i):
         r = pl.ds(pl.multiple_of(i * rb, rb), rb)
-        kb[r, :] = rmsnorm(ab[r, :]).astype(BF)
+        hi, mid, lo = split3(rmsnorm(ab[r, :]))
+        kb[r, :] = hi
+        ne = wr_ref.shape[1]
+        part = lambda v, k: v[:, k * ne:(k + 1) * ne]
+        p1, p2, p3 = dot(hi, rb3[:]), dot(mid, rb3[:, :2 * ne]), dot(lo, rb3[:, :2 * ne])
+        lg_ref[r, :] = part(p1, 0) + ((part(p1, 1) + part(p2, 0)) + (part(p1, 2) + part(p2, 1) + part(p3, 0)))
 
     uout = [pltpu.make_async_copy(kb.at[pl.ds(p * t // 2, t // 2), :], o, iosem.at[1 + p]) for p, o in enumerate((ut_ref, ub_ref))]
     for c in uout:
         c.start()
     while waiting:
         swap()
-    for c in swaps:
+    for c in swaps + ids:
         c.wait()
     for w in range(4):
         for c in own(w) + [onward(w, OT), onward(w, OB)] + [across(w, k) for k in where]:
@@ -253,7 +275,7 @@
         c.wait()
 
 
-def attention_layer(nx, x, wv, wk, wq, wo, cos, sin, w1, w3):
+def attention_layer(nx, x, wv, wk, wq, wo, cos, sin, w1, w3, wr, ids):
     t, d = x.shape
     hb = pl.BlockSpec(memory_space=pl.ANY)
     vm = pl.BlockSpec(memory_space=pltpu.VMEM)
@@ -261,17 +283,19 @@
     act = pltpu.VMEM((t, d), BF)
     return pl.pallas_call(
         functools.partial(layer_kernel, nx),
-        in_specs=[hb] * 5 + [vm] * 2 + [hb] * 2,
-        out_specs=[hb] * 5,
+        in_specs=[hb] * 5 + [vm] * 2 + [hb] * 2 + [vm, hb],
+        out_specs=[hb] * 5 + [vm, hb],
         out_shape=[jax.ShapeDtypeStruct((t, d), BF), half, half, jax.ShapeDtypeStruct(w1.shape, BF),
-                   jax.ShapeDtypeStruct(w3.shape, BF)],
-        scratch_shapes=[pltpu.VMEM((4, d, d), BF), act, act, act, act,
+                   jax.ShapeDtypeStruct(w3.shape, BF), jax.ShapeDtypeStruct((t, wr.shape[1]), F32),
+                   jax.ShapeDtypeStruct((nx, *ids.shape), I32)],
+        scratch_shapes=[pltpu.VMEM((4, d, d), BF), act, act, act, act, pltpu.VMEM((d, 4 * wr.shape[1]), BF),
                         pltpu.SemaphoreType.DMA((4, 13)), pltpu.SemaphoreType.DMA((4, 13)),
                         pltpu.SemaphoreType.DMA((4,)), pltpu.SemaphoreType.DMA((3,)),
-                        pltpu.SemaphoreType.DMA((2 * w1.shape[0],)), pltpu.SemaphoreType.DMA((2 * w1.shape[0],))],
+                        pltpu.SemaphoreType.DMA((2 * w1.shape[0],)), pltpu.SemaphoreType.DMA((2 * w1.shape[0],)),
+                        pltpu.SemaphoreType.DMA((nx,)), pltpu.SemaphoreType.DMA((nx,))],
         compiler_params=params(collective_id=0, has_side_effects=True),
         cost_estimate=cost(8 * t * d * d, 24 * t * d),
-    )(x, wv, wk, wq, wo, cos, sin, w1, w3)
+    )(x, wv, wk, wq, wo, cos, sin, w1, w3, wr, ids)
 
 
 def fetch_expert(l, slot, own, other, bufs, sem):
@@ -328,12 +352,16 @@
         n = sum(ns)
 
         def entry(i):
-            p = jnp.where(i < ns[0], 0, nblk - 1)
-            return p, hl_ref[jnp.where(p == 0, js[0], js[-1]) * nl + i - jnp.where(p == 0, 0, ns[0])]
+            p, j, k, end = 0, js[0], i, 0
+            for q in range(nblk - 1):
+                end = end + ns[q]
+                past = i >= end
+                p, j, k = jnp.where(past, q + 1, p), jnp.where(past, js[q + 1], j), jnp.where(past, i - end, k)
+            return p, j, hl_ref[j * nl + k]
 
         @pl.when(n > 0)
         def _():
-            fetch_expert(entry(0)[1], 0, own, other, bufs, sem)
+            fetch_expert(entry(0)[-1], 0, own, other, bufs, sem)
 
         ucp = [pltpu.make_async_copy(us[p], ubuf.at[pl.ds(p * t, t), :], usem) for p in range(nblk)]
         for cp in ucp:
@@ -404,10 +432,9 @@
 
             @pl.when(i + 1 < n)
             def _():
-                fetch_expert(entry(i + 1)[1], 1 - slot, own, other, bufs, sem)
-
-            p, e = entry(i)
-            blk = jnp.where(p == 0, js[0], js[-1])
+                fetch_expert(entry(i + 1)[-1], 1 - slot, own, other, bufs, sem)
+
+            p, blk, e = entry(i)
 
             @loop(t // tm)
             def _(m):
@@ -466,14 +493,6 @@
     )(*args)
 
 
-def split3(g):
-    hi = g.astype(BF)
-    r = g - hi.astype(F32)
-    mid = r.astype(BF)
-    lo = (r - mid.astype(F32)).astype(BF)
-    return hi, mid, lo
-
-
 def selection(j, i, eg_ref, pos_ref):
     t = pos_ref.shape[2]
     it = lax.broadcasted_iota(I32, (2 * PIECE, t), 0)
@@ -488,17 +507,22 @@
     return jnp.concatenate(hits, axis=0), ls
 
 
-def gather_kernel(js, nch_ref, eg_ref, pos_ref, *refs):
-    us = refs[:len(js)]
-    x_ref, xbuf, sem = refs[-3:]
+def gather_kernel(nch_ref, eg_ref, pos_ref, *refs):
+    us, (x_ref, ubuf, xbuf, usem, sem) = refs[:-5], refs[-5:]
     cap = x_ref.shape[0] // pos_ref.shape[0]
-    for p, j in enumerate(js):
+    cps = [pltpu.make_async_copy(u, ubuf.at[j % 2], usem.at[j % 2]) for j, u in enumerate(us)]
+    cps[0].start()
+    for j in range(len(us)):
         nch = nch_ref[j]
 
         def out(i, slot):
             dst = pl.multiple_of(j * cap + i * CHUNK, CHUNK)
             return pltpu.make_async_copy(xbuf.at[slot], x_ref.at[pl.ds(dst, CHUNK), :], sem.at[slot])
 
+        if j + 1 < len(us):
+            cps[j + 1].start()
+        cps[j].wait()
+
         @loop(nch)
         def _(i):
             slot = parity(i)
@@ -507,7 +531,7 @@
             def _():
                 out(i - 2, slot).wait()
 
-            xbuf[slot] = dot(selection(j, i, eg_ref, pos_ref)[0], us[p][:]).astype(BF)
+            xbuf[slot] = dot(selection(j, i, eg_ref, pos_ref)[0], ubuf[j % 2]).astype(BF)
             out(i, slot).start()
 
         for k in (2, 1):
@@ -516,24 +540,21 @@
                 out(nch - k, parity(nch - k)).wait()
 
 
-def gather(js, r, us, x):
-    nblk = len(js)
+def gather(r, us):
     t, d = us[0].shape
-    nb = r.eg.shape[0]
-    cap = r.eg.shape[1] * PIECE
+    rows = r.eg.size * PIECE
     vm = pl.BlockSpec(memory_space=pltpu.VMEM)
     sm = pl.BlockSpec(memory_space=pltpu.SMEM)
     hb = pl.BlockSpec(memory_space=pl.ANY)
     return pl.pallas_call(
-        functools.partial(gather_kernel, js),
-        in_specs=[sm, sm, vm] + [vm] * nblk + ([hb] if x is not None else []),
+        gather_kernel,
+        in_specs=[sm, sm, vm] + [hb] * len(us),
         out_specs=hb,
-        out_shape=jax.ShapeDtypeStruct((nb * cap, d), BF),
-        input_output_aliases={3 + nblk: 0} if x is not None else {},
-        scratch_shapes=[pltpu.VMEM((2, CHUNK, d), BF), DMA2],
+        out_shape=jax.ShapeDtypeStruct((rows, d), BF),
+        scratch_shapes=[pltpu.VMEM((2, t, d), BF), pltpu.VMEM((2, CHUNK, d), BF), DMA2, DMA2],
         compiler_params=params(),
         cost_estimate=cost(t * d, 4 * CHUNK * d),
-    )(r.nch, r.eg.reshape(-1), r.pos, *us, *([x] if x is not None else []))
+    )(r.nch, r.eg.reshape(-1), r.pos, *us)
 
 
 def cold_kernel(nt_ref, tl_ref, tp_ref, tn_ref, tw_ref, tf_ref, nx_ref, pc_ref, x_ref, *refs):
@@ -757,14 +778,12 @@
         x = x.reshape(t, d)
         ids = idx.reshape(t, k)
 
-        ids4 = jnp.stack([ids, shift(ids, 1), shift(ids, -1), shift(ids, 2)])
         hd = HEAD // 2
-        freq = THETA ** (-jnp.arange(hd, dtype=F32) / hd)
-        ang = (jnp.arange(t) % s).astype(F32)[:, None] * freq
-        c, sn = jnp.cos(ang), jnp.sin(ang)
-        cos, sin = jnp.concatenate([c, c], axis=1), jnp.concatenate([-sn, sn], axis=1)
-        x, cos, sin, ids4 = lax.optimization_barrier((x, cos, sin, ids4))
-        h, ut, ub, o1, o3 = attention_layer(nx, x, wv, wk, wq, wo, cos, sin, w1, w3)
+        ang = (np.arange(t) % s).astype(np.float32)[:, None] * np.float32(THETA) ** (-np.arange(hd, dtype=np.float32) / hd)
+        c, sn = np.cos(ang), np.sin(ang)
+        cos, sin = [jnp.asarray(np.concatenate(v, axis=1), F32) for v in ((c, c), (-sn, sn))]
+        h, ut, ub, o1, o3, logits, ids4 = attention_layer(nx, x, wv, wk, wq, wo, cos, sin, w1, w3, wr, ids.T)
+        ids4 = jnp.swapaxes(ids4, 1, 2)
         ids4, w2, ut, ub = lax.optimization_barrier((ids4, w2, ut, ub))
         o2 = partner(w2)
         own, other = (w1, w3, w2), (o1, o3, o2)
@@ -774,47 +793,39 @@
         lid = halves((ids4 - me * ne) % nl)
         r, plan = routing_plan(lid, is_local, nl)
         ohl = (lid[:, None] == jnp.arange(nl, dtype=I32)[:, None, None]) & is_local[:, None]
-        A, R, L, O = (0, 1), (2, 3), (4, 5), (6, 7)
-        ra = r._replace(pos=r.pos[:2])
 
         u1t, u2b = shift(ut, 1), shift(ub, -1)
-        logits = jnp.dot(rmsnorm(h), wr, precision=lax.Precision.HIGHEST, preferred_element_type=F32)
         oh = ids[..., None] == jnp.arange(wr.shape[1], dtype=I32)
         g = jax.nn.softmax(jnp.sum(jnp.where(oh, logits[:, None, :], 0.0), axis=-1), axis=-1)
         ut2, ub2, g = lax.optimization_barrier((ut, ub, g))
         g4 = [g, shift(g, 1), shift(g, -1), shift(g, 2)]
         u1b, u2t = shift(ub2, 1), shift(ut2, -1)
         spread = lambda o, v: jnp.sum(jnp.where(o, halves(v)[:, None], 0.0), axis=3)
-        ra = ra._replace(gt=spread(ohl[:2], g[None]))
         r = r._replace(gt=spread(ohl, jnp.stack(g4)))
 
-        x = gather(A, r, (ut, ub), None)
-        a0, = block((0,), ra, None, (ut,), (None,), own, other, F32, ON, comb=False)
-        a0, x, u1t, u2b = lax.optimization_barrier((a0, x, u1t, u2b))
         u3t, u3b = shift(u1t, 1), shift(u2b, -1)
-        d2, d5 = block((2, 5), r, None, (u1t, u2b), (None, None), own, other, F32, 2 * ON, comb=False)
+        a0, d2, d5 = block((0, 2, 5), r, None, (ut, u1t, u2b), 3 * (None,), own, other, F32, 3 * ON, comb=False)
         u1b, d2 = lax.optimization_barrier((u1b, d2))
-        x = gather(R, r, (u1t, u1b), x)
-        x = gather(L, r, (u2t, u2b), x)
-        u3t, x = lax.optimization_barrier((u3t, x))
-        x = gather(O, r, (u3t, u3b), x)
+        x = gather(r, (ut, ub, u1t, u1b, u2t, u2b, u3t, u3b))
         z = cold(plan, x, own, other)
 
         tie = lambda r, *v: (lambda w: (r._replace(nch=w[0]), *w[1:]))(lax.optimization_barrier((r.nch, *v)))
         b2, b5 = block((2, 5), r, z, (), (d2, d5), own, other, BF, (False, False))
         r, b2, b5 = tie(r, b2, b5)
         b2, b5 = shift(b2, -1), shift(b5, 1)
-        b6, b7 = block(O, r, z, (u3t, u3b), (None, None), own, other, BF, 2 * ON)
-        r, b6, b7 = tie(r, b6, b7)
-        c6, c7 = shift(b6, 1), shift(b7, -1)
+        b6, = block((6,), r, z, (u3t,), (None,), own, other, BF, ON)
+        r, b6 = tie(r, b6)
+        c6 = shift(b6, 1)
+        b7, = block((7,), r, z, (u3b,), (None,), own, other, BF, ON)
+        r, b7 = tie(r, b7)
+        c7 = shift(b7, -1)
         b3, = block((3,), r, z, (u1b,), (None,), own, other, BF, ON)
-        r, b3 = tie(r, b3)
-        b3 = shift(b3, -1)
+        r, b3, c6 = tie(r, b3, c6)
+        b3, b6 = shift(b3, -1), shift(c6, 1)
         b4, = block((4,), r, z, (u2t,), (None,), own, other, BF, ON)
-        r, b4, c6, c7 = tie(r, b4, c6, c7)
-        b4 = shift(b4, 1)
-        b6, b7 = shift(c6, 1), shift(c7, -1)
-        accs = block(A, r, z, (ut, ub), (a0, None), own, other, F32, (False, True))
+        r, b4, c7 = tie(r, b4, c7)
+        b4, b7 = shift(b4, 1), shift(c7, -1)
+        accs = block((0, 1), r, z, (ut, ub), (a0, None), own, other, F32, (False, True))
         y = final(h, accs, [(b2, b3), (b4, b5), (b6, b7)])
         return y.reshape(b, s, d)
 

time: 772 us -> 733 us (0.949); the launches traced: 767 us -> 719 us
  waiting for transfers between devices: 108 us -> 82.6 us
  starting transfers between devices: 23.3 us -> 12.9 us
  matrix products: 8.98 us -> 0.24 us
    ppermute x1, waiting for transfers between devices: 15.9 us -> 0.01 us  [partner(): return lax.ppermute(v, 'ep', [(i, i ^ 1) for i in range(nd)])]
    ppermute x20 -> x17, starting transfers between devices: 22.2 us -> 11.9 us  [shift(): lax.ppermute(v, 'ep', [(2 * i + c, 2 * ((i + s) % nx) + c) for i in range...]
    ppermute x20 -> x17, waiting for transfers between devices: 92 us -> 82.6 us  [shift(): lax.ppermute(v, 'ep', [(2 * i + c, 2 * ((i + s) % nx) + c) for i in range...]
    dot_general x1 -> x0, matrix products: 8.73 us -> none  [local(): jnp.dot(rmsnorm(h), wr, precision=lax.Precision.HIGHEST, preferred_elemen...]
    pallas_call x4 -> x1, Pallas kernels: 29.1 us -> 22.2 us  [gather(): pl.pallas_call(gather_kernel, in_specs=[sm, sm, vm] + [hb] * len(us), out...]
  transfers between devices with their start and end apart: 21 -> 18, of which waited for: 5 -> 3; matrix products, arithmetic and copies ran while one was open for 4% -> 3% of each run, Pallas kernels for 33% -> 37%
where the time goes in v5:
time: 733 us; the launch traced here: 719 us
  Pallas kernels  601 us (82%)
  waiting for transfers between devices  82.6 us (11%)
  other arithmetic  14.6 us (2%)
  starting transfers between devices  12.9 us (2%)
    pallas_call x7, Pallas kernels, block(): pl.pallas_call(functools.partial(block_kernel, js, [v is not None for v i...  323 us
    pallas_call x1, Pallas kernels, attention_layer(): pl.pallas_call(functools.partial(layer_kernel, nx), in_specs=[hb] * 5 + [...  173 us
    ppermute x17, waiting for transfers between devices, shift(): lax.ppermute(v, 'ep', [(2 * i + c, 2 * ((i + s) % nx) + c) for i in range...  82.6 us
    pallas_call x1, Pallas kernels, cold(): pl.pallas_call(cold_kernel, in_specs=[sm] * len(plan) + [hb] * 7, out_spe...  70.1 us
    pallas_call x1, Pallas kernels, gather(): pl.pallas_call(gather_kernel, in_specs=[sm, sm, vm] + [hb] * len(us), out...  22.2 us
  transfers between devices with their start and end apart: 18, of which 3 were waited for; matrix products, arithmetic and copies ran while one was open for 3% of the time, Pallas kernels for 37%

profile of v5, /device:TPU:113, one launch (start us, length us, event | category | flops | bytes accessed | tf_op | source)
XLA Modules:
  0.0 719.4 jit_solution(17096740221827661900)
XLA Ops:
  0.0 2.4 copy.61.wr_ref
  2.4 173.3 %shard_map.118 = (bf16[1024,2048]{1,0:T(8,128)(2,1)}, bf16[512,2048]{1,0:T(8,128)(2,1)}, bf16[512,2048]{1,0:T(8,128)(2,1)}, bf16[8,2048,1024]{2,1,0:T(8,128)(2,1...) custom-call(bf16[1024,2048]{1,0:T(8,128)(2,1)} %bitcast.42, ...), custom_call_target="tpu_custom_call" | custom-call | flops 34359738368 | bytes 50331648 | tf_op jit(solution)/shard_map/pallas_call | solution.py:284
  175.7 1.1 collective-permute-start.6
  176.7 1.2 copy.62
  178.0 0.3 select_reduce_fusion.2
  178.3 1.6 collective-permute-start.2
  180.0 1.6 collective-permute-start.1
  181.6 0.1 collective-permute-start.5
  181.7 1.3 collective-permute-start.3
  183.0 1.0 fusion.6
  184.0 1.0 add_select_fusion.2
  185.0 0.8 fusion.1
  185.8 0.2 convolution_convert_fusion
  186.1 0.3 slice_reduce_fusion
  186.4 0.2 reduce_window_sum.37
  186.6 0.2 reduce_window_sum.38
  186.9 0.1 reduce.5
  187.2 0.2 convert_reduce_fusion.2
  187.9 0.1 reduce.7
  188.2 0.1 reduce.6
  188.3 0.2 reduce-window.32
  188.5 0.1 reduce.8
  188.6 0.1 copy.63
  188.7 0.1 convert_reduce_fusion.1
  188.9 0.7 select_reduce_fusion.3
  189.6 0.3 fusion.12
  189.9 0.7 convert_reduce_fusion
  190.6 0.3 fusion.14
  191.0 0.2 multiply_reduce_fusion
  191.2 0.9 collective-permute-start.4
  192.1 38.1 %collective-permute-done = f32[1024,8]{0,1:T(8,128)S(1)} collective-permute-done((f32[1024,8]{0,1:T(8,128)S(1)}, f32[1024,8]{0,1:T(8,128)S(1)}, u32[]{:S(2)}, u32[]{:S(2)}) %collective-permute-start) | collective-permute-done | bytes 32800 | tf_op jit(solution)/shard_map/ppermute | solution.py:767
  230.2 0.1 collective-permute-start.7
  230.4 0.8 collective-permute-start.9
  231.2 0.7 collective-permute-start.8
  231.9 0.7 slice_reduce_fusion.1.refs_0_
  232.5 0.6 slice.21
  233.1 0.6 min.52.refs_1_
  233.7 0.7 min.55.eg_ref.refs_2_.refs_4_
  234.4 2.5 select_reduce_fusion
  237.0 0.5 negate_maximum_fusion.nch_ref.refs_1_.refs_3_
  237.5 0.5 compare_select_fusion.2.nx_ref
  238.0 0.6 compare_convert_fusion.1.tf_ref
  238.6 0.5 subtract_clamp_fusion
  239.1 0.6 add_clamp_fusion.pc_ref
  239.7 0.8 add_select_fusion.pos_ref.refs_3_.refs_5_
  240.6 1.6 select_reduce_fusion.1.refs_2_.refs_0_
  242.1 94.8 %shard_map.119 = (f32[512,2048]{1,0:T(8,128)}, f32[512,2048]{1,0:T(8,128)}, f32[512,2048]{1,0:T(8,128)}) custom-call(s32[8]{0:T(128)} %slice_reduce_fusion.1.refs_0_, s32[128]{0:T(128)} %min.52.refs_1_, f32[8,16,512]{2,1,0:T(8,128)} %select_reduce_fusion.1.refs_2_.refs_0_, bf16[512,2048]{1,0:T(8,128)(2,1)} %get-tuple-element.56.refs_3_.refs_0_.refs_7_, ...), custom_call_target="tpu_custom_call" | custom-call | flops 1048576 | bytes 12582912 | tf_op jit(solution)/shard_map/pallas_call | solution.py:488
  337.0 22.2 %shard_map.120.x_ref = bf16[34816,2048]{1,0:T(8,128)(2,1)} custom-call(s32[8]{0:T(128)} %negate_maximum_fusion.nch_ref.refs_1_.refs_3_, s32[4352]{0:T(1024)} %min.55.eg_ref.refs_2_.refs_4_, s32[8,16,512]{2,1,0:T(8,128)} %add_select_fusion.pos_ref.refs_3_.refs_5_, bf16[512,2048]{1,0:T(8,128)(2,1)} %get-tuple-element.56.refs_3_.refs_0_.refs_7_, ...), custom_call_target="tpu_custom_call" | custom-call | flops 1048576 | bytes 2097152 | tf_op jit(solution)/shard_map/pallas_call | solution.py:549
  359.2 70.1 %shard_map.121.refs_4_.refs_6_ = bf16[34816,2048]{1,0:T(8,128)(2,1)} custom-call(s32[1]{0:T(128)} %bitcast.14.nt_ref, s32[115]{0:T(128)} %copy-done.1, s32[115]{0:T(128)} %get-tuple-element.87.tp_ref, s32[115]{0:T(128)} %get-tuple-element.86.tn_ref, s32[115]{0:T(128)} %get-tuple-element.78.tw_ref, ...), custom_call_target="tpu_custom_call", output_to_operand_aliasing={{}: (8, {})} | custom-call | flops 70866960384 | bytes 201326592 | tf_op jit(solution)/shard_map/pallas_call | solution.py:651
  429.3 17.9 %shard_map.122 = (bf16[512,2048]{1,0:T(8,128)(2,1)}, bf16[512,2048]{1,0:T(8,128)(2,1)}) custom-call(f32[8,16,512]{2,1,0:T(8,128)} %select_reduce_fusion.1.refs_2_.refs_0_, s32[8]{0:T(128)} %negate_maximum_fusion.nch_ref.refs_1_.refs_3_, s32[4352]{0:T(1024)} %min.55.eg_ref.refs_2_.refs_4_, s32[8,16,512]{2,1,0:T(8,128)} %add_select_fusion.pos_ref.refs_3_.refs_5_, ...), custom_call_target="tpu_custom_call" | custom-call | flops 1048576 | bytes 12582912 | tf_op jit(solution)/shard_map/pallas_call | solution.py:488
  447.2 40.6 %shard_map.123 = bf16[512,2048]{1,0:T(8,128)(2,1)} custom-call(s32[8]{0:T(128)} %slice_reduce_fusion.1.refs_0_, s32[128]{0:T(128)} %min.52.refs_1_, f32[8,16,512]{2,1,0:T(8,128)} %select_reduce_fusion.1.refs_2_.refs_0_, s32[8]{0:T(128)} %negate_maximum_fusion.nch_ref.refs_1_.refs_3_, s32[4352]{0:T(1024)} %min.55.eg_ref.refs_2_.refs_4_, ...), custom_call_target="tpu_custom_call" | custom-call | flops 1048576 | bytes 12582912 | tf_op jit(solution)/shard_map/pallas_call | solution.py:488
  487.8 0.1 collective-permute-start.10
  487.9 40.1 %shard_map.124 = bf16[512,2048]{1,0:T(8,128)(2,1)} custom-call(s32[8]{0:T(128)} %slice_reduce_fusion.1.refs_0_, s32[128]{0:T(128)} %min.52.refs_1_, f32[8,16,512]{2,1,0:T(8,128)} %select_reduce_fusion.1.refs_2_.refs_0_, s32[8]{0:T(128)} %negate_maximum_fusion.nch_ref.refs_1_.refs_3_, s32[4352]{0:T(1024)} %min.55.eg_ref.refs_2_.refs_4_, ...), custom_call_target="tpu_custom_call" | custom-call | flops 1048576 | bytes 12582912 | tf_op jit(solution)/shard_map/pallas_call | solution.py:488
  528.1 0.1 collective-permute-start.11
  528.2 0.1 collective-permute-start.12
  528.3 1.4 collective-permute-start.15
  529.8 40.1 %shard_map.125 = bf16[512,2048]{1,0:T(8,128)(2,1)} custom-call(s32[8]{0:T(128)} %slice_reduce_fusion.1.refs_0_, s32[128]{0:T(128)} %min.52.refs_1_, f32[8,16,512]{2,1,0:T(8,128)} %select_reduce_fusion.1.refs_2_.refs_0_, s32[8]{0:T(128)} %negate_maximum_fusion.nch_ref.refs_1_.refs_3_, s32[4352]{0:T(1024)} %min.55.eg_ref.refs_2_.refs_4_, ...), custom_call_target="tpu_custom_call" | custom-call | flops 1048576 | bytes 12582912 | tf_op jit(solution)/shard_map/pallas_call | solution.py:488
  569.9 40.1 %shard_map.126 = bf16[512,2048]{1,0:T(8,128)(2,1)} custom-call(s32[8]{0:T(128)} %slice_reduce_fusion.1.refs_0_, s32[128]{0:T(128)} %min.52.refs_1_, f32[8,16,512]{2,1,0:T(8,128)} %select_reduce_fusion.1.refs_2_.refs_0_, s32[8]{0:T(128)} %negate_maximum_fusion.nch_ref.refs_1_.refs_3_, s32[4352]{0:T(1024)} %min.55.eg_ref.refs_2_.refs_4_, ...), custom_call_target="tpu_custom_call" | custom-call | flops 1048576 | bytes 12582912 | tf_op jit(solution)/shard_map/pallas_call | solution.py:488
  610.1 0.1 collective-permute-start.14
  610.2 2.6 collective-permute-start.17
  612.8 3.9 collective-permute-done.12.refs_2_
  616.8 49.4 %shard_map.127 = (f32[512,2048]{1,0:T(8,128)}, f32[512,2048]{1,0:T(8,128)}) custom-call(s32[8]{0:T(128)} %slice_reduce_fusion.1.refs_0_, s32[128]{0:T(128)} %min.52.refs_1_, f32[8,16,512]{2,1,0:T(8,128)} %select_reduce_fusion.1.refs_2_.refs_0_, s32[8]{0:T(128)} %negate_maximum_fusion.nch_ref.refs_1_.refs_3_, s32[4352]{0:T(1024)} %min.55.eg_ref.refs_2_.refs_4_, ...), custom_call_target="tpu_custom_call" | custom-call | flops 1048576 | bytes 12582912 | tf_op jit(solution)/shard_map/pallas_call | solution.py:488
  666.2 40.5 %collective-permute-done.13.refs_3_ = bf16[512,2048]{1,0:T(8,128)(2,1)} collective-permute-done((bf16[512,2048]{1,0:T(8,128)(2,1)}, bf16[512,2048]{1,0:T(8,128)(2,1)}, u32[]{:S(2)}, u32[]{:S(2)}) %collective-permute-start.13) | collective-permute-done | bytes 2097184 | tf_op jit(solution)/shard_map/ppermute | solution.py:767
  706.6 12.6 %shard_map.128 = bf16[1024,2048]{1,0:T(8,128)(2,1)} custom-call(bf16[1024,2048]{1,0:T(8,128)(2,1)} %get-tuple-element.41.h_ref, f32[512,2048]{1,0:T(8,128)} %get-tuple-element.69.refs_0_, f32[512,2048]{1,0:T(8,128)} %get-tuple-element.70.refs_1_, bf16[512,2048]{1,0:T(8,128)(2,1)} %collective-permute-done.12.refs_2_, ...), custom_call_target="tpu_custom_call" | custom-call | flops 12582912 | bytes 41943040 | tf_op jit(solution)/shard_map/pallas_call | solution.py:687
  (52 shorter events, 1.3 us)
Async XLA Ops:
  2.4 175.6 %copy-start = (s32[1,1024,8]{1,2,0:T(8,128)S(1)}, s32[1,1024,8]{1,2,0:T(8,128)}, u32[]{:S(2)}) copy-start(s32[1,1024,8]{1,2,0:T(8,128)} %param.21) | copy-start | bytes 98308
  175.7 66.5 %collective-permute-start.6 = (bf16[8,1024,2048]{2,1,0:T(8,128)(2,1)}, bf16[8,1024,2048]{2,1,0:T(8,128)(2,1)}, u32[]{:S(2)}, u32[]{:S(2)}) collective-permute-start(bf16[8,1024,2048]{2,1,0:T(8,128)(2,1)} %refs_11_), channel_id=1, source_target_pairs={{0,1},{1,0},{2,3},{3,2},{4,5},{5,4},{6,7},{7,6},{8,9},{9,8},{10,11... | collective-permute-start | bytes 100663304 | tf_op jit(solution)/shard_map/ppermute | solution.py:770
  178.3 12.5 %collective-permute-start.2 = (f32[1024,8]{0,1:T(8,128)S(1)}, f32[1024,8]{0,1:T(8,128)S(1)}, u32[]{:S(2)}, u32[]{:S(2)}) collective-permute-start(f32[1024,8]{0,1:T(8,128)S(1)} %fusion.15), channel_id=1, source_target_pairs={{0,4},{1,5},{2,6},{3,7},{4,0},{5,1},{6,2},{7,3},{8,12},{9,13},{10,... | collective-permute-start | bytes 98312 | tf_op jit(solution)/shard_map/ppermute | solution.py:767
  180.0 11.2 %collective-permute-start.1 = (f32[1024,8]{0,1:T(8,128)S(1)}, f32[1024,8]{0,1:T(8,128)S(1)}, u32[]{:S(2)}, u32[]{:S(2)}) collective-permute-start(f32[1024,8]{0,1:T(8,128)S(1)} %fusion.15), channel_id=1, source_target_pairs={{0,6},{1,7},{2,0},{3,1},{4,2},{5,3},{6,4},{7,5},{8,14},{9,15},{10,... | collective-permute-start | bytes 98312 | tf_op jit(solution)/shard_map/ppermute | solution.py:767
  181.6 48.8 %collective-permute-start.5 = (bf16[512,2048]{1,0:T(8,128)(2,1)}, bf16[512,2048]{1,0:T(8,128)(2,1)}, u32[]{:S(2)}, u32[]{:S(2)}) collective-permute-start(bf16[512,2048]{1,0:T(8,128)(2,1)} %get-tuple-element.50.refs_1_.refs_8_), channel_id=1, source_target_pairs={{0,6},{1,7},{2,0},{3,1},{4,2},{5,3},{6,4},{7,5},{8,14},{9,15},{10,... | collective-permute-start | bytes 6291464 | tf_op jit(solution)/shard_map/ppermute | solution.py:767
  181.7 49.4 %collective-permute-start.3 = (bf16[512,2048]{1,0:T(8,128)(2,1)}, bf16[512,2048]{1,0:T(8,128)(2,1)}, u32[]{:S(2)}, u32[]{:S(2)}) collective-permute-start(bf16[512,2048]{1,0:T(8,128)(2,1)} %get-tuple-element.56.refs_3_.refs_0_.refs_7_), channel_id=1, source_target_pairs={{0,2},{1,3},{2,4},{3,5},{4,6},{5,7},{6,0},{7,1},{8,10},{9,11},{10,... | collective-permute-start | bytes 6291464 | tf_op jit(solution)/shard_map/ppermute | solution.py:767
  187.1 149.9 %copy-start.1 = (s32[115]{0:T(128)}, s32[115]{0:T(128)S(1)}, u32[]{:S(2)}) copy-start(s32[115]{0:T(128)S(1)} %broadcast_minimum_fusion.3.tl_ref) | copy-start | bytes 1384
  190.9 39.4 %collective-permute-start = (f32[1024,8]{0,1:T(8,128)S(1)}, f32[1024,8]{0,1:T(8,128)S(1)}, u32[]{:S(2)}, u32[]{:S(2)}) collective-permute-start(f32[1024,8]{0,1:T(8,128)S(1)} %fusion.15), channel_id=1, source_target_pairs={{0,2},{1,3},{2,4},{3,5},{4,6},{5,7},{6,0},{7,1},{8,10},{9,11},{10,... | collective-permute-start | bytes 98312 | tf_op jit(solution)/shard_map/ppermute | solution.py:767
  191.2 145.8 %collective-permute-start.4 = (bf16[512,2048]{1,0:T(8,128)(2,1)}, bf16[512,2048]{1,0:T(8,128)(2,1)}, u32[]{:S(2)}, u32[]{:S(2)}) collective-permute-start(bf16[512,2048]{1,0:T(8,128)(2,1)} %get-tuple-element.50.refs_1_.refs_8_), channel_id=1, source_target_pairs={{0,2},{1,3},{2,4},{3,5},{4,6},{5,7},{6,0},{7,1},{8,10},{9,11},{10,... | collective-permute-start | bytes 6291464 | tf_op jit(solution)/shard_map/ppermute | solution.py:767
  230.2 106.7 %collective-permute-start.7 = (bf16[512,2048]{1,0:T(8,128)(2,1)}, bf16[512,2048]{1,0:T(8,128)(2,1)}, u32[]{:S(2)}, u32[]{:S(2)}) collective-permute-start(bf16[512,2048]{1,0:T(8,128)(2,1)} %get-tuple-element.56.refs_3_.refs_0_.refs_7_), channel_id=1, source_target_pairs={{0,6},{1,7},{2,0},{3,1},{4,2},{5,3},{6,4},{7,5},{8,14},{9,15},{10,... | collective-permute-start | bytes 6291464 | tf_op jit(solution)/shard_map/ppermute | solution.py:767
  230.4 106.6 %collective-permute-start.9 = (bf16[512,2048]{1,0:T(8,128)(2,1)}, bf16[512,2048]{1,0:T(8,128)(2,1)}, u32[]{:S(2)}, u32[]{:S(2)}) collective-permute-start(bf16[512,2048]{1,0:T(8,128)(2,1)} %collective-permute-done.5.refs_5_), channel_id=1, source_target_pairs={{0,6},{1,7},{2,0},{3,1},{4,2},{5,3},{6,4},{7,5},{8,14},{9,15},{10,... | collective-permute-start | bytes 6291464 | tf_op jit(solution)/shard_map/ppermute | solution.py:767
  231.2 105.9 %collective-permute-start.8 = (bf16[512,2048]{1,0:T(8,128)(2,1)}, bf16[512,2048]{1,0:T(8,128)(2,1)}, u32[]{:S(2)}, u32[]{:S(2)}) collective-permute-start(bf16[512,2048]{1,0:T(8,128)(2,1)} %collective-permute-done.3.refs_4_.refs_2_), channel_id=1, source_target_pairs={{0,2},{1,3},{2,4},{3,5},{4,6},{5,7},{6,0},{7,1},{8,10},{9,11},{10,... | collective-permute-start | bytes 6291464 | tf_op jit(solution)/shard_map/ppermute | solution.py:767
  487.8 82.1 %collective-permute-start.10 = (bf16[512,2048]{1,0:T(8,128)(2,1)}, bf16[512,2048]{1,0:T(8,128)(2,1)}, u32[]{:S(2)}, u32[]{:S(2)}) collective-permute-start(bf16[512,2048]{1,0:T(8,128)(2,1)} %shard_map.123), channel_id=1, source_target_pairs={{0,2},{1,3},{2,4},{3,5},{4,6},{5,7},{6,0},{7,1},{8,10},{9,11},{10,... | collective-permute-start | bytes 6291464 | tf_op jit(solution)/shard_map/ppermute | solution.py:767
  528.1 82.0 %collective-permute-start.11 = (bf16[512,2048]{1,0:T(8,128)(2,1)}, bf16[512,2048]{1,0:T(8,128)(2,1)}, u32[]{:S(2)}, u32[]{:S(2)}) collective-permute-start(bf16[512,2048]{1,0:T(8,128)(2,1)} %shard_map.124), channel_id=1, source_target_pairs={{0,6},{1,7},{2,0},{3,1},{4,2},{5,3},{6,4},{7,5},{8,14},{9,15},{10,... | collective-permute-start | bytes 6291464 | tf_op jit(solution)/shard_map/ppermute | solution.py:767
  528.2 88.6 %collective-permute-start.12 = (bf16[512,2048]{1,0:T(8,128)(2,1)}, bf16[512,2048]{1,0:T(8,128)(2,1)}, u32[]{:S(2)}, u32[]{:S(2)}) collective-permute-start(bf16[512,2048]{1,0:T(8,128)(2,1)} %get-tuple-element.71), channel_id=1, source_target_pairs={{0,6},{1,7},{2,0},{3,1},{4,2},{5,3},{6,4},{7,5},{8,14},{9,15},{10,... | collective-permute-start | bytes 6291464 | tf_op jit(solution)/shard_map/ppermute | solution.py:767
  528.3 137.8 %collective-permute-start.15 = (bf16[512,2048]{1,0:T(8,128)(2,1)}, bf16[512,2048]{1,0:T(8,128)(2,1)}, u32[]{:S(2)}, u32[]{:S(2)}) collective-permute-start(bf16[512,2048]{1,0:T(8,128)(2,1)} %get-tuple-element.74), channel_id=1, source_target_pairs={{0,2},{1,3},{2,4},{3,5},{4,6},{5,7},{6,0},{7,1},{8,10},{9,11},{10,... | collective-permute-start | bytes 6291464 | tf_op jit(solution)/shard_map/ppermute | solution.py:767
  610.1 56.1 %collective-permute-start.14 = (bf16[512,2048]{1,0:T(8,128)(2,1)}, bf16[512,2048]{1,0:T(8,128)(2,1)}, u32[]{:S(2)}, u32[]{:S(2)}) collective-permute-start(bf16[512,2048]{1,0:T(8,128)(2,1)} %shard_map.126), channel_id=1, source_target_pairs={{0,2},{1,3},{2,4},{3,5},{4,6},{5,7},{6,0},{7,1},{8,10},{9,11},{10,... | collective-permute-start | bytes 6291464 | tf_op jit(solution)/shard_map/ppermute | solution.py:767
  610.2 56.0 %collective-permute-start.17 = (bf16[512,2048]{1,0:T(8,128)(2,1)}, bf16[512,2048]{1,0:T(8,128)(2,1)}, u32[]{:S(2)}, u32[]{:S(2)}) collective-permute-start(bf16[512,2048]{1,0:T(8,128)(2,1)} %collective-permute-done.11), channel_id=1, source_target_pairs={{0,6},{1,7},{2,0},{3,1},{4,2},{5,3},{6,4},{7,5},{8,14},{9,15},{10,... | collective-permute-start | bytes 6291464 | tf_op jit(solution)/shard_map/ppermute | solution.py:767
  612.8 93.8 %collective-permute-start.13 = (bf16[512,2048]{1,0:T(8,128)(2,1)}, bf16[512,2048]{1,0:T(8,128)(2,1)}, u32[]{:S(2)}, u32[]{:S(2)}) collective-permute-start(bf16[512,2048]{1,0:T(8,128)(2,1)} %shard_map.125), channel_id=1, source_target_pairs={{0,6},{1,7},{2,0},{3,1},{4,2},{5,3},{6,4},{7,5},{8,14},{9,15},{10,... | collective-permute-start | bytes 6291464 | tf_op jit(solution)/shard_map/ppermute | solution.py:767
  616.8 89.9 %collective-permute-start.16 = (bf16[512,2048]{1,0:T(8,128)(2,1)}, bf16[512,2048]{1,0:T(8,128)(2,1)}, u32[]{:S(2)}, u32[]{:S(2)}) collective-permute-start(bf16[512,2048]{1,0:T(8,128)(2,1)} %collective-permute-done.10), channel_id=1, source_target_pairs={{0,2},{1,3},{2,4},{3,5},{4,6},{5,7},{6,0},{7,1},{8,10},{9,11},{10,... | collective-permute-start | bytes 6291464 | tf_op jit(solution)/shard_map/ppermute | solution.py:767

commit v6 on v5

--- a/solution.py
+++ b/solution.py
@@ -62,12 +62,13 @@
     return hi, mid, lo
 
 
-LT, LB, RT, RB, OT, OB, PO, PASS = 0, 1, 2, 3, 4, 5, 6, 7
+LT, LB, RT, RB, OT, OB, PO, PASS = range(8)
+SWAPS = "41111111210032329"
 MESH = pl.DeviceIdType.MESH
 
 
-def layer_kernel(nx, x_ref, wv_ref, wk_ref, wq_ref, wo_ref, cos_ref, sin_ref, w1_ref, w3_ref, wr_ref, id_ref,
-                 h_ref, ut_ref, ub_ref, o1_ref, o3_ref, lg_ref, id4_ref,
+def layer_kernel(nx, x_ref, wv_ref, wk_ref, wq_ref, wo_ref, cos_ref, sin_ref, w1_ref, w3_ref, w2_ref, wr_ref, id_ref,
+                 h_ref, ut_ref, ub_ref, o1_ref, o3_ref, o2_ref, lg_ref, id4_ref,
                  w_ref, ab, qb, kb, vb, rb3, ssem, rsem, lsem, iosem, swap_send, swap_recv, id_send, id_recv):
     shards = (wv_ref, wk_ref, wq_ref, wo_ref)
     sh = wv_ref.shape[0]
@@ -137,30 +138,26 @@
         for k in (LB, RT):
             arrive(w, k)
             across(w, k).start()
-        if w != 2:
-            swap()
-        if w == 3:
-            swap()
+        swap()
 
     def stage_c(w):
         for k in (OT, OB):
             arrive(w, k)
             across(w, k).start()
-        if w != 2:
-            swap()
+        swap()
 
     def stage_d(w):
         for k in (PO, PASS + LT, PASS + RB, PASS + LB, PASS + RT, PASS + OT, PASS + OB):
             arrive(w, k)
         mine(w).wait()
 
-    pieces = [(src.at[e], dst.at[e]) for e in range(w1_ref.shape[0]) for src, dst in ((w1_ref, o1_ref), (w3_ref, o3_ref))]
+    pieces = [(src.at[e], dst.at[e]) for e in range(w1_ref.shape[0]) for src, dst in ((w1_ref, o1_ref), (w3_ref, o3_ref), (w2_ref, o2_ref))]
     swaps = [pltpu.make_async_remote_copy(src_ref=src, dst_ref=dst, send_sem=swap_send.at[i], recv_sem=swap_recv.at[i],
                                           device_id={"ep": partner}, device_id_type=MESH) for i, (src, dst) in enumerate(pieces)]
-    waiting = list(swaps)
+    waiting, quota = list(swaps), iter(SWAPS)
 
     def swap():
-        if waiting:
+        for _ in range(min(int(next(quota)), len(waiting))):
             waiting.pop(0).start()
 
     ids = [pltpu.make_async_remote_copy(src_ref=id_ref, dst_ref=id4_ref.at[k + 1], send_sem=id_send.at[k], recv_sem=id_recv.at[k],
@@ -174,7 +171,7 @@
     xin.start()
     xin.wait()
     rb = min(256, t)
-    rb3[:] = jnp.concatenate([*split3(wr_ref[:]), jnp.zeros(wr_ref.shape, BF)], axis=1)
+    rb3[:] = jnp.concatenate(split3(wr_ref[:]), axis=0)
 
     @loop(t // rb)
     def _(i):
@@ -202,8 +199,6 @@
         stage_c(w)
         stage_d(w)
         swap()
-        if w == 2:
-            swap()
         project(w, dst, rope)
     stage_a(3)
 
@@ -233,6 +228,7 @@
                 p = (p * (1.0 / jnp.sum(p, axis=0, keepdims=True))).astype(BF)
                 qb[r, c] = lax.dot_general(p, vb[:n, c], TN, preferred_element_type=F32).astype(BF)
 
+    swap()
     xin = pltpu.make_async_copy(x_ref, vb, iosem.at[0])
     xin.start()
     stage_d(3)
@@ -255,16 +251,15 @@
         r = pl.ds(pl.multiple_of(i * rb, rb), rb)
         hi, mid, lo = split3(rmsnorm(ab[r, :]))
         kb[r, :] = hi
-        ne = wr_ref.shape[1]
+        ne = wr_ref.shape[0]
         part = lambda v, k: v[:, k * ne:(k + 1) * ne]
-        p1, p2, p3 = dot(hi, rb3[:]), dot(mid, rb3[:, :2 * ne]), dot(lo, rb3[:, :2 * ne])
+        p1, p2, p3 = [lax.dot_general(v, rb3[:n * ne], NT, preferred_element_type=F32) for v, n in ((hi, 3), (mid, 2), (lo, 1))]
         lg_ref[r, :] = part(p1, 0) + ((part(p1, 1) + part(p2, 0)) + (part(p1, 2) + part(p2, 1) + part(p3, 0)))
 
     uout = [pltpu.make_async_copy(kb.at[pl.ds(p * t // 2, t // 2), :], o, iosem.at[1 + p]) for p, o in enumerate((ut_ref, ub_ref))]
     for c in uout:
         c.start()
-    while waiting:
-        swap()
+    assert not waiting
     for c in swaps + ids:
         c.wait()
     for w in range(4):
@@ -275,7 +270,7 @@
         c.wait()
 
 
-def attention_layer(nx, x, wv, wk, wq, wo, cos, sin, w1, w3, wr, ids):
+def attention_layer(nx, x, wv, wk, wq, wo, cos, sin, w1, w3, w2, wr, ids):
     t, d = x.shape
     hb = pl.BlockSpec(memory_space=pl.ANY)
     vm = pl.BlockSpec(memory_space=pltpu.VMEM)
@@ -283,19 +278,19 @@
     act = pltpu.VMEM((t, d), BF)
     return pl.pallas_call(
         functools.partial(layer_kernel, nx),
-        in_specs=[hb] * 5 + [vm] * 2 + [hb] * 2 + [vm, hb],
-        out_specs=[hb] * 5 + [vm, hb],
+        in_specs=[hb] * 5 + [vm] * 2 + [hb] * 3 + [vm, hb],
+        out_specs=[hb] * 6 + [vm, hb],
         out_shape=[jax.ShapeDtypeStruct((t, d), BF), half, half, jax.ShapeDtypeStruct(w1.shape, BF),
-                   jax.ShapeDtypeStruct(w3.shape, BF), jax.ShapeDtypeStruct((t, wr.shape[1]), F32),
+                   *[jax.ShapeDtypeStruct(v.shape, BF) for v in (w3, w2)], jax.ShapeDtypeStruct((t, wr.shape[0]), F32),
                    jax.ShapeDtypeStruct((nx, *ids.shape), I32)],
-        scratch_shapes=[pltpu.VMEM((4, d, d), BF), act, act, act, act, pltpu.VMEM((d, 4 * wr.shape[1]), BF),
+        scratch_shapes=[pltpu.VMEM((4, d, d), BF), act, act, act, act, pltpu.VMEM((3 * wr.shape[0], d), BF),
                         pltpu.SemaphoreType.DMA((4, 13)), pltpu.SemaphoreType.DMA((4, 13)),
                         pltpu.SemaphoreType.DMA((4,)), pltpu.SemaphoreType.DMA((3,)),
-                        pltpu.SemaphoreType.DMA((2 * w1.shape[0],)), pltpu.SemaphoreType.DMA((2 * w1.shape[0],)),
+                        pltpu.SemaphoreType.DMA((3 * w1.shape[0],)), pltpu.SemaphoreType.DMA((3 * w1.shape[0],)),
                         pltpu.SemaphoreType.DMA((nx,)), pltpu.SemaphoreType.DMA((nx,))],
         compiler_params=params(collective_id=0, has_side_effects=True),
         cost_estimate=cost(8 * t * d * d, 24 * t * d),
-    )(x, wv, wk, wq, wo, cos, sin, w1, w3, wr, ids)
+    )(x, wv, wk, wq, wo, cos, sin, w1, w3, w2, wr, ids)
 
 
 def fetch_expert(l, slot, own, other, bufs, sem):
@@ -507,54 +502,56 @@
     return jnp.concatenate(hits, axis=0), ls
 
 
-def gather_kernel(nch_ref, eg_ref, pos_ref, *refs):
-    us, (x_ref, ubuf, xbuf, usem, sem) = refs[:-5], refs[-5:]
+def gather_kernel(js, nch_ref, eg_ref, pos_ref, *refs):
+    us, (x_ref, ubuf, xbuf, usem, sem) = refs[:len(js)], refs[-5:]
     cap = x_ref.shape[0] // pos_ref.shape[0]
-    cps = [pltpu.make_async_copy(u, ubuf.at[j % 2], usem.at[j % 2]) for j, u in enumerate(us)]
+    cps = [pltpu.make_async_copy(u, ubuf.at[p % 2], usem.at[p % 2]) for p, u in enumerate(us)]
     cps[0].start()
-    for j in range(len(us)):
-        nch = nch_ref[j]
-
-        def out(i, slot):
-            dst = pl.multiple_of(j * cap + i * CHUNK, CHUNK)
-            return pltpu.make_async_copy(xbuf.at[slot], x_ref.at[pl.ds(dst, CHUNK), :], sem.at[slot])
-
-        if j + 1 < len(us):
-            cps[j + 1].start()
-        cps[j].wait()
-
-        @loop(nch)
+
+    def out(slot, row):
+        return pltpu.make_async_copy(xbuf.at[slot], x_ref.at[pl.ds(pl.multiple_of(row, CHUNK), CHUNK), :], sem.at[slot])
+
+    made = 0
+    for p, j in enumerate(js):
+        if p + 1 < len(js):
+            cps[p + 1].start()
+        cps[p].wait()
+
+        @loop(nch_ref[j])
         def _(i):
-            slot = parity(i)
-
-            @pl.when(i >= 2)
+            slot = parity(made + i)
+
+            @pl.when(made + i >= 2)
             def _():
-                out(i - 2, slot).wait()
-
-            xbuf[slot] = dot(selection(j, i, eg_ref, pos_ref)[0], ubuf[j % 2]).astype(BF)
-            out(i, slot).start()
-
-        for k in (2, 1):
-            @pl.when(nch >= k)
-            def _():
-                out(nch - k, parity(nch - k)).wait()
-
-
-def gather(r, us):
+                out(slot, 0).wait()
+
+            xbuf[slot] = dot(selection(j, i, eg_ref, pos_ref)[0], ubuf[p % 2]).astype(BF)
+            out(slot, j * cap + i * CHUNK).start()
+
+        made = made + nch_ref[j]
+    for k in (2, 1):
+        @pl.when(made >= k)
+        def _():
+            out(parity(made - k), 0).wait()
+
+
+def gather(js, r, us, x):
     t, d = us[0].shape
     rows = r.eg.size * PIECE
     vm = pl.BlockSpec(memory_space=pltpu.VMEM)
     sm = pl.BlockSpec(memory_space=pltpu.SMEM)
     hb = pl.BlockSpec(memory_space=pl.ANY)
+    more = [] if x is None else [x]
     return pl.pallas_call(
-        gather_kernel,
-        in_specs=[sm, sm, vm] + [hb] * len(us),
+        functools.partial(gather_kernel, js),
+        in_specs=[sm, sm, vm] + [hb] * len(us + more),
         out_specs=hb,
         out_shape=jax.ShapeDtypeStruct((rows, d), BF),
+        input_output_aliases={3 + len(us): 0} if more else {},
         scratch_shapes=[pltpu.VMEM((2, t, d), BF), pltpu.VMEM((2, CHUNK, d), BF), DMA2, DMA2],
         compiler_params=params(),
         cost_estimate=cost(t * d, 4 * CHUNK * d),
-    )(r.nch, r.eg.reshape(-1), r.pos, *us)
+    )(r.nch, r.eg.reshape(-1), r.pos, *us, *more)
 
 
 def cold_kernel(nt_ref, tl_ref, tp_ref, tn_ref, tw_ref, tf_ref, nx_ref, pc_ref, x_ref, *refs):
@@ -674,7 +671,7 @@
 def final(h, accs, parts):
     t, d = h.shape
     half = t // 2
-    tm = min(128, half)
+    tm = min(256, half)
     n = half // tm
 
     def body(h_ref, *refs):
@@ -766,9 +763,6 @@
     def shift(v, s):
         return lax.ppermute(v, 'ep', [(2 * i + c, 2 * ((i + s) % nx) + c) for i in range(nx) for c in range(2)])
 
-    def partner(v):
-        return lax.ppermute(v, 'ep', [(i, i ^ 1) for i in range(nd)])
-
     def local(x, wq, wk, wv, wo, wr, w1, w3, w2, idx):
         b, s, d = x.shape
         t, k, ne = b * s, idx.shape[-1], w1.shape[0]
@@ -782,10 +776,8 @@
         ang = (np.arange(t) % s).astype(np.float32)[:, None] * np.float32(THETA) ** (-np.arange(hd, dtype=np.float32) / hd)
         c, sn = np.cos(ang), np.sin(ang)
         cos, sin = [jnp.asarray(np.concatenate(v, axis=1), F32) for v in ((c, c), (-sn, sn))]
-        h, ut, ub, o1, o3, logits, ids4 = attention_layer(nx, x, wv, wk, wq, wo, cos, sin, w1, w3, wr, ids.T)
+        h, ut, ub, o1, o3, o2, logits, ids4 = attention_layer(nx, x, wv, wk, wq, wo, cos, sin, w1, w3, w2, wr.T, ids.T)
         ids4 = jnp.swapaxes(ids4, 1, 2)
-        ids4, w2, ut, ub = lax.optimization_barrier((ids4, w2, ut, ub))
-        o2 = partner(w2)
         own, other = (w1, w3, w2), (o1, o3, o2)
 
         halves = lambda v: v.reshape(2 * v.shape[0], half, *v.shape[2:])
@@ -801,27 +793,32 @@
         g4 = [g, shift(g, 1), shift(g, -1), shift(g, 2)]
         u1b, u2t = shift(ub2, 1), shift(ut2, -1)
         spread = lambda o, v: jnp.sum(jnp.where(o, halves(v)[:, None], 0.0), axis=3)
+        ra = r._replace(gt=spread(ohl[:2], g[None]))
         r = r._replace(gt=spread(ohl, jnp.stack(g4)))
 
+        a0, = block((0,), ra, None, (ut,), (None,), own, other, F32, ON, comb=False)
+        a0, u1t, u2b = lax.optimization_barrier((a0, u1t, u2b))
         u3t, u3b = shift(u1t, 1), shift(u2b, -1)
-        a0, d2, d5 = block((0, 2, 5), r, None, (ut, u1t, u2b), 3 * (None,), own, other, F32, 3 * ON, comb=False)
+        d2, d5 = block((2, 5), r, None, (u1t, u2b), 2 * (None,), own, other, F32, 2 * ON, comb=False)
         u1b, d2 = lax.optimization_barrier((u1b, d2))
-        x = gather(r, (ut, ub, u1t, u1b, u2t, u2b, u3t, u3b))
+        x = gather(tuple(range(6)), r, [ut, ub, u1t, u1b, u2t, u2b], None)
+        u3t, x = lax.optimization_barrier((u3t, x))
+        x = gather((6, 7), r, [u3t, u3b], x)
         z = cold(plan, x, own, other)
 
         tie = lambda r, *v: (lambda w: (r._replace(nch=w[0]), *w[1:]))(lax.optimization_barrier((r.nch, *v)))
+        b6, = block((6,), r, z, (u3t,), (None,), own, other, BF, ON)
+        r, b6 = tie(r, b6)
+        c6 = shift(b6, 1)
         b2, b5 = block((2, 5), r, z, (), (d2, d5), own, other, BF, (False, False))
         r, b2, b5 = tie(r, b2, b5)
         b2, b5 = shift(b2, -1), shift(b5, 1)
-        b6, = block((6,), r, z, (u3t,), (None,), own, other, BF, ON)
-        r, b6 = tie(r, b6)
-        c6 = shift(b6, 1)
         b7, = block((7,), r, z, (u3b,), (None,), own, other, BF, ON)
-        r, b7 = tie(r, b7)
-        c7 = shift(b7, -1)
+        r, b7, c6 = tie(r, b7, c6)
+        c7, b6 = shift(b7, -1), shift(c6, 1)
         b3, = block((3,), r, z, (u1b,), (None,), own, other, BF, ON)
-        r, b3, c6 = tie(r, b3, c6)
-        b3, b6 = shift(b3, -1), shift(c6, 1)
+        r, b3 = tie(r, b3)
+        b3 = shift(b3, -1)
         b4, = block((4,), r, z, (u2t,), (None,), own, other, BF, ON)
         r, b4, c7 = tie(r, b4, c7)
         b4, b7 = shift(b4, 1), shift(c7, -1)

time: 733 us -> 787 us (1.074)
  waiting for transfers between devices: 82.6 us -> 122 us
  Pallas kernels: 601 us -> 616 us
    ppermute x17, waiting for transfers between devices: 82.6 us -> 122 us  [shift(): lax.ppermute(v, 'ep', [(2 * i + c, 2 * ((i + s) % nx) + c) for i in range...]
    pallas_call x1, Pallas kernels: 173 us -> 184 us  [attention_layer(): pl.pallas_call(functools.partial(layer_kernel, nx), in_specs=[hb] * 5 + [...]
    pallas_call x7 -> x8, Pallas kernels: 323 us -> 329 us  [block(): pl.pallas_call(functools.partial(block_kernel, js, [v is not None for v i...]
    pallas_call x1 -> x2, Pallas kernels: 22.2 us -> 20.5 us  [gather(): pl.pallas_call(functools.partial(gather_kernel, js), in_specs=[sm, sm, vm...]
  transfers between devices with their start and end apart: 18 -> 17, of which waited for: 3 -> 4; matrix products, arithmetic and copies ran while one was open for 3% -> 3% of each run, Pallas kernels for 37% -> 39%
where the time goes in v6:
time: 787 us; the launch traced here: 773 us
  Pallas kernels  616 us (78%)
  waiting for transfers between devices  122 us (16%)
  other arithmetic  15.5 us (2%)
  starting transfers between devices  14.4 us (2%)
    pallas_call x8, Pallas kernels, block(): pl.pallas_call(functools.partial(block_kernel, js, [v is not None for v i...  329 us
    pallas_call x1, Pallas kernels, attention_layer(): pl.pallas_call(functools.partial(layer_kernel, nx), in_specs=[hb] * 5 + [...  184 us
    ppermute x17, waiting for transfers between devices, shift(): lax.ppermute(v, 'ep', [(2 * i + c, 2 * ((i + s) % nx) + c) for i in range...  122 us
    pallas_call x1, Pallas kernels, cold(): pl.pallas_call(cold_kernel, in_specs=[sm] * len(plan) + [hb] * 7, out_spe...  70.1 us
    pallas_call x2, Pallas kernels, gather(): pl.pallas_call(functools.partial(gather_kernel, js), in_specs=[sm, sm, vm...  20.5 us
  transfers between devices with their start and end apart: 17, of which 4 were waited for; matrix products, arithmetic and copies ran while one was open for 3% of the time, Pallas kernels for 39%

profile of v6, /device:TPU:113, one launch (start us, length us, event | category | flops | bytes accessed | tf_op | source)
XLA Modules:
  0.0 773.4 jit_solution(15480639802796070169)
XLA Ops:
  0.0 184.2 %shard_map.118 = (bf16[1024,2048]{1,0:T(8,128)(2,1)}, bf16[512,2048]{1,0:T(8,128)(2,1)}, bf16[512,2048]{1,0:T(8,128)(2,1)}, bf16[8,2048,1024]{2,1,0:T(8,128)(2,1...) custom-call(bf16[1024,2048]{1,0:T(8,128)(2,1)} %bitcast.63, ...), custom_call_target="tpu_custom_call" | custom-call | flops 34359738368 | bytes 50331648 | tf_op jit(solution)/shard_map/pallas_call | solution.py:279
  184.3 1.3 collective-permute-start.4
  185.6 0.3 collective-permute-start.3
  185.8 1.2 copy.60
  187.0 0.3 select_reduce_fusion.2
  187.4 1.6 collective-permute-start.2
  189.0 1.5 collective-permute-start.6
  190.5 1.2 collective-permute-start.7
  191.7 1.0 fusion.5
  192.7 1.0 add_select_fusion.2
  193.7 0.9 fusion
  194.5 0.2 convolution_convert_fusion
  194.8 0.3 slice_reduce_fusion
  195.1 0.2 reduce_window_sum.37
  195.3 0.7 slice_reduce_fusion.1.refs_0_
  196.0 0.2 convert_reduce_fusion.2
  196.2 0.2 reduce_window_sum.38
  196.7 0.6 min.52.refs_1_
  197.6 0.1 reduce.7
  197.9 0.1 reduce.5
  198.1 0.1 reduce.6
  198.2 0.2 reduce-window.32
  198.5 0.1 copy.61
  198.6 0.8 select_reduce_fusion.3.refs_2_
  199.4 35.7 %shard_map.119.refs_15_ = f32[512,2048]{1,0:T(8,128)} custom-call(s32[8]{0:T(128)} %slice_reduce_fusion.1.refs_0_, s32[128]{0:T(128)} %min.52.refs_1_, f32[2,16,512]{2,1,0:T(8,128)} %select_reduce_fusion.3.refs_2_, bf16[512,2048]{1,0:T(8,128)(2,1)} %get-tuple-element.56.refs_3_.refs_0_.refs_7_, bf16[8,2048,1024]{2,1,0:T(8,128)(2,1)} %refs_9_.9, ...), custom_call_target="tpu_custom_call" | custom-call | flops 1048576 | bytes 12582912 | tf_op jit(solution)/shard_map/pallas_call | solution.py:483
  235.3 0.1 convert_reduce_fusion.1
  235.5 0.7 select_reduce_fusion.4
  236.1 0.3 fusion.12
  236.4 0.7 convert_reduce_fusion
  237.1 2.6 select_reduce_fusion
  239.7 0.1 collective-permute-start.5
  239.9 2.6 collective-permute-start.8
  242.5 0.3 fusion.14
  242.8 0.5 compare_convert_fusion.1.tf_ref
  243.3 0.6 subtract_clamp_fusion
  243.9 0.6 add_clamp_fusion.pc_ref
  244.5 0.8 add_select_fusion.pos_ref.refs_5_.refs_3_
  245.3 0.2 multiply_reduce_fusion
  245.6 0.5 negate_maximum_fusion.nch_ref.refs_3_.refs_1_
  246.2 75.6 %collective-permute-done.1 = f32[1024,8]{0,1:T(8,128)S(1)} collective-permute-done((f32[1024,8]{0,1:T(8,128)S(1)}, f32[1024,8]{0,1:T(8,128)S(1)}, u32[]{:S(2)}, u32[]{:S(2)}) %collective-permute-start.1) | collective-permute-done | bytes 32800 | tf_op jit(solution)/shard_map/ppermute | solution.py:764
  321.8 0.7 collective-permute-start
  322.5 0.5 compare_select_fusion.2.nx_ref
  323.0 0.6 slice.25
  323.6 0.7 min.55.eg_ref.refs_4_.refs_2_
  324.3 1.4 collective-permute-done
  325.7 1.6 select_reduce_fusion.1.refs_2_.refs_0_
  327.3 65.4 %shard_map.120 = (f32[512,2048]{1,0:T(8,128)}, f32[512,2048]{1,0:T(8,128)}) custom-call(s32[8]{0:T(128)} %slice_reduce_fusion.1.refs_0_, s32[128]{0:T(128)} %min.52.refs_1_, f32[8,16,512]{2,1,0:T(8,128)} %select_reduce_fusion.1.refs_2_.refs_0_, bf16[512,2048]{1,0:T(8,128)(2,1)} %collective-permute-done.3.refs_3_.refs_2_, ...), custom_call_target="tpu_custom_call" | custom-call | flops 1048576 | bytes 12582912 | tf_op jit(solution)/shard_map/pallas_call | solution.py:483
  392.8 13.8 %shard_map.121.refs_2_ = bf16[34816,2048]{1,0:T(8,128)(2,1)} custom-call(s32[8]{0:T(128)} %negate_maximum_fusion.nch_ref.refs_3_.refs_1_, s32[4352]{0:T(1024)} %min.55.eg_ref.refs_4_.refs_2_, s32[8,16,512]{2,1,0:T(8,128)} %add_select_fusion.pos_ref.refs_5_.refs_3_, bf16[512,2048]{1,0:T(8,128)(2,1)} %get-tuple-element.56.refs_3_.refs_0_.refs_7_, ...), custom_call_target="tpu_custom_call" | custom-call | flops 1048576 | bytes 2097152 | tf_op jit(solution)/shard_map/pallas_call | solution.py:545
  406.6 6.8 shard_map.122.x_ref
  413.3 70.1 %shard_map.123.refs_6_.refs_4_ = bf16[34816,2048]{1,0:T(8,128)(2,1)} custom-call(s32[1]{0:T(128)} %bitcast.15.nt_ref, s32[115]{0:T(128)} %copy-done.1, s32[115]{0:T(128)} %get-tuple-element.91.tp_ref, s32[115]{0:T(128)} %get-tuple-element.90.tn_ref, s32[115]{0:T(128)} %get-tuple-element.80.tw_ref, ...), custom_call_target="tpu_custom_call", output_to_operand_aliasing={{}: (8, {})} | custom-call | flops 70866960384 | bytes 201326592 | tf_op jit(solution)/shard_map/pallas_call | solution.py:648
  483.4 40.1 %shard_map.124 = bf16[512,2048]{1,0:T(8,128)(2,1)} custom-call(s32[8]{0:T(128)} %slice_reduce_fusion.1.refs_0_, s32[128]{0:T(128)} %min.52.refs_1_, f32[8,16,512]{2,1,0:T(8,128)} %select_reduce_fusion.1.refs_2_.refs_0_, s32[8]{0:T(128)} %negate_maximum_fusion.nch_ref.refs_3_.refs_1_, s32[4352]{0:T(1024)} %min.55.eg_ref.refs_4_.refs_2_, ...), custom_call_target="tpu_custom_call" | custom-call | flops 1048576 | bytes 12582912 | tf_op jit(solution)/shard_map/pallas_call | solution.py:483
  523.5 0.1 collective-permute-start.9
  523.6 17.9 %shard_map.125 = (bf16[512,2048]{1,0:T(8,128)(2,1)}, bf16[512,2048]{1,0:T(8,128)(2,1)}) custom-call(f32[8,16,512]{2,1,0:T(8,128)} %select_reduce_fusion.1.refs_2_.refs_0_, s32[8]{0:T(128)} %negate_maximum_fusion.nch_ref.refs_3_.refs_1_, s32[4352]{0:T(1024)} %min.55.eg_ref.refs_4_.refs_2_, s32[8,16,512]{2,1,0:T(8,128)} %add_select_fusion.pos_ref.refs_5_.refs_3_, ...), custom_call_target="tpu_custom_call" | custom-call | flops 1048576 | bytes 12582912 | tf_op jit(solution)/shard_map/pallas_call | solution.py:483
  541.6 40.1 %shard_map.126 = bf16[512,2048]{1,0:T(8,128)(2,1)} custom-call(s32[8]{0:T(128)} %slice_reduce_fusion.1.refs_0_, s32[128]{0:T(128)} %min.52.refs_1_, f32[8,16,512]{2,1,0:T(8,128)} %select_reduce_fusion.1.refs_2_.refs_0_, s32[8]{0:T(128)} %negate_maximum_fusion.nch_ref.refs_3_.refs_1_, s32[4352]{0:T(1024)} %min.55.eg_ref.refs_4_.refs_2_, ...), custom_call_target="tpu_custom_call" | custom-call | flops 1048576 | bytes 12582912 | tf_op jit(solution)/shard_map/pallas_call | solution.py:483
  581.7 0.1 collective-permute-start.10
  581.9 1.4 collective-permute-start.14
  583.4 40.1 %shard_map.127 = bf16[512,2048]{1,0:T(8,128)(2,1)} custom-call(s32[8]{0:T(128)} %slice_reduce_fusion.1.refs_0_, s32[128]{0:T(128)} %min.52.refs_1_, f32[8,16,512]{2,1,0:T(8,128)} %select_reduce_fusion.1.refs_2_.refs_0_, s32[8]{0:T(128)} %negate_maximum_fusion.nch_ref.refs_3_.refs_1_, s32[4352]{0:T(1024)} %min.55.eg_ref.refs_4_.refs_2_, ...), custom_call_target="tpu_custom_call" | custom-call | flops 1048576 | bytes 12582912 | tf_op jit(solution)/shard_map/pallas_call | solution.py:483
  623.6 1.4 collective-permute-start.15
  625.0 40.1 %shard_map.128 = bf16[512,2048]{1,0:T(8,128)(2,1)} custom-call(s32[8]{0:T(128)} %slice_reduce_fusion.1.refs_0_, s32[128]{0:T(128)} %min.52.refs_1_, f32[8,16,512]{2,1,0:T(8,128)} %select_reduce_fusion.1.refs_2_.refs_0_, s32[8]{0:T(128)} %negate_maximum_fusion.nch_ref.refs_3_.refs_1_, s32[4352]{0:T(1024)} %min.55.eg_ref.refs_4_.refs_2_, ...), custom_call_target="tpu_custom_call" | custom-call | flops 1048576 | bytes 12582912 | tf_op jit(solution)/shard_map/pallas_call | solution.py:483
  665.3 5.6 collective-permute-done.11.refs_2_
  670.9 1.5 collective-permute-start.16
  672.4 49.4 %shard_map.129 = (f32[512,2048]{1,0:T(8,128)}, f32[512,2048]{1,0:T(8,128)}) custom-call(s32[8]{0:T(128)} %slice_reduce_fusion.1.refs_0_, s32[128]{0:T(128)} %min.52.refs_1_, f32[8,16,512]{2,1,0:T(8,128)} %select_reduce_fusion.1.refs_2_.refs_0_, s32[8]{0:T(128)} %negate_maximum_fusion.nch_ref.refs_3_.refs_1_, s32[4352]{0:T(1024)} %min.55.eg_ref.refs_4_.refs_2_, ...), custom_call_target="tpu_custom_call" | custom-call | flops 1048576 | bytes 12582912 | tf_op jit(solution)/shard_map/pallas_call | solution.py:483
  721.9 38.9 %collective-permute-done.16.refs_7_ = bf16[512,2048]{1,0:T(8,128)(2,1)} collective-permute-done((bf16[512,2048]{1,0:T(8,128)(2,1)}, bf16[512,2048]{1,0:T(8,128)(2,1)}, u32[]{:S(2)}, u32[]{:S(2)}) %collective-permute-start.16) | collective-permute-done | bytes 2097184 | tf_op jit(solution)/shard_map/ppermute | solution.py:764
  760.8 12.2 %shard_map.130 = bf16[1024,2048]{1,0:T(8,128)(2,1)} custom-call(bf16[1024,2048]{1,0:T(8,128)(2,1)} %get-tuple-element.42.h_ref, f32[512,2048]{1,0:T(8,128)} %get-tuple-element.71.refs_0_, f32[512,2048]{1,0:T(8,128)} %get-tuple-element.72.refs_1_, bf16[512,2048]{1,0:T(8,128)(2,1)} %collective-permute-done.11.refs_2_, ...), custom_call_target="tpu_custom_call" | custom-call | flops 12582912 | bytes 41943040 | tf_op jit(solution)/shard_map/pallas_call | solution.py:684
  (52 shorter events, 1.7 us)
Async XLA Ops:
  0.0 187.0 %copy-start = (s32[1,1024,8]{1,2,0:T(8,128)S(1)}, s32[1,1024,8]{1,2,0:T(8,128)}, u32[]{:S(2)}) copy-start(s32[1,1024,8]{1,2,0:T(8,128)} %param.21) | copy-start | bytes 98308
  184.3 55.5 %collective-permute-start.4 = (bf16[512,2048]{1,0:T(8,128)(2,1)}, bf16[512,2048]{1,0:T(8,128)(2,1)}, u32[]{:S(2)}, u32[]{:S(2)}) collective-permute-start(bf16[512,2048]{1,0:T(8,128)(2,1)} %get-tuple-element.52.refs_1_.refs_8_), channel_id=1, source_target_pairs={{0,6},{1,7},{2,0},{3,1},{4,2},{5,3},{6,4},{7,5},{8,14},{9,15},{10,... | collective-permute-start | bytes 6291464 | tf_op jit(solution)/shard_map/ppermute | solution.py:764
  185.6 54.2 %collective-permute-start.3 = (bf16[512,2048]{1,0:T(8,128)(2,1)}, bf16[512,2048]{1,0:T(8,128)(2,1)}, u32[]{:S(2)}, u32[]{:S(2)}) collective-permute-start(bf16[512,2048]{1,0:T(8,128)(2,1)} %get-tuple-element.56.refs_3_.refs_0_.refs_7_), channel_id=1, source_target_pairs={{0,2},{1,3},{2,4},{3,5},{4,6},{5,7},{6,0},{7,1},{8,10},{9,11},{10,... | collective-permute-start | bytes 6291464 | tf_op jit(solution)/shard_map/ppermute | solution.py:764
  187.4 58.1 %collective-permute-start.2 = (f32[1024,8]{0,1:T(8,128)S(1)}, f32[1024,8]{0,1:T(8,128)S(1)}, u32[]{:S(2)}, u32[]{:S(2)}) collective-permute-start(f32[1024,8]{0,1:T(8,128)S(1)} %fusion.15), channel_id=1, source_target_pairs={{0,4},{1,5},{2,6},{3,7},{4,0},{5,1},{6,2},{7,3},{8,12},{9,13},{10,... | collective-permute-start | bytes 98312 | tf_op jit(solution)/shard_map/ppermute | solution.py:764
  189.0 203.7 %collective-permute-start.6 = (bf16[512,2048]{1,0:T(8,128)(2,1)}, bf16[512,2048]{1,0:T(8,128)(2,1)}, u32[]{:S(2)}, u32[]{:S(2)}) collective-permute-start(bf16[512,2048]{1,0:T(8,128)(2,1)} %get-tuple-element.52.refs_1_.refs_8_), channel_id=1, source_target_pairs={{0,2},{1,3},{2,4},{3,5},{4,6},{5,7},{6,0},{7,1},{8,10},{9,11},{10,... | collective-permute-start | bytes 6291464 | tf_op jit(solution)/shard_map/ppermute | solution.py:764
  190.5 202.2 %collective-permute-start.7 = (bf16[512,2048]{1,0:T(8,128)(2,1)}, bf16[512,2048]{1,0:T(8,128)(2,1)}, u32[]{:S(2)}, u32[]{:S(2)}) collective-permute-start(bf16[512,2048]{1,0:T(8,128)(2,1)} %get-tuple-element.56.refs_3_.refs_0_.refs_7_), channel_id=1, source_target_pairs={{0,6},{1,7},{2,0},{3,1},{4,2},{5,3},{6,4},{7,5},{8,14},{9,15},{10,... | collective-permute-start | bytes 6291464 | tf_op jit(solution)/shard_map/ppermute | solution.py:764
  235.4 0.7 copy-start.1
  239.7 166.8 %collective-permute-start.5 = (bf16[512,2048]{1,0:T(8,128)(2,1)}, bf16[512,2048]{1,0:T(8,128)(2,1)}, u32[]{:S(2)}, u32[]{:S(2)}) collective-permute-start(bf16[512,2048]{1,0:T(8,128)(2,1)} %collective-permute-done.3.refs_3_.refs_2_), channel_id=1, source_target_pairs={{0,2},{1,3},{2,4},{3,5},{4,6},{5,7},{6,0},{7,1},{8,10},{9,11},{10,... | collective-permute-start | bytes 6291464 | tf_op jit(solution)/shard_map/ppermute | solution.py:764
  239.9 166.7 %collective-permute-start.8 = (bf16[512,2048]{1,0:T(8,128)(2,1)}, bf16[512,2048]{1,0:T(8,128)(2,1)}, u32[]{:S(2)}, u32[]{:S(2)}) collective-permute-start(bf16[512,2048]{1,0:T(8,128)(2,1)} %collective-permute-done.4.refs_4_.refs_5_), channel_id=1, source_target_pairs={{0,6},{1,7},{2,0},{3,1},{4,2},{5,3},{6,4},{7,5},{8,14},{9,15},{10,... | collective-permute-start | bytes 6291464 | tf_op jit(solution)/shard_map/ppermute | solution.py:764
  245.5 76.2 %collective-permute-start.1 = (f32[1024,8]{0,1:T(8,128)S(1)}, f32[1024,8]{0,1:T(8,128)S(1)}, u32[]{:S(2)}, u32[]{:S(2)}) collective-permute-start(f32[1024,8]{0,1:T(8,128)S(1)} %fusion.15), channel_id=1, source_target_pairs={{0,6},{1,7},{2,0},{3,1},{4,2},{5,3},{6,4},{7,5},{8,14},{9,15},{10,... | collective-permute-start | bytes 98312 | tf_op jit(solution)/shard_map/ppermute | solution.py:764
  321.8 4.0 collective-permute-start
  523.5 58.2 %collective-permute-start.9 = (bf16[512,2048]{1,0:T(8,128)(2,1)}, bf16[512,2048]{1,0:T(8,128)(2,1)}, u32[]{:S(2)}, u32[]{:S(2)}) collective-permute-start(bf16[512,2048]{1,0:T(8,128)(2,1)} %shard_map.124), channel_id=1, source_target_pairs={{0,2},{1,3},{2,4},{3,5},{4,6},{5,7},{6,0},{7,1},{8,10},{9,11},{10,... | collective-permute-start | bytes 6291464 | tf_op jit(solution)/shard_map/ppermute | solution.py:764
  581.7 83.4 %collective-permute-start.10 = (bf16[512,2048]{1,0:T(8,128)(2,1)}, bf16[512,2048]{1,0:T(8,128)(2,1)}, u32[]{:S(2)}, u32[]{:S(2)}) collective-permute-start(bf16[512,2048]{1,0:T(8,128)(2,1)} %shard_map.126), channel_id=1, source_target_pairs={{0,6},{1,7},{2,0},{3,1},{4,2},{5,3},{6,4},{7,5},{8,14},{9,15},{10,... | collective-permute-start | bytes 6291464 | tf_op jit(solution)/shard_map/ppermute | solution.py:764
  581.8 89.1 %collective-permute-start.11 = (bf16[512,2048]{1,0:T(8,128)(2,1)}, bf16[512,2048]{1,0:T(8,128)(2,1)}, u32[]{:S(2)}, u32[]{:S(2)}) collective-permute-start(bf16[512,2048]{1,0:T(8,128)(2,1)} %get-tuple-element.73), channel_id=1, source_target_pairs={{0,6},{1,7},{2,0},{3,1},{4,2},{5,3},{6,4},{7,5},{8,14},{9,15},{10,... | collective-permute-start | bytes 6291464 | tf_op jit(solution)/shard_map/ppermute | solution.py:764
  581.9 139.9 %collective-permute-start.14 = (bf16[512,2048]{1,0:T(8,128)(2,1)}, bf16[512,2048]{1,0:T(8,128)(2,1)}, u32[]{:S(2)}, u32[]{:S(2)}) collective-permute-start(bf16[512,2048]{1,0:T(8,128)(2,1)} %get-tuple-element.76), channel_id=1, source_target_pairs={{0,2},{1,3},{2,4},{3,5},{4,6},{5,7},{6,0},{7,1},{8,10},{9,11},{10,... | collective-permute-start | bytes 6291464 | tf_op jit(solution)/shard_map/ppermute | solution.py:764
  623.5 98.4 %collective-permute-start.12 = (bf16[512,2048]{1,0:T(8,128)(2,1)}, bf16[512,2048]{1,0:T(8,128)(2,1)}, u32[]{:S(2)}, u32[]{:S(2)}) collective-permute-start(bf16[512,2048]{1,0:T(8,128)(2,1)} %shard_map.127), channel_id=1, source_target_pairs={{0,6},{1,7},{2,0},{3,1},{4,2},{5,3},{6,4},{7,5},{8,14},{9,15},{10,... | collective-permute-start | bytes 6291464 | tf_op jit(solution)/shard_map/ppermute | solution.py:764
  623.6 98.3 %collective-permute-start.15 = (bf16[512,2048]{1,0:T(8,128)(2,1)}, bf16[512,2048]{1,0:T(8,128)(2,1)}, u32[]{:S(2)}, u32[]{:S(2)}) collective-permute-start(bf16[512,2048]{1,0:T(8,128)(2,1)} %collective-permute-done.9), channel_id=1, source_target_pairs={{0,2},{1,3},{2,4},{3,5},{4,6},{5,7},{6,0},{7,1},{8,10},{9,11},{10,... | collective-permute-start | bytes 6291464 | tf_op jit(solution)/shard_map/ppermute | solution.py:764
  665.2 56.7 %collective-permute-start.13 = (bf16[512,2048]{1,0:T(8,128)(2,1)}, bf16[512,2048]{1,0:T(8,128)(2,1)}, u32[]{:S(2)}, u32[]{:S(2)}) collective-permute-start(bf16[512,2048]{1,0:T(8,128)(2,1)} %shard_map.128), channel_id=1, source_target_pairs={{0,2},{1,3},{2,4},{3,5},{4,6},{5,7},{6,0},{7,1},{8,10},{9,11},{10,... | collective-permute-start | bytes 6291464 | tf_op jit(solution)/shard_map/ppermute | solution.py:764
  670.9 89.9 %collective-permute-start.16 = (bf16[512,2048]{1,0:T(8,128)(2,1)}, bf16[512,2048]{1,0:T(8,128)(2,1)}, u32[]{:S(2)}, u32[]{:S(2)}) collective-permute-start(bf16[512,2048]{1,0:T(8,128)(2,1)} %collective-permute-done.10), channel_id=1, source_target_pairs={{0,6},{1,7},{2,0},{3,1},{4,2},{5,3},{6,4},{7,5},{8,14},{9,15},{10,... | collective-permute-start | bytes 6291464 | tf_op jit(solution)/shard_map/ppermute | solution.py:764

commit v7 on v6

--- a/solution.py
+++ b/solution.py
@@ -15,7 +15,7 @@
 PIECE = 8
 CHUNK = 256
 MT = 352
-HM = 256
+HM = 512
 VMEM = 66_000_000
 BF, F32, I32 = jnp.bfloat16, jnp.float32, jnp.int32
 
@@ -63,12 +63,13 @@
 
 
 LT, LB, RT, RB, OT, OB, PO, PASS = range(8)
-SWAPS = "41111111210032329"
+LATE = 3
+SWAPS = "41111111110022229"
 MESH = pl.DeviceIdType.MESH
 
 
 def layer_kernel(nx, x_ref, wv_ref, wk_ref, wq_ref, wo_ref, cos_ref, sin_ref, w1_ref, w3_ref, w2_ref, wr_ref, id_ref,
-                 h_ref, ut_ref, ub_ref, o1_ref, o3_ref, o2_ref, lg_ref, id4_ref,
+                 h_ref, ut_ref, ub_ref, o1_ref, o3_ref, o2_ref, late_ref, lg_ref, id4_ref,
                  w_ref, ab, qb, kb, vb, rb3, ssem, rsem, lsem, iosem, swap_send, swap_recv, id_send, id_recv):
     shards = (wv_ref, wk_ref, wq_ref, wo_ref)
     sh = wv_ref.shape[0]
@@ -151,7 +152,8 @@
             arrive(w, k)
         mine(w).wait()
 
-    pieces = [(src.at[e], dst.at[e]) for e in range(w1_ref.shape[0]) for src, dst in ((w1_ref, o1_ref), (w3_ref, o3_ref), (w2_ref, o2_ref))]
+    pieces = [(src.at[e], dst.at[e]) for e in range(w1_ref.shape[0]) for src, dst in ((w1_ref, o1_ref), (w3_ref, o3_ref), (w2_ref, o2_ref))
+              if e < dst.shape[0]]
     swaps = [pltpu.make_async_remote_copy(src_ref=src, dst_ref=dst, send_sem=swap_send.at[i], recv_sem=swap_recv.at[i],
                                           device_id={"ep": partner}, device_id_type=MESH) for i, (src, dst) in enumerate(pieces)]
     waiting, quota = list(swaps), iter(SWAPS)
@@ -172,6 +174,13 @@
     xin.wait()
     rb = min(256, t)
     rb3[:] = jnp.concatenate(split3(wr_ref[:]), axis=0)
+
+    for e in range(LATE):
+        room = w_ref.at[3, pl.ds(0, w2_ref.shape[1]), :]
+        for c in (pltpu.make_async_copy(w2_ref.at[o2_ref.shape[0] + e], room, iosem.at[3]),
+                  pltpu.make_async_copy(room, late_ref.at[e], iosem.at[3])):
+            c.start()
+            c.wait()
 
     @loop(t // rb)
     def _(i):
@@ -279,13 +288,14 @@
     return pl.pallas_call(
         functools.partial(layer_kernel, nx),
         in_specs=[hb] * 5 + [vm] * 2 + [hb] * 3 + [vm, hb],
-        out_specs=[hb] * 6 + [vm, hb],
+        out_specs=[hb] * 7 + [vm, hb],
         out_shape=[jax.ShapeDtypeStruct((t, d), BF), half, half, jax.ShapeDtypeStruct(w1.shape, BF),
-                   *[jax.ShapeDtypeStruct(v.shape, BF) for v in (w3, w2)], jax.ShapeDtypeStruct((t, wr.shape[0]), F32),
+                   jax.ShapeDtypeStruct(w3.shape, BF),
+                   *[jax.ShapeDtypeStruct((n, *w2.shape[1:]), BF) for n in (w2.shape[0] - LATE, LATE)], jax.ShapeDtypeStruct((t, wr.shape[0]), F32),
                    jax.ShapeDtypeStruct((nx, *ids.shape), I32)],
         scratch_shapes=[pltpu.VMEM((4, d, d), BF), act, act, act, act, pltpu.VMEM((3 * wr.shape[0], d), BF),
                         pltpu.SemaphoreType.DMA((4, 13)), pltpu.SemaphoreType.DMA((4, 13)),
-                        pltpu.SemaphoreType.DMA((4,)), pltpu.SemaphoreType.DMA((3,)),
+                        pltpu.SemaphoreType.DMA((4,)), pltpu.SemaphoreType.DMA((4,)),
                         pltpu.SemaphoreType.DMA((3 * w1.shape[0],)), pltpu.SemaphoreType.DMA((3 * w1.shape[0],)),
                         pltpu.SemaphoreType.DMA((nx,)), pltpu.SemaphoreType.DMA((nx,))],
         compiler_params=params(collective_id=0, has_side_effects=True),
@@ -294,17 +304,26 @@
 
 
 def fetch_expert(l, slot, own, other, bufs, sem):
-    ne = own[0].shape[0]
+    ne, split = own[0].shape[0], other[2].shape[0]
+    start = lambda src, dst: pltpu.make_async_copy(src, dst.at[slot], sem.at[slot]).start()
 
     @pl.when(l < ne)
     def _():
         for src, dst in zip(own, bufs):
-            pltpu.make_async_copy(src.at[l], dst.at[slot], sem.at[slot]).start()
+            start(src.at[l], dst)
 
     @pl.when(l >= ne)
     def _():
-        for src, dst in zip(other, bufs):
-            pltpu.make_async_copy(src.at[l - ne], dst.at[slot], sem.at[slot]).start()
+        for src, dst in zip(other[:2], bufs):
+            start(src.at[l - ne], dst)
+
+    @pl.when(jnp.logical_and(l >= ne, l < ne + split))
+    def _():
+        start(other[2].at[l - ne], bufs[2])
+
+    @pl.when(l >= ne + split)
+    def _():
+        start(other[3].at[l - ne - split], bufs[2])
 
 
 def wait_expert(slot, own, bufs, sem):
@@ -324,14 +343,14 @@
     nblk = len(js)
     take = lambda n: [refs.pop(0) for _ in range(n)]
     if any(dense):
-        nh_ref, hl_ref = take(2)
+        hot_ref, = take(1)
     gt_ref, = take(1)
     if comb:
         nch_ref, eg_ref, pos_ref, z_ref = take(4)
         cap = z_ref.shape[0] // pos_ref.shape[0]
     if any(dense):
         us = take(nblk)
-        own, other = take(3), take(3)
+        own, other = take(3), take(4)
         nl = 2 * own[0].shape[0]
     accs = [take(1)[0] if h else None for h in has_acc]
     outs = take(nblk)
@@ -339,24 +358,22 @@
     if comb:
         cbuf, zbuf, zsem = take(3)
     if any(dense):
-        bufs, (ubuf, sem, usem) = take(3), take(3)
+        bufs, (ubuf, sem, usem, ent_ref) = take(3), take(4)
     t, d = outs[0].shape
 
     if any(dense):
-        ns = [nh_ref[j] if on else 0 for j, on in zip(js, dense)]
-        n = sum(ns)
-
-        def entry(i):
-            p, j, k, end = 0, js[0], i, 0
-            for q in range(nblk - 1):
-                end = end + ns[q]
-                past = i >= end
-                p, j, k = jnp.where(past, q + 1, p), jnp.where(past, js[q + 1], j), jnp.where(past, i - end, k)
-            return p, j, hl_ref[j * nl + k]
+        n = 0
+        for p in range(nblk):
+            def note(l, n, p=p):
+                ent_ref[n] = p * nl + l
+                return n + hot_ref[js[p] * nl + l]
+
+            if dense[p]:
+                n = lax.fori_loop(0, nl, note, n)
 
         @pl.when(n > 0)
         def _():
-            fetch_expert(entry(0)[-1], 0, own, other, bufs, sem)
+            fetch_expert(lax.rem(ent_ref[0], nl), 0, own, other, bufs, sem)
 
         ucp = [pltpu.make_async_copy(us[p], ubuf.at[pl.ds(p * t, t), :], usem) for p in range(nblk)]
         for cp in ucp:
@@ -427,9 +444,12 @@
 
             @pl.when(i + 1 < n)
             def _():
-                fetch_expert(entry(i + 1)[-1], 1 - slot, own, other, bufs, sem)
-
-            p, blk, e = entry(i)
+                fetch_expert(lax.rem(ent_ref[i + 1], nl), 1 - slot, own, other, bufs, sem)
+
+            p, e = lax.div(ent_ref[i], nl), lax.rem(ent_ref[i], nl)
+            blk = js[0]
+            for q in range(1, nblk):
+                blk = jnp.where(p == q, js[q], blk)
 
             @loop(t // tm)
             def _(m):
@@ -456,13 +476,14 @@
     t = r.pos.shape[2]
     d = own[0].shape[1]
     ff = own[0].shape[2]
+    nl = r.pos.shape[1]
     vm = pl.BlockSpec(memory_space=pltpu.VMEM)
     sm = pl.BlockSpec(memory_space=pltpu.SMEM)
     hb = pl.BlockSpec(memory_space=pl.ANY)
     args, specs, scratch = [], [], []
     if any(dense):
-        args += [r.nh, r.hl.reshape(-1)]
-        specs += [sm, sm]
+        args += [r.hot.reshape(-1)]
+        specs += [sm]
     args += [r.gt]
     specs += [vm]
     if comb:
@@ -470,7 +491,7 @@
         specs += [sm, sm, vm, hb]
     if any(dense):
         args += list(us) + list(own) + list(other)
-        specs += [hb] * (nblk + 6)
+        specs += [hb] * (nblk + 7)
     args += [v for v in accs if v is not None]
     specs += [hb for v in accs if v is not None]
     scratch += [pltpu.VMEM((nblk * t, d), F32), pltpu.SemaphoreType.DMA((nblk,))]
@@ -478,7 +499,8 @@
         scratch += [pltpu.VMEM((t, 3 * CHUNK), BF), pltpu.VMEM((2, CHUNK, d), BF), DMA2]
     if any(dense):
         scratch += [*expert_buffers(d, ff),
-                    pltpu.VMEM((nblk * t, d), BF), DMA2, pltpu.SemaphoreType.DMA]
+                    pltpu.VMEM((nblk * t, d), BF), DMA2, pltpu.SemaphoreType.DMA,
+                    pltpu.SMEM((nblk * nl,), I32)]
     out = jax.ShapeDtypeStruct((t, d), dtype)
     return pl.pallas_call(
         functools.partial(block_kernel, js, [v is not None for v in accs], comb, dense),
@@ -554,10 +576,27 @@
     )(r.nch, r.eg.reshape(-1), r.pos, *us, *more)
 
 
-def cold_kernel(nt_ref, tl_ref, tp_ref, tn_ref, tw_ref, tf_ref, nx_ref, pc_ref, x_ref, *refs):
-    own, other, z_ref, refs = refs[:3], refs[3:6], refs[6], refs[7:]
-    bufs, (xbuf, zbuf, wsem, xsem, zsem) = refs[:3], refs[3:]
-    nt = nt_ref[0]
+def cold_kernel(np_ref, pc_ref, x_ref, *refs):
+    own, other, z_ref, refs = refs[:3], refs[3:7], refs[7], refs[8:]
+    bufs, (xbuf, zbuf, wsem, xsem, zsem, tl_ref, tp_ref, tn_ref, tw_ref, nx_ref) = refs[:3], refs[3:]
+    ppt = MT // PIECE
+
+    def tiles(l, carry):
+        q, turn, p = carry
+        n = np_ref[l]
+        more = lax.div(n + ppt - 1, ppt)
+
+        @loop(more)
+        def _(i):
+            tl_ref[q + i] = l
+            tp_ref[q + i] = p + i * ppt
+            tn_ref[q + i] = jnp.minimum(n - i * ppt, ppt)
+            tw_ref[q + i] = turn
+            nx_ref[q + i] = jnp.where(i == 0, q + more, 0)
+
+        return q + more, turn + jnp.minimum(n, 1), p + n
+
+    nt = lax.fori_loop(0, np_ref.shape[0], tiles, (0, 0, 0))[0]
 
     def each(n, fn):
         @loop(lax.div(n, 2))
@@ -614,13 +653,13 @@
         slot = parity(q)
         ws = parity(tw_ref[q])
 
-        @pl.when(tf_ref[q] == 1)
+        @pl.when(nx_ref[q] > 0)
         def _():
             wait_expert(ws, own, bufs, wsem)
 
-            @pl.when(nx_ref[q] >= 0)
+            @pl.when(nx_ref[q] < nt)
             def _():
-                fetch_expert(nx_ref[q], 1 - ws, own, other, bufs, wsem)
+                fetch_expert(tl_ref[nx_ref[q]], 1 - ws, own, other, bufs, wsem)
 
         @pl.when(q + 1 < nt)
         def _():
@@ -647,12 +686,12 @@
     hb = pl.BlockSpec(memory_space=pl.ANY)
     return pl.pallas_call(
         cold_kernel,
-        in_specs=[sm] * len(plan) + [hb] * 7,
+        in_specs=[sm] * len(plan) + [hb] * 8,
         out_specs=hb,
         out_shape=jax.ShapeDtypeStruct(x.shape, BF),
         scratch_shapes=[*expert_buffers(d, ff),
                         pltpu.VMEM((2, MT, d), BF), pltpu.VMEM((2, MT, d), BF),
-                        DMA2, DMA2, DMA2],
+                        DMA2, DMA2, DMA2, *5 * [pltpu.SMEM((plan[1].size * PIECE // MT + plan[0].size + 1,), I32)]],
         input_output_aliases={len(plan): 0},
         compiler_params=params(),
         cost_estimate=cost(6 * 16 * MT * d * ff, 96 * d * ff),
@@ -692,8 +731,7 @@
 
 
 class Routing(typing.NamedTuple):
-    nh: typing.Any
-    hl: typing.Any
+    hot: typing.Any
     nch: typing.Any
     eg: typing.Any
     pos: typing.Any
@@ -725,29 +763,7 @@
     inseg = seg[:, None] == jnp.arange(nl * nb, dtype=I32)
     shift_ = jnp.tile(jnp.arange(nb, dtype=I32) * npb, nl) + (pend - pcs).T.reshape(-1) - (fend - flat)
     pc = jnp.clip(p[:, 0] + jnp.sum(jnp.where(inseg, shift_, 0), axis=1), 0, nb * npb - 1)
-    ppt = MT // PIECE
-    ptot = jnp.sum(pcs, axis=0)
-    pstart = jnp.cumsum(ptot) - ptot
-    tiles = (ptot + ppt - 1) // ppt
-    tend = jnp.cumsum(tiles)
-    nq = -(-(nb * npb) // ppt) + nl
-    q = jnp.arange(nq, dtype=I32)
-    tl = jnp.minimum(below(tend[None, :], q[:, None]), nl - 1)
-    one = tl[:, None] == le
-    pick = lambda v: jnp.sum(jnp.where(one, v[None, :], 0), axis=1)
-    ti = q - pick(tend - tiles)
-    tp = pick(pstart) + ti * ppt
-    tn = jnp.clip(pick(ptot) - ti * ppt, 0, ppt)
-    active = (tiles > 0).astype(I32)
-    tw = pick(jnp.cumsum(active) - active)
-    tf = (ti == 0).astype(I32)
-    later = (le[None, :] > tl[:, None]) & (active[None, :] > 0)
-    nxt = jnp.min(jnp.where(later, le[None, :], nl), axis=1)
-    nxt = jnp.where(nxt < nl, nxt, -1)
-    plan = tuple(v.astype(I32) for v in (tend[-1:], tl, tp, tn, tw, tf, nxt, pc))
-    hend = jnp.cumsum(hotm.astype(I32), axis=1)
-    hl = jnp.minimum(below(hend[:, None, :], le[None, :, None]), nl - 1)
-    return Routing(hend[:, -1], hl, nch, eg, pos, None), plan
+    return Routing(hotm.astype(I32), nch, eg, pos, None), (jnp.sum(pcs, axis=0), pc)
 
 
 ON = (True,)
@@ -776,9 +792,10 @@
         ang = (np.arange(t) % s).astype(np.float32)[:, None] * np.float32(THETA) ** (-np.arange(hd, dtype=np.float32) / hd)
         c, sn = np.cos(ang), np.sin(ang)
         cos, sin = [jnp.asarray(np.concatenate(v, axis=1), F32) for v in ((c, c), (-sn, sn))]
-        h, ut, ub, o1, o3, o2, logits, ids4 = attention_layer(nx, x, wv, wk, wq, wo, cos, sin, w1, w3, w2, wr.T, ids.T)
+        h, ut, ub, o1, o3, o2, late, logits, ids4 = attention_layer(nx, x, wv, wk, wq, wo, cos, sin, w1, w3, w2, wr.T, ids.T)
         ids4 = jnp.swapaxes(ids4, 1, 2)
-        own, other = (w1, w3, w2), (o1, o3, o2)
+        late = lax.ppermute(late, 'ep', [(i, i ^ 1) for i in range(nd)])
+        own, other = (w1, w3, w2), (o1, o3, o2, late)
 
         halves = lambda v: v.reshape(2 * v.shape[0], half, *v.shape[2:])
         is_local = halves(ids4 // nl == me // 2)

time: 787 us -> 773 us (0.982)
  Pallas kernels: 616 us -> 594 us
  waiting for transfers between devices: 122 us -> 130 us
    pallas_call x1, Pallas kernels: 184 us -> 173 us  [attention_layer(): pl.pallas_call(functools.partial(layer_kernel, nx), in_specs=[hb] * 5 + [...]
    pallas_call x8, Pallas kernels: 329 us -> 318 us  [block(): pl.pallas_call(functools.partial(block_kernel, js, [v is not None for v i...]
  transfers between devices with their start and end apart: 17 -> 18, of which waited for: 4 -> 5; matrix products, arithmetic and copies ran while one was open for 3% -> 2% of each run, Pallas kernels for 39% -> 39%
where the time goes in v7:
time: 773 us; the launch traced here: 758 us
  Pallas kernels  594 us (77%)
  waiting for transfers between devices  130 us (17%)
  starting transfers between devices  17.1 us (2%)
  other arithmetic  12.9 us (2%)
    pallas_call x8, Pallas kernels, block(): pl.pallas_call(functools.partial(block_kernel, js, [v is not None for v i...  318 us
    pallas_call x1, Pallas kernels, attention_layer(): pl.pallas_call(functools.partial(layer_kernel, nx), in_specs=[hb] * 5 + [...  173 us
    ppermute x17, waiting for transfers between devices, shift(): lax.ppermute(v, 'ep', [(2 * i + c, 2 * ((i + s) % nx) + c) for i in range...  125 us
    pallas_call x1, Pallas kernels, cold(): pl.pallas_call(cold_kernel, in_specs=[sm] * len(plan) + [hb] * 8, out_spe...  69.8 us
    pallas_call x2, Pallas kernels, gather(): pl.pallas_call(functools.partial(gather_kernel, js), in_specs=[sm, sm, vm...  20.5 us
    ppermute x17, starting transfers between devices, shift(): lax.ppermute(v, 'ep', [(2 * i + c, 2 * ((i + s) % nx) + c) for i in range...  16 us
  transfers between devices with their start and end apart: 18, of which 5 were waited for; matrix products, arithmetic and copies ran while one was open for 2% of the time, Pallas kernels for 39%

profile of v7, /device:TPU:113, one launch (start us, length us, event | category | flops | bytes accessed | tf_op | source)
XLA Modules:
  0.0 758.4 jit_solution(861662964667771070)
XLA Ops:
  0.0 173.0 %shard_map.118 = (bf16[1024,2048]{1,0:T(8,128)(2,1)}, bf16[512,2048]{1,0:T(8,128)(2,1)}, bf16[512,2048]{1,0:T(8,128)(2,1)}, bf16[8,2048,1024]{2,1,0:T(8,128)(2,1...) custom-call(bf16[1024,2048]{1,0:T(8,128)(2,1)} %bitcast.57, ...), custom_call_target="tpu_custom_call" | custom-call | flops 34359738368 | bytes 50331648 | tf_op jit(solution)/shard_map/pallas_call | solution.py:288
  173.0 1.1 collective-permute-start.3
  174.1 1.9 collective-permute-start.5
  176.1 1.2 copy.48
  177.3 0.3 select_reduce_fusion.2
  177.7 1.3 collective-permute-start.2
  178.9 2.1 collective-permute-start.7
  181.0 1.0 fusion.5
  182.0 1.0 add_select_fusion.2
  183.0 0.9 fusion
  183.9 0.2 convolution_convert_fusion
  184.1 0.3 slice_reduce_fusion
  184.4 0.6 fusion.19
  184.9 0.2 reduce_window_sum.20
  185.1 0.1 copy.49
  185.2 0.3 not_reduce_fusion
  185.5 0.4 fusion.11
  186.0 0.6 reshape.90.refs_0_
  186.6 0.8 select_reduce_fusion.3.refs_1_
  187.4 5.8 collective-permute-done.3.refs_9_.refs_10_.refs_6_.refs_13_.refs_14_
  193.2 1.9 collective-permute-start.8
  195.2 35.0 %shard_map.119.refs_15_ = f32[512,2048]{1,0:T(8,128)} custom-call(s32[128]{0:T(128)} %reshape.90.refs_0_, f32[2,16,512]{2,1,0:T(8,128)} %select_reduce_fusion.3.refs_1_, bf16[512,2048]{1,0:T(8,128)(2,1)} %get-tuple-element.58.refs_2_.refs_0_.refs_6_, bf16[8,2048,1024]{2,1,0:T(8,128)(2,1)} %refs_8_.9, bf16[8,2048,1024]{2,1,0:T(8,128)(2,1)} %refs_9_.9, ...), custom_call_target="tpu_custom_call" | custom-call | flops 1048576 | bytes 12582912 | tf_op jit(solution)/shard_map/pallas_call | solution.py:505
  230.2 0.1 collective-permute-start.6
  230.3 2.6 collective-permute-start.9
  233.0 0.1 convert_reduce_fusion.1
  233.1 0.1 copy.50
  233.2 0.1 reshape.88
  233.3 0.1 reshape.92
  233.3 0.1 copy.52
  233.4 0.1 add.48
  233.5 0.2 reduce-window.8
  233.7 0.1 reduce.5
  233.8 0.7 convert_reduce_fusion
  234.5 2.6 select_reduce_fusion
  237.1 0.8 add_select_fusion.pos_ref.refs_4_.refs_3_
  237.9 0.6 add_clamp_fusion.pc_ref
  238.5 0.2 multiply_reduce_fusion
  238.7 74.1 %collective-permute-done.1 = f32[1024,8]{0,1:T(8,128)S(1)} collective-permute-done((f32[1024,8]{0,1:T(8,128)S(1)}, f32[1024,8]{0,1:T(8,128)S(1)}, u32[]{:S(2)}, u32[]{:S(2)}) %collective-permute-start.1) | collective-permute-done | bytes 32800 | tf_op jit(solution)/shard_map/ppermute | solution.py:780
  312.8 0.9 collective-permute-start
  313.7 0.5 negate_maximum_fusion.nch_ref.refs_2_.refs_1_
  314.2 0.7 min.30.eg_ref.refs_3_.refs_2_
  314.9 2.5 collective-permute-done
  317.4 1.6 select_reduce_fusion.1.refs_1_.refs_0_
  319.0 63.8 %shard_map.120 = (f32[512,2048]{1,0:T(8,128)}, f32[512,2048]{1,0:T(8,128)}) custom-call(s32[128]{0:T(128)} %reshape.90.refs_0_, f32[8,16,512]{2,1,0:T(8,128)} %select_reduce_fusion.1.refs_1_.refs_0_, bf16[512,2048]{1,0:T(8,128)(2,1)} %collective-permute-done.4.refs_2_, bf16[512,2048]{1,0:T(8,128)(2,1)} %collective-permute-done.5.refs_3_.refs_5_, ...), custom_call_target="tpu_custom_call" | custom-call | flops 1048576 | bytes 12582912 | tf_op jit(solution)/shard_map/pallas_call | solution.py:505
  382.8 13.8 %shard_map.121.refs_2_ = bf16[34816,2048]{1,0:T(8,128)(2,1)} custom-call(s32[8]{0:T(128)} %negate_maximum_fusion.nch_ref.refs_2_.refs_1_, s32[4352]{0:T(1024)} %min.30.eg_ref.refs_3_.refs_2_, s32[8,16,512]{2,1,0:T(8,128)} %add_select_fusion.pos_ref.refs_4_.refs_3_, bf16[512,2048]{1,0:T(8,128)(2,1)} %get-tuple-element.58.refs_2_.refs_0_.refs_6_, ...), custom_call_target="tpu_custom_call" | custom-call | flops 1048576 | bytes 2097152 | tf_op jit(solution)/shard_map/pallas_call | solution.py:567
  396.6 6.8 shard_map.122.x_ref
  403.4 69.8 %shard_map.123.refs_5_.refs_4_ = bf16[34816,2048]{1,0:T(8,128)(2,1)} custom-call(s32[16]{0:T(128)} %get-tuple-element.83.np_ref, s32[4352]{0:T(1024)} %add_clamp_fusion.pc_ref, bf16[34816,2048]{1,0:T(8,128)(2,1)} %shard_map.122.x_ref, bf16[8,2048,1024]{2,1,0:T(8,128)(2,1)} %refs_8_.9, ...), custom_call_target="tpu_custom_call", output_to_operand_aliasing={{}: (2, {})} | custom-call | flops 70866960384 | bytes 201326592 | tf_op jit(solution)/shard_map/pallas_call | solution.py:687
  473.2 38.2 %shard_map.124 = bf16[512,2048]{1,0:T(8,128)(2,1)} custom-call(s32[128]{0:T(128)} %reshape.90.refs_0_, f32[8,16,512]{2,1,0:T(8,128)} %select_reduce_fusion.1.refs_1_.refs_0_, s32[8]{0:T(128)} %negate_maximum_fusion.nch_ref.refs_2_.refs_1_, s32[4352]{0:T(1024)} %min.30.eg_ref.refs_3_.refs_2_, s32[8,16,512]{2,1,0:T(8,128)} %add_select_fusion.pos_ref.refs_4_.refs_3_, ...), custom_call_target="tpu_custom_call" | custom-call | flops 1048576 | bytes 12582912 | tf_op jit(solution)/shard_map/pallas_call | solution.py:505
  511.4 0.1 collective-permute-start.10
  511.5 18.0 %shard_map.125 = (bf16[512,2048]{1,0:T(8,128)(2,1)}, bf16[512,2048]{1,0:T(8,128)(2,1)}) custom-call(f32[8,16,512]{2,1,0:T(8,128)} %select_reduce_fusion.1.refs_1_.refs_0_, s32[8]{0:T(128)} %negate_maximum_fusion.nch_ref.refs_2_.refs_1_, s32[4352]{0:T(1024)} %min.30.eg_ref.refs_3_.refs_2_, s32[8,16,512]{2,1,0:T(8,128)} %add_select_fusion.pos_ref.refs_4_.refs_3_, ...), custom_call_target="tpu_custom_call" | custom-call | flops 1048576 | bytes 12582912 | tf_op jit(solution)/shard_map/pallas_call | solution.py:505
  529.5 38.2 %shard_map.126 = bf16[512,2048]{1,0:T(8,128)(2,1)} custom-call(s32[128]{0:T(128)} %reshape.90.refs_0_, f32[8,16,512]{2,1,0:T(8,128)} %select_reduce_fusion.1.refs_1_.refs_0_, s32[8]{0:T(128)} %negate_maximum_fusion.nch_ref.refs_2_.refs_1_, s32[4352]{0:T(1024)} %min.30.eg_ref.refs_3_.refs_2_, s32[8,16,512]{2,1,0:T(8,128)} %add_select_fusion.pos_ref.refs_4_.refs_3_, ...), custom_call_target="tpu_custom_call" | custom-call | flops 1048576 | bytes 12582912 | tf_op jit(solution)/shard_map/pallas_call | solution.py:505
  567.7 0.1 collective-permute-start.11
  567.9 0.1 collective-permute-start.12
  568.0 1.4 collective-permute-start.15
  569.4 38.2 %shard_map.127 = bf16[512,2048]{1,0:T(8,128)(2,1)} custom-call(s32[128]{0:T(128)} %reshape.90.refs_0_, f32[8,16,512]{2,1,0:T(8,128)} %select_reduce_fusion.1.refs_1_.refs_0_, s32[8]{0:T(128)} %negate_maximum_fusion.nch_ref.refs_2_.refs_1_, s32[4352]{0:T(1024)} %min.30.eg_ref.refs_3_.refs_2_, s32[8,16,512]{2,1,0:T(8,128)} %add_select_fusion.pos_ref.refs_4_.refs_3_, ...), custom_call_target="tpu_custom_call" | custom-call | flops 1048576 | bytes 12582912 | tf_op jit(solution)/shard_map/pallas_call | solution.py:505
  607.6 0.1 collective-permute-start.13
  607.7 1.6 collective-permute-start.16
  609.3 38.2 %shard_map.128 = bf16[512,2048]{1,0:T(8,128)(2,1)} custom-call(s32[128]{0:T(128)} %reshape.90.refs_0_, f32[8,16,512]{2,1,0:T(8,128)} %select_reduce_fusion.1.refs_1_.refs_0_, s32[8]{0:T(128)} %negate_maximum_fusion.nch_ref.refs_2_.refs_1_, s32[4352]{0:T(1024)} %min.30.eg_ref.refs_3_.refs_2_, s32[8,16,512]{2,1,0:T(8,128)} %add_select_fusion.pos_ref.refs_4_.refs_3_, ...), custom_call_target="tpu_custom_call" | custom-call | flops 1048576 | bytes 12582912 | tf_op jit(solution)/shard_map/pallas_call | solution.py:505
  647.5 0.1 collective-permute-start.14
  647.7 8.4 %collective-permute-done.12.refs_2_ = bf16[512,2048]{1,0:T(8,128)(2,1)} collective-permute-done((bf16[512,2048]{1,0:T(8,128)(2,1)}, bf16[512,2048]{1,0:T(8,128)(2,1)}, u32[]{:S(2)}, u32[]{:S(2)}) %collective-permute-start.12) | collective-permute-done | bytes 2097184 | tf_op jit(solution)/shard_map/ppermute | solution.py:780
  656.1 1.5 collective-permute-start.17
  657.6 48.8 %shard_map.129 = (f32[512,2048]{1,0:T(8,128)}, f32[512,2048]{1,0:T(8,128)}) custom-call(s32[128]{0:T(128)} %reshape.90.refs_0_, f32[8,16,512]{2,1,0:T(8,128)} %select_reduce_fusion.1.refs_1_.refs_0_, s32[8]{0:T(128)} %negate_maximum_fusion.nch_ref.refs_2_.refs_1_, s32[4352]{0:T(1024)} %min.30.eg_ref.refs_3_.refs_2_, ...), custom_call_target="tpu_custom_call" | custom-call | flops 1048576 | bytes 12582912 | tf_op jit(solution)/shard_map/pallas_call | solution.py:505
  706.5 39.5 %collective-permute-done.17.refs_7_ = bf16[512,2048]{1,0:T(8,128)(2,1)} collective-permute-done((bf16[512,2048]{1,0:T(8,128)(2,1)}, bf16[512,2048]{1,0:T(8,128)(2,1)}, u32[]{:S(2)}, u32[]{:S(2)}) %collective-permute-start.17) | collective-permute-done | bytes 2097184 | tf_op jit(solution)/shard_map/ppermute | solution.py:780
  746.0 12.2 %shard_map.130 = bf16[1024,2048]{1,0:T(8,128)(2,1)} custom-call(bf16[1024,2048]{1,0:T(8,128)(2,1)} %get-tuple-element.43.h_ref, f32[512,2048]{1,0:T(8,128)} %get-tuple-element.73.refs_0_, f32[512,2048]{1,0:T(8,128)} %get-tuple-element.74.refs_1_, bf16[512,2048]{1,0:T(8,128)(2,1)} %collective-permute-done.12.refs_2_, ...), custom_call_target="tpu_custom_call" | custom-call | flops 12582912 | bytes 41943040 | tf_op jit(solution)/shard_map/pallas_call | solution.py:723
  (26 shorter events, 0.2 us)
Async XLA Ops:
  0.0 177.3 %copy-start = (s32[1,1024,8]{1,2,0:T(8,128)S(1)}, s32[1,1024,8]{1,2,0:T(8,128)}, u32[]{:S(2)}) copy-start(s32[1,1024,8]{1,2,0:T(8,128)} %param.21) | copy-start | bytes 98308
  173.0 20.2 %collective-permute-start.3 = (bf16[3,1024,2048]{2,1,0:T(8,128)(2,1)}, bf16[3,1024,2048]{2,1,0:T(8,128)(2,1)}, u32[]{:S(2)}, u32[]{:S(2)}) collective-permute-start(bf16[3,1024,2048]{2,1,0:T(8,128)(2,1)} %get-tuple-element.52), channel_id=1, source_target_pairs={{0,1},{1,0},{2,3},{3,2},{4,5},{5,4},{6,7},{7,6},{8,9},{9,8},{10,11... | collective-permute-start | bytes 37748744 | tf_op jit(solution)/shard_map/ppermute | solution.py:797
  174.1 56.1 %collective-permute-start.5 = (bf16[512,2048]{1,0:T(8,128)(2,1)}, bf16[512,2048]{1,0:T(8,128)(2,1)}, u32[]{:S(2)}, u32[]{:S(2)}) collective-permute-start(bf16[512,2048]{1,0:T(8,128)(2,1)} %get-tuple-element.54.refs_1_.refs_7_), channel_id=1, source_target_pairs={{0,6},{1,7},{2,0},{3,1},{4,2},{5,3},{6,4},{7,5},{8,14},{9,15},{10,... | collective-permute-start | bytes 6291464 | tf_op jit(solution)/shard_map/ppermute | solution.py:780
  176.1 54.1 %collective-permute-start.4 = (bf16[512,2048]{1,0:T(8,128)(2,1)}, bf16[512,2048]{1,0:T(8,128)(2,1)}, u32[]{:S(2)}, u32[]{:S(2)}) collective-permute-start(bf16[512,2048]{1,0:T(8,128)(2,1)} %get-tuple-element.58.refs_2_.refs_0_.refs_6_), channel_id=1, source_target_pairs={{0,2},{1,3},{2,4},{3,5},{4,6},{5,7},{6,0},{7,1},{8,10},{9,11},{10,... | collective-permute-start | bytes 6291464 | tf_op jit(solution)/shard_map/ppermute | solution.py:780
  177.7 60.8 %collective-permute-start.2 = (f32[1024,8]{0,1:T(8,128)S(1)}, f32[1024,8]{0,1:T(8,128)S(1)}, u32[]{:S(2)}, u32[]{:S(2)}) collective-permute-start(f32[1024,8]{0,1:T(8,128)S(1)} %fusion.13), channel_id=1, source_target_pairs={{0,4},{1,5},{2,6},{3,7},{4,0},{5,1},{6,2},{7,3},{8,12},{9,13},{10,... | collective-permute-start | bytes 98312 | tf_op jit(solution)/shard_map/ppermute | solution.py:780
  178.9 203.9 %collective-permute-start.7 = (bf16[512,2048]{1,0:T(8,128)(2,1)}, bf16[512,2048]{1,0:T(8,128)(2,1)}, u32[]{:S(2)}, u32[]{:S(2)}) collective-permute-start(bf16[512,2048]{1,0:T(8,128)(2,1)} %get-tuple-element.54.refs_1_.refs_7_), channel_id=1, source_target_pairs={{0,2},{1,3},{2,4},{3,5},{4,6},{5,7},{6,0},{7,1},{8,10},{9,11},{10,... | collective-permute-start | bytes 6291464 | tf_op jit(solution)/shard_map/ppermute | solution.py:780
  193.2 189.6 %collective-permute-start.8 = (bf16[512,2048]{1,0:T(8,128)(2,1)}, bf16[512,2048]{1,0:T(8,128)(2,1)}, u32[]{:S(2)}, u32[]{:S(2)}) collective-permute-start(bf16[512,2048]{1,0:T(8,128)(2,1)} %get-tuple-element.58.refs_2_.refs_0_.refs_6_), channel_id=1, source_target_pairs={{0,6},{1,7},{2,0},{3,1},{4,2},{5,3},{6,4},{7,5},{8,14},{9,15},{10,... | collective-permute-start | bytes 6291464 | tf_op jit(solution)/shard_map/ppermute | solution.py:780
  230.2 166.4 %collective-permute-start.6 = (bf16[512,2048]{1,0:T(8,128)(2,1)}, bf16[512,2048]{1,0:T(8,128)(2,1)}, u32[]{:S(2)}, u32[]{:S(2)}) collective-permute-start(bf16[512,2048]{1,0:T(8,128)(2,1)} %collective-permute-done.4.refs_2_), channel_id=1, source_target_pairs={{0,2},{1,3},{2,4},{3,5},{4,6},{5,7},{6,0},{7,1},{8,10},{9,11},{10,... | collective-permute-start | bytes 6291464 | tf_op jit(solution)/shard_map/ppermute | solution.py:780
  230.3 166.3 %collective-permute-start.9 = (bf16[512,2048]{1,0:T(8,128)(2,1)}, bf16[512,2048]{1,0:T(8,128)(2,1)}, u32[]{:S(2)}, u32[]{:S(2)}) collective-permute-start(bf16[512,2048]{1,0:T(8,128)(2,1)} %collective-permute-done.5.refs_3_.refs_5_), channel_id=1, source_target_pairs={{0,6},{1,7},{2,0},{3,1},{4,2},{5,3},{6,4},{7,5},{8,14},{9,15},{10,... | collective-permute-start | bytes 6291464 | tf_op jit(solution)/shard_map/ppermute | solution.py:780
  238.5 74.3 %collective-permute-start.1 = (f32[1024,8]{0,1:T(8,128)S(1)}, f32[1024,8]{0,1:T(8,128)S(1)}, u32[]{:S(2)}, u32[]{:S(2)}) collective-permute-start(f32[1024,8]{0,1:T(8,128)S(1)} %fusion.13), channel_id=1, source_target_pairs={{0,6},{1,7},{2,0},{3,1},{4,2},{5,3},{6,4},{7,5},{8,14},{9,15},{10,... | collective-permute-start | bytes 98312 | tf_op jit(solution)/shard_map/ppermute | solution.py:780
  312.8 4.6 collective-permute-start
  511.4 56.3 %collective-permute-start.10 = (bf16[512,2048]{1,0:T(8,128)(2,1)}, bf16[512,2048]{1,0:T(8,128)(2,1)}, u32[]{:S(2)}, u32[]{:S(2)}) collective-permute-start(bf16[512,2048]{1,0:T(8,128)(2,1)} %shard_map.124), channel_id=1, source_target_pairs={{0,2},{1,3},{2,4},{3,5},{4,6},{5,7},{6,0},{7,1},{8,10},{9,11},{10,... | collective-permute-start | bytes 6291464 | tf_op jit(solution)/shard_map/ppermute | solution.py:780
  567.7 79.8 %collective-permute-start.11 = (bf16[512,2048]{1,0:T(8,128)(2,1)}, bf16[512,2048]{1,0:T(8,128)(2,1)}, u32[]{:S(2)}, u32[]{:S(2)}) collective-permute-start(bf16[512,2048]{1,0:T(8,128)(2,1)} %shard_map.126), channel_id=1, source_target_pairs={{0,6},{1,7},{2,0},{3,1},{4,2},{5,3},{6,4},{7,5},{8,14},{9,15},{10,... | collective-permute-start | bytes 6291464 | tf_op jit(solution)/shard_map/ppermute | solution.py:780
  567.9 88.2 %collective-permute-start.12 = (bf16[512,2048]{1,0:T(8,128)(2,1)}, bf16[512,2048]{1,0:T(8,128)(2,1)}, u32[]{:S(2)}, u32[]{:S(2)}) collective-permute-start(bf16[512,2048]{1,0:T(8,128)(2,1)} %get-tuple-element.75), channel_id=1, source_target_pairs={{0,6},{1,7},{2,0},{3,1},{4,2},{5,3},{6,4},{7,5},{8,14},{9,15},{10,... | collective-permute-start | bytes 6291464 | tf_op jit(solution)/shard_map/ppermute | solution.py:780
  568.0 138.4 %collective-permute-start.15 = (bf16[512,2048]{1,0:T(8,128)(2,1)}, bf16[512,2048]{1,0:T(8,128)(2,1)}, u32[]{:S(2)}, u32[]{:S(2)}) collective-permute-start(bf16[512,2048]{1,0:T(8,128)(2,1)} %get-tuple-element.78), channel_id=1, source_target_pairs={{0,2},{1,3},{2,4},{3,5},{4,6},{5,7},{6,0},{7,1},{8,10},{9,11},{10,... | collective-permute-start | bytes 6291464 | tf_op jit(solution)/shard_map/ppermute | solution.py:780
  607.6 98.8 %collective-permute-start.13 = (bf16[512,2048]{1,0:T(8,128)(2,1)}, bf16[512,2048]{1,0:T(8,128)(2,1)}, u32[]{:S(2)}, u32[]{:S(2)}) collective-permute-start(bf16[512,2048]{1,0:T(8,128)(2,1)} %shard_map.127), channel_id=1, source_target_pairs={{0,6},{1,7},{2,0},{3,1},{4,2},{5,3},{6,4},{7,5},{8,14},{9,15},{10,... | collective-permute-start | bytes 6291464 | tf_op jit(solution)/shard_map/ppermute | solution.py:780
  607.7 98.7 %collective-permute-start.16 = (bf16[512,2048]{1,0:T(8,128)(2,1)}, bf16[512,2048]{1,0:T(8,128)(2,1)}, u32[]{:S(2)}, u32[]{:S(2)}) collective-permute-start(bf16[512,2048]{1,0:T(8,128)(2,1)} %collective-permute-done.10), channel_id=1, source_target_pairs={{0,2},{1,3},{2,4},{3,5},{4,6},{5,7},{6,0},{7,1},{8,10},{9,11},{10,... | collective-permute-start | bytes 6291464 | tf_op jit(solution)/shard_map/ppermute | solution.py:780
  647.5 58.9 %collective-permute-start.14 = (bf16[512,2048]{1,0:T(8,128)(2,1)}, bf16[512,2048]{1,0:T(8,128)(2,1)}, u32[]{:S(2)}, u32[]{:S(2)}) collective-permute-start(bf16[512,2048]{1,0:T(8,128)(2,1)} %shard_map.128), channel_id=1, source_target_pairs={{0,2},{1,3},{2,4},{3,5},{4,6},{5,7},{6,0},{7,1},{8,10},{9,11},{10,... | collective-permute-start | bytes 6291464 | tf_op jit(solution)/shard_map/ppermute | solution.py:780
  656.1 89.9 %collective-permute-start.17 = (bf16[512,2048]{1,0:T(8,128)(2,1)}, bf16[512,2048]{1,0:T(8,128)(2,1)}, u32[]{:S(2)}, u32[]{:S(2)}) collective-permute-start(bf16[512,2048]{1,0:T(8,128)(2,1)} %collective-permute-done.11), channel_id=1, source_target_pairs={{0,6},{1,7},{2,0},{3,1},{4,2},{5,3},{6,4},{7,5},{8,14},{9,15},{10,... | collective-permute-start | bytes 6291464 | tf_op jit(solution)/shard_map/ppermute | solution.py:780

commit v8 on v7

--- a/solution.py
+++ b/solution.py
@@ -70,8 +70,9 @@
 
 def layer_kernel(nx, x_ref, wv_ref, wk_ref, wq_ref, wo_ref, cos_ref, sin_ref, w1_ref, w3_ref, w2_ref, wr_ref, id_ref,
                  h_ref, ut_ref, ub_ref, o1_ref, o3_ref, o2_ref, late_ref, lg_ref, id4_ref,
-                 w_ref, ab, qb, kb, vb, rb3, ssem, rsem, lsem, iosem, swap_send, swap_recv, id_send, id_recv):
+                 w_ref, ab, qb, kb, vb, rb3, fb, ssem, rsem, lsem, iosem, swap_send, swap_recv, id_send, id_recv):
     shards = (wv_ref, wk_ref, wq_ref, wo_ref)
+    last = len(shards) - 1
     sh = wv_ref.shape[0]
     hs = sh // 2
     t, d = ab.shape
@@ -97,7 +98,7 @@
 
     def own(w):
         src = shards[w]
-        top, bot = src.at[pl.ds(0, hs), :], src.at[pl.ds(hs, hs), :]
+        top, bot = src.at[:hs, :], src.at[hs:, :]
         return [remote(w, top, rows(me, 0), right, 0, LT), remote(w, bot, rows(me, 1), left, 1, RB),
                 remote(w, bot, rows(me, 1), right, 2, LB), remote(w, top, rows(me, 0), left, 3, RT),
                 remote(w, src, rows(me), partner, 6, PO)]
@@ -129,7 +130,7 @@
         onward(w, OT).start()
         arrive(w, RB)
         onward(w, OB).start()
-        if w + 1 < 4:
+        if w < last:
             begin(w + 1)
         across(w, LT).start()
         across(w, RB).start()
@@ -147,10 +148,14 @@
             across(w, k).start()
         swap()
 
-    def stage_d(w):
-        for k in (PO, PASS + LT, PASS + RB, PASS + LB, PASS + RT, PASS + OT, PASS + OB):
+    def near(w):
+        for k in (PO, PASS + LT, PASS + RB, PASS + LB, PASS + RT):
             arrive(w, k)
         mine(w).wait()
+
+    def far(w):
+        for k in (PASS + OT, PASS + OB):
+            arrive(w, k)
 
     pieces = [(src.at[e], dst.at[e]) for e in range(w1_ref.shape[0]) for src, dst in ((w1_ref, o1_ref), (w3_ref, o3_ref), (w2_ref, o2_ref))
               if e < dst.shape[0]]
@@ -176,7 +181,7 @@
     rb3[:] = jnp.concatenate(split3(wr_ref[:]), axis=0)
 
     for e in range(LATE):
-        room = w_ref.at[3, pl.ds(0, w2_ref.shape[1]), :]
+        room = w_ref.at[last, :w2_ref.shape[1], :]
         for c in (pltpu.make_async_copy(w2_ref.at[o2_ref.shape[0] + e], room, iosem.at[3]),
                   pltpu.make_async_copy(room, late_ref.at[e], iosem.at[3])):
             c.start()
@@ -187,45 +192,66 @@
         r = pl.ds(pl.multiple_of(i * rb, rb), rb)
         ab[r, :] = rmsnorm(kb[r, :]).astype(BF)
 
-    tm, tn = min(512, t), min(512, d)
-
-    def project(w, dst, rope):
-        @loop(d // tn)
+    tm, tn = [min(512, v) for v in (t, d)]
+
+    def tiles(lo, hi, fn):
+        @pl.loop(lo, hi)
         def _(n):
             @loop(t // tm)
             def _(m):
-                r = pl.ds(pl.multiple_of(m * tm, tm), tm)
-                z = dot(ab[r, :], w_ref[w, :, pl.ds(pl.multiple_of(n * tn, tn), tn)])
-                for j in range(tn // HEAD):
-                    zj = z[:, j * HEAD:(j + 1) * HEAD]
-                    if rope:
-                        zj = zj * cos_ref[r, :] + pltpu.roll(zj, HEAD // 2, 1) * sin_ref[r, :]
-                    dst[r, pl.ds(pl.multiple_of(n * tn + j * HEAD, HEAD), HEAD)] = zj.astype(BF)
-
-    for w, (dst, rope) in enumerate(((vb, False), (kb, True), (qb, True))):
+                fn(pl.ds(pl.multiple_of(m * tm, tm), tm), pl.multiple_of(n * tn, tn))
+
+    def some(a, w, r, n, chips):
+        ks = [pl.ds(pl.multiple_of(2 * sh * c, 2 * sh), 2 * sh) for c in chips]
+        return functools.reduce(jnp.add, [dot(a[r, k], w_ref[w, k, pl.ds(n, tn)]) for k in ks])
+
+    close, across_ = (chip, left // 2, right // 2), (opp // 2,)
+
+    def ahead(a, w):
+        def fn(r, n):
+            fb[r, pl.ds(n, tn)] = some(a, w, r, n, close)
+
+        near(w)
+        tiles(0, d // tn // 2, fn)
+        stage_c(w)
+        tiles(d // tn // 2, d // tn, fn)
+        far(w)
+
+    def put(dst, rope, r, n, z):
+        for j in range(tn // HEAD):
+            zj = z[:, j * HEAD:(j + 1) * HEAD]
+            if rope:
+                zj = zj * cos_ref[r, :] + pltpu.roll(zj, HEAD // 2, 1) * sin_ref[r, :]
+            dst[r, pl.ds(pl.multiple_of(n + j * HEAD, HEAD), HEAD)] = zj.astype(BF)
+
+    for w, (dst, rope) in enumerate(((vb, False), (kb, True))):
         stage_a(w)
         stage_b(w)
         stage_c(w)
-        stage_d(w)
+        near(w)
+        far(w)
         swap()
-        project(w, dst, rope)
-    stage_a(3)
-
-    tq = min(256, t)
+        tiles(0, d // tn, lambda r, n: put(dst, rope, r, n, dot(ab[r, :], w_ref[w, :, pl.ds(n, tn)])))
+    w = last - 1
+    stage_a(w)
+    stage_b(w)
+    ahead(ab, w)
+    swap()
+    tiles(0, d // tn, lambda r, n: put(qb, True, r, n, fb[r, pl.ds(n, tn)] + some(ab, w, r, n, across_)))
+    stage_a(last)
+
+    tq = rb
     scale = math.log2(math.e) / math.sqrt(HEAD)
     causal = lax.broadcasted_iota(I32, (tq, tq), 0) <= lax.broadcasted_iota(I32, (tq, tq), 1)
     group = min(4, d // HEAD)
     steps = d // HEAD // group
-    marks = {1: stage_b, steps - 1: stage_c}
-    if len(marks) > steps - 1:
-        marks = {}
-        stage_b(3)
-        stage_c(3)
+    if steps == 1:
+        stage_b(last)
 
     @loop(steps)
     def _(jj):
-        for at, stage in marks.items():
-            pl.when(jj == at)(functools.partial(stage, 3))
+        if steps > 1:
+            pl.when(jj == 1)(functools.partial(stage_b, last))
         for j in range(group):
             c = pl.ds(pl.multiple_of((jj * group + j) * HEAD, HEAD), HEAD)
             for i in range(t // tq):
@@ -240,18 +266,14 @@
     swap()
     xin = pltpu.make_async_copy(x_ref, vb, iosem.at[0])
     xin.start()
-    stage_d(3)
+    ahead(qb, last)
     xin.wait()
 
-    @loop(d // tn)
-    def _(n):
-        c = pl.ds(pl.multiple_of(n * tn, tn), tn)
-
-        @loop(t // tm)
-        def _(m):
-            r = pl.ds(pl.multiple_of(m * tm, tm), tm)
-            ab[r, c] = (vb[r, c].astype(F32) + dot(qb[r, :], w_ref[3, :, c])).astype(BF)
-
+    def residual(r, n):
+        c = pl.ds(n, tn)
+        ab[r, c] = (vb[r, c].astype(F32) + (fb[r, c] + some(qb, last, r, n, across_))).astype(BF)
+
+    tiles(0, d // tn, residual)
     hout = pltpu.make_async_copy(ab, h_ref, iosem.at[0])
     hout.start()
 
@@ -271,7 +293,7 @@
     assert not waiting
     for c in swaps + ids:
         c.wait()
-    for w in range(4):
+    for w in range(last + 1):
         for c in own(w) + [onward(w, OT), onward(w, OB)] + [across(w, k) for k in where]:
             c.wait_send()
     hout.wait()
@@ -293,7 +315,7 @@
                    jax.ShapeDtypeStruct(w3.shape, BF),
                    *[jax.ShapeDtypeStruct((n, *w2.shape[1:]), BF) for n in (w2.shape[0] - LATE, LATE)], jax.ShapeDtypeStruct((t, wr.shape[0]), F32),
                    jax.ShapeDtypeStruct((nx, *ids.shape), I32)],
-        scratch_shapes=[pltpu.VMEM((4, d, d), BF), act, act, act, act, pltpu.VMEM((3 * wr.shape[0], d), BF),
+        scratch_shapes=[pltpu.VMEM((4, d, d), BF), act, act, act, act, pltpu.VMEM((3 * wr.shape[0], d), BF), pltpu.VMEM((t, d), F32),
                         pltpu.SemaphoreType.DMA((4, 13)), pltpu.SemaphoreType.DMA((4, 13)),
                         pltpu.SemaphoreType.DMA((4,)), pltpu.SemaphoreType.DMA((4,)),
                         pltpu.SemaphoreType.DMA((3 * w1.shape[0],)), pltpu.SemaphoreType.DMA((3 * w1.shape[0],)),
@@ -524,8 +546,7 @@
     return jnp.concatenate(hits, axis=0), ls
 
 
-def gather_kernel(js, nch_ref, eg_ref, pos_ref, *refs):
-    us, (x_ref, ubuf, xbuf, usem, sem) = refs[:len(js)], refs[-5:]
+def gather_rows(js, nch_ref, eg_ref, pos_ref, us, x_ref, ubuf, xbuf, usem, sem):
     cap = x_ref.shape[0] // pos_ref.shape[0]
     cps = [pltpu.make_async_copy(u, ubuf.at[p % 2], usem.at[p % 2]) for p, u in enumerate(us)]
     cps[0].start()
@@ -557,28 +578,31 @@
             out(parity(made - k), 0).wait()
 
 
-def gather(js, r, us, x):
+def gather_kernel(js, nch_ref, eg_ref, pos_ref, *refs):
+    gather_rows(js, nch_ref, eg_ref, pos_ref, refs[:len(js)], *refs[len(js):])
+
+
+def gather(js, r, us):
     t, d = us[0].shape
-    rows = r.eg.size * PIECE
     vm = pl.BlockSpec(memory_space=pltpu.VMEM)
     sm = pl.BlockSpec(memory_space=pltpu.SMEM)
     hb = pl.BlockSpec(memory_space=pl.ANY)
-    more = [] if x is None else [x]
     return pl.pallas_call(
         functools.partial(gather_kernel, js),
-        in_specs=[sm, sm, vm] + [hb] * len(us + more),
+        in_specs=[sm, sm, vm] + [hb] * len(us),
         out_specs=hb,
-        out_shape=jax.ShapeDtypeStruct((rows, d), BF),
-        input_output_aliases={3 + len(us): 0} if more else {},
+        out_shape=jax.ShapeDtypeStruct((r.eg.size * PIECE, d), BF),
         scratch_shapes=[pltpu.VMEM((2, t, d), BF), pltpu.VMEM((2, CHUNK, d), BF), DMA2, DMA2],
         compiler_params=params(),
         cost_estimate=cost(t * d, 4 * CHUNK * d),
-    )(r.nch, r.eg.reshape(-1), r.pos, *us, *more)
-
-
-def cold_kernel(np_ref, pc_ref, x_ref, *refs):
+    )(r.nch, r.eg.reshape(-1), r.pos, *us)
+
+
+def cold_kernel(js, np_ref, pc_ref, nch_ref, eg_ref, pos_ref, *refs):
+    us, refs = refs[:len(js)], refs[len(js) + 1:]
     own, other, z_ref, refs = refs[:3], refs[3:7], refs[7], refs[8:]
-    bufs, (xbuf, zbuf, wsem, xsem, zsem, tl_ref, tp_ref, tn_ref, tw_ref, nx_ref) = refs[:3], refs[3:]
+    x_ref = z_ref
+    bufs, (ubuf, gbuf, usem, gsem, xbuf, zbuf, wsem, xsem, zsem, tl_ref, tp_ref, tn_ref, tw_ref, nx_ref) = refs[:3], refs[3:]
     ppt = MT // PIECE
 
     def tiles(l, carry):
@@ -646,6 +670,11 @@
     @pl.when(nt > 0)
     def _():
         fetch_expert(tl_ref[0], 0, own, other, bufs, wsem)
+
+    gather_rows(js, nch_ref, eg_ref, pos_ref, us, z_ref, ubuf, gbuf, usem, gsem)
+
+    @pl.when(nt > 0)
+    def _():
         xin(0, 0)
 
     @loop(nt)
@@ -680,22 +709,25 @@
             zwait(nt - k, parity(nt - k))
 
 
-def cold(plan, x, own, other):
+def cold(plan, js, r, us, x, own, other):
     d, ff = own[0].shape[1:]
+    t = us[0].shape[0]
+    vm = pl.BlockSpec(memory_space=pltpu.VMEM)
     sm = pl.BlockSpec(memory_space=pltpu.SMEM)
     hb = pl.BlockSpec(memory_space=pl.ANY)
+    args = (*plan, r.nch, r.eg.reshape(-1), r.pos, *us)
     return pl.pallas_call(
-        cold_kernel,
-        in_specs=[sm] * len(plan) + [hb] * 8,
+        functools.partial(cold_kernel, js),
+        in_specs=[sm] * 4 + [vm] + [hb] * (len(us) + 8),
         out_specs=hb,
         out_shape=jax.ShapeDtypeStruct(x.shape, BF),
-        scratch_shapes=[*expert_buffers(d, ff),
+        scratch_shapes=[*expert_buffers(d, ff), pltpu.VMEM((2, t, d), BF), pltpu.VMEM((2, CHUNK, d), BF), DMA2, DMA2,
                         pltpu.VMEM((2, MT, d), BF), pltpu.VMEM((2, MT, d), BF),
                         DMA2, DMA2, DMA2, *5 * [pltpu.SMEM((plan[1].size * PIECE // MT + plan[0].size + 1,), I32)]],
-        input_output_aliases={len(plan): 0},
+        input_output_aliases={len(args): 0},
         compiler_params=params(),
         cost_estimate=cost(6 * 16 * MT * d * ff, 96 * d * ff),
-    )(*plan, x, *own, *other)
+    )(*args, x, *own, *other)
 
 
 def final_kernel(h_ref, *refs):
@@ -818,10 +850,9 @@
         u3t, u3b = shift(u1t, 1), shift(u2b, -1)
         d2, d5 = block((2, 5), r, None, (u1t, u2b), 2 * (None,), own, other, F32, 2 * ON, comb=False)
         u1b, d2 = lax.optimization_barrier((u1b, d2))
-        x = gather(tuple(range(6)), r, [ut, ub, u1t, u1b, u2t, u2b], None)
+        x = gather(tuple(range(6)), r, [ut, ub, u1t, u1b, u2t, u2b])
         u3t, x = lax.optimization_barrier((u3t, x))
-        x = gather((6, 7), r, [u3t, u3b], x)
-        z = cold(plan, x, own, other)
+        z = cold(plan, (6, 7), r, [u3t, u3b], x, own, other)
 
         tie = lambda r, *v: (lambda w: (r._replace(nch=w[0]), *w[1:]))(lax.optimization_barrier((r.nch, *v)))
         b6, = block((6,), r, z, (u3t,), (None,), own, other, BF, ON)

time: 773 us -> 779 us (level)
    pallas_call x2 -> x1, Pallas kernels: 20.5 us -> 13.8 us  [gather(): pl.pallas_call(functools.partial(gather_kernel, js), in_specs=[sm, sm, vm...]
where the time goes in v8:
time: 779 us; the launch traced here: 763 us
  Pallas kernels  600 us (77%)
  waiting for transfers between devices  130 us (17%)
  starting transfers between devices  15.9 us (2%)
  other arithmetic  13.1 us (2%)
    pallas_call x8, Pallas kernels, block(): pl.pallas_call(functools.partial(block_kernel, js, [v is not None for v i...  319 us
    pallas_call x1, Pallas kernels, attention_layer(): pl.pallas_call(functools.partial(layer_kernel, nx), in_specs=[hb] * 5 + [...  181 us
    ppermute x17, waiting for transfers between devices, shift(): lax.ppermute(v, 'ep', [(2 * i + c, 2 * ((i + s) % nx) + c) for i in range...  124 us
    pallas_call x1, Pallas kernels, cold(): pl.pallas_call(functools.partial(cold_kernel, js), in_specs=[sm] * 4 + [v...  75.3 us
    ppermute x17, starting transfers between devices, shift(): lax.ppermute(v, 'ep', [(2 * i + c, 2 * ((i + s) % nx) + c) for i in range...  15.8 us
  transfers between devices with their start and end apart: 18, of which 5 were waited for; matrix products, arithmetic and copies ran while one was open for 2% of the time, Pallas kernels for 39%

profile of v8, /device:TPU:113, one launch (start us, length us, event | category | flops | bytes accessed | tf_op | source)
XLA Modules:
  0.0 763.5 jit_solution(5778270650334625158)
XLA Ops:
  0.0 180.6 %shard_map.118 = (bf16[1024,2048]{1,0:T(8,128)(2,1)}, bf16[512,2048]{1,0:T(8,128)(2,1)}, bf16[512,2048]{1,0:T(8,128)(2,1)}, bf16[8,2048,1024]{2,1,0:T(8,128)(2,1...) custom-call(bf16[1024,2048]{1,0:T(8,128)(2,1)} %bitcast.57, ...), custom_call_target="tpu_custom_call" | custom-call | flops 34359738368 | bytes 50331648 | tf_op jit(solution)/shard_map/pallas_call | solution.py:310
  180.6 0.1 collective-permute-start.3
  180.7 2.0 collective-permute-start.5
  182.8 1.2 copy.47
  184.0 0.3 select_reduce_fusion.2
  184.4 1.4 collective-permute-start.2
  185.8 2.0 collective-permute-start.7
  187.7 1.0 fusion.5
  188.7 1.0 add_select_fusion.2
  189.7 0.9 fusion
  190.5 0.2 convolution_convert_fusion
  190.8 0.3 slice_reduce_fusion
  191.1 0.6 fusion.19
  191.6 0.2 reduce_window_sum.20
  191.8 0.1 copy.48
  191.9 0.3 not_reduce_fusion
  192.2 0.4 fusion.11
  192.7 0.6 reshape.90.refs_0_
  193.3 0.8 select_reduce_fusion.3.refs_1_
  194.1 0.1 add_bitcast_fusion
  194.1 6.0 collective-permute-done.3.refs_9_.refs_10_.refs_13_.refs_14_
  200.2 1.9 collective-permute-start.8
  202.1 35.0 %shard_map.119.refs_15_ = f32[512,2048]{1,0:T(8,128)} custom-call(s32[128]{0:T(128)} %reshape.90.refs_0_, f32[2,16,512]{2,1,0:T(8,128)} %select_reduce_fusion.3.refs_1_, bf16[512,2048]{1,0:T(8,128)(2,1)} %get-tuple-element.58.refs_2_.refs_0_.refs_6_, bf16[8,2048,1024]{2,1,0:T(8,128)(2,1)} %refs_8_.9, bf16[8,2048,1024]{2,1,0:T(8,128)(2,1)} %refs_9_.9, ...), custom_call_target="tpu_custom_call" | custom-call | flops 1048576 | bytes 12582912 | tf_op jit(solution)/shard_map/pallas_call | solution.py:527
  237.1 0.1 collective-permute-start.6
  237.3 2.6 collective-permute-start.9
  239.9 0.1 convert_reduce_fusion.1
  240.0 0.1 copy.49
  240.1 0.1 reshape.88
  240.2 0.1 reshape.92
  240.3 0.1 copy.51
  240.4 0.1 add.48
  240.5 0.2 reduce-window.8
  240.6 0.1 reduce.5
  240.7 0.7 convert_reduce_fusion
  241.4 2.8 select_reduce_fusion
  244.2 0.8 add_select_fusion.pos_ref.refs_4_.refs_3_
  245.1 0.6 add_clamp_fusion.pc_ref
  245.7 0.2 multiply_reduce_fusion
  245.9 73.3 %collective-permute-done.1 = f32[1024,8]{0,1:T(8,128)S(1)} collective-permute-done((f32[1024,8]{0,1:T(8,128)S(1)}, f32[1024,8]{0,1:T(8,128)S(1)}, u32[]{:S(2)}, u32[]{:S(2)}) %collective-permute-start.1) | collective-permute-done | bytes 32800 | tf_op jit(solution)/shard_map/ppermute | solution.py:812
  319.2 0.7 collective-permute-start
  319.9 0.5 negate_maximum_fusion.nch_ref.refs_2_.refs_1_
  320.5 0.7 min.30.eg_ref.refs_3_.refs_2_
  321.1 2.5 collective-permute-done
  323.7 1.6 select_reduce_fusion.1.refs_1_.refs_0_
  325.2 63.8 %shard_map.120 = (f32[512,2048]{1,0:T(8,128)}, f32[512,2048]{1,0:T(8,128)}) custom-call(s32[128]{0:T(128)} %reshape.90.refs_0_, f32[8,16,512]{2,1,0:T(8,128)} %select_reduce_fusion.1.refs_1_.refs_0_, bf16[512,2048]{1,0:T(8,128)(2,1)} %collective-permute-done.4.refs_2_, bf16[512,2048]{1,0:T(8,128)(2,1)} %collective-permute-done.5.refs_3_.refs_5_, ...), custom_call_target="tpu_custom_call" | custom-call | flops 1048576 | bytes 12582912 | tf_op jit(solution)/shard_map/pallas_call | solution.py:527
  389.1 13.8 %shard_map.121.refs_2_ = bf16[34816,2048]{1,0:T(8,128)(2,1)} custom-call(s32[8]{0:T(128)} %negate_maximum_fusion.nch_ref.refs_2_.refs_1_, s32[4352]{0:T(1024)} %min.30.eg_ref.refs_3_.refs_2_, s32[8,16,512]{2,1,0:T(8,128)} %add_select_fusion.pos_ref.refs_4_.refs_3_, bf16[512,2048]{1,0:T(8,128)(2,1)} %get-tuple-element.58.refs_2_.refs_0_.refs_6_, ...), custom_call_target="tpu_custom_call" | custom-call | flops 1048576 | bytes 2097152 | tf_op jit(solution)/shard_map/pallas_call | solution.py:590
  402.9 75.3 %shard_map.122.refs_5_.refs_4_ = bf16[34816,2048]{1,0:T(8,128)(2,1)} custom-call(s32[16]{0:T(128)} %get-tuple-element.83.np_ref, s32[4352]{0:T(1024)} %add_clamp_fusion.pc_ref, s32[8]{0:T(128)} %negate_maximum_fusion.nch_ref.refs_2_.refs_1_, s32[4352]{0:T(1024)} %min.30.eg_ref.refs_3_.refs_2_, ...), custom_call_target="tpu_custom_call", output_to_operand_aliasing={{}: (7, {})} | custom-call | flops 70866960384 | bytes 201326592 | tf_op jit(solution)/shard_map/pallas_call | solution.py:719
  478.2 38.2 %shard_map.123 = bf16[512,2048]{1,0:T(8,128)(2,1)} custom-call(s32[128]{0:T(128)} %reshape.90.refs_0_, f32[8,16,512]{2,1,0:T(8,128)} %select_reduce_fusion.1.refs_1_.refs_0_, s32[8]{0:T(128)} %negate_maximum_fusion.nch_ref.refs_2_.refs_1_, s32[4352]{0:T(1024)} %min.30.eg_ref.refs_3_.refs_2_, s32[8,16,512]{2,1,0:T(8,128)} %add_select_fusion.pos_ref.refs_4_.refs_3_, ...), custom_call_target="tpu_custom_call" | custom-call | flops 1048576 | bytes 12582912 | tf_op jit(solution)/shard_map/pallas_call | solution.py:527
  516.4 0.1 collective-permute-start.10
  516.5 18.0 %shard_map.124 = (bf16[512,2048]{1,0:T(8,128)(2,1)}, bf16[512,2048]{1,0:T(8,128)(2,1)}) custom-call(f32[8,16,512]{2,1,0:T(8,128)} %select_reduce_fusion.1.refs_1_.refs_0_, s32[8]{0:T(128)} %negate_maximum_fusion.nch_ref.refs_2_.refs_1_, s32[4352]{0:T(1024)} %min.30.eg_ref.refs_3_.refs_2_, s32[8,16,512]{2,1,0:T(8,128)} %add_select_fusion.pos_ref.refs_4_.refs_3_, ...), custom_call_target="tpu_custom_call" | custom-call | flops 1048576 | bytes 12582912 | tf_op jit(solution)/shard_map/pallas_call | solution.py:527
  534.5 38.4 %shard_map.125 = bf16[512,2048]{1,0:T(8,128)(2,1)} custom-call(s32[128]{0:T(128)} %reshape.90.refs_0_, f32[8,16,512]{2,1,0:T(8,128)} %select_reduce_fusion.1.refs_1_.refs_0_, s32[8]{0:T(128)} %negate_maximum_fusion.nch_ref.refs_2_.refs_1_, s32[4352]{0:T(1024)} %min.30.eg_ref.refs_3_.refs_2_, s32[8,16,512]{2,1,0:T(8,128)} %add_select_fusion.pos_ref.refs_4_.refs_3_, ...), custom_call_target="tpu_custom_call" | custom-call | flops 1048576 | bytes 12582912 | tf_op jit(solution)/shard_map/pallas_call | solution.py:527
  572.9 0.1 collective-permute-start.11
  573.0 0.1 collective-permute-start.12
  573.1 1.4 collective-permute-start.15
  574.5 38.2 %shard_map.126 = bf16[512,2048]{1,0:T(8,128)(2,1)} custom-call(s32[128]{0:T(128)} %reshape.90.refs_0_, f32[8,16,512]{2,1,0:T(8,128)} %select_reduce_fusion.1.refs_1_.refs_0_, s32[8]{0:T(128)} %negate_maximum_fusion.nch_ref.refs_2_.refs_1_, s32[4352]{0:T(1024)} %min.30.eg_ref.refs_3_.refs_2_, s32[8,16,512]{2,1,0:T(8,128)} %add_select_fusion.pos_ref.refs_4_.refs_3_, ...), custom_call_target="tpu_custom_call" | custom-call | flops 1048576 | bytes 12582912 | tf_op jit(solution)/shard_map/pallas_call | solution.py:527
  612.7 0.1 collective-permute-start.13
  612.8 1.4 collective-permute-start.16
  614.3 38.2 %shard_map.127 = bf16[512,2048]{1,0:T(8,128)(2,1)} custom-call(s32[128]{0:T(128)} %reshape.90.refs_0_, f32[8,16,512]{2,1,0:T(8,128)} %select_reduce_fusion.1.refs_1_.refs_0_, s32[8]{0:T(128)} %negate_maximum_fusion.nch_ref.refs_2_.refs_1_, s32[4352]{0:T(1024)} %min.30.eg_ref.refs_3_.refs_2_, s32[8,16,512]{2,1,0:T(8,128)} %add_select_fusion.pos_ref.refs_4_.refs_3_, ...), custom_call_target="tpu_custom_call" | custom-call | flops 1048576 | bytes 12582912 | tf_op jit(solution)/shard_map/pallas_call | solution.py:527
  652.5 0.1 collective-permute-start.14
  652.6 8.3 %collective-permute-done.12.refs_2_ = bf16[512,2048]{1,0:T(8,128)(2,1)} collective-permute-done((bf16[512,2048]{1,0:T(8,128)(2,1)}, bf16[512,2048]{1,0:T(8,128)(2,1)}, u32[]{:S(2)}, u32[]{:S(2)}) %collective-permute-start.12) | collective-permute-done | bytes 2097184 | tf_op jit(solution)/shard_map/ppermute | solution.py:812
  661.0 1.5 collective-permute-start.17
  662.5 48.9 %shard_map.128 = (f32[512,2048]{1,0:T(8,128)}, f32[512,2048]{1,0:T(8,128)}) custom-call(s32[128]{0:T(128)} %reshape.90.refs_0_, f32[8,16,512]{2,1,0:T(8,128)} %select_reduce_fusion.1.refs_1_.refs_0_, s32[8]{0:T(128)} %negate_maximum_fusion.nch_ref.refs_2_.refs_1_, s32[4352]{0:T(1024)} %min.30.eg_ref.refs_3_.refs_2_, ...), custom_call_target="tpu_custom_call" | custom-call | flops 1048576 | bytes 12582912 | tf_op jit(solution)/shard_map/pallas_call | solution.py:527
  711.4 39.5 %collective-permute-done.17.refs_7_ = bf16[512,2048]{1,0:T(8,128)(2,1)} collective-permute-done((bf16[512,2048]{1,0:T(8,128)(2,1)}, bf16[512,2048]{1,0:T(8,128)(2,1)}, u32[]{:S(2)}, u32[]{:S(2)}) %collective-permute-start.17) | collective-permute-done | bytes 2097184 | tf_op jit(solution)/shard_map/ppermute | solution.py:812
  750.8 12.2 %shard_map.129 = bf16[1024,2048]{1,0:T(8,128)(2,1)} custom-call(bf16[1024,2048]{1,0:T(8,128)(2,1)} %get-tuple-element.43.h_ref, f32[512,2048]{1,0:T(8,128)} %get-tuple-element.73.refs_0_, f32[512,2048]{1,0:T(8,128)} %get-tuple-element.74.refs_1_, bf16[512,2048]{1,0:T(8,128)(2,1)} %collective-permute-done.12.refs_2_, ...), custom_call_target="tpu_custom_call" | custom-call | flops 12582912 | bytes 41943040 | tf_op jit(solution)/shard_map/pallas_call | solution.py:755
  (25 shorter events, 0.1 us)
Async XLA Ops:
  0.0 184.0 %copy-start = (s32[1,1024,8]{1,2,0:T(8,128)S(1)}, s32[1,1024,8]{1,2,0:T(8,128)}, u32[]{:S(2)}) copy-start(s32[1,1024,8]{1,2,0:T(8,128)} %param.21) | copy-start | bytes 98308
  180.6 19.6 %collective-permute-start.3 = (bf16[3,1024,2048]{2,1,0:T(8,128)(2,1)}, bf16[3,1024,2048]{2,1,0:T(8,128)(2,1)}, u32[]{:S(2)}, u32[]{:S(2)}) collective-permute-start(bf16[3,1024,2048]{2,1,0:T(8,128)(2,1)} %get-tuple-element.52), channel_id=1, source_target_pairs={{0,1},{1,0},{2,3},{3,2},{4,5},{5,4},{6,7},{7,6},{8,9},{9,8},{10,11... | collective-permute-start | bytes 37748744 | tf_op jit(solution)/shard_map/ppermute | solution.py:829
  180.7 56.4 %collective-permute-start.5 = (bf16[512,2048]{1,0:T(8,128)(2,1)}, bf16[512,2048]{1,0:T(8,128)(2,1)}, u32[]{:S(2)}, u32[]{:S(2)}) collective-permute-start(bf16[512,2048]{1,0:T(8,128)(2,1)} %get-tuple-element.54.refs_1_.refs_7_), channel_id=1, source_target_pairs={{0,6},{1,7},{2,0},{3,1},{4,2},{5,3},{6,4},{7,5},{8,14},{9,15},{10,... | collective-permute-start | bytes 6291464 | tf_op jit(solution)/shard_map/ppermute | solution.py:812
  182.7 54.4 %collective-permute-start.4 = (bf16[512,2048]{1,0:T(8,128)(2,1)}, bf16[512,2048]{1,0:T(8,128)(2,1)}, u32[]{:S(2)}, u32[]{:S(2)}) collective-permute-start(bf16[512,2048]{1,0:T(8,128)(2,1)} %get-tuple-element.58.refs_2_.refs_0_.refs_6_), channel_id=1, source_target_pairs={{0,2},{1,3},{2,4},{3,5},{4,6},{5,7},{6,0},{7,1},{8,10},{9,11},{10,... | collective-permute-start | bytes 6291464 | tf_op jit(solution)/shard_map/ppermute | solution.py:812
  184.4 61.3 %collective-permute-start.2 = (f32[1024,8]{0,1:T(8,128)S(1)}, f32[1024,8]{0,1:T(8,128)S(1)}, u32[]{:S(2)}, u32[]{:S(2)}) collective-permute-start(f32[1024,8]{0,1:T(8,128)S(1)} %fusion.13), channel_id=1, source_target_pairs={{0,4},{1,5},{2,6},{3,7},{4,0},{5,1},{6,2},{7,3},{8,12},{9,13},{10,... | collective-permute-start | bytes 98312 | tf_op jit(solution)/shard_map/ppermute | solution.py:812
  185.8 203.3 %collective-permute-start.7 = (bf16[512,2048]{1,0:T(8,128)(2,1)}, bf16[512,2048]{1,0:T(8,128)(2,1)}, u32[]{:S(2)}, u32[]{:S(2)}) collective-permute-start(bf16[512,2048]{1,0:T(8,128)(2,1)} %get-tuple-element.54.refs_1_.refs_7_), channel_id=1, source_target_pairs={{0,2},{1,3},{2,4},{3,5},{4,6},{5,7},{6,0},{7,1},{8,10},{9,11},{10,... | collective-permute-start | bytes 6291464 | tf_op jit(solution)/shard_map/ppermute | solution.py:812
  200.2 188.9 %collective-permute-start.8 = (bf16[512,2048]{1,0:T(8,128)(2,1)}, bf16[512,2048]{1,0:T(8,128)(2,1)}, u32[]{:S(2)}, u32[]{:S(2)}) collective-permute-start(bf16[512,2048]{1,0:T(8,128)(2,1)} %get-tuple-element.58.refs_2_.refs_0_.refs_6_), channel_id=1, source_target_pairs={{0,6},{1,7},{2,0},{3,1},{4,2},{5,3},{6,4},{7,5},{8,14},{9,15},{10,... | collective-permute-start | bytes 6291464 | tf_op jit(solution)/shard_map/ppermute | solution.py:812
  237.1 165.7 %collective-permute-start.6 = (bf16[512,2048]{1,0:T(8,128)(2,1)}, bf16[512,2048]{1,0:T(8,128)(2,1)}, u32[]{:S(2)}, u32[]{:S(2)}) collective-permute-start(bf16[512,2048]{1,0:T(8,128)(2,1)} %collective-permute-done.4.refs_2_), channel_id=1, source_target_pairs={{0,2},{1,3},{2,4},{3,5},{4,6},{5,7},{6,0},{7,1},{8,10},{9,11},{10,... | collective-permute-start | bytes 6291464 | tf_op jit(solution)/shard_map/ppermute | solution.py:812
  237.3 165.6 %collective-permute-start.9 = (bf16[512,2048]{1,0:T(8,128)(2,1)}, bf16[512,2048]{1,0:T(8,128)(2,1)}, u32[]{:S(2)}, u32[]{:S(2)}) collective-permute-start(bf16[512,2048]{1,0:T(8,128)(2,1)} %collective-permute-done.5.refs_3_.refs_5_), channel_id=1, source_target_pairs={{0,6},{1,7},{2,0},{3,1},{4,2},{5,3},{6,4},{7,5},{8,14},{9,15},{10,... | collective-permute-start | bytes 6291464 | tf_op jit(solution)/shard_map/ppermute | solution.py:812
  245.7 73.5 %collective-permute-start.1 = (f32[1024,8]{0,1:T(8,128)S(1)}, f32[1024,8]{0,1:T(8,128)S(1)}, u32[]{:S(2)}, u32[]{:S(2)}) collective-permute-start(f32[1024,8]{0,1:T(8,128)S(1)} %fusion.13), channel_id=1, source_target_pairs={{0,6},{1,7},{2,0},{3,1},{4,2},{5,3},{6,4},{7,5},{8,14},{9,15},{10,... | collective-permute-start | bytes 98312 | tf_op jit(solution)/shard_map/ppermute | solution.py:812
  319.2 4.5 collective-permute-start
  516.4 56.5 %collective-permute-start.10 = (bf16[512,2048]{1,0:T(8,128)(2,1)}, bf16[512,2048]{1,0:T(8,128)(2,1)}, u32[]{:S(2)}, u32[]{:S(2)}) collective-permute-start(bf16[512,2048]{1,0:T(8,128)(2,1)} %shard_map.123), channel_id=1, source_target_pairs={{0,2},{1,3},{2,4},{3,5},{4,6},{5,7},{6,0},{7,1},{8,10},{9,11},{10,... | collective-permute-start | bytes 6291464 | tf_op jit(solution)/shard_map/ppermute | solution.py:812
  572.9 79.6 %collective-permute-start.11 = (bf16[512,2048]{1,0:T(8,128)(2,1)}, bf16[512,2048]{1,0:T(8,128)(2,1)}, u32[]{:S(2)}, u32[]{:S(2)}) collective-permute-start(bf16[512,2048]{1,0:T(8,128)(2,1)} %shard_map.125), channel_id=1, source_target_pairs={{0,6},{1,7},{2,0},{3,1},{4,2},{5,3},{6,4},{7,5},{8,14},{9,15},{10,... | collective-permute-start | bytes 6291464 | tf_op jit(solution)/shard_map/ppermute | solution.py:812
  573.0 88.0 %collective-permute-start.12 = (bf16[512,2048]{1,0:T(8,128)(2,1)}, bf16[512,2048]{1,0:T(8,128)(2,1)}, u32[]{:S(2)}, u32[]{:S(2)}) collective-permute-start(bf16[512,2048]{1,0:T(8,128)(2,1)} %get-tuple-element.75), channel_id=1, source_target_pairs={{0,6},{1,7},{2,0},{3,1},{4,2},{5,3},{6,4},{7,5},{8,14},{9,15},{10,... | collective-permute-start | bytes 6291464 | tf_op jit(solution)/shard_map/ppermute | solution.py:812
  573.1 138.2 %collective-permute-start.15 = (bf16[512,2048]{1,0:T(8,128)(2,1)}, bf16[512,2048]{1,0:T(8,128)(2,1)}, u32[]{:S(2)}, u32[]{:S(2)}) collective-permute-start(bf16[512,2048]{1,0:T(8,128)(2,1)} %get-tuple-element.78), channel_id=1, source_target_pairs={{0,2},{1,3},{2,4},{3,5},{4,6},{5,7},{6,0},{7,1},{8,10},{9,11},{10,... | collective-permute-start | bytes 6291464 | tf_op jit(solution)/shard_map/ppermute | solution.py:812
  612.7 98.6 %collective-permute-start.13 = (bf16[512,2048]{1,0:T(8,128)(2,1)}, bf16[512,2048]{1,0:T(8,128)(2,1)}, u32[]{:S(2)}, u32[]{:S(2)}) collective-permute-start(bf16[512,2048]{1,0:T(8,128)(2,1)} %shard_map.126), channel_id=1, source_target_pairs={{0,6},{1,7},{2,0},{3,1},{4,2},{5,3},{6,4},{7,5},{8,14},{9,15},{10,... | collective-permute-start | bytes 6291464 | tf_op jit(solution)/shard_map/ppermute | solution.py:812
  612.8 98.5 %collective-permute-start.16 = (bf16[512,2048]{1,0:T(8,128)(2,1)}, bf16[512,2048]{1,0:T(8,128)(2,1)}, u32[]{:S(2)}, u32[]{:S(2)}) collective-permute-start(bf16[512,2048]{1,0:T(8,128)(2,1)} %collective-permute-done.10), channel_id=1, source_target_pairs={{0,2},{1,3},{2,4},{3,5},{4,6},{5,7},{6,0},{7,1},{8,10},{9,11},{10,... | collective-permute-start | bytes 6291464 | tf_op jit(solution)/shard_map/ppermute | solution.py:812
  652.5 58.9 %collective-permute-start.14 = (bf16[512,2048]{1,0:T(8,128)(2,1)}, bf16[512,2048]{1,0:T(8,128)(2,1)}, u32[]{:S(2)}, u32[]{:S(2)}) collective-permute-start(bf16[512,2048]{1,0:T(8,128)(2,1)} %shard_map.127), channel_id=1, source_target_pairs={{0,2},{1,3},{2,4},{3,5},{4,6},{5,7},{6,0},{7,1},{8,10},{9,11},{10,... | collective-permute-start | bytes 6291464 | tf_op jit(solution)/shard_map/ppermute | solution.py:812
  661.0 89.9 %collective-permute-start.17 = (bf16[512,2048]{1,0:T(8,128)(2,1)}, bf16[512,2048]{1,0:T(8,128)(2,1)}, u32[]{:S(2)}, u32[]{:S(2)}) collective-permute-start(bf16[512,2048]{1,0:T(8,128)(2,1)} %collective-permute-done.11), channel_id=1, source_target_pairs={{0,6},{1,7},{2,0},{3,1},{4,2},{5,3},{6,4},{7,5},{8,14},{9,15},{10,... | collective-permute-start | bytes 6291464 | tf_op jit(solution)/shard_map/ppermute | solution.py:812

commit v9 on v7

--- a/solution.py
+++ b/solution.py
@@ -524,8 +524,7 @@
     return jnp.concatenate(hits, axis=0), ls
 
 
-def gather_kernel(js, nch_ref, eg_ref, pos_ref, *refs):
-    us, (x_ref, ubuf, xbuf, usem, sem) = refs[:len(js)], refs[-5:]
+def gather_rows(js, nch_ref, eg_ref, pos_ref, us, x_ref, ubuf, xbuf, usem, sem):
     cap = x_ref.shape[0] // pos_ref.shape[0]
     cps = [pltpu.make_async_copy(u, ubuf.at[p % 2], usem.at[p % 2]) for p, u in enumerate(us)]
     cps[0].start()
@@ -557,28 +556,31 @@
             out(parity(made - k), 0).wait()
 
 
-def gather(js, r, us, x):
+def gather_kernel(js, nch_ref, eg_ref, pos_ref, *refs):
+    gather_rows(js, nch_ref, eg_ref, pos_ref, refs[:len(js)], *refs[len(js):])
+
+
+def gather(js, r, us):
     t, d = us[0].shape
-    rows = r.eg.size * PIECE
     vm = pl.BlockSpec(memory_space=pltpu.VMEM)
     sm = pl.BlockSpec(memory_space=pltpu.SMEM)
     hb = pl.BlockSpec(memory_space=pl.ANY)
-    more = [] if x is None else [x]
     return pl.pallas_call(
         functools.partial(gather_kernel, js),
-        in_specs=[sm, sm, vm] + [hb] * len(us + more),
+        in_specs=[sm, sm, vm] + [hb] * len(us),
         out_specs=hb,
-        out_shape=jax.ShapeDtypeStruct((rows, d), BF),
-        input_output_aliases={3 + len(us): 0} if more else {},
+        out_shape=jax.ShapeDtypeStruct((r.eg.size * PIECE, d), BF),
         scratch_shapes=[pltpu.VMEM((2, t, d), BF), pltpu.VMEM((2, CHUNK, d), BF), DMA2, DMA2],
         compiler_params=params(),
         cost_estimate=cost(t * d, 4 * CHUNK * d),
-    )(r.nch, r.eg.reshape(-1), r.pos, *us, *more)
-
-
-def cold_kernel(np_ref, pc_ref, x_ref, *refs):
+    )(r.nch, r.eg.reshape(-1), r.pos, *us)
+
+
+def cold_kernel(js, np_ref, pc_ref, nch_ref, eg_ref, pos_ref, *refs):
+    us, refs = refs[:len(js)], refs[len(js) + 1:]
     own, other, z_ref, refs = refs[:3], refs[3:7], refs[7], refs[8:]
-    bufs, (xbuf, zbuf, wsem, xsem, zsem, tl_ref, tp_ref, tn_ref, tw_ref, nx_ref) = refs[:3], refs[3:]
+    x_ref = z_ref
+    bufs, (ubuf, gbuf, usem, gsem, xbuf, zbuf, wsem, xsem, zsem, tl_ref, tp_ref, tn_ref, tw_ref, nx_ref) = refs[:3], refs[3:]
     ppt = MT // PIECE
 
     def tiles(l, carry):
@@ -599,14 +601,14 @@
     nt = lax.fori_loop(0, np_ref.shape[0], tiles, (0, 0, 0))[0]
 
     def each(n, fn):
-        @loop(lax.div(n, 2))
+        whole = lax.div(n, 4)
+
+        @loop(whole)
         def _(i):
-            fn(2 * i)
-            fn(2 * i + 1)
-
-        @pl.when(parity(n) == 1)
-        def _():
-            fn(n - 1)
+            for k in range(4):
+                fn(4 * i + k)
+
+        pl.loop(4 * whole, n)(fn)
 
     def xin(q, slot):
         p0 = tp_ref[q]
@@ -646,6 +648,11 @@
     @pl.when(nt > 0)
     def _():
         fetch_expert(tl_ref[0], 0, own, other, bufs, wsem)
+
+    gather_rows(js, nch_ref, eg_ref, pos_ref, us, z_ref, ubuf, gbuf, usem, gsem)
+
+    @pl.when(nt > 0)
+    def _():
         xin(0, 0)
 
     @loop(nt)
@@ -680,54 +687,51 @@
             zwait(nt - k, parity(nt - k))
 
 
-def cold(plan, x, own, other):
+def cold(plan, js, r, us, x, own, other):
     d, ff = own[0].shape[1:]
+    t = us[0].shape[0]
+    vm = pl.BlockSpec(memory_space=pltpu.VMEM)
     sm = pl.BlockSpec(memory_space=pltpu.SMEM)
     hb = pl.BlockSpec(memory_space=pl.ANY)
+    args = (*plan, r.nch, r.eg.reshape(-1), r.pos, *us)
     return pl.pallas_call(
-        cold_kernel,
-        in_specs=[sm] * len(plan) + [hb] * 8,
+        functools.partial(cold_kernel, js),
+        in_specs=[sm] * 4 + [vm] + [hb] * (len(us) + 8),
         out_specs=hb,
         out_shape=jax.ShapeDtypeStruct(x.shape, BF),
-        scratch_shapes=[*expert_buffers(d, ff),
+        scratch_shapes=[*expert_buffers(d, ff), pltpu.VMEM((2, t, d), BF), pltpu.VMEM((2, CHUNK, d), BF), DMA2, DMA2,
                         pltpu.VMEM((2, MT, d), BF), pltpu.VMEM((2, MT, d), BF),
                         DMA2, DMA2, DMA2, *5 * [pltpu.SMEM((plan[1].size * PIECE // MT + plan[0].size + 1,), I32)]],
-        input_output_aliases={len(plan): 0},
+        input_output_aliases={len(args): 0},
         compiler_params=params(),
         cost_estimate=cost(6 * 16 * MT * d * ff, 96 * d * ff),
-    )(*plan, x, *own, *other)
+    )(*args, x, *own, *other)
 
 
 def final_kernel(h_ref, *refs):
     y_ref = refs[-1]
-    acc, parts = refs[0], refs[1:-1]
-    y = h_ref[:].astype(F32) + acc[:]
-    for v in parts:
-        y = y + v[:].astype(F32)
-    y_ref[:] = y.astype(BF)
+    half = refs[0].shape[0]
+    for p in range(2):
+        rows = pl.ds(p * half, half)
+        y = h_ref[rows, :].astype(F32)
+        for v in refs[p:-1:2]:
+            y = y + v[:].astype(F32)
+        y_ref[rows, :] = y.astype(BF)
 
 
 def final(h, accs, parts):
     t, d = h.shape
-    half = t // 2
-    tm = min(256, half)
-    n = half // tm
-
-    def body(h_ref, *refs):
-        for p in range(2):
-            @pl.when(pl.program_id(0) // n == p)
-            def _():
-                final_kernel(h_ref, refs[p], *refs[2 + p:-1:2], refs[-1])
-
-    spec = lambda p: pl.BlockSpec((tm, d), lambda i: (jnp.minimum(i, n - 1) if p == 0 else jnp.maximum(i - n, 0), 0))
+    tn = min(256, d)
+    cols = lambda rows: pl.BlockSpec((rows, tn), lambda i: (0, i))
+    args = [*accs, *[v for part in parts for v in part]]
     return pl.pallas_call(
-        body, grid=(2 * n,),
-        in_specs=[pl.BlockSpec((tm, d), lambda i: (i, 0))] + [spec(0), spec(1)] * (1 + len(parts)),
-        out_specs=pl.BlockSpec((tm, d), lambda i: (i, 0)),
+        final_kernel, grid=(d // tn,),
+        in_specs=[cols(t)] + [cols(t // 2)] * len(args),
+        out_specs=cols(t),
         out_shape=jax.ShapeDtypeStruct((t, d), BF),
         compiler_params=params(),
         cost_estimate=cost(6 * t * d, 20 * t * d),
-    )(h, *accs, *[v for part in parts for v in part])
+    )(h, *args)
 
 
 class Routing(typing.NamedTuple):
@@ -818,10 +822,9 @@
         u3t, u3b = shift(u1t, 1), shift(u2b, -1)
         d2, d5 = block((2, 5), r, None, (u1t, u2b), 2 * (None,), own, other, F32, 2 * ON, comb=False)
         u1b, d2 = lax.optimization_barrier((u1b, d2))
-        x = gather(tuple(range(6)), r, [ut, ub, u1t, u1b, u2t, u2b], None)
+        x = gather(tuple(range(6)), r, [ut, ub, u1t, u1b, u2t, u2b])
         u3t, x = lax.optimization_barrier((u3t, x))
-        x = gather((6, 7), r, [u3t, u3b], x)
-        z = cold(plan, x, own, other)
+        z = cold(plan, (6, 7), r, [u3t, u3b], x, own, other)
 
         tie = lambda r, *v: (lambda w: (r._replace(nch=w[0]), *w[1:]))(lax.optimization_barrier((r.nch, *v)))
         b6, = block((6,), r, z, (u3t,), (None,), own, other, BF, ON)

time: 773 us -> 771 us (level)
    pallas_call x2 -> x1, Pallas kernels: 20.5 us -> 13.8 us  [gather(): pl.pallas_call(functools.partial(gather_kernel, js), in_specs=[sm, sm, vm...]
where the time goes in v9:
time: 771 us; the launch traced here: 756 us
  Pallas kernels  591 us (77%)
  waiting for transfers between devices  130 us (17%)
  starting transfers between devices  17.1 us (2%)
  other arithmetic  12.9 us (2%)
    pallas_call x8, Pallas kernels, block(): pl.pallas_call(functools.partial(block_kernel, js, [v is not None for v i...  318 us
    pallas_call x1, Pallas kernels, attention_layer(): pl.pallas_call(functools.partial(layer_kernel, nx), in_specs=[hb] * 5 + [...  173 us
    ppermute x17, waiting for transfers between devices, shift(): lax.ppermute(v, 'ep', [(2 * i + c, 2 * ((i + s) % nx) + c) for i in range...  125 us
    pallas_call x1, Pallas kernels, cold(): pl.pallas_call(functools.partial(cold_kernel, js), in_specs=[sm] * 4 + [v...  74.3 us
    ppermute x17, starting transfers between devices, shift(): lax.ppermute(v, 'ep', [(2 * i + c, 2 * ((i + s) % nx) + c) for i in range...  16 us
  transfers between devices with their start and end apart: 18, of which 5 were waited for; matrix products, arithmetic and copies ran while one was open for 2% of the time, Pallas kernels for 39%

profile of v9, /device:TPU:113, one launch (start us, length us, event | category | flops | bytes accessed | tf_op | source)
XLA Modules:
  0.0 756.0 jit_solution(9589325594204422193)
XLA Ops:
  0.0 173.0 %shard_map.118 = (bf16[1024,2048]{1,0:T(8,128)(2,1)}, bf16[512,2048]{1,0:T(8,128)(2,1)}, bf16[512,2048]{1,0:T(8,128)(2,1)}, bf16[8,2048,1024]{2,1,0:T(8,128)(2,1...) custom-call(bf16[1024,2048]{1,0:T(8,128)(2,1)} %bitcast.57, ...), custom_call_target="tpu_custom_call" | custom-call | flops 34359738368 | bytes 50331648 | tf_op jit(solution)/shard_map/pallas_call | solution.py:288
  173.0 1.1 collective-permute-start.3
  174.1 1.9 collective-permute-start.5
  176.1 1.2 copy.47
  177.3 0.3 select_reduce_fusion.2
  177.7 1.3 collective-permute-start.2
  178.9 2.1 collective-permute-start.7
  181.0 1.0 fusion.5
  182.0 1.0 add_select_fusion.2
  183.0 0.9 fusion
  183.9 0.2 convolution_convert_fusion
  184.1 0.3 slice_reduce_fusion
  184.4 0.6 fusion.19
  184.9 0.2 reduce_window_sum.20
  185.1 0.1 copy.48
  185.2 0.3 not_reduce_fusion
  185.5 0.4 fusion.11
  186.0 0.6 reshape.90.refs_0_
  186.6 0.8 select_reduce_fusion.3.refs_1_
  187.4 0.1 add_bitcast_fusion
  187.4 5.8 collective-permute-done.3.refs_9_.refs_10_.refs_13_.refs_14_
  193.2 1.9 collective-permute-start.8
  195.2 35.0 %shard_map.119.refs_15_ = f32[512,2048]{1,0:T(8,128)} custom-call(s32[128]{0:T(128)} %reshape.90.refs_0_, f32[2,16,512]{2,1,0:T(8,128)} %select_reduce_fusion.3.refs_1_, bf16[512,2048]{1,0:T(8,128)(2,1)} %get-tuple-element.58.refs_2_.refs_0_.refs_6_, bf16[8,2048,1024]{2,1,0:T(8,128)(2,1)} %refs_8_.9, bf16[8,2048,1024]{2,1,0:T(8,128)(2,1)} %refs_9_.9, ...), custom_call_target="tpu_custom_call" | custom-call | flops 1048576 | bytes 12582912 | tf_op jit(solution)/shard_map/pallas_call | solution.py:505
  230.2 0.1 collective-permute-start.6
  230.3 2.6 collective-permute-start.9
  233.0 0.1 convert_reduce_fusion.1
  233.1 0.1 copy.49
  233.2 0.1 reshape.88
  233.3 0.1 reshape.92
  233.3 0.1 copy.51
  233.4 0.1 add.48
  233.5 0.2 reduce-window.8
  233.7 0.1 reduce.5
  233.8 0.7 convert_reduce_fusion
  234.5 2.6 select_reduce_fusion
  237.1 0.8 add_select_fusion.pos_ref.refs_4_.refs_3_
  237.9 0.6 add_clamp_fusion.pc_ref
  238.5 0.2 multiply_reduce_fusion
  238.7 74.1 %collective-permute-done.1 = f32[1024,8]{0,1:T(8,128)S(1)} collective-permute-done((f32[1024,8]{0,1:T(8,128)S(1)}, f32[1024,8]{0,1:T(8,128)S(1)}, u32[]{:S(2)}, u32[]{:S(2)}) %collective-permute-start.1) | collective-permute-done | bytes 32800 | tf_op jit(solution)/shard_map/ppermute | solution.py:784
  312.8 0.9 collective-permute-start
  313.7 0.5 negate_maximum_fusion.nch_ref.refs_2_.refs_1_
  314.2 0.7 min.30.eg_ref.refs_3_.refs_2_
  314.9 2.5 collective-permute-done
  317.4 1.6 select_reduce_fusion.1.refs_1_.refs_0_
  319.0 63.8 %shard_map.120 = (f32[512,2048]{1,0:T(8,128)}, f32[512,2048]{1,0:T(8,128)}) custom-call(s32[128]{0:T(128)} %reshape.90.refs_0_, f32[8,16,512]{2,1,0:T(8,128)} %select_reduce_fusion.1.refs_1_.refs_0_, bf16[512,2048]{1,0:T(8,128)(2,1)} %collective-permute-done.4.refs_2_, bf16[512,2048]{1,0:T(8,128)(2,1)} %collective-permute-done.5.refs_3_.refs_5_, ...), custom_call_target="tpu_custom_call" | custom-call | flops 1048576 | bytes 12582912 | tf_op jit(solution)/shard_map/pallas_call | solution.py:505
  382.8 13.8 %shard_map.121.refs_2_ = bf16[34816,2048]{1,0:T(8,128)(2,1)} custom-call(s32[8]{0:T(128)} %negate_maximum_fusion.nch_ref.refs_2_.refs_1_, s32[4352]{0:T(1024)} %min.30.eg_ref.refs_3_.refs_2_, s32[8,16,512]{2,1,0:T(8,128)} %add_select_fusion.pos_ref.refs_4_.refs_3_, bf16[512,2048]{1,0:T(8,128)(2,1)} %get-tuple-element.58.refs_2_.refs_0_.refs_6_, ...), custom_call_target="tpu_custom_call" | custom-call | flops 1048576 | bytes 2097152 | tf_op jit(solution)/shard_map/pallas_call | solution.py:568
  396.6 74.3 %shard_map.122.refs_5_.refs_4_ = bf16[34816,2048]{1,0:T(8,128)(2,1)} custom-call(s32[16]{0:T(128)} %get-tuple-element.83.np_ref, s32[4352]{0:T(1024)} %add_clamp_fusion.pc_ref, s32[8]{0:T(128)} %negate_maximum_fusion.nch_ref.refs_2_.refs_1_, s32[4352]{0:T(1024)} %min.30.eg_ref.refs_3_.refs_2_, ...), custom_call_target="tpu_custom_call", output_to_operand_aliasing={{}: (7, {})} | custom-call | flops 70866960384 | bytes 201326592 | tf_op jit(solution)/shard_map/pallas_call | solution.py:697
  470.9 38.2 %shard_map.123 = bf16[512,2048]{1,0:T(8,128)(2,1)} custom-call(s32[128]{0:T(128)} %reshape.90.refs_0_, f32[8,16,512]{2,1,0:T(8,128)} %select_reduce_fusion.1.refs_1_.refs_0_, s32[8]{0:T(128)} %negate_maximum_fusion.nch_ref.refs_2_.refs_1_, s32[4352]{0:T(1024)} %min.30.eg_ref.refs_3_.refs_2_, s32[8,16,512]{2,1,0:T(8,128)} %add_select_fusion.pos_ref.refs_4_.refs_3_, ...), custom_call_target="tpu_custom_call" | custom-call | flops 1048576 | bytes 12582912 | tf_op jit(solution)/shard_map/pallas_call | solution.py:505
  509.1 0.1 collective-permute-start.10
  509.2 18.0 %shard_map.124 = (bf16[512,2048]{1,0:T(8,128)(2,1)}, bf16[512,2048]{1,0:T(8,128)(2,1)}) custom-call(f32[8,16,512]{2,1,0:T(8,128)} %select_reduce_fusion.1.refs_1_.refs_0_, s32[8]{0:T(128)} %negate_maximum_fusion.nch_ref.refs_2_.refs_1_, s32[4352]{0:T(1024)} %min.30.eg_ref.refs_3_.refs_2_, s32[8,16,512]{2,1,0:T(8,128)} %add_select_fusion.pos_ref.refs_4_.refs_3_, ...), custom_call_target="tpu_custom_call" | custom-call | flops 1048576 | bytes 12582912 | tf_op jit(solution)/shard_map/pallas_call | solution.py:505
  527.2 38.2 %shard_map.125 = bf16[512,2048]{1,0:T(8,128)(2,1)} custom-call(s32[128]{0:T(128)} %reshape.90.refs_0_, f32[8,16,512]{2,1,0:T(8,128)} %select_reduce_fusion.1.refs_1_.refs_0_, s32[8]{0:T(128)} %negate_maximum_fusion.nch_ref.refs_2_.refs_1_, s32[4352]{0:T(1024)} %min.30.eg_ref.refs_3_.refs_2_, s32[8,16,512]{2,1,0:T(8,128)} %add_select_fusion.pos_ref.refs_4_.refs_3_, ...), custom_call_target="tpu_custom_call" | custom-call | flops 1048576 | bytes 12582912 | tf_op jit(solution)/shard_map/pallas_call | solution.py:505
  565.5 0.1 collective-permute-start.11
  565.6 0.1 collective-permute-start.12
  565.7 1.4 collective-permute-start.15
  567.1 38.2 %shard_map.126 = bf16[512,2048]{1,0:T(8,128)(2,1)} custom-call(s32[128]{0:T(128)} %reshape.90.refs_0_, f32[8,16,512]{2,1,0:T(8,128)} %select_reduce_fusion.1.refs_1_.refs_0_, s32[8]{0:T(128)} %negate_maximum_fusion.nch_ref.refs_2_.refs_1_, s32[4352]{0:T(1024)} %min.30.eg_ref.refs_3_.refs_2_, s32[8,16,512]{2,1,0:T(8,128)} %add_select_fusion.pos_ref.refs_4_.refs_3_, ...), custom_call_target="tpu_custom_call" | custom-call | flops 1048576 | bytes 12582912 | tf_op jit(solution)/shard_map/pallas_call | solution.py:505
  605.3 0.1 collective-permute-start.13
  605.4 1.6 collective-permute-start.16
  607.0 38.2 %shard_map.127 = bf16[512,2048]{1,0:T(8,128)(2,1)} custom-call(s32[128]{0:T(128)} %reshape.90.refs_0_, f32[8,16,512]{2,1,0:T(8,128)} %select_reduce_fusion.1.refs_1_.refs_0_, s32[8]{0:T(128)} %negate_maximum_fusion.nch_ref.refs_2_.refs_1_, s32[4352]{0:T(1024)} %min.30.eg_ref.refs_3_.refs_2_, s32[8,16,512]{2,1,0:T(8,128)} %add_select_fusion.pos_ref.refs_4_.refs_3_, ...), custom_call_target="tpu_custom_call" | custom-call | flops 1048576 | bytes 12582912 | tf_op jit(solution)/shard_map/pallas_call | solution.py:505
  645.3 0.1 collective-permute-start.14
  645.4 8.5 %collective-permute-done.12.refs_2_ = bf16[512,2048]{1,0:T(8,128)(2,1)} collective-permute-done((bf16[512,2048]{1,0:T(8,128)(2,1)}, bf16[512,2048]{1,0:T(8,128)(2,1)}, u32[]{:S(2)}, u32[]{:S(2)}) %collective-permute-start.12) | collective-permute-done | bytes 2097184 | tf_op jit(solution)/shard_map/ppermute | solution.py:784
  653.8 1.5 collective-permute-start.17
  655.4 48.8 %shard_map.128 = (f32[512,2048]{1,0:T(8,128)}, f32[512,2048]{1,0:T(8,128)}) custom-call(s32[128]{0:T(128)} %reshape.90.refs_0_, f32[8,16,512]{2,1,0:T(8,128)} %select_reduce_fusion.1.refs_1_.refs_0_, s32[8]{0:T(128)} %negate_maximum_fusion.nch_ref.refs_2_.refs_1_, s32[4352]{0:T(1024)} %min.30.eg_ref.refs_3_.refs_2_, ...), custom_call_target="tpu_custom_call" | custom-call | flops 1048576 | bytes 12582912 | tf_op jit(solution)/shard_map/pallas_call | solution.py:505
  704.2 39.5 %collective-permute-done.17.refs_7_ = bf16[512,2048]{1,0:T(8,128)(2,1)} collective-permute-done((bf16[512,2048]{1,0:T(8,128)(2,1)}, bf16[512,2048]{1,0:T(8,128)(2,1)}, u32[]{:S(2)}, u32[]{:S(2)}) %collective-permute-start.17) | collective-permute-done | bytes 2097184 | tf_op jit(solution)/shard_map/ppermute | solution.py:784
  743.7 12.0 %shard_map.129 = bf16[1024,2048]{1,0:T(8,128)(2,1)} custom-call(bf16[1024,2048]{1,0:T(8,128)(2,1)} %get-tuple-element.43.h_ref, f32[512,2048]{1,0:T(8,128)} %get-tuple-element.73.refs_0_, f32[512,2048]{1,0:T(8,128)} %get-tuple-element.74.refs_1_, bf16[512,2048]{1,0:T(8,128)(2,1)} %collective-permute-done.12.refs_2_, ...), custom_call_target="tpu_custom_call" | custom-call | flops 12582912 | bytes 41943040 | tf_op jit(solution)/shard_map/pallas_call | solution.py:727
  (25 shorter events, 0.1 us)
Async XLA Ops:
  0.0 177.3 %copy-start = (s32[1,1024,8]{1,2,0:T(8,128)S(1)}, s32[1,1024,8]{1,2,0:T(8,128)}, u32[]{:S(2)}) copy-start(s32[1,1024,8]{1,2,0:T(8,128)} %param.21) | copy-start | bytes 98308
  173.0 20.2 %collective-permute-start.3 = (bf16[3,1024,2048]{2,1,0:T(8,128)(2,1)}, bf16[3,1024,2048]{2,1,0:T(8,128)(2,1)}, u32[]{:S(2)}, u32[]{:S(2)}) collective-permute-start(bf16[3,1024,2048]{2,1,0:T(8,128)(2,1)} %get-tuple-element.52), channel_id=1, source_target_pairs={{0,1},{1,0},{2,3},{3,2},{4,5},{5,4},{6,7},{7,6},{8,9},{9,8},{10,11... | collective-permute-start | bytes 37748744 | tf_op jit(solution)/shard_map/ppermute | solution.py:801
  174.1 56.1 %collective-permute-start.5 = (bf16[512,2048]{1,0:T(8,128)(2,1)}, bf16[512,2048]{1,0:T(8,128)(2,1)}, u32[]{:S(2)}, u32[]{:S(2)}) collective-permute-start(bf16[512,2048]{1,0:T(8,128)(2,1)} %get-tuple-element.54.refs_1_.refs_7_), channel_id=1, source_target_pairs={{0,6},{1,7},{2,0},{3,1},{4,2},{5,3},{6,4},{7,5},{8,14},{9,15},{10,... | collective-permute-start | bytes 6291464 | tf_op jit(solution)/shard_map/ppermute | solution.py:784
  176.1 54.1 %collective-permute-start.4 = (bf16[512,2048]{1,0:T(8,128)(2,1)}, bf16[512,2048]{1,0:T(8,128)(2,1)}, u32[]{:S(2)}, u32[]{:S(2)}) collective-permute-start(bf16[512,2048]{1,0:T(8,128)(2,1)} %get-tuple-element.58.refs_2_.refs_0_.refs_6_), channel_id=1, source_target_pairs={{0,2},{1,3},{2,4},{3,5},{4,6},{5,7},{6,0},{7,1},{8,10},{9,11},{10,... | collective-permute-start | bytes 6291464 | tf_op jit(solution)/shard_map/ppermute | solution.py:784
  177.7 60.8 %collective-permute-start.2 = (f32[1024,8]{0,1:T(8,128)S(1)}, f32[1024,8]{0,1:T(8,128)S(1)}, u32[]{:S(2)}, u32[]{:S(2)}) collective-permute-start(f32[1024,8]{0,1:T(8,128)S(1)} %fusion.13), channel_id=1, source_target_pairs={{0,4},{1,5},{2,6},{3,7},{4,0},{5,1},{6,2},{7,3},{8,12},{9,13},{10,... | collective-permute-start | bytes 98312 | tf_op jit(solution)/shard_map/ppermute | solution.py:784
  178.9 203.9 %collective-permute-start.7 = (bf16[512,2048]{1,0:T(8,128)(2,1)}, bf16[512,2048]{1,0:T(8,128)(2,1)}, u32[]{:S(2)}, u32[]{:S(2)}) collective-permute-start(bf16[512,2048]{1,0:T(8,128)(2,1)} %get-tuple-element.54.refs_1_.refs_7_), channel_id=1, source_target_pairs={{0,2},{1,3},{2,4},{3,5},{4,6},{5,7},{6,0},{7,1},{8,10},{9,11},{10,... | collective-permute-start | bytes 6291464 | tf_op jit(solution)/shard_map/ppermute | solution.py:784
  193.2 189.6 %collective-permute-start.8 = (bf16[512,2048]{1,0:T(8,128)(2,1)}, bf16[512,2048]{1,0:T(8,128)(2,1)}, u32[]{:S(2)}, u32[]{:S(2)}) collective-permute-start(bf16[512,2048]{1,0:T(8,128)(2,1)} %get-tuple-element.58.refs_2_.refs_0_.refs_6_), channel_id=1, source_target_pairs={{0,6},{1,7},{2,0},{3,1},{4,2},{5,3},{6,4},{7,5},{8,14},{9,15},{10,... | collective-permute-start | bytes 6291464 | tf_op jit(solution)/shard_map/ppermute | solution.py:784
  230.2 166.4 %collective-permute-start.6 = (bf16[512,2048]{1,0:T(8,128)(2,1)}, bf16[512,2048]{1,0:T(8,128)(2,1)}, u32[]{:S(2)}, u32[]{:S(2)}) collective-permute-start(bf16[512,2048]{1,0:T(8,128)(2,1)} %collective-permute-done.4.refs_2_), channel_id=1, source_target_pairs={{0,2},{1,3},{2,4},{3,5},{4,6},{5,7},{6,0},{7,1},{8,10},{9,11},{10,... | collective-permute-start | bytes 6291464 | tf_op jit(solution)/shard_map/ppermute | solution.py:784
  230.3 166.3 %collective-permute-start.9 = (bf16[512,2048]{1,0:T(8,128)(2,1)}, bf16[512,2048]{1,0:T(8,128)(2,1)}, u32[]{:S(2)}, u32[]{:S(2)}) collective-permute-start(bf16[512,2048]{1,0:T(8,128)(2,1)} %collective-permute-done.5.refs_3_.refs_5_), channel_id=1, source_target_pairs={{0,6},{1,7},{2,0},{3,1},{4,2},{5,3},{6,4},{7,5},{8,14},{9,15},{10,... | collective-permute-start | bytes 6291464 | tf_op jit(solution)/shard_map/ppermute | solution.py:784
  238.5 74.3 %collective-permute-start.1 = (f32[1024,8]{0,1:T(8,128)S(1)}, f32[1024,8]{0,1:T(8,128)S(1)}, u32[]{:S(2)}, u32[]{:S(2)}) collective-permute-start(f32[1024,8]{0,1:T(8,128)S(1)} %fusion.13), channel_id=1, source_target_pairs={{0,6},{1,7},{2,0},{3,1},{4,2},{5,3},{6,4},{7,5},{8,14},{9,15},{10,... | collective-permute-start | bytes 98312 | tf_op jit(solution)/shard_map/ppermute | solution.py:784
  312.8 4.6 collective-permute-start
  509.1 56.3 %collective-permute-start.10 = (bf16[512,2048]{1,0:T(8,128)(2,1)}, bf16[512,2048]{1,0:T(8,128)(2,1)}, u32[]{:S(2)}, u32[]{:S(2)}) collective-permute-start(bf16[512,2048]{1,0:T(8,128)(2,1)} %shard_map.123), channel_id=1, source_target_pairs={{0,2},{1,3},{2,4},{3,5},{4,6},{5,7},{6,0},{7,1},{8,10},{9,11},{10,... | collective-permute-start | bytes 6291464 | tf_op jit(solution)/shard_map/ppermute | solution.py:784
  565.5 79.8 %collective-permute-start.11 = (bf16[512,2048]{1,0:T(8,128)(2,1)}, bf16[512,2048]{1,0:T(8,128)(2,1)}, u32[]{:S(2)}, u32[]{:S(2)}) collective-permute-start(bf16[512,2048]{1,0:T(8,128)(2,1)} %shard_map.125), channel_id=1, source_target_pairs={{0,6},{1,7},{2,0},{3,1},{4,2},{5,3},{6,4},{7,5},{8,14},{9,15},{10,... | collective-permute-start | bytes 6291464 | tf_op jit(solution)/shard_map/ppermute | solution.py:784
  565.6 88.3 %collective-permute-start.12 = (bf16[512,2048]{1,0:T(8,128)(2,1)}, bf16[512,2048]{1,0:T(8,128)(2,1)}, u32[]{:S(2)}, u32[]{:S(2)}) collective-permute-start(bf16[512,2048]{1,0:T(8,128)(2,1)} %get-tuple-element.75), channel_id=1, source_target_pairs={{0,6},{1,7},{2,0},{3,1},{4,2},{5,3},{6,4},{7,5},{8,14},{9,15},{10,... | collective-permute-start | bytes 6291464 | tf_op jit(solution)/shard_map/ppermute | solution.py:784
  565.7 138.5 %collective-permute-start.15 = (bf16[512,2048]{1,0:T(8,128)(2,1)}, bf16[512,2048]{1,0:T(8,128)(2,1)}, u32[]{:S(2)}, u32[]{:S(2)}) collective-permute-start(bf16[512,2048]{1,0:T(8,128)(2,1)} %get-tuple-element.78), channel_id=1, source_target_pairs={{0,2},{1,3},{2,4},{3,5},{4,6},{5,7},{6,0},{7,1},{8,10},{9,11},{10,... | collective-permute-start | bytes 6291464 | tf_op jit(solution)/shard_map/ppermute | solution.py:784
  605.3 98.9 %collective-permute-start.13 = (bf16[512,2048]{1,0:T(8,128)(2,1)}, bf16[512,2048]{1,0:T(8,128)(2,1)}, u32[]{:S(2)}, u32[]{:S(2)}) collective-permute-start(bf16[512,2048]{1,0:T(8,128)(2,1)} %shard_map.126), channel_id=1, source_target_pairs={{0,6},{1,7},{2,0},{3,1},{4,2},{5,3},{6,4},{7,5},{8,14},{9,15},{10,... | collective-permute-start | bytes 6291464 | tf_op jit(solution)/shard_map/ppermute | solution.py:784
  605.4 98.8 %collective-permute-start.16 = (bf16[512,2048]{1,0:T(8,128)(2,1)}, bf16[512,2048]{1,0:T(8,128)(2,1)}, u32[]{:S(2)}, u32[]{:S(2)}) collective-permute-start(bf16[512,2048]{1,0:T(8,128)(2,1)} %collective-permute-done.10), channel_id=1, source_target_pairs={{0,2},{1,3},{2,4},{3,5},{4,6},{5,7},{6,0},{7,1},{8,10},{9,11},{10,... | collective-permute-start | bytes 6291464 | tf_op jit(solution)/shard_map/ppermute | solution.py:784
  645.3 59.0 %collective-permute-start.14 = (bf16[512,2048]{1,0:T(8,128)(2,1)}, bf16[512,2048]{1,0:T(8,128)(2,1)}, u32[]{:S(2)}, u32[]{:S(2)}) collective-permute-start(bf16[512,2048]{1,0:T(8,128)(2,1)} %shard_map.127), channel_id=1, source_target_pairs={{0,2},{1,3},{2,4},{3,5},{4,6},{5,7},{6,0},{7,1},{8,10},{9,11},{10,... | collective-permute-start | bytes 6291464 | tf_op jit(solution)/shard_map/ppermute | solution.py:784
  653.8 89.9 %collective-permute-start.17 = (bf16[512,2048]{1,0:T(8,128)(2,1)}, bf16[512,2048]{1,0:T(8,128)(2,1)}, u32[]{:S(2)}, u32[]{:S(2)}) collective-permute-start(bf16[512,2048]{1,0:T(8,128)(2,1)} %collective-permute-done.11), channel_id=1, source_target_pairs={{0,6},{1,7},{2,0},{3,1},{4,2},{5,3},{6,4},{7,5},{8,14},{9,15},{10,... | collective-permute-start | bytes 6291464 | tf_op jit(solution)/shard_map/ppermute | solution.py:784
